TPU v7x, 256 devices: a whole 4x4x8 slice. The times are simulated.
256 devices in a mesh: band: 128 (over z, y, x), chan: 2 (over core).
Axes of the slice: x: 4, y: 4, z: 8, core: 2. Of those that a mesh axis runs over, the one named last changes fastest.
Arguments:
- grid_latent: bfloat16 [147456, 512], P(('band', 'chan')), may hold values from -6 to 6
- edge_latent: bfloat16 [294912, 512], P(('band', 'chan')), may hold values from -6 to 6
- mesh_latent: bfloat16 [40960, 512], P(('band', 'chan')), may hold values from -6 to 6
- mesh_cotangent: bfloat16 [40960, 512], P(('band', 'chan')), may hold values from -6 to 6
- w_grid: bfloat16 [512, 512], P(None, 'chan'), may hold values from -0.15625 to 0.15625
- w_mesh: bfloat16 [512, 512], P(None, 'chan'), may hold values from -0.15625 to 0.15625
- w_edge: bfloat16 [512, 512], P(None, 'chan'), may hold values from -0.15625 to 0.15625
- bias: float32 [512], P('chan'), may hold values from -3 to 3
- w_out: bfloat16 [512, 512], P('chan'), may hold values from -0.25 to 0.25
- senders: int32 [294912], P('band'), may hold values from 0 to 147455, as said below
- receivers: int32 [294912], P('band'), may hold values from 0 to 40959, as said below
- edge_count: int32 [128], P('band'), may hold values from 1152 to 2304, as said below
Outputs:
- grad_grid: bfloat16 [147456, 512], P(('band', 'chan'))
- grad_edge: bfloat16 [294912, 512], P(('band', 'chan'))
- grad_mesh: bfloat16 [40960, 512], P(('band', 'chan'))
- grad_w_grid: float32 [512, 512], P(None, 'chan')
- grad_w_mesh: float32 [512, 512], P(None, 'chan')
- grad_w_edge: float32 [512, 512], P(None, 'chan')
- grad_bias: float32 [512], P('chan')
- grad_w_out: float32 [512, 512], P('chan')
Inputs may be any that keep to these rules, and one draw needn't show every extreme that they name: `senders`: an edge of band j (rows j * 2304 to (j + 1) * 2304 - 1) has its sender among grid rows j * 1152 to (j + 1) * 1152 - 1. `receivers`: an edge of band j has its receiver among mesh rows of owners j - 1, j, j + 1 (owner i holds rows i * 320 to (i + 1) * 320 - 1). `edge_count`: some band uses all 2304 slots.
All inputs are finite; a program needn't handle non-finite values.
Results may differ from a plain program's by a relative error of at most 0.0059.
Values may be sent and summed in bfloat16 or wider, within the bound.
No kernel may reach another device: no remote copies, remote signals or barrier semaphores. Data moves between devices by JAX's collectives and lax.ppermute only.
A program may use at most 64 MiB of HBM per device.

v0:
```python
import jax
import jax.numpy as jnp
from jax import lax
from jax.sharding import PartitionSpec as P


def shifted(x, axis, by):
    devices = lax.axis_size(axis)
    pairs = [(i, i + by) for i in range(devices) if 0 <= i + by < devices]
    return lax.ppermute(x, axis, pairs)


def from_everyone(x, axis):
    devices = lax.axis_size(axis)
    return lax.all_to_all(jnp.broadcast_to(x[None], (devices, *x.shape)), axis, 0, 0, tiled=True)


def in_order(pieces, dim):
    pieces = jnp.moveaxis(pieces, 0, dim)
    lengths = pieces.shape
    return pieces.reshape(*lengths[:dim], lengths[dim] * lengths[dim + 1], *lengths[dim + 2 :])


def collect(x, axis, dim):
    pieces = from_everyone(x, axis)
    return in_order(pieces, dim)


def with_halo(x, sides, width):
    for axis, dim in sides:
        devices, length = (lax.axis_size(axis), x.shape[dim])
        up = [(i, (i + 1) % devices) for i in range(devices - 1)]
        down = [(j, i) for i, j in up]
        last = lax.slice_in_dim(x, length - width, length, axis=dim)
        initial = lax.slice_in_dim(x, 0, width, axis=dim)
        before = lax.ppermute(last, axis, up)
        after = lax.ppermute(initial, axis, down)
        x = jnp.concatenate([before, x, after], axis=dim)
    return x


def packed_total(arrays, axis):
    ravelled, at, gathered = (jnp.concatenate([a.reshape(-1) for a in arrays]), 0, [])
    so_far = lax.psum(ravelled, axis)
    for a in arrays:
        gathered.append(so_far[at : at + a.size].reshape(a.shape))
        at += a.size
    return tuple(gathered)


def cut_along(x, dim, devices):
    before, after = (x.shape[:dim], x.shape[dim + 1 :])
    return jnp.moveaxis(x.reshape(*before, devices, -1, *after), dim, 0)


def summed_on_arrival(x, axis, dim):
    pieces = cut_along(x, dim, lax.axis_size(axis))
    arrived = lax.all_to_all(pieces, axis, split_axis=0, concat_axis=0, tiled=True)
    return arrived.astype(jnp.float32).sum(axis=0)


def sum_at_owner(x, axis, dim):
    pieces = cut_along(x, dim, lax.axis_size(axis))
    arrived = lax.all_to_all(pieces, axis, split_axis=0, concat_axis=0, tiled=True)
    return arrived.sum(axis=0)


def pass_rims(partial_value):
    from_lower = shifted(partial_value[2].astype(jnp.bfloat16), "band", 1).astype(jnp.float32)
    from_upper = shifted(partial_value[0], "band", -1)
    return partial_value[1] + from_lower + from_upper


def body(
    grid_latent,
    edge_latent,
    mesh_latent,
    mesh_cotangent,
    w_grid,
    w_mesh,
    w_edge,
    bias,
    w_out,
    senders,
    receivers,
    edge_count,
):
    band_index = lax.axis_index("band")
    grid_full = collect(grid_latent, "chan", 0)
    edge_full = collect(edge_latent, "chan", 0)
    stacked = collect(jnp.stack([mesh_latent, mesh_cotangent]), "chan", 1)
    grid_rows = grid_full.shape[0]
    edge_rows = edge_full.shape[0]
    mesh_rows = stacked.shape[1]
    width = mesh_latent.shape[1]
    window = with_halo(stacked, (("band", 1),), mesh_rows)
    local_send = senders - band_index * grid_rows
    local_recv = receivers - (band_index - 1) * mesh_rows
    live = jnp.arange(edge_rows, dtype=jnp.int32) < edge_count[0]
    gsend = grid_full[local_send]
    mrecv = window[0][local_recv]
    message_cot = jnp.where(live[:, None], window[1][local_recv], jnp.zeros((), jnp.bfloat16))
    pre = (
        jnp.dot(gsend, w_grid, preferred_element_type=jnp.float32)
        + jnp.dot(mrecv, w_mesh, preferred_element_type=jnp.float32)
        + jnp.dot(edge_full, w_edge, preferred_element_type=jnp.float32)
        + bias
    )
    sig = jax.nn.sigmoid(pre)
    act = (pre * sig).astype(jnp.bfloat16)
    hidden_cot = lax.dot_general(
        message_cot, w_out, (((1,), (1,)), ((), ())), preferred_element_type=jnp.float32
    )
    pre_cot = (hidden_cot * sig * (1.0 + pre * (1.0 - sig))).astype(jnp.bfloat16)
    contract_rows = (((0,), (0,)), ((), ()))
    weight_terms = (
        lax.dot_general(gsend, pre_cot, contract_rows, preferred_element_type=jnp.float32),
        lax.dot_general(mrecv, pre_cot, contract_rows, preferred_element_type=jnp.float32),
        lax.dot_general(edge_full, pre_cot, contract_rows, preferred_element_type=jnp.float32),
        jnp.sum(pre_cot.astype(jnp.float32), axis=0),
        lax.dot_general(act, message_cot, contract_rows, preferred_element_type=jnp.float32),
    )
    grad_w_grid, grad_w_mesh, grad_w_edge, grad_bias, grad_w_out = packed_total(
        (weight_terms[0], weight_terms[1], weight_terms[2], weight_terms[3], weight_terms[4]),
        "band",
    )
    contract_hidden = (((1,), (1,)), ((), ()))
    edge_terms = lax.dot_general(
        pre_cot, w_edge, contract_hidden, preferred_element_type=jnp.float32
    )
    grad_edge = summed_on_arrival(edge_terms.astype(jnp.bfloat16), "chan", 0).astype(jnp.bfloat16)
    grid_terms = lax.dot_general(
        pre_cot, w_grid, contract_hidden, preferred_element_type=jnp.float32
    )
    grid_terms = jax.ops.segment_sum(grid_terms, local_send, num_segments=grid_rows)
    grad_grid = summed_on_arrival(grid_terms.astype(jnp.bfloat16), "chan", 0).astype(jnp.bfloat16)
    mesh_terms = lax.dot_general(
        pre_cot, w_mesh, contract_hidden, preferred_element_type=jnp.float32
    )
    mesh_terms = jax.ops.segment_sum(mesh_terms, local_recv, num_segments=3 * mesh_rows)
    mesh_terms = mesh_terms.reshape(3, mesh_rows, width)
    reduced = sum_at_owner(mesh_terms, "chan", 1)
    grad_mesh = pass_rims(reduced)
    return (
        grad_grid,
        grad_edge,
        grad_mesh.astype(jnp.bfloat16),
        grad_w_grid,
        grad_w_mesh,
        grad_w_edge,
        grad_bias,
        grad_w_out,
    )


def solution(mesh):
    return jax.shard_map(
        body,
        mesh=mesh,
        in_specs=(
            P(("band", "chan"), None),
            P(("band", "chan"), None),
            P(("band", "chan"), None),
            P(("band", "chan"), None),
            P(None, "chan"),
            P(None, "chan"),
            P(None, "chan"),
            P("chan"),
            P("chan", None),
            P("band"),
            P("band"),
            P("band"),
        ),
        out_specs=(
            P(("band", "chan"), None),
            P(("band", "chan"), None),
            P(("band", "chan"), None),
            P(None, "chan"),
            P(None, "chan"),
            P(None, "chan"),
            P("chan"),
            P("chan", None),
        ),
        check_vma=False,
    )
```

profile of v0, /device:TPU:32, one launch (start us, length us, event | category | flops | bytes accessed | tf_op | source)
XLA Modules:
  0.0 329.7 jit_solution(12943352725146437569)
XLA Ops:
  7.2 0.0 copy-start
  7.2 1.1 pad_maximum_fusion.1
  8.4 4.3 %all_to_all.30 = bf16[2,2,160,512]{3,2,1,0:T(8,128)(2,1)S(1)} all-to-all(bf16[2,2,160,512]{3,2,1,0:T(8,128)(2,1)S(1)} %broadcast_in_dim.54), channel_id=1, replica_groups=mesh['band'=128,'chan'=2] {'chan'}, dimensions={0} | all-to-all | bytes 1310720 | tf_op jit(solution)/shard_map/all_to_all | solution.py:15
  12.7 0.0 copy-start.12
  12.7 0.0 copy-start.7
  12.7 3.5 %collective-permute-start = (bf16[2,320,512]{2,1,0:T(8,128)(2,1)S(1)}, bf16[2,320,512]{2,1,0:T(8,128)(2,1)}, u32[]{:S(2)}, u32[]{:S(2)}) collective-permute-start(bf16[2,320,512]{2,1,0:T(8,128)(2,1)S(1)} %bitcast.65), channel_id=1, source_target_pairs={{0,2},{2,4},{4,6},{6,8},{8,10},{10,12},{12,14},{14,16},{16,18},{18... | collective-permute-start | bytes 1966088 | tf_op jit(solution)/shard_map/ppermute | solution.py:36
  16.2 6.7 %collective-permute-start.1 = (bf16[2,320,512]{2,1,0:T(8,128)(2,1)S(1)}, bf16[2,320,512]{2,1,0:T(8,128)(2,1)}, u32[]{:S(2)}, u32[]{:S(2)}) collective-permute-start(bf16[2,320,512]{2,1,0:T(8,128)(2,1)S(1)} %bitcast.66), channel_id=1, source_target_pairs={{2,0},{4,2},{6,4},{8,6},{10,8},{12,10},{14,12},{16,14},{18,16},{20... | collective-permute-start | bytes 1966088 | tf_op jit(solution)/shard_map/ppermute | solution.py:37
  22.9 1.1 broadcast_in_dim.57
  24.0 3.6 %all-to-all-start.1 = ((bf16[2,576,512]{2,1,0:T(8,128)(2,1)}), bf16[2,576,512]{2,1,0:T(8,128)(2,1)S(1)}, u32[]{:S(2)}, u32[]{:S(2)}) async-start(bf16[2,576,512]{2,1,0:T(8,128)(2,1)} %broadcast_in_dim.57), calls=%async_computation.1 | async-start | bytes 2359296 | tf_op jit(solution)/shard_map/all_to_all | solution.py:15
  28.3 1.5 all-to-all-done.1
  29.8 1.6 broadcast_in_dim.59
  31.4 4.9 %all-to-all-start.2 = ((bf16[2,1152,512]{2,1,0:T(8,128)(2,1)}), bf16[2,1152,512]{2,1,0:T(8,128)(2,1)}, u32[]{:S(2)}, u32[]{:S(2)}) async-start(bf16[2,1152,512]{2,1,0:T(8,128)(2,1)} %broadcast_in_dim.59), calls=%async_computation.2 | async-start | bytes 4718592 | tf_op jit(solution)/shard_map/all_to_all | solution.py:15
  36.3 0.0 all-reduce.2.cloned.1.call-start
  36.4 0.0 copy-start.13
  36.4 7.5 %gather_fusion.1 = bf16[2304,512]{1,0:T(8,128)(2,1)} fusion(bf16[1152,512]{1,0:T(8,128)(2,1)S(1)} %bitcast.61, s32[3072]{0:T(1024)S(1)} %pad_clamp_fusion), kind=kCustom, calls=%fused_computation.1 | custom fusion | bytes 4727808 | tf_op jit(solution)/shard_map/gather | solution.py:100
  43.9 0.6 compare_select_fusion.1
  44.5 3.9 %fusion.15 = f32[2304,256]{1,0:T(8,128)} fusion(bf16[2304,512]{1,0:T(8,128)(2,1)} %gather_fusion.1, bf16[512,256]{1,0:T(8,128)(2,1)S(1)} %copy-done.10), kind=kOutput, calls=%fused_computation.51 | convolution fusion | flops 603979776 | bytes 4980736 | tf_op jit(solution)/shard_map/dot_general | solution.py:104
  48.5 1.4 pad_maximum_fusion
  49.9 0.1 slice_bitcast_fusion.1
  50.0 7.5 %gather_fusion.2 = bf16[2304,512]{1,0:T(8,128)(2,1)} fusion(bf16[960,512]{1,0:T(8,128)(2,1)S(1)} %get-tuple-element.17, s32[3072]{0:T(1024)S(1)} %pad_clamp_fusion.1), kind=kCustom, calls=%fused_computation.2 | custom fusion | bytes 4727808 | tf_op jit(solution)/shard_map/gather | solution.py:101
  57.5 7.5 %gather_fusion = bf16[2304,512]{1,0:T(8,128)(2,1)} fusion(bf16[960,512]{1,0:T(8,128)(2,1)S(1)} %get-tuple-element.16, s32[3072]{0:T(1024)S(1)} %pad_clamp_fusion.1), kind=kCustom, calls=%fused_computation | custom fusion | bytes 4727808 | tf_op jit(solution)/shard_map/gather | solution.py:102
  65.1 3.2 convolution_add_fusion.1
  68.3 2.6 fusion
  70.9 2.9 convert_reduce_fusion
  73.8 0.8 convolution_bitcast_fusion.2
  74.6 0.8 copy-done.2
  75.5 0.8 convolution_bitcast_fusion.3
  76.3 3.3 convolution_bitcast_fusion.1
  79.5 1.9 convolution_bitcast_fusion
  81.4 1.1 copy.30
  82.5 0.3 copy.29
  82.8 2.0 copy.28
  84.9 1.4 copy.31
  86.2 1.2 copy.32
  87.5 0.1 constant_dynamic-update-slice_fusion
  87.7 1.3 copy-done.4
  89.0 0.0 all-reduce.2.cloned.1.call-update
  89.0 2.9 fusion.17
  92.0 16.9 %scatter_custom_fusion.1 = f32[960,512]{1,0:T(8,128)S(1)} fusion(s32[2304]{0:T(1024)} %get-tuple-element.9, f32[2304,512]{1,0:T(8,128)} %fusion.17, f32[]{:T(128)} %constant.10.clone.1), kind=kCustom, calls=%fused_computation.25 | custom fusion | flops 1179648 | bytes 1966592 | tf_op jit(solution)/shard_map/scatter-add | solution.py:140
  108.9 0.2 copy.27
  109.1 5.3 %all_to_all.31 = f32[2,3,160,512]{3,2,1,0:T(8,128)S(1)} all-to-all(f32[2,3,160,512]{3,2,1,0:T(8,128)S(1)} %copy.27), channel_id=1, replica_groups=mesh['band'=128,'chan'=2] {'chan'}, dimensions={0} | all-to-all | bytes 3932160 | tf_op jit(solution)/shard_map/all_to_all | solution.py:64
  114.4 1.2 reduce_sum.44
  115.6 1.0 slice_bitcast_fusion.2
  116.6 2.4 collective-permute-start.3
  119.0 3.9 %fusion.16 = f32[2304,512]{1,0:T(8,128)} fusion(bf16[2304,256]{1,0:T(8,128)(2,1)S(1)} %get-tuple-element.19, bf16[512,256]{1,0:T(8,128)(2,1)} %param.16), kind=kOutput, calls=%fused_computation.52 | convolution fusion | flops 603979776 | bytes 6160384 | tf_op jit(solution)/shard_map/dot_general | solution.py:132
  122.9 1.7 fusion.10
  124.6 3.4 %collective-permute-start.2 = (bf16[160,512]{1,0:T(8,128)(2,1)}, bf16[160,512]{1,0:T(8,128)(2,1)}, u32[]{:S(2)}, u32[]{:S(2)}) collective-permute-start(bf16[160,512]{1,0:T(8,128)(2,1)} %fusion.10), channel_id=1, source_target_pairs={{0,2},{2,4},{4,6},{6,8},{8,10},{10,12},{12,14},{14,16},{16,18},{18... | collective-permute-start | bytes 491528 | tf_op jit(solution)/shard_map/ppermute | solution.py:10
  128.0 17.8 %scatter_custom_fusion = f32[1152,512]{1,0:T(8,128)} fusion(s32[2304]{0:T(1024)S(1)} %get-tuple-element.11, f32[2304,512]{1,0:T(8,128)} %fusion.16, f32[]{:T(128)} %constant.10.clone.1), kind=kCustom, calls=%fused_computation.21 | custom fusion | flops 1179648 | bytes 2359808 | tf_op jit(solution)/shard_map/scatter-add | solution.py:135
  145.8 2.9 convert_element_type.30
  148.6 3.6 %all-to-all-start.3 = ((bf16[2,576,512]{2,1,0:T(8,128)(2,1)}), bf16[2,576,512]{2,1,0:T(8,128)(2,1)S(1)}, u32[]{:S(2)}, u32[]{:S(2)}) async-start(bf16[2,576,512]{2,1,0:T(8,128)(2,1)} %bitcast.9), calls=%async_computation.3 | async-start | bytes 2359296 | tf_op jit(solution)/shard_map/all_to_all | solution.py:58
  152.3 2.2 convolution_convert_fusion
  154.5 1.0 copy-done.3
  155.5 3.8 %all-to-all-start.4 = ((bf16[2,1152,512]{2,1,0:T(8,128)(2,1)}), bf16[2,1152,512]{2,1,0:T(8,128)(2,1)S(1)}, u32[]{:S(2)}, u32[]{:S(2)}) async-start(bf16[2,1152,512]{2,1,0:T(8,128)(2,1)} %bitcast.62), calls=%async_computation.4 | async-start | bytes 4718592 | tf_op jit(solution)/shard_map/all_to_all | solution.py:58
  159.3 2.5 reduce_sum.42
  161.8 0.6 all-to-all-done.4
  162.4 1.8 reduce_sum.43
  164.2 1.8 fusion.9
  165.9 150.3 %all-reduce.2.cloned.1.call-done = f32[524544]{0:T(1024)} async-done(((f32[524544]{0:T(1024)}), f32[524544]{0:T(1024)}) %all-reduce.2.cloned.1.call-update) | async-done | bytes 2098192 | tf_op jit(solution)/shard_map/psum | solution.py:44
  316.2 1.7 fusion.14
  317.9 0.9 reshape.91
  318.8 0.9 slice.67
  319.7 0.9 slice.69
  320.6 0.9 slice.71
  321.6 1.2 slice.88
  (43 shorter events, 0.3 us)
Async XLA Ops:
  7.2 57.9 %copy-start = (bf16[512,256]{1,0:T(8,128)(2,1)S(1)}, bf16[512,256]{1,0:T(8,128)(2,1)}, u32[]{:S(2)}) copy-start(bf16[512,256]{1,0:T(8,128)(2,1)} %param.17) | copy-start | bytes 786436
  7.2 15.7 %copy-start.11 = (bf16[576,512]{1,0:T(8,128)(2,1)S(1)}, bf16[576,512]{1,0:T(8,128)(2,1)}, u32[]{:S(2)}) copy-start(bf16[576,512]{1,0:T(8,128)(2,1)} %param.12) | copy-start | bytes 1769476
  12.7 15.0 %copy-start.12 = (s32[2304]{0:T(1024)S(1)}, s32[2304]{0:T(1024)}, u32[]{:S(2)}) copy-start(s32[2304]{0:T(1024)} %param.21) | copy-start | bytes 27652
  12.7 17.1 %copy-start.7 = (bf16[1152,512]{1,0:T(8,128)(2,1)S(1)}, bf16[1152,512]{1,0:T(8,128)(2,1)}, u32[]{:S(2)}) copy-start(bf16[1152,512]{1,0:T(8,128)(2,1)} %param.13) | copy-start | bytes 3538948
  12.7 35.8 %collective-permute-start = (bf16[2,320,512]{2,1,0:T(8,128)(2,1)S(1)}, bf16[2,320,512]{2,1,0:T(8,128)(2,1)}, u32[]{:S(2)}, u32[]{:S(2)}) collective-permute-start(bf16[2,320,512]{2,1,0:T(8,128)(2,1)S(1)} %bitcast.65), channel_id=1, source_target_pairs={{0,2},{2,4},{4,6},{6,8},{8,10},{10,12},{12,14},{14,16},{16,18},{18... | collective-permute-start | bytes 1966088 | tf_op jit(solution)/shard_map/ppermute | solution.py:36
  16.2 32.2 %collective-permute-start.1 = (bf16[2,320,512]{2,1,0:T(8,128)(2,1)S(1)}, bf16[2,320,512]{2,1,0:T(8,128)(2,1)}, u32[]{:S(2)}, u32[]{:S(2)}) collective-permute-start(bf16[2,320,512]{2,1,0:T(8,128)(2,1)S(1)} %bitcast.66), channel_id=1, source_target_pairs={{2,0},{4,2},{6,4},{8,6},{10,8},{12,10},{14,12},{16,14},{18,16},{20... | collective-permute-start | bytes 1966088 | tf_op jit(solution)/shard_map/ppermute | solution.py:37
  24.0 5.8 %all-to-all-start.1 = ((bf16[2,576,512]{2,1,0:T(8,128)(2,1)}), bf16[2,576,512]{2,1,0:T(8,128)(2,1)S(1)}, u32[]{:S(2)}, u32[]{:S(2)}) async-start(bf16[2,576,512]{2,1,0:T(8,128)(2,1)} %broadcast_in_dim.57), calls=%async_computation.1 | async-start | bytes 2359296 | tf_op jit(solution)/shard_map/all_to_all | solution.py:15
  31.4 36.8 %all-to-all-start.2 = ((bf16[2,1152,512]{2,1,0:T(8,128)(2,1)}), bf16[2,1152,512]{2,1,0:T(8,128)(2,1)}, u32[]{:S(2)}, u32[]{:S(2)}) async-start(bf16[2,1152,512]{2,1,0:T(8,128)(2,1)} %broadcast_in_dim.59), calls=%async_computation.2 | async-start | bytes 4718592 | tf_op jit(solution)/shard_map/all_to_all | solution.py:15
  36.3 279.9 %all-reduce.2.cloned.1.call-start = ((), (), s32[]{:S(2)}) async-start(), calls=%async_computation.6 | async-start | bytes 4202496 | tf_op jit(solution)/shard_map/psum | solution.py:44
  36.4 7.5 %copy-start.13 = (s32[2304]{0:T(1024)S(1)}, s32[2304]{0:T(1024)}, u32[]{:S(2)}) copy-start(s32[2304]{0:T(1024)} %param.22) | copy-start | bytes 27652
  36.4 8.1 %copy-start.10 = (bf16[512,256]{1,0:T(8,128)(2,1)S(1)}, bf16[512,256]{1,0:T(8,128)(2,1)}, u32[]{:S(2)}) copy-start(bf16[512,256]{1,0:T(8,128)(2,1)} %param.16) | copy-start | bytes 786436
  65.1 3.2 copy-start.8
  65.1 3.2 copy-start.14
  68.3 2.6 copy-start.5
  68.3 2.6 copy-start.16
  70.9 2.9 copy-start.1
  73.8 1.7 copy-start.2
  84.9 2.6 copy-start.6
  84.9 2.7 copy-start.15
  87.7 1.3 copy-start.4
  116.6 47.6 %collective-permute-start.3 = (f32[160,512]{1,0:T(8,128)S(1)}, f32[160,512]{1,0:T(8,128)S(1)}, u32[]{:S(2)}, u32[]{:S(2)}) collective-permute-start(f32[160,512]{1,0:T(8,128)S(1)} %slice_bitcast_fusion.2), channel_id=1, source_target_pairs={{2,0},{4,2},{6,4},{8,6},{10,8},{12,10},{14,12},{16,14},{18,16},{20... | collective-permute-start | bytes 983048 | tf_op jit(solution)/shard_map/ppermute | solution.py:10
  124.6 39.6 %collective-permute-start.2 = (bf16[160,512]{1,0:T(8,128)(2,1)}, bf16[160,512]{1,0:T(8,128)(2,1)}, u32[]{:S(2)}, u32[]{:S(2)}) collective-permute-start(bf16[160,512]{1,0:T(8,128)(2,1)} %fusion.10), channel_id=1, source_target_pairs={{0,2},{2,4},{4,6},{6,8},{8,10},{10,12},{12,14},{14,16},{16,18},{18... | collective-permute-start | bytes 491528 | tf_op jit(solution)/shard_map/ppermute | solution.py:10
  145.8 6.5 %copy-start.9 = (bf16[512,256]{1,0:T(8,128)(2,1)S(1)}, bf16[512,256]{1,0:T(8,128)(2,1)}, u32[]{:S(2)}) copy-start(bf16[512,256]{1,0:T(8,128)(2,1)} %param.18) | copy-start | bytes 786436
  148.6 5.9 %all-to-all-start.3 = ((bf16[2,576,512]{2,1,0:T(8,128)(2,1)}), bf16[2,576,512]{2,1,0:T(8,128)(2,1)S(1)}, u32[]{:S(2)}, u32[]{:S(2)}) async-start(bf16[2,576,512]{2,1,0:T(8,128)(2,1)} %bitcast.9), calls=%async_computation.3 | async-start | bytes 2359296 | tf_op jit(solution)/shard_map/all_to_all | solution.py:58
  154.5 1.0 copy-start.3
  155.5 6.9 %all-to-all-start.4 = ((bf16[2,1152,512]{2,1,0:T(8,128)(2,1)}), bf16[2,1152,512]{2,1,0:T(8,128)(2,1)S(1)}, u32[]{:S(2)}, u32[]{:S(2)}) async-start(bf16[2,1152,512]{2,1,0:T(8,128)(2,1)} %bitcast.62), calls=%async_computation.4 | async-start | bytes 4718592 | tf_op jit(solution)/shard_map/all_to_all | solution.py:58
Sparse Core Ops, SparseCore 0:
  89.1 227.0 all-reduce.1
where the time goes:
time: 332 us; the launch traced here: 330 us
  waiting for transfers between devices  152 us (46%)
  other arithmetic  47.9 us (14%)
  local copies, waits for them, and re-layouts  44.3 us (13%)
  starting transfers between devices  32 us (10%)
  matrix products  28.4 us (9%)
  between operations  15.1 us (5%)
  blocking collectives  9.57 us (3%)
    psum x1, waiting for transfers between devices, packed_total(): so_far = lax.psum(ravelled, axis)  150 us
    scatter-add x1, other arithmetic, body(): jax.ops.segment_sum(grid_terms, local_send, num_segments=grid_rows)  17.8 us
    scatter-add x1, other arithmetic, body(): jax.ops.segment_sum(mesh_terms, local_recv, num_segments=3 * mesh_rows)  16.9 us
    all_to_all x2, starting transfers between devices, from_everyone(): lax.all_to_all(jnp.broadcast_to(x[None], (devices, *x.shape)), axis, 0, 0...  8.52 us
    gather x1, local copies, waits for them, and re-layouts, body(): mrecv = window[0][local_recv]  7.52 us
    gather x1, local copies, waits for them, and re-layouts, body(): gsend = grid_full[local_send]  7.52 us
    gather x1, local copies, waits for them, and re-layouts, body(): window[1][local_recv]  7.5 us
    all_to_all x2, starting transfers between devices, summed_on_arrival(): lax.all_to_all(pieces, axis, split_axis=0, concat_axis=0, tiled=True)  7.42 us
  transfers between devices with their start and end apart: 9, of which 3 were waited for; matrix products, arithmetic and copies ran while one was open for 28% of the time, Pallas kernels for 0%

commit v1 on v0

v1 whole, which is shorter than its diff:
```python
import functools

import jax
import jax.numpy as jnp
import numpy as np
from jax import lax
from jax.experimental import pallas as pl
from jax.experimental.pallas import tpu as pltpu
from jax.sharding import Mesh, PartitionSpec as P

BF = jnp.bfloat16
F32 = jnp.float32
BAND = ("z", "y", "x")
PLANE = ("y", "x")
LANES = 128
EDGE_BLOCK = 384
TAIL = 16


def dot(a, b):
    return jnp.dot(a, b, preferred_element_type=F32)


def dot_t(a, b):
    return lax.dot_general(a, b, (((1,), (1,)), ((), ())), preferred_element_type=F32)


def dot_rows(a, b):
    return lax.dot_general(a, b, (((0,), (0,)), ((), ())), preferred_element_type=F32)


def edge_kernel(
    grid_own,
    grid_far,
    edge_own,
    edge_far,
    m0,
    m1,
    m2,
    m3,
    m4,
    m5,
    w_grid,
    w_mesh,
    w_edge,
    w_out,
    bias,
    send_col,
    recv_col,
    send_row,
    recv_row,
    wire,
    cot_own,
    cot_far,
    seg_grid,
    rim_low,
    rim_mid,
    rim_high,
    lat,
    cot,
    table,
    cot_table,
    left,
    right,
    sums,
    act_sums,
    edge_sum,
    bias_sum,
):
    half_edges = edge_own.shape[0]
    half_grid = grid_own.shape[0]
    n_grid = 2 * half_grid
    piece = m0.shape[1]
    n_mesh = 6 * piece
    pad_mesh = lat.shape[0]
    n_rows = n_grid + pad_mesh
    block = left.shape[0]
    hidden = w_grid.shape[1]
    for k, m in enumerate((m0, m1, m2, m3, m4, m5)):
        lat[k * piece : (k + 1) * piece] = m[0]
        cot[k * piece : (k + 1) * piece] = m[1]
    if pad_mesh > n_mesh:
        lat[n_mesh:] = jnp.zeros((pad_mesh - n_mesh, lat.shape[1]), BF)
        cot[n_mesh:] = jnp.zeros((pad_mesh - n_mesh, cot.shape[1]), BF)
    table[0:half_grid] = dot(grid_own[...], w_grid[...]).astype(BF)
    table[half_grid:n_grid] = dot(grid_far[...], w_grid[...]).astype(BF)
    table[n_grid:n_rows] = dot(lat[...], w_mesh[...]).astype(BF)
    table[n_rows:] = w_edge[...]
    cot_table[...] = dot_t(cot[...], w_out[...]).astype(BF)
    sums[...] = jnp.zeros_like(sums)
    act_sums[...] = jnp.zeros_like(act_sums)
    edge_sum[...] = jnp.zeros_like(edge_sum)
    bias_sum[...] = jnp.zeros_like(bias_sum)

    def run(edges, cot_out, base):
        def step(i, carry):
            at = pl.multiple_of(i * block, block)
            rows = pl.ds(at, block)
            wide = pl.ds(pl.multiple_of(base + at, block), block)
            lane = lax.broadcasted_iota(jnp.int32, (block, LANES), 1)
            sender = send_col[wide, :]
            receiver = recv_col[wide, :]
            for k in range(n_grid // LANES):
                left[:, k * LANES : (k + 1) * LANES] = jnp.where(sender == lane + k * LANES, 1.0, 0.0).astype(BF)
            for k in range(pad_mesh // LANES):
                at_lane = n_grid + k * LANES
                left[:, at_lane : at_lane + LANES] = jnp.where(receiver == lane + k * LANES, 1.0, 0.0).astype(BF)
            left[:, n_rows:] = edges[rows, :]
            pre = dot(left[...], table[...]) + bias[...]
            hidden_cot = dot(left[:, n_grid:n_rows], cot_table[...])
            sig = jax.nn.sigmoid(pre)
            act = (pre * sig).astype(BF)
            pre_cot = (hidden_cot * sig * (1.0 + pre * (1.0 - sig))).astype(BF)
            cot_out[rows, :] = pre_cot
            sub = lax.broadcasted_iota(jnp.int32, (LANES, block), 0)
            sender_row = jnp.broadcast_to(send_row[:, wide], (LANES, block))
            receiver_row = jnp.broadcast_to(recv_row[:, wide], (LANES, block))
            for k in range(n_grid // LANES):
                right[k * LANES : (k + 1) * LANES, :] = jnp.where(sender_row == sub + k * LANES, 1.0, 0.0).astype(BF)
            for k in range(pad_mesh // LANES):
                at_row = n_grid + k * LANES
                right[at_row : at_row + LANES, :] = jnp.where(receiver_row == sub + k * LANES, 1.0, 0.0).astype(BF)
            sums[...] += dot(right[...], pre_cot)
            act_sums[...] += dot(right[n_grid:, :], act)
            edge_sum[...] += dot_rows(edges[rows, :], pre_cot)
            bias_sum[...] += jnp.sum(pre_cot.astype(F32), axis=0, keepdims=True)
            return carry

        lax.fori_loop(0, half_edges // block, step, 0)

    run(edge_own, cot_own, 0)
    run(edge_far, cot_far, half_edges)

    seg_grid[...] = sums[:n_grid].astype(BF)
    seg_mesh = sums[n_grid:].astype(BF)
    grads = (
        dot_rows(grid_own[...], seg_grid[:half_grid]) + dot_rows(grid_far[...], seg_grid[half_grid:]),
        dot_rows(lat[...], seg_mesh),
        edge_sum[...],
    )
    rows = 128
    at = 0

    def put(at, value):
        wire[at, 0:rows, :] = value[:, :LANES].astype(BF)
        wire[at, rows : 2 * rows, :] = value[:, LANES:].astype(BF)

    for g in grads:
        for k in range(g.shape[0] // rows):
            put(at, g[k * rows : (k + 1) * rows])
            at += 1
    g = dot_rows(act_sums[...].astype(BF), cot[...])
    for c in range(2):
        for k in range(g.shape[0] // rows):
            put(at, g[k * rows : (k + 1) * rows, c * hidden : (c + 1) * hidden])
            at += 1
    sub = lax.broadcasted_iota(jnp.int32, (TAIL, LANES), 0)
    low = jnp.broadcast_to(bias_sum[:, :LANES], (TAIL, LANES))
    high = jnp.broadcast_to(bias_sum[:, LANES:], (TAIL, LANES))
    tail = jnp.where(sub == 0, low, jnp.where(sub == 1, high, 0.0)).astype(BF)
    for k in range(wire.shape[0]):
        wire[k, 2 * rows :, :] = tail
    for ref, o, kind in ((rim_low, 0, BF), (rim_mid, 1, F32), (rim_high, 2, BF)):
        for h in range(2):
            start = n_grid + (3 * h + o) * piece
            ref[h * piece : (h + 1) * piece] = sums[start : start + piece].astype(kind)


def swap(x):
    return lax.ppermute(x, "chan", [(0, 1), (1, 0)])


def shifted(x, by):
    n = lax.axis_size(BAND)
    return lax.ppermute(x, BAND, [(i, i + by) for i in range(n) if 0 <= i + by < n])


def plane_total(wire):
    arrived = lax.all_to_all(wire, PLANE, 0, 0, tiled=True)
    total = arrived.astype(F32).sum(axis=0)
    depth = lax.axis_size("z")
    step = 1
    while step < depth:
        mine = total.astype(BF)
        other = lax.ppermute(mine, "z", [(i, i ^ step) for i in range(depth)])
        total = mine.astype(F32) + other.astype(F32)
        step *= 2
    chunk = total[:-TAIL].astype(BF)
    bias_total = total[-TAIL:]
    members = wire.shape[0]
    everyone = lax.all_to_all(jnp.broadcast_to(chunk[None], (members, *chunk.shape)), PLANE, 0, 0, tiled=True)
    return everyone, bias_total


def body(
    grid_latent,
    edge_latent,
    mesh_latent,
    mesh_cotangent,
    w_grid,
    w_mesh,
    w_edge,
    bias,
    w_out,
    senders,
    receivers,
    edge_count,
):
    band = lax.axis_index(BAND)
    chan = lax.axis_index("chan")
    half_grid = grid_latent.shape[0]
    half_edges = edge_latent.shape[0]
    piece, width = mesh_latent.shape
    hidden = w_grid.shape[1]
    n_grid = 2 * half_grid
    n_edges = 2 * half_edges
    pad_mesh = -(-6 * piece // LANES) * LANES

    mesh_own = jnp.stack([mesh_latent, mesh_cotangent])
    mesh_below = shifted(mesh_own, 1)
    mesh_above = shifted(mesh_own, -1)
    edge_far = swap(edge_latent)
    grid_far = swap(grid_latent)
    mesh_near = (mesh_below, mesh_own, mesh_above)
    mesh_far = tuple(swap(m) for m in mesh_near)

    at = senders - band * n_grid - chan * half_grid
    local_send = jnp.where(at < 0, at + n_grid, at)
    at = receivers - (band - 1) * (2 * piece)
    owner = at // (2 * piece)
    within = at - owner * (2 * piece)
    half = within // piece
    local_recv = ((half ^ chan) * 3 + owner) * piece + within - half * piece
    live = jnp.arange(n_edges, dtype=jnp.int32) < edge_count[0]
    local_recv = jnp.where(live, local_recv, -1)

    def own_first(v):
        return jnp.where(chan == 0, v, jnp.concatenate([v[half_edges:], v[:half_edges]]))

    local_send = own_first(local_send)
    local_recv = own_first(local_recv)
    columns = [jnp.broadcast_to(v[:, None], (n_edges, LANES)) for v in (local_send, local_recv)]
    rows = [v.reshape(1, n_edges) for v in (local_send, local_recv)]

    members = lax.axis_size(PLANE)
    shape = jax.ShapeDtypeStruct
    vmem = pl.BlockSpec(memory_space=pltpu.VMEM)
    wire, cot_own, cot_far, seg_grid, rim_low, rim_mid, rim_high = pl.pallas_call(
        edge_kernel,
        out_shape=(
            shape((16, 256 + TAIL, LANES), BF),
            shape((half_edges, hidden), BF),
            shape((half_edges, hidden), BF),
            shape((n_grid, hidden), BF),
            shape((2 * piece, hidden), BF),
            shape((2 * piece, hidden), F32),
            shape((2 * piece, hidden), BF),
        ),
        in_specs=[vmem] * 19,
        out_specs=(vmem,) * 7,
        scratch_shapes=[
            pltpu.VMEM((pad_mesh, width), BF),
            pltpu.VMEM((pad_mesh, width), BF),
            pltpu.VMEM((n_grid + pad_mesh + width, hidden), BF),
            pltpu.VMEM((pad_mesh, hidden), BF),
            pltpu.VMEM((EDGE_BLOCK, n_grid + pad_mesh + width), BF),
            pltpu.VMEM((n_grid + pad_mesh, EDGE_BLOCK), BF),
            pltpu.VMEM((n_grid + pad_mesh, hidden), F32),
            pltpu.VMEM((pad_mesh, hidden), F32),
            pltpu.VMEM((width, hidden), F32),
            pltpu.VMEM((1, hidden), F32),
        ],
        compiler_params=pltpu.CompilerParams(vmem_limit_bytes=56 * 1024 * 1024),
        name="edge_step",
    )(
        grid_latent,
        grid_far,
        edge_latent,
        edge_far,
        *mesh_near,
        *mesh_far,
        w_grid,
        w_mesh,
        w_edge,
        w_out,
        bias.reshape(1, hidden),
        *columns,
        *rows,
    )

    from_above = shifted(rim_low, -1)
    from_below = shifted(rim_high, 1)
    edge_back = swap(dot_t(cot_far, w_edge).astype(BF))
    grid_back = swap(dot_t(seg_grid[half_grid:], w_grid).astype(BF))
    everyone, bias_total = plane_total(wire.reshape(members, -1, LANES))

    grad_edge = (dot_t(cot_own, w_edge) + edge_back.astype(F32)).astype(BF)
    grad_grid = (dot_t(seg_grid[:half_grid], w_grid) + grid_back.astype(F32)).astype(BF)
    seg_mesh = (rim_mid + from_above.astype(F32) + from_below.astype(F32)).astype(BF)
    mesh_back = swap(dot_t(seg_mesh[piece:], w_mesh).astype(BF))
    grad_mesh = (dot_t(seg_mesh[:piece], w_mesh) + mesh_back.astype(F32)).astype(BF)

    def wide(chunks):
        n = chunks.shape[0]
        pair = chunks.astype(F32).reshape(n, 2, 128, LANES)
        return jnp.concatenate([pair[:, 0], pair[:, 1]], axis=-1).reshape(n * 128, 2 * LANES)

    grad_w_grid = wide(everyone[0:4])
    grad_w_mesh = wide(everyone[4:8])
    grad_w_edge = wide(everyone[8:12])
    grad_w_out = jnp.concatenate([wide(everyone[12:14]), wide(everyone[14:16])], axis=1)
    grad_bias = jnp.concatenate([bias_total[0], bias_total[1]])
    return (
        grad_grid,
        grad_edge,
        grad_mesh,
        grad_w_grid,
        grad_w_mesh,
        grad_w_edge,
        grad_bias,
        grad_w_out,
    )


def solution(mesh):
    bands, chans = (mesh.shape["band"], mesh.shape["chan"])
    side = 4
    inner = Mesh(np.asarray(mesh.devices).reshape(bands // side**2, side, side, chans), (*BAND, "chan"))
    every = P((*BAND, "chan"), None)
    return jax.shard_map(
        body,
        mesh=inner,
        in_specs=(
            every,
            every,
            every,
            every,
            P(None, "chan"),
            P(None, "chan"),
            P(None, "chan"),
            P("chan"),
            P("chan", None),
            P(BAND),
            P(BAND),
            P(BAND),
        ),
        out_specs=(
            every,
            every,
            every,
            P(None, "chan"),
            P(None, "chan"),
            P(None, "chan"),
            P("chan"),
            P("chan", None),
        ),
        check_vma=False,
    )
```

time: 332 us -> 127 us (0.38)
  waiting for transfers between devices: 152 us -> 41.1 us
  other arithmetic: 47.9 us -> 7.49 us
  local copies, waits for them, and re-layouts: 44.3 us -> 6.47 us
  Pallas kernels: 0 us -> 24.9 us
  matrix products: 28.4 us -> 8.63 us
  between operations: 15.1 us -> 1.72 us
  blocking collectives: 9.57 us -> 0 us
    psum x1 -> x0, waiting for transfers between devices: 150 us -> none  [packed_total(): so_far = lax.psum(ravelled, axis)]
    scatter-add x2 -> x0, other arithmetic: 34.7 us -> none  [the longest x1 17.8 us: body(): jax.ops.segment_sum(grid_terms, local_send, num_segments=grid_rows)]
    pallas_call x0 -> x1, Pallas kernels: none -> 24.9 us  [body(): pl.pallas_call(edge_kernel, out_shape=(shape((16, 256 + TAIL, LANES), BF)...]
    gather x3 -> x0, local copies, waits for them, and re-layouts: 22.5 us -> none  [the longest x1 7.52 us: body(): mrecv = window[0][local_recv]]
    all_to_all x4 -> x2, waiting for transfers between devices: 2.07 us -> 22.9 us  [the longest x1 13 us: plane_total(): arrived = lax.all_to_all(wire, PLANE, 0, 0, tiled=True)]
    dot_general x11 -> x6, matrix products: 28.4 us -> 8.63 us  [dot_t(): lax.dot_general(a, b, (((1,), (1,)), ((), ())), preferred_element_type=F32)]
    ppermute x4 -> x15, waiting for transfers between devices: 0.01 us -> 18.2 us  [the longest x4 11.3 us: shifted(): lax.ppermute(x, BAND, [(i, i + by) for i in range(n) if 0 <= i + by < n])]
    ppermute x4 -> x15, starting transfers between devices: 16 us -> 27.3 us  [the longest x4 15.2 us: shifted(): lax.ppermute(x, BAND, [(i, i + by) for i in range(n) if 0 <= i + by < n])]
  transfers between devices with their start and end apart: 9 -> 17, of which waited for: 3 -> 7; matrix products, arithmetic and copies ran while one was open for 28% -> 12% of each run, Pallas kernels for 0% -> 0%
where the time goes in v1:
time: 127 us; the launch traced here: 125 us
  waiting for transfers between devices  41.1 us (32%)
  starting transfers between devices  35 us (28%)
  Pallas kernels  24.9 us (20%)
  matrix products  8.63 us (7%)
  other arithmetic  7.49 us (6%)
  local copies, waits for them, and re-layouts  6.47 us (5%)
  between operations  1.72 us (1%)
    pallas_call x1, Pallas kernels, body(): pl.pallas_call(edge_kernel, out_shape=(shape((16, 256 + TAIL, LANES), BF)...  24.9 us
    ppermute x4, starting transfers between devices, shifted(): lax.ppermute(x, BAND, [(i, i + by) for i in range(n) if 0 <= i + by < n])  15.2 us
    all_to_all x1, waiting for transfers between devices, plane_total(): arrived = lax.all_to_all(wire, PLANE, 0, 0, tiled=True)  13 us
    ppermute x4, waiting for transfers between devices, shifted(): lax.ppermute(x, BAND, [(i, i + by) for i in range(n) if 0 <= i + by < n])  11.3 us
    ppermute x3, starting transfers between devices, plane_total(): other = lax.ppermute(mine, 'z', [(i, i ^ step) for i in range(depth)])  11.3 us
    all_to_all x1, waiting for transfers between devices, plane_total(): lax.all_to_all(jnp.broadcast_to(chunk[None], (members, *chunk.shape)), PL...  9.92 us
    dot_general x6, matrix products, dot_t(): lax.dot_general(a, b, (((1,), (1,)), ((), ())), preferred_element_type=F32)  8.63 us
    ppermute x3, waiting for transfers between devices, plane_total(): other = lax.ppermute(mine, 'z', [(i, i ^ step) for i in range(depth)])  6.91 us
  transfers between devices with their start and end apart: 17, of which 7 were waited for; matrix products, arithmetic and copies ran while one was open for 12% of the time, Pallas kernels for 0%

profile of v1, /device:TPU:32, one launch (start us, length us, event | category | flops | bytes accessed | tf_op | source)
XLA Modules:
  0.0 125.4 jit_solution(8845790672654650223)
XLA Ops:
  0.6 0.1 collective-permute-start.1
  0.7 1.0 pad_maximum_fusion.4.m1
  1.8 0.0 copy-start.3
  1.8 0.6 collective-permute-start.5
  2.4 6.7 %collective-permute-start.3 = (bf16[2,160,512]{2,1,0:T(8,128)(2,1)S(1)}, bf16[2,160,512]{2,1,0:T(8,128)(2,1)S(1)}, u32[]{:S(2)}, u32[]{:S(2)}) collective-permute-start(bf16[2,160,512]{2,1,0:T(8,128)(2,1)S(1)} %pad_maximum_fusion.4.m1), channel_id=1, source_target_pairs={{2,0},{4,2},{6,4},{8,6},{10,8},{12,10},{14,12},{16,14},{18,16},{20... | collective-permute-start | bytes 983048 | tf_op jit(solution)/shard_map/ppermute | solution.py:175
  9.0 1.9 %collective-permute-start.2 = (bf16[2,160,512]{2,1,0:T(8,128)(2,1)S(1)}, bf16[2,160,512]{2,1,0:T(8,128)(2,1)S(1)}, u32[]{:S(2)}, u32[]{:S(2)}) collective-permute-start(bf16[2,160,512]{2,1,0:T(8,128)(2,1)S(1)} %pad_maximum_fusion.4.m1), channel_id=1, source_target_pairs={{0,2},{2,4},{4,6},{6,8},{8,10},{10,12},{12,14},{14,16},{16,18},{18... | collective-permute-start | bytes 983048 | tf_op jit(solution)/shard_map/ppermute | solution.py:175
  10.9 0.1 collective-permute-start
  11.1 0.7 compare_select_fusion
  12.4 0.7 subtract_select_fusion
  13.2 3.0 %collective-permute-done.3.m2 = bf16[2,160,512]{2,1,0:T(8,128)(2,1)S(1)} collective-permute-done((bf16[2,160,512]{2,1,0:T(8,128)(2,1)S(1)}, bf16[2,160,512]{2,1,0:T(8,128)(2,1)S(1)}, u32[]{:S(2)}, u32[]{:S(2)}) %collective-permute-start.3) | collective-permute-done | bytes 327712 | tf_op jit(solution)/shard_map/ppermute | solution.py:175
  16.2 0.0 collective-permute-start.6
  16.2 8.3 %collective-permute-done.2.m0 = bf16[2,160,512]{2,1,0:T(8,128)(2,1)S(1)} collective-permute-done((bf16[2,160,512]{2,1,0:T(8,128)(2,1)S(1)}, bf16[2,160,512]{2,1,0:T(8,128)(2,1)S(1)}, u32[]{:S(2)}, u32[]{:S(2)}) %collective-permute-start.2) | collective-permute-done | bytes 327712 | tf_op jit(solution)/shard_map/ppermute | solution.py:175
  24.5 0.0 collective-permute-start.4
  24.5 0.9 add_select_fusion.2
  25.4 0.6 reshape.84.send_row
  26.0 0.6 reshape.85.recv_row
  26.6 0.0 collective-permute-done.5.m4
  26.6 0.0 collective-permute-done.grid_far
  26.6 0.0 copy-start.8
  26.6 0.0 collective-permute-done.6.m5
  26.6 0.0 collective-permute-done.4.m3
  26.6 0.0 collective-permute-done.1.edge_far
  26.6 0.0 copy-start.4
  26.6 1.9 %broadcast_in_dim.9.recv_col = s32[2304,128]{1,0:T(8,128)} broadcast(s32[2304]{0:T(1024)S(1)} %get-tuple-element.44), dimensions={0} | broadcast | bytes 1188864 | tf_op jit(solution)/shard_map/broadcast_in_dim | solution.py:242
  28.5 1.9 %broadcast_in_dim.8.send_col = s32[2304,128]{1,0:T(8,128)} broadcast(s32[2304]{0:T(1024)S(1)} %get-tuple-element.43), dimensions={0} | broadcast | bytes 1188864 | tf_op jit(solution)/shard_map/broadcast_in_dim | solution.py:242
  30.4 24.9 %edge_step.1 = (bf16[16,272,128]{2,1,0:T(8,128)(2,1)}, bf16[1152,256]{1,0:T(8,128)(2,1)}, bf16[1152,256]{1,0:T(8,128)(2,1)}, bf16[1152,256]{1,0:T(8,128)(2,1)}, ...) custom-call(bf16[576,512]{1,0:T(8,128)(2,1)} %grid_own.1, bf16[576,512]{1,0:T(8,128)(2,1)} %copy-done.8, ...), custom_call_target="tpu_custom_call" | custom-call | tf_op jit(solution)/shard_map/edge_step/pallas_call | solution.py:248
  55.3 0.0 copy-start.15
  55.4 0.0 copy-start.1
  55.4 3.8 %all-to-all-start = ((bf16[16,272,128]{2,1,0:T(8,128)(2,1)}), bf16[16,272,128]{2,1,0:T(8,128)(2,1)S(1)}, u32[]{:S(2)}, u32[]{:S(2)}) async-start(bf16[16,272,128]{2,1,0:T(8,128)(2,1)} %get-tuple-element.21), calls=%async_computation | async-start | bytes 2228224 | tf_op jit(solution)/shard_map/all_to_all | solution.py:179
  59.2 0.0 copy-start.2
  59.3 4.5 %collective-permute-start.9 = (bf16[320,256]{1,0:T(8,128)(2,1)S(1)}, bf16[320,256]{1,0:T(8,128)(2,1)S(1)}, u32[]{:S(2)}, u32[]{:S(2)}) collective-permute-start(bf16[320,256]{1,0:T(8,128)(2,1)S(1)} %copy-done.15), channel_id=1, source_target_pairs={{2,0},{4,2},{6,4},{8,6},{10,8},{12,10},{14,12},{16,14},{18,16},{20... | collective-permute-start | bytes 491528 | tf_op jit(solution)/shard_map/ppermute | solution.py:175
  63.8 2.1 %collective-permute-start.10 = (bf16[320,256]{1,0:T(8,128)(2,1)S(1)}, bf16[320,256]{1,0:T(8,128)(2,1)S(1)}, u32[]{:S(2)}, u32[]{:S(2)}) collective-permute-start(bf16[320,256]{1,0:T(8,128)(2,1)S(1)} %copy-done.14), channel_id=1, source_target_pairs={{0,2},{2,4},{4,6},{6,8},{8,10},{10,12},{12,14},{14,16},{16,18},{18... | collective-permute-start | bytes 491528 | tf_op jit(solution)/shard_map/ppermute | solution.py:175
  65.9 1.2 convolution_convert_fusion.1
  67.1 0.0 collective-permute-start.7
  67.1 13.0 %all-to-all-done = bf16[16,272,128]{2,1,0:T(8,128)(2,1)S(1)} async-done(((bf16[16,272,128]{2,1,0:T(8,128)(2,1)}), bf16[16,272,128]{2,1,0:T(8,128)(2,1)S(1)}, u32[]{:S(2)}, u32[]{:S(2)}) %all-to-all-start) | async-done | bytes 1114144 | tf_op jit(solution)/shard_map/all_to_all | solution.py:179
  80.1 0.2 reduce_sum.12
  80.2 0.1 collective-permute-start.12
  80.4 0.0 copy-start
  80.4 1.5 %convolution_convert_fusion = bf16[1152,512]{1,0:T(8,128)(2,1)} fusion(bf16[1152,256]{1,0:T(8,128)(2,1)S(1)} %copy-done.7, bf16[512,256]{1,0:T(8,128)(2,1)S(1)} %copy-done.2), kind=kOutput, calls=%fused_computation.2 | convolution fusion | flops 302579712 | bytes 2031616 | tf_op jit(solution)/shard_map/dot_general | solution.py:25
  81.9 0.0 collective-permute-start.8
  81.9 2.7 %collective-permute-done.12 = bf16[272,128]{1,0:T(8,128)(2,1)S(1)} collective-permute-done((bf16[272,128]{1,0:T(8,128)(2,1)S(1)}, bf16[272,128]{1,0:T(8,128)(2,1)S(1)}, u32[]{:S(2)}, u32[]{:S(2)}) %collective-permute-start.12) | collective-permute-done | bytes 69664 | tf_op jit(solution)/shard_map/ppermute | solution.py:185
  84.7 3.3 %collective-permute-start.13 = (bf16[272,128]{1,0:T(8,128)(2,1)S(1)}, bf16[272,128]{1,0:T(8,128)(2,1)S(1)}, u32[]{:S(2)}, u32[]{:S(2)}) collective-permute-start(bf16[272,128]{1,0:T(8,128)(2,1)S(1)} %add_convert_fusion.2), channel_id=1, source_target_pairs={{0,64},{32,96},{64,0},{96,32},{128,192},{160,224},{192,128},{224,1... | collective-permute-start | bytes 208904 | tf_op jit(solution)/shard_map/ppermute | solution.py:185
  88.0 0.0 collective-permute-done.9
  88.0 0.0 collective-permute-done.10
  88.0 0.1 add_convert_fusion
  88.1 2.2 %collective-permute-done.13 = bf16[272,128]{1,0:T(8,128)(2,1)S(1)} collective-permute-done((bf16[272,128]{1,0:T(8,128)(2,1)S(1)}, bf16[272,128]{1,0:T(8,128)(2,1)S(1)}, u32[]{:S(2)}, u32[]{:S(2)}) %collective-permute-start.13) | collective-permute-done | bytes 69664 | tf_op jit(solution)/shard_map/ppermute | solution.py:185
  90.3 7.8 %collective-permute-start.14 = (bf16[272,128]{1,0:T(8,128)(2,1)S(1)}, bf16[272,128]{1,0:T(8,128)(2,1)S(1)}, u32[]{:S(2)}, u32[]{:S(2)}) collective-permute-start(bf16[272,128]{1,0:T(8,128)(2,1)S(1)} %add_convert_fusion.1), channel_id=1, source_target_pairs={{0,128},{32,160},{64,192},{96,224},{128,0},{160,32},{192,64},{224,... | collective-permute-start | bytes 208904 | tf_op jit(solution)/shard_map/ppermute | solution.py:185
  98.1 0.2 convolution_convert_fusion.2
  98.4 0.1 collective-permute-start.11
  98.5 1.9 %collective-permute-done.14 = bf16[272,128]{1,0:T(8,128)(2,1)S(1)} collective-permute-done((bf16[272,128]{1,0:T(8,128)(2,1)S(1)}, bf16[272,128]{1,0:T(8,128)(2,1)S(1)}, u32[]{:S(2)}, u32[]{:S(2)}) %collective-permute-start.14) | collective-permute-done | bytes 69664 | tf_op jit(solution)/shard_map/ppermute | solution.py:185
  100.5 1.2 broadcast_in_dim.10
  101.6 3.9 %all-to-all-start.1 = ((bf16[16,256,128]{2,1,0:T(8,128)(2,1)}), bf16[16,256,128]{2,1,0:T(8,128)(2,1)S(1)}, u32[]{:S(2)}, u32[]{:S(2)}) async-start(bf16[16,256,128]{2,1,0:T(8,128)(2,1)} %broadcast_in_dim.10), calls=%async_computation.1 | async-start | bytes 2097152 | tf_op jit(solution)/shard_map/all_to_all | solution.py:191
  105.6 1.9 %fusion.2 = bf16[160,512]{1,0:T(8,128)(2,1)} fusion(bf16[512,256]{1,0:T(8,128)(2,1)S(1)} %copy-done, bf16[160,512]{1,0:T(8,128)(2,1)} %collective-permute-done.11, bf16[320,256]{1,0:T(8,128)(2,1)S(1)} %add_convert_fusion), kind=kOutput, calls=%fused_computation.7 | convolution fusion | flops 42188800 | bytes 671744 | tf_op jit(solution)/shard_map/dot_general | solution.py:25
  107.4 0.0 collective-permute-done.7
  107.4 2.3 %fusion.1 = bf16[576,512]{1,0:T(8,128)(2,1)} fusion(bf16[512,256]{1,0:T(8,128)(2,1)S(1)} %copy-done.1, bf16[576,512]{1,0:T(8,128)(2,1)} %collective-permute-done.7, bf16[1152,256]{1,0:T(8,128)(2,1)} %get-tuple-element.15), kind=kOutput, calls=%fused_computation.4 | convolution fusion | flops 151879680 | bytes 1736704 | tf_op jit(solution)/shard_map/dot_general | solution.py:25
  109.8 0.0 collective-permute-done.8
  109.8 1.5 %fusion = bf16[1152,512]{1,0:T(8,128)(2,1)} fusion(bf16[1152,256]{1,0:T(8,128)(2,1)S(1)} %copy-done.6, bf16[512,256]{1,0:T(8,128)(2,1)S(1)} %copy-done.2, bf16[1152,512]{1,0:T(8,128)(2,1)S(1)} %collective-permute-done.8), kind=kOutput, calls=%fused_computation.1 | convolution fusion | flops 303759360 | bytes 3211264 | tf_op jit(solution)/shard_map/dot_general | solution.py:25
  111.3 0.6 pad_maximum_fusion.5
  111.9 9.9 %all-to-all-done.1 = bf16[16,256,128]{2,1,0:T(8,128)(2,1)S(1)} async-done(((bf16[16,256,128]{2,1,0:T(8,128)(2,1)}), bf16[16,256,128]{2,1,0:T(8,128)(2,1)S(1)}, u32[]{:S(2)}, u32[]{:S(2)}) %all-to-all-start.1) | async-done | bytes 1048608 | tf_op jit(solution)/shard_map/all_to_all | solution.py:191
  121.9 0.1 fusion.10
  122.1 0.8 pad_maximum_fusion.1
  122.9 0.8 pad_maximum_fusion.2
  123.7 0.8 pad_maximum_fusion
  124.5 0.8 pad_maximum_fusion.3
  (39 shorter events, 0.3 us)
Async XLA Ops:
  0.6 26.0 %collective-permute-start.1 = (bf16[1152,512]{1,0:T(8,128)(2,1)}, bf16[1152,512]{1,0:T(8,128)(2,1)S(1)}, u32[]{:S(2)}, u32[]{:S(2)}) collective-permute-start(bf16[1152,512]{1,0:T(8,128)(2,1)} %edge_own.1), channel_id=1, source_target_pairs={{0,1},{1,0},{2,3},{3,2},{4,5},{5,4},{6,7},{7,6},{8,9},{9,8},{10,11... | collective-permute-start | bytes 3538952 | tf_op jit(solution)/shard_map/ppermute | solution.py:170
  1.8 28.6 %copy-start.3 = (bf16[2,160,512]{2,1,0:T(8,128)(2,1)}, bf16[2,160,512]{2,1,0:T(8,128)(2,1)S(1)}, u32[]{:S(2)}) copy-start(bf16[2,160,512]{2,1,0:T(8,128)(2,1)S(1)} %pad_maximum_fusion.4.m1) | copy-start | bytes 983044
  1.8 24.8 %collective-permute-start.5 = (bf16[2,160,512]{2,1,0:T(8,128)(2,1)S(1)}, bf16[2,160,512]{2,1,0:T(8,128)(2,1)S(1)}, u32[]{:S(2)}, u32[]{:S(2)}) collective-permute-start(bf16[2,160,512]{2,1,0:T(8,128)(2,1)S(1)} %pad_maximum_fusion.4.m1), channel_id=1, source_target_pairs={{0,1},{1,0},{2,3},{3,2},{4,5},{5,4},{6,7},{7,6},{8,9},{9,8},{10,11... | collective-permute-start | bytes 983048 | tf_op jit(solution)/shard_map/ppermute | solution.py:170
  2.4 13.8 %collective-permute-start.3 = (bf16[2,160,512]{2,1,0:T(8,128)(2,1)S(1)}, bf16[2,160,512]{2,1,0:T(8,128)(2,1)S(1)}, u32[]{:S(2)}, u32[]{:S(2)}) collective-permute-start(bf16[2,160,512]{2,1,0:T(8,128)(2,1)S(1)} %pad_maximum_fusion.4.m1), channel_id=1, source_target_pairs={{2,0},{4,2},{6,4},{8,6},{10,8},{12,10},{14,12},{16,14},{18,16},{20... | collective-permute-start | bytes 983048 | tf_op jit(solution)/shard_map/ppermute | solution.py:175
  9.0 15.5 %collective-permute-start.2 = (bf16[2,160,512]{2,1,0:T(8,128)(2,1)S(1)}, bf16[2,160,512]{2,1,0:T(8,128)(2,1)S(1)}, u32[]{:S(2)}, u32[]{:S(2)}) collective-permute-start(bf16[2,160,512]{2,1,0:T(8,128)(2,1)S(1)} %pad_maximum_fusion.4.m1), channel_id=1, source_target_pairs={{0,2},{2,4},{4,6},{6,8},{8,10},{10,12},{12,14},{14,16},{16,18},{18... | collective-permute-start | bytes 983048 | tf_op jit(solution)/shard_map/ppermute | solution.py:175
  10.9 15.6 %collective-permute-start = (bf16[576,512]{1,0:T(8,128)(2,1)}, bf16[576,512]{1,0:T(8,128)(2,1)S(1)}, u32[]{:S(2)}, u32[]{:S(2)}) collective-permute-start(bf16[576,512]{1,0:T(8,128)(2,1)} %grid_own.1), channel_id=1, source_target_pairs={{0,1},{1,0},{2,3},{3,2},{4,5},{5,4},{6,7},{7,6},{8,9},{9,8},{10,11... | collective-permute-start | bytes 1769480 | tf_op jit(solution)/shard_map/ppermute | solution.py:170
  16.2 14.2 %copy-start.11 = (bf16[2,160,512]{2,1,0:T(8,128)(2,1)}, bf16[2,160,512]{2,1,0:T(8,128)(2,1)S(1)}, u32[]{:S(2)}) copy-start(bf16[2,160,512]{2,1,0:T(8,128)(2,1)S(1)} %collective-permute-done.3.m2) | copy-start | bytes 983044
  16.2 10.4 %collective-permute-start.6 = (bf16[2,160,512]{2,1,0:T(8,128)(2,1)S(1)}, bf16[2,160,512]{2,1,0:T(8,128)(2,1)S(1)}, u32[]{:S(2)}, u32[]{:S(2)}) collective-permute-start(bf16[2,160,512]{2,1,0:T(8,128)(2,1)S(1)} %collective-permute-done.3.m2), channel_id=1, source_target_pairs={{0,1},{1,0},{2,3},{3,2},{4,5},{5,4},{6,7},{7,6},{8,9},{9,8},{10,11... | collective-permute-start | bytes 983048 | tf_op jit(solution)/shard_map/ppermute | solution.py:170
  24.5 5.9 %copy-start.12 = (bf16[2,160,512]{2,1,0:T(8,128)(2,1)}, bf16[2,160,512]{2,1,0:T(8,128)(2,1)S(1)}, u32[]{:S(2)}) copy-start(bf16[2,160,512]{2,1,0:T(8,128)(2,1)S(1)} %collective-permute-done.2.m0) | copy-start | bytes 983044
  24.5 2.1 %collective-permute-start.4 = (bf16[2,160,512]{2,1,0:T(8,128)(2,1)S(1)}, bf16[2,160,512]{2,1,0:T(8,128)(2,1)}, u32[]{:S(2)}, u32[]{:S(2)}) collective-permute-start(bf16[2,160,512]{2,1,0:T(8,128)(2,1)S(1)} %collective-permute-done.2.m0), channel_id=1, source_target_pairs={{0,1},{1,0},{2,3},{3,2},{4,5},{5,4},{6,7},{7,6},{8,9},{9,8},{10,11... | collective-permute-start | bytes 983048 | tf_op jit(solution)/shard_map/ppermute | solution.py:170
  26.6 3.8 %copy-start.10 = (bf16[2,160,512]{2,1,0:T(8,128)(2,1)}, bf16[2,160,512]{2,1,0:T(8,128)(2,1)S(1)}, u32[]{:S(2)}) copy-start(bf16[2,160,512]{2,1,0:T(8,128)(2,1)S(1)} %collective-permute-done.5.m4) | copy-start | bytes 983044
  26.6 3.8 %copy-start.8 = (bf16[576,512]{1,0:T(8,128)(2,1)}, bf16[576,512]{1,0:T(8,128)(2,1)S(1)}, u32[]{:S(2)}) copy-start(bf16[576,512]{1,0:T(8,128)(2,1)S(1)} %collective-permute-done.grid_far) | copy-start | bytes 1769476
  26.6 3.8 %copy-start.13 = (bf16[2,160,512]{2,1,0:T(8,128)(2,1)}, bf16[2,160,512]{2,1,0:T(8,128)(2,1)S(1)}, u32[]{:S(2)}) copy-start(bf16[2,160,512]{2,1,0:T(8,128)(2,1)S(1)} %collective-permute-done.6.m5) | copy-start | bytes 983044
  26.6 3.8 %copy-start.4 = (bf16[1152,512]{1,0:T(8,128)(2,1)}, bf16[1152,512]{1,0:T(8,128)(2,1)S(1)}, u32[]{:S(2)}) copy-start(bf16[1152,512]{1,0:T(8,128)(2,1)S(1)} %collective-permute-done.1.edge_far) | copy-start | bytes 3538948
  55.3 3.9 %copy-start.15 = (bf16[320,256]{1,0:T(8,128)(2,1)S(1)}, bf16[320,256]{1,0:T(8,128)(2,1)}, u32[]{:S(2)}) copy-start(bf16[320,256]{1,0:T(8,128)(2,1)} %get-tuple-element.19) | copy-start | bytes 491524
  55.3 8.4 %copy-start.14 = (bf16[320,256]{1,0:T(8,128)(2,1)S(1)}, bf16[320,256]{1,0:T(8,128)(2,1)}, u32[]{:S(2)}) copy-start(bf16[320,256]{1,0:T(8,128)(2,1)} %get-tuple-element.20) | copy-start | bytes 491524
  55.4 10.6 %copy-start.1 = (bf16[512,256]{1,0:T(8,128)(2,1)S(1)}, bf16[512,256]{1,0:T(8,128)(2,1)}, u32[]{:S(2)}) copy-start(bf16[512,256]{1,0:T(8,128)(2,1)} %w_grid.1) | copy-start | bytes 786436
  55.4 10.6 %copy-start.5 = (bf16[1152,256]{1,0:T(8,128)(2,1)S(1)}, bf16[1152,256]{1,0:T(8,128)(2,1)}, u32[]{:S(2)}) copy-start(bf16[1152,256]{1,0:T(8,128)(2,1)} %get-tuple-element.15) | copy-start | bytes 1769476
  55.4 24.7 %all-to-all-start = ((bf16[16,272,128]{2,1,0:T(8,128)(2,1)}), bf16[16,272,128]{2,1,0:T(8,128)(2,1)S(1)}, u32[]{:S(2)}, u32[]{:S(2)}) async-start(bf16[16,272,128]{2,1,0:T(8,128)(2,1)} %get-tuple-element.21), calls=%async_computation | async-start | bytes 2228224 | tf_op jit(solution)/shard_map/all_to_all | solution.py:179
  59.2 21.1 %copy-start.2 = (bf16[512,256]{1,0:T(8,128)(2,1)S(1)}, bf16[512,256]{1,0:T(8,128)(2,1)}, u32[]{:S(2)}) copy-start(bf16[512,256]{1,0:T(8,128)(2,1)} %w_edge.1) | copy-start | bytes 786436
  59.2 21.1 %copy-start.7 = (bf16[1152,256]{1,0:T(8,128)(2,1)S(1)}, bf16[1152,256]{1,0:T(8,128)(2,1)}, u32[]{:S(2)}) copy-start(bf16[1152,256]{1,0:T(8,128)(2,1)} %get-tuple-element.17) | copy-start | bytes 1769476
  59.3 28.7 %collective-permute-start.9 = (bf16[320,256]{1,0:T(8,128)(2,1)S(1)}, bf16[320,256]{1,0:T(8,128)(2,1)S(1)}, u32[]{:S(2)}, u32[]{:S(2)}) collective-permute-start(bf16[320,256]{1,0:T(8,128)(2,1)S(1)} %copy-done.15), channel_id=1, source_target_pairs={{2,0},{4,2},{6,4},{8,6},{10,8},{12,10},{14,12},{16,14},{18,16},{20... | collective-permute-start | bytes 491528 | tf_op jit(solution)/shard_map/ppermute | solution.py:175
  63.8 24.2 %collective-permute-start.10 = (bf16[320,256]{1,0:T(8,128)(2,1)S(1)}, bf16[320,256]{1,0:T(8,128)(2,1)S(1)}, u32[]{:S(2)}, u32[]{:S(2)}) collective-permute-start(bf16[320,256]{1,0:T(8,128)(2,1)S(1)} %copy-done.14), channel_id=1, source_target_pairs={{0,2},{2,4},{4,6},{6,8},{8,10},{10,12},{12,14},{14,16},{16,18},{18... | collective-permute-start | bytes 491528 | tf_op jit(solution)/shard_map/ppermute | solution.py:175
  67.1 40.3 %collective-permute-start.7 = (bf16[576,512]{1,0:T(8,128)(2,1)}, bf16[576,512]{1,0:T(8,128)(2,1)}, u32[]{:S(2)}, u32[]{:S(2)}) collective-permute-start(bf16[576,512]{1,0:T(8,128)(2,1)} %convolution_convert_fusion.1), channel_id=1, source_target_pairs={{0,1},{1,0},{2,3},{3,2},{4,5},{5,4},{6,7},{7,6},{8,9},{9,8},{10,11... | collective-permute-start | bytes 1769480 | tf_op jit(solution)/shard_map/ppermute | solution.py:170
  80.2 7.8 %copy-start.9 = (f32[320,256]{1,0:T(8,128)S(1)}, f32[320,256]{1,0:T(8,128)}, u32[]{:S(2)}) copy-start(f32[320,256]{1,0:T(8,128)} %get-tuple-element.18) | copy-start | bytes 983044
  80.2 4.4 %collective-permute-start.12 = (bf16[272,128]{1,0:T(8,128)(2,1)S(1)}, bf16[272,128]{1,0:T(8,128)(2,1)S(1)}, u32[]{:S(2)}, u32[]{:S(2)}) collective-permute-start(bf16[272,128]{1,0:T(8,128)(2,1)S(1)} %reduce_sum.12), channel_id=1, source_target_pairs={{0,32},{32,0},{64,96},{96,64},{128,160},{160,128},{192,224},{224,1... | collective-permute-start | bytes 208904 | tf_op jit(solution)/shard_map/ppermute | solution.py:185
  80.4 17.8 %copy-start = (bf16[512,256]{1,0:T(8,128)(2,1)S(1)}, bf16[512,256]{1,0:T(8,128)(2,1)}, u32[]{:S(2)}) copy-start(bf16[512,256]{1,0:T(8,128)(2,1)} %w_mesh.1) | copy-start | bytes 786436
  81.9 27.9 %collective-permute-start.8 = (bf16[1152,512]{1,0:T(8,128)(2,1)}, bf16[1152,512]{1,0:T(8,128)(2,1)S(1)}, u32[]{:S(2)}, u32[]{:S(2)}) collective-permute-start(bf16[1152,512]{1,0:T(8,128)(2,1)} %convolution_convert_fusion), channel_id=1, source_target_pairs={{0,1},{1,0},{2,3},{3,2},{4,5},{5,4},{6,7},{7,6},{8,9},{9,8},{10,11... | collective-permute-start | bytes 3538952 | tf_op jit(solution)/shard_map/ppermute | solution.py:170
  84.7 5.6 %collective-permute-start.13 = (bf16[272,128]{1,0:T(8,128)(2,1)S(1)}, bf16[272,128]{1,0:T(8,128)(2,1)S(1)}, u32[]{:S(2)}, u32[]{:S(2)}) collective-permute-start(bf16[272,128]{1,0:T(8,128)(2,1)S(1)} %add_convert_fusion.2), channel_id=1, source_target_pairs={{0,64},{32,96},{64,0},{96,32},{128,192},{160,224},{192,128},{224,1... | collective-permute-start | bytes 208904 | tf_op jit(solution)/shard_map/ppermute | solution.py:185
  90.3 10.1 %collective-permute-start.14 = (bf16[272,128]{1,0:T(8,128)(2,1)S(1)}, bf16[272,128]{1,0:T(8,128)(2,1)S(1)}, u32[]{:S(2)}, u32[]{:S(2)}) collective-permute-start(bf16[272,128]{1,0:T(8,128)(2,1)S(1)} %add_convert_fusion.1), channel_id=1, source_target_pairs={{0,128},{32,160},{64,192},{96,224},{128,0},{160,32},{192,64},{224,... | collective-permute-start | bytes 208904 | tf_op jit(solution)/shard_map/ppermute | solution.py:185
  98.4 7.2 %collective-permute-start.11 = (bf16[160,512]{1,0:T(8,128)(2,1)S(1)}, bf16[160,512]{1,0:T(8,128)(2,1)}, u32[]{:S(2)}, u32[]{:S(2)}) collective-permute-start(bf16[160,512]{1,0:T(8,128)(2,1)S(1)} %convolution_convert_fusion.2), channel_id=1, source_target_pairs={{0,1},{1,0},{2,3},{3,2},{4,5},{5,4},{6,7},{7,6},{8,9},{9,8},{10,11... | collective-permute-start | bytes 491528 | tf_op jit(solution)/shard_map/ppermute | solution.py:170
  101.6 20.1 %all-to-all-start.1 = ((bf16[16,256,128]{2,1,0:T(8,128)(2,1)}), bf16[16,256,128]{2,1,0:T(8,128)(2,1)S(1)}, u32[]{:S(2)}, u32[]{:S(2)}) async-start(bf16[16,256,128]{2,1,0:T(8,128)(2,1)} %broadcast_in_dim.10), calls=%async_computation.1 | async-start | bytes 2097152 | tf_op jit(solution)/shard_map/all_to_all | solution.py:191
  105.5 4.2 %copy-start.6 = (bf16[1152,256]{1,0:T(8,128)(2,1)S(1)}, bf16[1152,256]{1,0:T(8,128)(2,1)}, u32[]{:S(2)}) copy-start(bf16[1152,256]{1,0:T(8,128)(2,1)} %get-tuple-element.16) | copy-start | bytes 1769476

commit v2 on v1

v2 whole, which is shorter than its diff:
```python
import functools

import jax
import jax.numpy as jnp
import numpy as np
from jax import lax
from jax.experimental import pallas as pl
from jax.experimental.pallas import tpu as pltpu
from jax.sharding import Mesh, PartitionSpec as P

BF = jnp.bfloat16
F32 = jnp.float32
BAND = ("z", "y", "x")
PLANE = ("y", "x")
LANES = 128
EDGE_BLOCK = 384
TAIL = 16
SENDER_FLOPS = 4 * 10**9
EDGE_FLOPS = 9 * 10**9


def dot(a, b):
    return jnp.dot(a, b, preferred_element_type=F32)


def dot_t(a, b):
    return lax.dot_general(a, b, (((1,), (1,)), ((), ())), preferred_element_type=F32)


def dot_rows(a, b):
    return lax.dot_general(a, b, (((0,), (0,)), ((), ())), preferred_element_type=F32)


def one_hot(column, offset):
    place = lax.broadcasted_iota(jnp.int32, column.shape, column.ndim - 1)
    return jnp.where(column == place + offset, 1.0, 0.0).astype(BF)


def one_hot_rows(row, offset):
    place = lax.broadcasted_iota(jnp.int32, row.shape, 0)
    return jnp.where(row == place + offset, 1.0, 0.0).astype(BF)


def local_senders(row, where, half_grid):
    at = row - where[0] * (2 * half_grid) - where[1] * half_grid
    return jnp.where(at < 0, at + 2 * half_grid, at)


def local_receivers(row, slot, where, piece):
    at = row - (where[0] - 1) * (2 * piece)
    owner = jnp.where(at >= 2 * piece, 1, 0) + jnp.where(at >= 4 * piece, 1, 0)
    within = at - owner * (2 * piece)
    half = jnp.where(within >= piece, 1, 0)
    flip = jnp.where(half == where[1], 0, 1)
    near = (flip * 3 + owner) * piece + within - half * piece
    return jnp.where(slot < where[2], near, -1)


def sender_kernel(
    where, grid_own, grid_far, edge_own, edge_far, w_grid, w_edge, bias, senders, pre_own, pre_far, table, left
):
    half_edges = edge_own.shape[0]
    half_grid = grid_own.shape[0]
    n_grid = 2 * half_grid
    block = left.shape[0]
    table[0:half_grid] = dot(grid_own[...], w_grid[...]).astype(BF)
    table[half_grid:n_grid] = dot(grid_far[...], w_grid[...]).astype(BF)
    table[n_grid:] = w_edge[...]
    parts = half_edges // LANES

    def run(edges, pre, base):
        def step(i, carry):
            rows = pl.ds(pl.multiple_of(i * block, block), block)
            for c in range(block // LANES):
                at = base + i * (block // LANES) + c
                row = local_senders(senders[pl.ds(at, 1), :], where, half_grid)
                column = jnp.broadcast_to(row, (LANES, LANES)).T
                for k in range(n_grid // LANES):
                    left[c * LANES : (c + 1) * LANES, k * LANES : (k + 1) * LANES] = one_hot(column, k * LANES)
            left[:, n_grid:] = edges[rows, :]
            pre[rows, :] = dot(left[...], table[...]) + bias[...]
            return carry

        lax.fori_loop(0, half_edges // block, step, 0)

    run(edge_own, pre_own, where[1] * parts)
    run(edge_far, pre_far, (1 - where[1]) * parts)


def edge_kernel(
    where,
    grid_own,
    grid_far,
    edge_own,
    edge_far,
    m0,
    m1,
    m2,
    m3,
    m4,
    m5,
    w_mesh,
    w_out,
    pre_own,
    pre_far,
    senders,
    receivers,
    wire,
    cot_own,
    cot_far,
    seg_grid,
    rim_low,
    rim_mid,
    rim_high,
    lat,
    cot,
    table,
    left,
    right,
    sums,
    act_sums,
    edge_sum,
    bias_sum,
):
    half_edges = edge_own.shape[0]
    half_grid = grid_own.shape[0]
    n_grid = 2 * half_grid
    piece = m0.shape[1]
    n_mesh = 6 * piece
    pad_mesh = lat.shape[0]
    n_rows = n_grid + pad_mesh
    block = left.shape[0]
    hidden = w_mesh.shape[1]
    for k, m in enumerate((m0, m1, m2, m3, m4, m5)):
        lat[k * piece : (k + 1) * piece] = m[0]
        cot[k * piece : (k + 1) * piece] = m[1]
    if pad_mesh > n_mesh:
        lat[n_mesh:] = jnp.zeros((pad_mesh - n_mesh, lat.shape[1]), BF)
        cot[n_mesh:] = jnp.zeros((pad_mesh - n_mesh, cot.shape[1]), BF)
    table[:, 0:hidden] = dot(lat[...], w_mesh[...]).astype(BF)
    cots = dot_t(cot[...], w_out[...])
    high = cots.astype(BF)
    table[:, hidden : 2 * hidden] = high
    table[:, 2 * hidden :] = (cots - high.astype(F32)).astype(BF)
    sums[...] = jnp.zeros_like(sums)
    act_sums[...] = jnp.zeros_like(act_sums)
    edge_sum[...] = jnp.zeros_like(edge_sum)
    bias_sum[...] = jnp.zeros_like(bias_sum)
    parts = half_edges // LANES

    def run(edges, pre_part, cot_out, base):
        def step(i, carry):
            rows = pl.ds(pl.multiple_of(i * block, block), block)
            for c in range(block // LANES):
                at = base + i * (block // LANES) + c
                mine = slice(c * LANES, (c + 1) * LANES)
                slot = at * LANES + lax.broadcasted_iota(jnp.int32, (1, LANES), 1)
                row = local_receivers(receivers[pl.ds(at, 1), :], slot, where, piece)
                row = jnp.broadcast_to(row, (LANES, LANES))
                column = row.T
                for k in range(pad_mesh // LANES):
                    left[mine, k * LANES : (k + 1) * LANES] = one_hot(column, k * LANES)
                    at_row = n_grid + k * LANES
                    right[at_row : at_row + LANES, mine] = one_hot_rows(row, k * LANES)
                row = local_senders(senders[pl.ds(at, 1), :], where, half_grid)
                row = jnp.broadcast_to(row, (LANES, LANES))
                for k in range(n_grid // LANES):
                    right[k * LANES : (k + 1) * LANES, mine] = one_hot_rows(row, k * LANES)
            got = dot(left[...], table[...])
            pre = pre_part[rows, :] + got[:, 0:hidden]
            hidden_cot = got[:, hidden : 2 * hidden] + got[:, 2 * hidden :]
            sig = jax.nn.sigmoid(pre)
            act = (pre * sig).astype(BF)
            pre_cot = (hidden_cot * sig * (1.0 + pre * (1.0 - sig))).astype(BF)
            cot_out[rows, :] = pre_cot
            sums[...] += dot(right[...], pre_cot)
            act_sums[...] += dot(right[n_grid:, :], act)
            edge_sum[...] += dot_rows(edges[rows, :], pre_cot)
            bias_sum[...] += jnp.sum(pre_cot.astype(F32), axis=0, keepdims=True)
            return carry

        lax.fori_loop(0, half_edges // block, step, 0)

    run(edge_own, pre_own, cot_own, where[1] * parts)
    run(edge_far, pre_far, cot_far, (1 - where[1]) * parts)

    seg_grid[...] = sums[:n_grid].astype(BF)
    seg_mesh = sums[n_grid:].astype(BF)
    grads = (
        dot_rows(grid_own[...], seg_grid[:half_grid]) + dot_rows(grid_far[...], seg_grid[half_grid:]),
        dot_rows(lat[...], seg_mesh),
        edge_sum[...],
    )
    rows = 128
    at = 0

    def put(at, value):
        wire[at, 0:rows, :] = value[:, :LANES].astype(BF)
        wire[at, rows : 2 * rows, :] = value[:, LANES:].astype(BF)

    for g in grads:
        for k in range(g.shape[0] // rows):
            put(at, g[k * rows : (k + 1) * rows])
            at += 1
    g = dot_rows(act_sums[...].astype(BF), cot[...])
    for c in range(2):
        for k in range(g.shape[0] // rows):
            put(at, g[k * rows : (k + 1) * rows, c * hidden : (c + 1) * hidden])
            at += 1
    sub = lax.broadcasted_iota(jnp.int32, (TAIL, LANES), 0)
    low = jnp.broadcast_to(bias_sum[:, :LANES], (TAIL, LANES))
    high = jnp.broadcast_to(bias_sum[:, LANES:], (TAIL, LANES))
    tail = jnp.where(sub == 0, low, jnp.where(sub == 1, high, 0.0)).astype(BF)
    for k in range(wire.shape[0]):
        wire[k, 2 * rows :, :] = tail
    for ref, o, kind in ((rim_low, 0, BF), (rim_mid, 1, F32), (rim_high, 2, BF)):
        for h in range(2):
            start = n_grid + (3 * h + o) * piece
            ref[h * piece : (h + 1) * piece] = sums[start : start + piece].astype(kind)


def last_sum_kernel(mine, other, spread, bias):
    total = mine[...].astype(F32) + other[...].astype(F32)
    rows = spread.shape[1]
    low, high = (total[:rows].astype(BF), total[rows : 2 * rows].astype(BF))
    for k in range(spread.shape[0]):
        spread[k, :, :LANES] = low
        spread[k, :, LANES:] = high
    bias[:, :LANES] = total[2 * rows : 2 * rows + 1]
    bias[:, LANES:] = total[2 * rows + 1 : 2 * rows + 2]


def swap(x):
    return lax.ppermute(x, "chan", [(0, 1), (1, 0)])


def shifted(x, by):
    n = lax.axis_size(BAND)
    return lax.ppermute(x, BAND, [(i, i + by) for i in range(n) if 0 <= i + by < n])


def depth_total(mine):
    depth = lax.axis_size("z")
    step = 1
    while True:
        other = lax.ppermute(mine, "z", [(i, i ^ step) for i in range(depth)])
        step *= 2
        if step == depth:
            return mine, other
        mine = (mine.astype(F32) + other.astype(F32)).astype(BF)


def body(
    grid_latent,
    edge_latent,
    mesh_latent,
    mesh_cotangent,
    w_grid,
    w_mesh,
    w_edge,
    bias,
    w_out,
    senders,
    receivers,
    edge_count,
):
    band = lax.axis_index(BAND)
    chan = lax.axis_index("chan")
    half_grid = grid_latent.shape[0]
    half_edges = edge_latent.shape[0]
    piece, width = mesh_latent.shape
    hidden = w_grid.shape[1]
    n_grid = 2 * half_grid
    pad_mesh = -(-6 * piece // LANES) * LANES

    mesh_own = jnp.stack([mesh_latent, mesh_cotangent])
    mesh_below = shifted(mesh_own, 1)
    mesh_above = shifted(mesh_own, -1)
    edge_far = swap(edge_latent)
    grid_far = swap(grid_latent)
    mesh_own_far = swap(mesh_own)

    where = jnp.stack([band, chan, edge_count[0]])
    senders = senders.reshape(-1, LANES)
    receivers = receivers.reshape(-1, LANES)
    shape = jax.ShapeDtypeStruct
    vmem = pl.BlockSpec(memory_space=pltpu.VMEM)
    smem = pl.BlockSpec(memory_space=pltpu.SMEM)
    params = pltpu.CompilerParams(vmem_limit_bytes=56 * 1024 * 1024)
    pre_own, pre_far = pl.pallas_call(
        sender_kernel,
        out_shape=(shape((half_edges, hidden), F32),) * 2,
        in_specs=[smem] + [vmem] * 8,
        out_specs=(vmem,) * 2,
        scratch_shapes=[
            pltpu.VMEM((n_grid + width, hidden), BF),
            pltpu.VMEM((EDGE_BLOCK, n_grid + width), BF),
        ],
        compiler_params=params,
        cost_estimate=pl.CostEstimate(flops=SENDER_FLOPS, transcendentals=0, bytes_accessed=1 << 22),
        name="sender_step",
    )(where, grid_latent, grid_far, edge_latent, edge_far, w_grid, w_edge, bias.reshape(1, hidden), senders)

    mesh_below, mesh_above, pre_own, pre_far = lax.optimization_barrier((mesh_below, mesh_above, pre_own, pre_far))
    mesh_near = (mesh_below, mesh_own, mesh_above)
    mesh_far = (swap(mesh_below), mesh_own_far, swap(mesh_above))
    wire, cot_own, cot_far, seg_grid, rim_low, rim_mid, rim_high = pl.pallas_call(
        edge_kernel,
        out_shape=(
            shape((16, 256 + TAIL, LANES), BF),
            shape((half_edges, hidden), BF),
            shape((half_edges, hidden), BF),
            shape((n_grid, hidden), BF),
            shape((2 * piece, hidden), BF),
            shape((2 * piece, hidden), F32),
            shape((2 * piece, hidden), BF),
        ),
        in_specs=[smem] + [vmem] * 16,
        out_specs=(vmem,) * 7,
        scratch_shapes=[
            pltpu.VMEM((pad_mesh, width), BF),
            pltpu.VMEM((pad_mesh, width), BF),
            pltpu.VMEM((pad_mesh, 3 * hidden), BF),
            pltpu.VMEM((EDGE_BLOCK, pad_mesh), BF),
            pltpu.VMEM((n_grid + pad_mesh, EDGE_BLOCK), BF),
            pltpu.VMEM((n_grid + pad_mesh, hidden), F32),
            pltpu.VMEM((pad_mesh, hidden), F32),
            pltpu.VMEM((width, hidden), F32),
            pltpu.VMEM((1, hidden), F32),
        ],
        compiler_params=params,
        cost_estimate=pl.CostEstimate(flops=EDGE_FLOPS, transcendentals=1 << 20, bytes_accessed=1 << 23),
        name="edge_step",
    )(
        where,
        grid_latent,
        grid_far,
        edge_latent,
        edge_far,
        *mesh_near,
        *mesh_far,
        w_mesh,
        w_out,
        pre_own,
        pre_far,
        senders,
        receivers,
    )

    arrived = lax.all_to_all(wire, PLANE, 0, 0, tiled=True)
    edge_term = dot_t(cot_far, w_edge).astype(BF)
    grid_term = dot_t(seg_grid[half_grid:], w_grid).astype(BF)
    edge_back = swap(edge_term)
    grid_back = swap(grid_term)
    total = arrived.astype(F32).sum(axis=0).astype(BF)
    total, rim_low, rim_high, _, _ = lax.optimization_barrier((total, rim_low, rim_high, edge_term, grid_term))
    from_above = shifted(rim_low, -1)
    from_below = shifted(rim_high, 1)
    mine, other = depth_total(total)
    spread, grad_bias = pl.pallas_call(
        last_sum_kernel,
        out_shape=(shape((16, 128, hidden), BF), shape((1, hidden), F32)),
        in_specs=[vmem] * 2,
        out_specs=(vmem,) * 2,
        name="last_sum",
    )(mine, other)
    everyone = lax.all_to_all(spread, PLANE, 0, 0, tiled=True)

    rim_mid, from_above, from_below, _ = lax.optimization_barrier((rim_mid, from_above, from_below, grad_bias))
    grad_edge = (dot_t(cot_own, w_edge) + edge_back.astype(F32)).astype(BF)
    grad_grid = (dot_t(seg_grid[:half_grid], w_grid) + grid_back.astype(F32)).astype(BF)
    seg_mesh = (rim_mid + from_above.astype(F32) + from_below.astype(F32)).astype(BF)
    mesh_back = swap(dot_t(seg_mesh[piece:], w_mesh).astype(BF))
    grad_mesh = (dot_t(seg_mesh[:piece], w_mesh) + mesh_back.astype(F32)).astype(BF)

    def rows_of(start, stop):
        return everyone[start:stop].astype(F32).reshape(-1, hidden)

    return (
        grad_grid,
        grad_edge,
        grad_mesh,
        rows_of(0, 4),
        rows_of(4, 8),
        rows_of(8, 12),
        grad_bias.reshape(hidden),
        jnp.concatenate([rows_of(12, 14), rows_of(14, 16)], axis=1),
    )


def solution(mesh):
    bands, chans = (mesh.shape["band"], mesh.shape["chan"])
    side = 4
    inner = Mesh(np.asarray(mesh.devices).reshape(bands // side**2, side, side, chans), (*BAND, "chan"))
    every = P((*BAND, "chan"), None)
    return jax.shard_map(
        body,
        mesh=inner,
        in_specs=(
            every,
            every,
            every,
            every,
            P(None, "chan"),
            P(None, "chan"),
            P(None, "chan"),
            P("chan"),
            P("chan", None),
            P(BAND),
            P(BAND),
            P(BAND),
        ),
        out_specs=(
            every,
            every,
            every,
            P(None, "chan"),
            P(None, "chan"),
            P(None, "chan"),
            P("chan"),
            P("chan", None),
        ),
        check_vma=False,
    )
```

time: 127 us -> 123 us (0.969)
  Pallas kernels: 24.9 us -> 31.1 us
  waiting for transfers between devices: 41.1 us -> 37.9 us
  local copies, waits for them, and re-layouts: 6.47 us -> 3.35 us
  matrix products: 8.63 us -> 6.44 us
  other arithmetic: 7.49 us -> 5.89 us
    pallas_call x0 -> x2, Pallas kernels: none -> 9.74 us  [the longest x1 7.64 us: body(): pl.pallas_call(sender_kernel, out_shape=(shape((half_edges, hidden), F32)...]
    ppermute x4, waiting for transfers between devices: 11.3 us -> 3.74 us  [shifted(): lax.ppermute(x, BAND, [(i, i + by) for i in range(n) if 0 <= i + by < n])]
    broadcast_in_dim x3 -> x0, local copies, waits for them, and re-layouts: 4.94 us -> none  [the longest x2 3.75 us: body(): jnp.broadcast_to(v[:, None], (n_edges, LANES))]
    pallas_call x1, Pallas kernels: 24.9 us -> 21.3 us  [body(): pl.pallas_call(edge_kernel, out_shape=(shape((16, 256 + TAIL, LANES), BF)...]
    unnamed x32 -> x36, local copies, waits for them, and re-layouts: 0.08 us -> 3.28 us
    concatenate x5 -> x1, other arithmetic: 3.88 us -> 0.85 us  [body(): jnp.concatenate([rows_of(12, 14), rows_of(14, 16)], axis=1)]
    all_to_all x2, starting transfers between devices: 7.72 us -> 10.7 us  [the longest x1 6.14 us: body(): everyone = lax.all_to_all(spread, PLANE, 0, 0, tiled=True)]
    ppermute x3, starting transfers between devices: 11.3 us -> 8.93 us  [depth_total(): other = lax.ppermute(mine, 'z', [(i, i ^ step) for i in range(depth)])]
  transfers between devices with their start and end apart: 17 -> 17, of which waited for: 7 -> 7; matrix products, arithmetic and copies ran while one was open for 12% -> 8% of each run, Pallas kernels for 0% -> 8%
where the time goes in v2:
time: 123 us; the launch traced here: 122 us
  waiting for transfers between devices  37.9 us (31%)
  starting transfers between devices  36 us (29%)
  Pallas kernels  31.1 us (25%)
  matrix products  6.44 us (5%)
  other arithmetic  5.89 us (5%)
  local copies, waits for them, and re-layouts  3.35 us (3%)
  between operations  1.58 us (1%)
    pallas_call x1, Pallas kernels, body(): pl.pallas_call(edge_kernel, out_shape=(shape((16, 256 + TAIL, LANES), BF)...  21.3 us
    all_to_all x1, waiting for transfers between devices, body(): arrived = lax.all_to_all(wire, PLANE, 0, 0, tiled=True)  17 us
    ppermute x4, starting transfers between devices, shifted(): lax.ppermute(x, BAND, [(i, i + by) for i in range(n) if 0 <= i + by < n])  14.4 us
    ppermute x3, starting transfers between devices, depth_total(): other = lax.ppermute(mine, 'z', [(i, i ^ step) for i in range(depth)])  8.93 us
    all_to_all x1, waiting for transfers between devices, body(): everyone = lax.all_to_all(spread, PLANE, 0, 0, tiled=True)  8.24 us
    pallas_call x1, Pallas kernels, body(): pl.pallas_call(sender_kernel, out_shape=(shape((half_edges, hidden), F32)...  7.64 us
    ppermute x3, waiting for transfers between devices, depth_total(): other = lax.ppermute(mine, 'z', [(i, i ^ step) for i in range(depth)])  7.34 us
    dot_general x6, matrix products, dot_t(): lax.dot_general(a, b, (((1,), (1,)), ((), ())), preferred_element_type=F32)  6.44 us
  transfers between devices with their start and end apart: 17, of which 7 were waited for; matrix products, arithmetic and copies ran while one was open for 8% of the time, Pallas kernels for 8%

profile of v2, /device:TPU:32, one launch (start us, length us, event | category | flops | bytes accessed | tf_op | source)
XLA Modules:
  0.0 122.1 jit_solution(2222725139724879752)
XLA Ops:
  0.6 0.1 collective-permute-start.1
  0.7 0.5 collective-permute-start
  1.2 1.0 pad_maximum_fusion.m1
  2.3 0.0 copy-start.7
  2.3 0.2 collective-permute-start.5
  2.5 6.7 %collective-permute-start.3 = (bf16[2,160,512]{2,1,0:T(8,128)(2,1)S(1)}, bf16[2,160,512]{2,1,0:T(8,128)(2,1)S(1)}, u32[]{:S(2)}, u32[]{:S(2)}) collective-permute-start(bf16[2,160,512]{2,1,0:T(8,128)(2,1)S(1)} %pad_maximum_fusion.m1), channel_id=1, source_target_pairs={{2,0},{4,2},{6,4},{8,6},{10,8},{12,10},{14,12},{16,14},{18,16},{20... | collective-permute-start | bytes 983048 | tf_op jit(solution)/shard_map/ppermute | solution.py:239
  9.1 1.9 %collective-permute-start.2 = (bf16[2,160,512]{2,1,0:T(8,128)(2,1)S(1)}, bf16[2,160,512]{2,1,0:T(8,128)(2,1)S(1)}, u32[]{:S(2)}, u32[]{:S(2)}) collective-permute-start(bf16[2,160,512]{2,1,0:T(8,128)(2,1)S(1)} %pad_maximum_fusion.m1), channel_id=1, source_target_pairs={{0,2},{2,4},{4,6},{6,8},{8,10},{10,12},{12,14},{14,16},{16,18},{18... | collective-permute-start | bytes 983048 | tf_op jit(solution)/shard_map/ppermute | solution.py:239
  11.7 0.7 pad_add_fusion.where
  12.4 0.0 collective-permute-done.grid_far
  12.4 0.0 collective-permute-done.1.edge_far
  12.4 0.0 copy-start.11
  12.4 0.8 copy-done.12
  13.2 0.4 copy-done.11
  13.6 7.6 %sender_step.1 = (f32[1152,256]{1,0:T(8,128)}, f32[1152,256]{1,0:T(8,128)}) custom-call(s32[3]{0:T(128)} %pad_add_fusion.where, bf16[576,512]{1,0:T(8,128)(2,1)} %grid_own.3, bf16[576,512]{1,0:T(8,128)(2,1)} %copy-done.12, bf16[1152,512]{1,0:T(8,128)(2,1)} %edge_own.3, bf16[1152,512]{1,0:T(8,128)(2,1)} %copy-done.11, bf16[512,256]{1,0:T(8,128)(2,1)} %w_grid.1, ...), custom_call_target="tpu_custom_call" | custom-call | flops 4000000000 | bytes 4194304 | tf_op jit(solution)/shard_map/sender_step/pallas_call | solution.py:290
  21.2 0.0 collective-permute-done.3.m2
  21.2 0.0 copy-start.14
  21.2 3.7 %collective-permute-done.2.m0 = bf16[2,160,512]{2,1,0:T(8,128)(2,1)S(1)} collective-permute-done((bf16[2,160,512]{2,1,0:T(8,128)(2,1)S(1)}, bf16[2,160,512]{2,1,0:T(8,128)(2,1)S(1)}, u32[]{:S(2)}, u32[]{:S(2)}) %collective-permute-start.2) | collective-permute-done | bytes 327712 | tf_op jit(solution)/shard_map/ppermute | solution.py:239
  25.0 0.0 collective-permute-start.4
  25.0 0.5 collective-permute-start.6
  25.5 0.0 collective-permute-done.5.m4
  25.5 1.1 collective-permute-done.4.m3
  26.6 0.5 collective-permute-done.6.m5
  27.1 0.2 copy-done.16
  27.3 0.5 copy-done.17
  27.8 21.3 %edge_step.1 = (bf16[16,272,128]{2,1,0:T(8,128)(2,1)}, bf16[1152,256]{1,0:T(8,128)(2,1)}, bf16[1152,256]{1,0:T(8,128)(2,1)}, bf16[1152,256]{1,0:T(8,128)(2,1)}, ...) custom-call(s32[3]{0:T(128)} %pad_add_fusion.where, bf16[576,512]{1,0:T(8,128)(2,1)} %grid_own.3, ...), custom_call_target="tpu_custom_call" | custom-call | flops 8999999488 | bytes 8388608 | tf_op jit(solution)/shard_map/edge_step/pallas_call | solution.py:307
  49.1 0.0 copy-start.1
  49.2 0.0 copy-start.2
  49.2 4.6 %all-to-all-start = ((bf16[16,272,128]{2,1,0:T(8,128)(2,1)}), bf16[16,272,128]{2,1,0:T(8,128)(2,1)S(1)}, u32[]{:S(2)}, u32[]{:S(2)}) async-start(bf16[16,272,128]{2,1,0:T(8,128)(2,1)} %get-tuple-element.39), calls=%async_computation | async-start | bytes 2228224 | tf_op jit(solution)/shard_map/all_to_all | solution.py:350
  53.8 1.2 convolution_convert_fusion.1
  55.0 0.5 convolution_convert_fusion
  55.5 17.0 %all-to-all-done = bf16[16,272,128]{2,1,0:T(8,128)(2,1)S(1)} async-done(((bf16[16,272,128]{2,1,0:T(8,128)(2,1)}), bf16[16,272,128]{2,1,0:T(8,128)(2,1)S(1)}, u32[]{:S(2)}, u32[]{:S(2)}) %all-to-all-start) | async-done | bytes 1114144 | tf_op jit(solution)/shard_map/all_to_all | solution.py:350
  72.4 0.2 reduce_sum.12
  72.6 0.2 collective-permute-start.11
  72.8 0.0 collective-permute-start.7
  72.8 0.5 collective-permute-start.8
  73.3 3.7 %collective-permute-done.11 = bf16[272,128]{1,0:T(8,128)(2,1)S(1)} collective-permute-done((bf16[272,128]{1,0:T(8,128)(2,1)S(1)}, bf16[272,128]{1,0:T(8,128)(2,1)S(1)}, u32[]{:S(2)}, u32[]{:S(2)}) %collective-permute-start.11) | collective-permute-done | bytes 69664 | tf_op jit(solution)/shard_map/ppermute | solution.py:246
  77.0 4.6 %collective-permute-start.12 = (bf16[272,128]{1,0:T(8,128)(2,1)S(1)}, bf16[272,128]{1,0:T(8,128)(2,1)S(1)}, u32[]{:S(2)}, u32[]{:S(2)}) collective-permute-start(bf16[272,128]{1,0:T(8,128)(2,1)S(1)} %add_convert_fusion.3), channel_id=1, source_target_pairs={{0,64},{32,96},{64,0},{96,32},{128,192},{160,224},{192,128},{224,1... | collective-permute-start | bytes 208904 | tf_op jit(solution)/shard_map/ppermute | solution.py:246
  81.6 2.6 %collective-permute-start.9 = (bf16[320,256]{1,0:T(8,128)(2,1)}, bf16[320,256]{1,0:T(8,128)(2,1)S(1)}, u32[]{:S(2)}, u32[]{:S(2)}) collective-permute-start(bf16[320,256]{1,0:T(8,128)(2,1)} %get-tuple-element.42), channel_id=1, source_target_pairs={{2,0},{4,2},{6,4},{8,6},{10,8},{12,10},{14,12},{16,14},{18,16},{20... | collective-permute-start | bytes 491528 | tf_op jit(solution)/shard_map/ppermute | solution.py:239
  84.2 3.3 %collective-permute-start.10 = (bf16[320,256]{1,0:T(8,128)(2,1)}, bf16[320,256]{1,0:T(8,128)(2,1)}, u32[]{:S(2)}, u32[]{:S(2)}) collective-permute-start(bf16[320,256]{1,0:T(8,128)(2,1)} %get-tuple-element.43), channel_id=1, source_target_pairs={{0,2},{2,4},{4,6},{6,8},{8,10},{10,12},{12,14},{14,16},{16,18},{18... | collective-permute-start | bytes 491528 | tf_op jit(solution)/shard_map/ppermute | solution.py:239
  87.4 0.0 collective-permute-done.12
  87.5 0.0 copy-start.8
  87.5 4.2 %collective-permute-start.13 = (bf16[272,128]{1,0:T(8,128)(2,1)S(1)}, bf16[272,128]{1,0:T(8,128)(2,1)S(1)}, u32[]{:S(2)}, u32[]{:S(2)}) collective-permute-start(bf16[272,128]{1,0:T(8,128)(2,1)S(1)} %add_convert_fusion.2.mine), channel_id=1, source_target_pairs={{0,128},{32,160},{64,192},{96,224},{128,0},{160,32},{192,64},{224,... | collective-permute-start | bytes 208904 | tf_op jit(solution)/shard_map/ppermute | solution.py:246
  91.7 0.0 collective-permute-done.7
  91.7 1.2 fusion.1
  92.8 3.6 %collective-permute-done.13.other = bf16[272,128]{1,0:T(8,128)(2,1)S(1)} collective-permute-done((bf16[272,128]{1,0:T(8,128)(2,1)S(1)}, bf16[272,128]{1,0:T(8,128)(2,1)S(1)}, u32[]{:S(2)}, u32[]{:S(2)}) %collective-permute-start.13) | collective-permute-done | bytes 69664 | tf_op jit(solution)/shard_map/ppermute | solution.py:246
  96.5 0.6 copy-done.10
  97.1 2.1 %last_sum.1 = (bf16[16,128,256]{2,1,0:T(8,128)(2,1)}, f32[1,256]{1,0:T(1,128)}) custom-call(bf16[272,128]{1,0:T(8,128)(2,1)} %copy-done.8, bf16[272,128]{1,0:T(8,128)(2,1)} %copy-done.10), custom_call_target="tpu_custom_call" | custom-call | tf_op jit(solution)/shard_map/last_sum/pallas_call | solution.py:360
  99.2 0.0 collective-permute-done.9
  99.2 0.0 collective-permute-done.10
  99.2 0.7 copy-done.9
  99.9 6.1 %all-to-all-start.1 = ((bf16[16,128,256]{2,1,0:T(8,128)(2,1)}), bf16[16,128,256]{2,1,0:T(8,128)(2,1)S(1)}, u32[]{:S(2)}, u32[]{:S(2)}) async-start(bf16[16,128,256]{2,1,0:T(8,128)(2,1)} %get-tuple-element.49), calls=%async_computation.1 | async-start | bytes 2097152 | tf_op jit(solution)/shard_map/all_to_all | solution.py:367
  106.0 0.0 copy-start.3
  106.1 1.2 add_convert_fusion.1
  107.3 1.2 convolution_convert_fusion.2
  108.5 0.1 collective-permute-start.14
  108.6 0.0 collective-permute-done.8
  108.6 0.0 copy-start
  108.6 1.5 %fusion = bf16[1152,512]{1,0:T(8,128)(2,1)} fusion(bf16[1152,256]{1,0:T(8,128)(2,1)S(1)} %copy-done.5, bf16[512,256]{1,0:T(8,128)(2,1)S(1)} %copy-done.3, bf16[1152,512]{1,0:T(8,128)(2,1)S(1)} %collective-permute-done.8), kind=kOutput, calls=%fused_computation.1 | convolution fusion | flops 303759360 | bytes 3211264 | tf_op jit(solution)/shard_map/dot_general | solution.py:27
  110.1 0.9 add_convert_fusion
  111.0 8.2 %all-to-all-done.1 = bf16[16,128,256]{2,1,0:T(8,128)(2,1)S(1)} async-done(((bf16[16,128,256]{2,1,0:T(8,128)(2,1)}), bf16[16,128,256]{2,1,0:T(8,128)(2,1)S(1)}, u32[]{:S(2)}, u32[]{:S(2)}) %all-to-all-start.1) | async-done | bytes 1048608 | tf_op jit(solution)/shard_map/all_to_all | solution.py:367
  119.3 0.1 fusion.10
  119.3 0.8 bitcast_convert_fusion.2
  120.2 0.9 maximum_convert_fusion
  121.1 1.1 bitcast_convert_fusion
  (26 shorter events, 0.1 us)
Async XLA Ops:
  0.6 11.7 %collective-permute-start.1 = (bf16[1152,512]{1,0:T(8,128)(2,1)}, bf16[1152,512]{1,0:T(8,128)(2,1)S(1)}, u32[]{:S(2)}, u32[]{:S(2)}) collective-permute-start(bf16[1152,512]{1,0:T(8,128)(2,1)} %edge_own.3), channel_id=1, source_target_pairs={{0,1},{1,0},{2,3},{3,2},{4,5},{5,4},{6,7},{7,6},{8,9},{9,8},{10,11... | collective-permute-start | bytes 3538952 | tf_op jit(solution)/shard_map/ppermute | solution.py:234
  0.7 11.6 %collective-permute-start = (bf16[576,512]{1,0:T(8,128)(2,1)}, bf16[576,512]{1,0:T(8,128)(2,1)S(1)}, u32[]{:S(2)}, u32[]{:S(2)}) collective-permute-start(bf16[576,512]{1,0:T(8,128)(2,1)} %grid_own.3), channel_id=1, source_target_pairs={{0,1},{1,0},{2,3},{3,2},{4,5},{5,4},{6,7},{7,6},{8,9},{9,8},{10,11... | collective-permute-start | bytes 1769480 | tf_op jit(solution)/shard_map/ppermute | solution.py:234
  2.3 19.0 %copy-start.7 = (bf16[2,160,512]{2,1,0:T(8,128)(2,1)}, bf16[2,160,512]{2,1,0:T(8,128)(2,1)S(1)}, u32[]{:S(2)}) copy-start(bf16[2,160,512]{2,1,0:T(8,128)(2,1)S(1)} %pad_maximum_fusion.m1) | copy-start | bytes 983044
  2.3 23.2 %collective-permute-start.5 = (bf16[2,160,512]{2,1,0:T(8,128)(2,1)S(1)}, bf16[2,160,512]{2,1,0:T(8,128)(2,1)S(1)}, u32[]{:S(2)}, u32[]{:S(2)}) collective-permute-start(bf16[2,160,512]{2,1,0:T(8,128)(2,1)S(1)} %pad_maximum_fusion.m1), channel_id=1, source_target_pairs={{0,1},{1,0},{2,3},{3,2},{4,5},{5,4},{6,7},{7,6},{8,9},{9,8},{10,11... | collective-permute-start | bytes 983048 | tf_op jit(solution)/shard_map/ppermute | solution.py:234
  2.5 18.8 %collective-permute-start.3 = (bf16[2,160,512]{2,1,0:T(8,128)(2,1)S(1)}, bf16[2,160,512]{2,1,0:T(8,128)(2,1)S(1)}, u32[]{:S(2)}, u32[]{:S(2)}) collective-permute-start(bf16[2,160,512]{2,1,0:T(8,128)(2,1)S(1)} %pad_maximum_fusion.m1), channel_id=1, source_target_pairs={{2,0},{4,2},{6,4},{8,6},{10,8},{12,10},{14,12},{16,14},{18,16},{20... | collective-permute-start | bytes 983048 | tf_op jit(solution)/shard_map/ppermute | solution.py:239
  9.1 15.9 %collective-permute-start.2 = (bf16[2,160,512]{2,1,0:T(8,128)(2,1)S(1)}, bf16[2,160,512]{2,1,0:T(8,128)(2,1)S(1)}, u32[]{:S(2)}, u32[]{:S(2)}) collective-permute-start(bf16[2,160,512]{2,1,0:T(8,128)(2,1)S(1)} %pad_maximum_fusion.m1), channel_id=1, source_target_pairs={{0,2},{2,4},{4,6},{6,8},{8,10},{10,12},{12,14},{14,16},{16,18},{18... | collective-permute-start | bytes 983048 | tf_op jit(solution)/shard_map/ppermute | solution.py:239
  12.4 0.8 copy-start.12
  12.4 1.2 copy-start.11
  21.2 5.8 %copy-start.14 = (bf16[2,160,512]{2,1,0:T(8,128)(2,1)}, bf16[2,160,512]{2,1,0:T(8,128)(2,1)S(1)}, u32[]{:S(2)}) copy-start(bf16[2,160,512]{2,1,0:T(8,128)(2,1)S(1)} %collective-permute-done.3.m2) | copy-start | bytes 983044
  25.0 2.1 %copy-start.15 = (bf16[2,160,512]{2,1,0:T(8,128)(2,1)}, bf16[2,160,512]{2,1,0:T(8,128)(2,1)S(1)}, u32[]{:S(2)}) copy-start(bf16[2,160,512]{2,1,0:T(8,128)(2,1)S(1)} %collective-permute-done.2.m0) | copy-start | bytes 983044
  25.0 1.6 %collective-permute-start.4 = (bf16[2,160,512]{2,1,0:T(8,128)(2,1)S(1)}, bf16[2,160,512]{2,1,0:T(8,128)(2,1)S(1)}, u32[]{:S(2)}, u32[]{:S(2)}) collective-permute-start(bf16[2,160,512]{2,1,0:T(8,128)(2,1)S(1)} %collective-permute-done.2.m0), channel_id=1, source_target_pairs={{0,1},{1,0},{2,3},{3,2},{4,5},{5,4},{6,7},{7,6},{8,9},{9,8},{10,11... | collective-permute-start | bytes 983048 | tf_op jit(solution)/shard_map/ppermute | solution.py:234
  25.0 2.1 %collective-permute-start.6 = (bf16[2,160,512]{2,1,0:T(8,128)(2,1)S(1)}, bf16[2,160,512]{2,1,0:T(8,128)(2,1)S(1)}, u32[]{:S(2)}, u32[]{:S(2)}) collective-permute-start(bf16[2,160,512]{2,1,0:T(8,128)(2,1)S(1)} %collective-permute-done.3.m2), channel_id=1, source_target_pairs={{0,1},{1,0},{2,3},{3,2},{4,5},{5,4},{6,7},{7,6},{8,9},{9,8},{10,11... | collective-permute-start | bytes 983048 | tf_op jit(solution)/shard_map/ppermute | solution.py:234
  25.5 1.6 %copy-start.13 = (bf16[2,160,512]{2,1,0:T(8,128)(2,1)}, bf16[2,160,512]{2,1,0:T(8,128)(2,1)S(1)}, u32[]{:S(2)}) copy-start(bf16[2,160,512]{2,1,0:T(8,128)(2,1)S(1)} %collective-permute-done.5.m4) | copy-start | bytes 983044
  26.6 0.7 copy-start.16
  27.1 0.7 copy-start.17
  49.1 4.7 %copy-start.1 = (bf16[512,256]{1,0:T(8,128)(2,1)S(1)}, bf16[512,256]{1,0:T(8,128)(2,1)}, u32[]{:S(2)}) copy-start(bf16[512,256]{1,0:T(8,128)(2,1)} %w_grid.1) | copy-start | bytes 786436
  49.2 4.6 %copy-start.4 = (bf16[1152,256]{1,0:T(8,128)(2,1)S(1)}, bf16[1152,256]{1,0:T(8,128)(2,1)}, u32[]{:S(2)}) copy-start(bf16[1152,256]{1,0:T(8,128)(2,1)} %get-tuple-element.35) | copy-start | bytes 1769476
  49.2 5.8 %copy-start.2 = (bf16[512,256]{1,0:T(8,128)(2,1)S(1)}, bf16[512,256]{1,0:T(8,128)(2,1)}, u32[]{:S(2)}) copy-start(bf16[512,256]{1,0:T(8,128)(2,1)} %w_edge.1) | copy-start | bytes 786436
  49.2 23.3 %all-to-all-start = ((bf16[16,272,128]{2,1,0:T(8,128)(2,1)}), bf16[16,272,128]{2,1,0:T(8,128)(2,1)S(1)}, u32[]{:S(2)}, u32[]{:S(2)}) async-start(bf16[16,272,128]{2,1,0:T(8,128)(2,1)} %get-tuple-element.39), calls=%async_computation | async-start | bytes 2228224 | tf_op jit(solution)/shard_map/all_to_all | solution.py:350
  53.8 1.2 copy-start.6
  72.6 4.4 %collective-permute-start.11 = (bf16[272,128]{1,0:T(8,128)(2,1)S(1)}, bf16[272,128]{1,0:T(8,128)(2,1)S(1)}, u32[]{:S(2)}, u32[]{:S(2)}) collective-permute-start(bf16[272,128]{1,0:T(8,128)(2,1)S(1)} %reduce_sum.12), channel_id=1, source_target_pairs={{0,32},{32,0},{64,96},{96,64},{128,160},{160,128},{192,224},{224,1... | collective-permute-start | bytes 208904 | tf_op jit(solution)/shard_map/ppermute | solution.py:246
  72.8 18.9 %collective-permute-start.7 = (bf16[576,512]{1,0:T(8,128)(2,1)}, bf16[576,512]{1,0:T(8,128)(2,1)S(1)}, u32[]{:S(2)}, u32[]{:S(2)}) collective-permute-start(bf16[576,512]{1,0:T(8,128)(2,1)} %convolution_convert_fusion.1), channel_id=1, source_target_pairs={{0,1},{1,0},{2,3},{3,2},{4,5},{5,4},{6,7},{7,6},{8,9},{9,8},{10,11... | collective-permute-start | bytes 1769480 | tf_op jit(solution)/shard_map/ppermute | solution.py:234
  72.8 35.8 %collective-permute-start.8 = (bf16[1152,512]{1,0:T(8,128)(2,1)S(1)}, bf16[1152,512]{1,0:T(8,128)(2,1)S(1)}, u32[]{:S(2)}, u32[]{:S(2)}) collective-permute-start(bf16[1152,512]{1,0:T(8,128)(2,1)S(1)} %convolution_convert_fusion), channel_id=1, source_target_pairs={{0,1},{1,0},{2,3},{3,2},{4,5},{5,4},{6,7},{7,6},{8,9},{9,8},{10,11... | collective-permute-start | bytes 3538952 | tf_op jit(solution)/shard_map/ppermute | solution.py:234
  77.0 10.4 %collective-permute-start.12 = (bf16[272,128]{1,0:T(8,128)(2,1)S(1)}, bf16[272,128]{1,0:T(8,128)(2,1)S(1)}, u32[]{:S(2)}, u32[]{:S(2)}) collective-permute-start(bf16[272,128]{1,0:T(8,128)(2,1)S(1)} %add_convert_fusion.3), channel_id=1, source_target_pairs={{0,64},{32,96},{64,0},{96,32},{128,192},{160,224},{192,128},{224,1... | collective-permute-start | bytes 208904 | tf_op jit(solution)/shard_map/ppermute | solution.py:246
  81.6 17.6 %collective-permute-start.9 = (bf16[320,256]{1,0:T(8,128)(2,1)}, bf16[320,256]{1,0:T(8,128)(2,1)S(1)}, u32[]{:S(2)}, u32[]{:S(2)}) collective-permute-start(bf16[320,256]{1,0:T(8,128)(2,1)} %get-tuple-element.42), channel_id=1, source_target_pairs={{2,0},{4,2},{6,4},{8,6},{10,8},{12,10},{14,12},{16,14},{18,16},{20... | collective-permute-start | bytes 491528 | tf_op jit(solution)/shard_map/ppermute | solution.py:239
  84.2 15.1 %collective-permute-start.10 = (bf16[320,256]{1,0:T(8,128)(2,1)}, bf16[320,256]{1,0:T(8,128)(2,1)}, u32[]{:S(2)}, u32[]{:S(2)}) collective-permute-start(bf16[320,256]{1,0:T(8,128)(2,1)} %get-tuple-element.43), channel_id=1, source_target_pairs={{0,2},{2,4},{4,6},{6,8},{8,10},{10,12},{12,14},{14,16},{16,18},{18... | collective-permute-start | bytes 491528 | tf_op jit(solution)/shard_map/ppermute | solution.py:239
  87.5 9.0 %copy-start.8 = (bf16[272,128]{1,0:T(8,128)(2,1)}, bf16[272,128]{1,0:T(8,128)(2,1)S(1)}, u32[]{:S(2)}) copy-start(bf16[272,128]{1,0:T(8,128)(2,1)S(1)} %add_convert_fusion.2.mine) | copy-start | bytes 208900
  87.5 9.0 %collective-permute-start.13 = (bf16[272,128]{1,0:T(8,128)(2,1)S(1)}, bf16[272,128]{1,0:T(8,128)(2,1)S(1)}, u32[]{:S(2)}, u32[]{:S(2)}) collective-permute-start(bf16[272,128]{1,0:T(8,128)(2,1)S(1)} %add_convert_fusion.2.mine), channel_id=1, source_target_pairs={{0,128},{32,160},{64,192},{96,224},{128,0},{160,32},{192,64},{224,... | collective-permute-start | bytes 208904 | tf_op jit(solution)/shard_map/ppermute | solution.py:246
  96.5 0.6 copy-start.10
  99.2 0.7 copy-start.9
  99.9 19.4 %all-to-all-start.1 = ((bf16[16,128,256]{2,1,0:T(8,128)(2,1)}), bf16[16,128,256]{2,1,0:T(8,128)(2,1)S(1)}, u32[]{:S(2)}, u32[]{:S(2)}) async-start(bf16[16,128,256]{2,1,0:T(8,128)(2,1)} %get-tuple-element.49), calls=%async_computation.1 | async-start | bytes 2097152 | tf_op jit(solution)/shard_map/all_to_all | solution.py:367
  106.0 2.5 %copy-start.3 = (bf16[512,256]{1,0:T(8,128)(2,1)S(1)}, bf16[512,256]{1,0:T(8,128)(2,1)}, u32[]{:S(2)}) copy-start(bf16[512,256]{1,0:T(8,128)(2,1)} %w_edge.1) | copy-start | bytes 786436
  106.0 2.5 %copy-start.5 = (bf16[1152,256]{1,0:T(8,128)(2,1)S(1)}, bf16[1152,256]{1,0:T(8,128)(2,1)}, u32[]{:S(2)}) copy-start(bf16[1152,256]{1,0:T(8,128)(2,1)} %get-tuple-element.36) | copy-start | bytes 1769476
  108.5 1.7 %collective-permute-start.14 = (bf16[160,512]{1,0:T(8,128)(2,1)S(1)}, bf16[160,512]{1,0:T(8,128)(2,1)S(1)}, u32[]{:S(2)}, u32[]{:S(2)}) collective-permute-start(bf16[160,512]{1,0:T(8,128)(2,1)S(1)} %convolution_convert_fusion.2), channel_id=1, source_target_pairs={{0,1},{1,0},{2,3},{3,2},{4,5},{5,4},{6,7},{7,6},{8,9},{9,8},{10,11... | collective-permute-start | bytes 491528 | tf_op jit(solution)/shard_map/ppermute | solution.py:234
  108.6 1.5 %copy-start = (bf16[512,256]{1,0:T(8,128)(2,1)S(1)}, bf16[512,256]{1,0:T(8,128)(2,1)}, u32[]{:S(2)}) copy-start(bf16[512,256]{1,0:T(8,128)(2,1)} %w_mesh.1) | copy-start | bytes 786436

commit v3 on v2

v3 whole, which is shorter than its diff:
```python
import functools

import jax
import jax.numpy as jnp
import numpy as np
from jax import lax
from jax.experimental import pallas as pl
from jax.experimental.pallas import tpu as pltpu
from jax.sharding import Mesh, PartitionSpec as P

BF = jnp.bfloat16
F32 = jnp.float32
BAND = ("z", "y", "x")
PLANE = ("y", "x")
LANES = 128
EDGE_BLOCK = 768
TAIL = 16
SENDER_FLOPS = 4 * 10**9
EDGE_FLOPS = 9 * 10**9


def dot(a, b):
    return jnp.dot(a, b, preferred_element_type=F32)


def dot_t(a, b):
    return lax.dot_general(a, b, (((1,), (1,)), ((), ())), preferred_element_type=F32)


def dot_rows(a, b):
    return lax.dot_general(a, b, (((0,), (0,)), ((), ())), preferred_element_type=F32)


def one_hot(column, offset):
    place = lax.broadcasted_iota(jnp.int32, column.shape, column.ndim - 1)
    return jnp.where(column == place + offset, 1.0, 0.0).astype(BF)


def one_hot_rows(row, offset):
    place = lax.broadcasted_iota(jnp.int32, row.shape, 0)
    return jnp.where(row == place + offset, 1.0, 0.0).astype(BF)


def local_senders(row, where, half_grid):
    at = row - where[0] * (2 * half_grid) - where[1] * half_grid
    return jnp.where(at < 0, at + 2 * half_grid, at)


def local_receivers(row, slot, where, piece):
    at = row - (where[0] - 1) * (2 * piece)
    owner = jnp.where(at >= 2 * piece, 1, 0) + jnp.where(at >= 4 * piece, 1, 0)
    within = at - owner * (2 * piece)
    half = jnp.where(within >= piece, 1, 0)
    flip = jnp.where(half == where[1], 0, 1)
    place = jnp.where(where[0] % 2 == 0, 2 - owner, owner)
    near = (flip * 3 + place) * piece + within - half * piece
    return jnp.where(slot < where[2], near, -1)


def index_row(group, groups, where):
    at = group + where[1] * (groups // 2)
    return jnp.where(at >= groups, at - groups, at)


def copies(pairs, sems):
    return [pltpu.make_async_copy(src, dst, sems.at[k]) for k, (src, dst) in enumerate(pairs)]


def sender_kernel(
    where,
    grid_own,
    grid_far,
    edge_own,
    edge_far,
    w_grid,
    w_edge,
    bias,
    senders,
    pre_out,
    grid,
    edge,
    pre,
    table,
    left,
    in_sems,
    out_sems,
):
    half_edges = edge_own.shape[0]
    half_grid = grid_own.shape[0]
    n_grid = 2 * half_grid
    block = left.shape[0]
    fetches = copies(
        (
            (grid_own, grid.at[0:half_grid]),
            (grid_far, grid.at[half_grid:]),
            (edge_own, edge.at[0:half_edges]),
            (edge_far, edge.at[half_edges:]),
        ),
        in_sems,
    )
    for f in fetches:
        f.start()
    table[n_grid:] = w_edge[...]
    fetches[0].wait()
    fetches[1].wait()
    table[0:n_grid] = dot(grid[...], w_grid[...]).astype(BF)
    fetches[2].wait()
    fetches[3].wait()
    groups = 2 * half_edges // LANES
    per = block // LANES
    steps = 2 * half_edges // block

    def step(i, carry):
        rows = pl.ds(pl.multiple_of(i * block, block), block)
        for c in range(per):
            at = index_row(i * per + c, groups, where)
            row = local_senders(senders[pl.ds(at, 1), :], where, half_grid)
            column = jnp.broadcast_to(row, (LANES, LANES)).T
            for k in range(n_grid // LANES):
                left[c * LANES : (c + 1) * LANES, k * LANES : (k + 1) * LANES] = one_hot(column, k * LANES)
        left[:, n_grid:] = edge[rows, :]
        pre[rows, :] = dot(left[...], table[...]) + bias[...]
        pltpu.make_async_copy(pre.at[rows], pre_out.at[rows], out_sems.at[i]).start()
        return carry

    lax.fori_loop(0, steps, step, 0)
    for k in range(steps):
        rows = pl.ds(k * block, block)
        pltpu.make_async_copy(pre.at[rows], pre_out.at[rows], out_sems.at[k]).wait()


def edge_kernel(
    where,
    grid_own,
    grid_far,
    edge_own,
    edge_far,
    m0,
    m1,
    m2,
    m3,
    m4,
    m5,
    w_mesh,
    w_out,
    pre_in,
    senders,
    receivers,
    wire_out,
    cot_own,
    cot_far,
    seg_out,
    rim_low,
    rim_mid,
    rim_high,
    grid,
    edge,
    pre_part,
    lat,
    cot,
    table,
    left,
    right,
    sums,
    act_sums,
    edge_sum,
    bias_sum,
    cots,
    seg_grid,
    wire,
    low_v,
    mid_v,
    high_v,
    in_sems,
    out_sems,
):
    half_edges = edge_own.shape[0]
    half_grid = grid_own.shape[0]
    n_grid = 2 * half_grid
    piece = m0.shape[1]
    n_mesh = 6 * piece
    pad_mesh = lat.shape[0]
    n_rows = n_grid + pad_mesh
    block = left.shape[0]
    hidden = w_mesh.shape[1]
    pieces = (m0, m1, m2, m3, m4, m5)
    lats = [(m.at[0], lat.at[k * piece : (k + 1) * piece]) for k, m in enumerate(pieces)]
    cot_pairs = [(m.at[1], cot.at[k * piece : (k + 1) * piece]) for k, m in enumerate(pieces)]
    rest = [
        (pre_in, pre_part),
        (edge_own, edge.at[0:half_edges]),
        (edge_far, edge.at[half_edges:]),
        (grid_own, grid.at[0:half_grid]),
        (grid_far, grid.at[half_grid:]),
    ]
    fetches = copies(lats + cot_pairs + rest, in_sems)
    for f in fetches:
        f.start()
    if pad_mesh > n_mesh:
        lat[n_mesh:] = jnp.zeros((pad_mesh - n_mesh, lat.shape[1]), BF)
        cot[n_mesh:] = jnp.zeros((pad_mesh - n_mesh, cot.shape[1]), BF)
    sums[...] = jnp.zeros_like(sums)
    act_sums[...] = jnp.zeros_like(act_sums)
    edge_sum[...] = jnp.zeros_like(edge_sum)
    bias_sum[...] = jnp.zeros_like(bias_sum)
    for f in fetches[0:12]:
        f.wait()
    table[:, 0:hidden] = dot(lat[...], w_mesh[...]).astype(BF)
    cot_terms = dot_t(cot[...], w_out[...])
    high = cot_terms.astype(BF)
    table[:, hidden : 2 * hidden] = high
    table[:, 2 * hidden :] = (cot_terms - high.astype(F32)).astype(BF)
    for f in fetches[12:]:
        f.wait()
    groups = 2 * half_edges // LANES
    per = block // LANES

    def step(i, carry):
        rows = pl.ds(pl.multiple_of(i * block, block), block)
        for c in range(per):
            at = index_row(i * per + c, groups, where)
            mine = slice(c * LANES, (c + 1) * LANES)
            slot = at * LANES + lax.broadcasted_iota(jnp.int32, (1, LANES), 1)
            row = local_receivers(receivers[pl.ds(at, 1), :], slot, where, piece)
            row = jnp.broadcast_to(row, (LANES, LANES))
            column = row.T
            for k in range(pad_mesh // LANES):
                left[mine, k * LANES : (k + 1) * LANES] = one_hot(column, k * LANES)
                at_row = n_grid + k * LANES
                right[at_row : at_row + LANES, mine] = one_hot_rows(row, k * LANES)
            row = local_senders(senders[pl.ds(at, 1), :], where, half_grid)
            row = jnp.broadcast_to(row, (LANES, LANES))
            for k in range(n_grid // LANES):
                right[k * LANES : (k + 1) * LANES, mine] = one_hot_rows(row, k * LANES)
        got = dot(left[...], table[...])
        pre = pre_part[rows, :] + got[:, 0:hidden]
        hidden_cot = got[:, hidden : 2 * hidden] + got[:, 2 * hidden :]
        sig = jax.nn.sigmoid(pre)
        act = (pre * sig).astype(BF)
        pre_cot = (hidden_cot * sig * (1.0 + pre * (1.0 - sig))).astype(BF)
        cots[rows, :] = pre_cot
        sums[...] += dot(right[...], pre_cot)
        act_sums[...] += dot(right[n_grid:, :], act)
        edge_sum[...] += dot_rows(edge[rows, :], pre_cot)
        bias_sum[...] += jnp.sum(pre_cot.astype(F32), axis=0, keepdims=True)
        return carry

    lax.fori_loop(0, 2 * half_edges // block, step, 0)

    seg_grid[...] = sums[:n_grid].astype(BF)
    for ref, o, kind in ((low_v, 0, BF), (mid_v, 1, F32), (high_v, 2, BF)):
        for h in range(2):
            start = n_grid + (3 * h + o) * piece
            ref[h * piece : (h + 1) * piece] = sums[start : start + piece].astype(kind)
    stores = copies(
        (
            (low_v, rim_low),
            (high_v, rim_high),
            (seg_grid, seg_out),
            (cots.at[0:half_edges], cot_own),
            (cots.at[half_edges:], cot_far),
            (mid_v, rim_mid),
            (wire.at[8:12], wire_out.at[8:12]),
            (wire.at[0:4], wire_out.at[0:4]),
            (wire.at[4:8], wire_out.at[4:8]),
            (wire.at[12:16], wire_out.at[12:16]),
        ),
        out_sems,
    )
    for f in stores[0:6]:
        f.start()
    rows = 128
    sub = lax.broadcasted_iota(jnp.int32, (TAIL, LANES), 0)
    low = jnp.broadcast_to(bias_sum[:, :LANES], (TAIL, LANES))
    high = jnp.broadcast_to(bias_sum[:, LANES:], (TAIL, LANES))
    tail = jnp.where(sub == 0, low, jnp.where(sub == 1, high, 0.0)).astype(BF)
    for k in range(wire.shape[0]):
        wire[k, 2 * rows :, :] = tail

    def put(at, value):
        wire[at, 0:rows, :] = value[:, :LANES].astype(BF)
        wire[at, rows : 2 * rows, :] = value[:, LANES:].astype(BF)

    def put_all(at, g):
        for k in range(g.shape[0] // rows):
            put(at + k, g[k * rows : (k + 1) * rows])

    put_all(8, edge_sum[...])
    stores[6].start()
    put_all(0, dot_rows(grid[...], seg_grid[...]))
    stores[7].start()
    put_all(4, dot_rows(lat[...], sums[n_grid:].astype(BF)))
    stores[8].start()
    g = dot_rows(act_sums[...].astype(BF), cot[...])
    put_all(12, g[:, 0:hidden])
    put_all(14, g[:, hidden:])
    stores[9].start()
    for f in stores:
        f.wait()


def last_sum_kernel(mine, other, spread, bias):
    total = mine[...].astype(F32) + other[...].astype(F32)
    rows = spread.shape[1]
    low, high = (total[:rows].astype(BF), total[rows : 2 * rows].astype(BF))
    for k in range(spread.shape[0]):
        spread[k, :, :LANES] = low
        spread[k, :, LANES:] = high
    bias[:, :LANES] = total[2 * rows : 2 * rows + 1]
    bias[:, LANES:] = total[2 * rows + 1 : 2 * rows + 2]


def swap(x):
    return lax.ppermute(x, "chan", [(0, 1), (1, 0)])


def pair_swap(x, first):
    n = lax.axis_size(BAND)
    pairs = [(i, i + 1) for i in range(first, n - 1, 2)]
    return lax.ppermute(x, BAND, pairs + [(j, i) for i, j in pairs])


def depth_total(mine):
    depth = lax.axis_size("z")
    step = 1
    while True:
        mask = depth - 1 if 2 * step == depth else step
        other = lax.ppermute(mine, "z", [(i, i ^ mask) for i in range(depth)])
        step *= 2
        if step == depth:
            return mine, other
        mine = (mine.astype(F32) + other.astype(F32)).astype(BF)


def body(
    grid_latent,
    edge_latent,
    mesh_latent,
    mesh_cotangent,
    w_grid,
    w_mesh,
    w_edge,
    bias,
    w_out,
    senders,
    receivers,
    edge_count,
):
    band = lax.axis_index(BAND)
    chan = lax.axis_index("chan")
    half_grid = grid_latent.shape[0]
    half_edges = edge_latent.shape[0]
    piece, width = mesh_latent.shape
    hidden = w_grid.shape[1]
    n_grid = 2 * half_grid
    pad_mesh = -(-6 * piece // LANES) * LANES

    mesh_own = jnp.stack([mesh_latent, mesh_cotangent])
    mesh_low = pair_swap(mesh_own, 0)
    mesh_high = pair_swap(mesh_own, 1)
    edge_far = swap(edge_latent)
    grid_far = swap(grid_latent)
    mesh_own_far = swap(mesh_own)

    where = jnp.stack([band, chan, edge_count[0]])
    senders = senders.reshape(-1, LANES)
    receivers = receivers.reshape(-1, LANES)
    shape = jax.ShapeDtypeStruct
    vmem = pl.BlockSpec(memory_space=pltpu.VMEM)
    smem = pl.BlockSpec(memory_space=pltpu.SMEM)
    params = pltpu.CompilerParams(vmem_limit_bytes=56 * 1024 * 1024)
    anywhere = pl.BlockSpec(memory_space=pl.ANY)
    dma = pltpu.SemaphoreType.DMA
    n_edges = 2 * half_edges
    pre = pl.pallas_call(
        sender_kernel,
        out_shape=shape((n_edges, hidden), F32),
        in_specs=[smem] + [anywhere] * 4 + [vmem] * 4,
        out_specs=anywhere,
        scratch_shapes=[
            pltpu.VMEM((n_grid, width), BF),
            pltpu.VMEM((n_edges, width), BF),
            pltpu.VMEM((n_edges, hidden), F32),
            pltpu.VMEM((n_grid + width, hidden), BF),
            pltpu.VMEM((EDGE_BLOCK, n_grid + width), BF),
            dma((4,)),
            dma((n_edges // EDGE_BLOCK,)),
        ],
        compiler_params=params,
        cost_estimate=pl.CostEstimate(flops=SENDER_FLOPS, transcendentals=0, bytes_accessed=1 << 22),
        name="sender_step",
    )(where, grid_latent, grid_far, edge_latent, edge_far, w_grid, w_edge, bias.reshape(1, hidden), senders)

    mesh_low, mesh_high, pre = lax.optimization_barrier((mesh_low, mesh_high, pre))
    mesh_near = (mesh_low, mesh_own, mesh_high)
    mesh_far = (swap(mesh_low), mesh_own_far, swap(mesh_high))
    wire, cot_own, cot_far, seg_grid, rim_low, rim_mid, rim_high = pl.pallas_call(
        edge_kernel,
        out_shape=(
            shape((16, 256 + TAIL, LANES), BF),
            shape((half_edges, hidden), BF),
            shape((half_edges, hidden), BF),
            shape((n_grid, hidden), BF),
            shape((2 * piece, hidden), BF),
            shape((2 * piece, hidden), F32),
            shape((2 * piece, hidden), BF),
        ),
        in_specs=[smem] + [anywhere] * 10 + [vmem] * 2 + [anywhere] + [vmem] * 2,
        out_specs=(anywhere,) * 7,
        scratch_shapes=[
            pltpu.VMEM((n_grid, width), BF),
            pltpu.VMEM((n_edges, width), BF),
            pltpu.VMEM((n_edges, hidden), F32),
            pltpu.VMEM((pad_mesh, width), BF),
            pltpu.VMEM((pad_mesh, width), BF),
            pltpu.VMEM((pad_mesh, 3 * hidden), BF),
            pltpu.VMEM((EDGE_BLOCK, pad_mesh), BF),
            pltpu.VMEM((n_grid + pad_mesh, EDGE_BLOCK), BF),
            pltpu.VMEM((n_grid + pad_mesh, hidden), F32),
            pltpu.VMEM((pad_mesh, hidden), F32),
            pltpu.VMEM((width, hidden), F32),
            pltpu.VMEM((1, hidden), F32),
            pltpu.VMEM((n_edges, hidden), BF),
            pltpu.VMEM((n_grid, hidden), BF),
            pltpu.VMEM((16, 256 + TAIL, LANES), BF),
            pltpu.VMEM((2 * piece, hidden), BF),
            pltpu.VMEM((2 * piece, hidden), F32),
            pltpu.VMEM((2 * piece, hidden), BF),
            dma((17,)),
            dma((10,)),
        ],
        compiler_params=params,
        cost_estimate=pl.CostEstimate(flops=EDGE_FLOPS, transcendentals=1 << 20, bytes_accessed=1 << 23),
        name="edge_step",
    )(
        where,
        grid_latent,
        grid_far,
        edge_latent,
        edge_far,
        *mesh_near,
        *mesh_far,
        w_mesh,
        w_out,
        pre,
        senders,
        receivers,
    )

    from_low = pair_swap(rim_low, 0)
    from_high = pair_swap(rim_high, 1)
    arrived = lax.all_to_all(wire, PLANE, 0, 0, tiled=True)
    edge_term = dot_t(cot_far, w_edge).astype(BF)
    grid_term = dot_t(seg_grid[half_grid:], w_grid).astype(BF)
    edge_back = swap(edge_term)
    grid_back = swap(grid_term)
    total = arrived.astype(F32).sum(axis=0).astype(BF)
    total, from_low, from_high, _, _ = lax.optimization_barrier((total, from_low, from_high, edge_term, grid_term))
    mine, other = depth_total(total)
    spread, grad_bias = pl.pallas_call(
        last_sum_kernel,
        out_shape=(shape((16, 128, hidden), BF), shape((1, hidden), F32)),
        in_specs=[vmem] * 2,
        out_specs=(vmem,) * 2,
        name="last_sum",
    )(mine, other)
    everyone = lax.all_to_all(spread, PLANE, 0, 0, tiled=True)

    grad_edge = (dot_t(cot_own, w_edge) + edge_back.astype(F32)).astype(BF)
    grad_grid = (dot_t(seg_grid[:half_grid], w_grid) + grid_back.astype(F32)).astype(BF)
    seg_mesh = (rim_mid + from_low.astype(F32) + from_high.astype(F32)).astype(BF)
    seg_mesh, _ = lax.optimization_barrier((seg_mesh, grad_bias))
    mesh_back = swap(dot_t(seg_mesh[piece:], w_mesh).astype(BF))
    grad_mesh = (dot_t(seg_mesh[:piece], w_mesh) + mesh_back.astype(F32)).astype(BF)

    def rows_of(start, stop):
        return everyone[start:stop].astype(F32).reshape(-1, hidden)

    return (
        grad_grid,
        grad_edge,
        grad_mesh,
        rows_of(0, 4),
        rows_of(4, 8),
        rows_of(8, 12),
        grad_bias.reshape(hidden),
        jnp.concatenate([rows_of(12, 14), rows_of(14, 16)], axis=1),
    )


def solution(mesh):
    bands, chans = (mesh.shape["band"], mesh.shape["chan"])
    side = 4
    inner = Mesh(np.asarray(mesh.devices).reshape(bands // side**2, side, side, chans), (*BAND, "chan"))
    every = P((*BAND, "chan"), None)
    return jax.shard_map(
        body,
        mesh=inner,
        in_specs=(
            every,
            every,
            every,
            every,
            P(None, "chan"),
            P(None, "chan"),
            P(None, "chan"),
            P("chan"),
            P("chan", None),
            P(BAND),
            P(BAND),
            P(BAND),
        ),
        out_specs=(
            every,
            every,
            every,
            P(None, "chan"),
            P(None, "chan"),
            P(None, "chan"),
            P("chan"),
            P("chan", None),
        ),
        check_vma=False,
    )
```

time: 123 us -> 112 us (0.911)
  waiting for transfers between devices: 37.9 us -> 27.9 us
  Pallas kernels: 31.1 us -> 28.1 us
  starting transfers between devices: 36 us -> 37.9 us
    all_to_all x1, waiting for transfers between devices: 17 us -> 9.06 us  [body(): arrived = lax.all_to_all(wire, PLANE, 0, 0, tiled=True)]
    ppermute x7, waiting for transfers between devices: 11.1 us -> 7.86 us  [the longest x3 7.85 us: depth_total(): other = lax.ppermute(mine, 'z', [(i, i ^ mask) for i in range(depth)])]
    pallas_call x1, Pallas kernels: 21.3 us -> 18.5 us  [body(): pl.pallas_call(edge_kernel, out_shape=(shape((16, 256 + TAIL, LANES), BF)...]
    all_to_all x1, starting transfers between devices: 4.6 us -> 6.17 us  [body(): arrived = lax.all_to_all(wire, PLANE, 0, 0, tiled=True)]
    unnamed x36 -> x32, local copies, waits for them, and re-layouts: 3.28 us -> 2.6 us
  transfers between devices with their start and end apart: 17 -> 17, of which waited for: 7 -> 7; matrix products, arithmetic and copies ran while one was open for 8% -> 9% of each run, Pallas kernels for 8% -> 9%
where the time goes in v3:
time: 112 us; the launch traced here: 111 us
  starting transfers between devices  37.9 us (34%)
  Pallas kernels  28.1 us (25%)
  waiting for transfers between devices  27.9 us (25%)
  matrix products  7.5 us (7%)
  other arithmetic  5.78 us (5%)
  local copies, waits for them, and re-layouts  2.67 us (2%)
  between operations  1.61 us (1%)
    pallas_call x1, Pallas kernels, body(): pl.pallas_call(edge_kernel, out_shape=(shape((16, 256 + TAIL, LANES), BF)...  18.5 us
    ppermute x4, starting transfers between devices, pair_swap(): return lax.ppermute(x, BAND, pairs + [(j, i) for i, j in pairs])  14.6 us
    all_to_all x1, waiting for transfers between devices, body(): everyone = lax.all_to_all(spread, PLANE, 0, 0, tiled=True)  9.39 us
    all_to_all x1, waiting for transfers between devices, body(): arrived = lax.all_to_all(wire, PLANE, 0, 0, tiled=True)  9.06 us
    ppermute x3, starting transfers between devices, depth_total(): other = lax.ppermute(mine, 'z', [(i, i ^ mask) for i in range(depth)])  9.04 us
    ppermute x3, waiting for transfers between devices, depth_total(): other = lax.ppermute(mine, 'z', [(i, i ^ mask) for i in range(depth)])  7.85 us
    dot_general x6, matrix products, dot_t(): lax.dot_general(a, b, (((1,), (1,)), ((), ())), preferred_element_type=F32)  7.5 us
    pallas_call x1, Pallas kernels, body(): pl.pallas_call(sender_kernel, out_shape=shape((n_edges, hidden), F32), in...  7.45 us
  transfers between devices with their start and end apart: 17, of which 7 were waited for; matrix products, arithmetic and copies ran while one was open for 9% of the time, Pallas kernels for 9%

profile of v3, /device:TPU:32, one launch (start us, length us, event | category | flops | bytes accessed | tf_op | source)
XLA Modules:
  0.0 111.4 jit_solution(16416588728394631741)
XLA Ops:
  0.6 0.1 collective-permute-start.1
  0.7 0.5 collective-permute-start
  1.2 1.0 pad_maximum_fusion.m1
  2.3 0.0 copy-start.6
  2.3 0.2 collective-permute-start.5
  2.5 6.7 %collective-permute-start.3 = (bf16[2,160,512]{2,1,0:T(8,128)(2,1)S(1)}, bf16[2,160,512]{2,1,0:T(8,128)(2,1)S(1)}, u32[]{:S(2)}, u32[]{:S(2)}) collective-permute-start(bf16[2,160,512]{2,1,0:T(8,128)(2,1)S(1)} %pad_maximum_fusion.m1), channel_id=1, source_target_pairs={{2,4},{6,8},{10,12},{14,16},{18,20},{22,24},{26,28},{30,32},{34,36... | collective-permute-start | bytes 983048 | tf_op jit(solution)/shard_map/ppermute | solution.py:320
  9.1 0.1 collective-permute-start.2
  9.9 0.6 pad_add_fusion.where
  10.4 0.0 collective-permute-done.grid_far
  10.4 0.0 collective-permute-done.1.edge_far
  10.4 0.0 copy-start.9
  10.5 0.8 copy-done.10
  11.2 0.4 copy-done.9
  11.6 7.4 %sender_step.1.pre_in = f32[2304,256]{1,0:T(8,128)} custom-call(s32[3]{0:T(128)} %pad_add_fusion.where, bf16[576,512]{1,0:T(8,128)(2,1)} %grid_own.3, bf16[576,512]{1,0:T(8,128)(2,1)} %copy-done.10, bf16[1152,512]{1,0:T(8,128)(2,1)} %edge_own.3, bf16[1152,512]{1,0:T(8,128)(2,1)} %copy-done.9, bf16[512,256]{1,0:T(8,128)(2,1)} %w_grid.1, ...), custom_call_target="tpu_custom_call" | custom-call | flops 4000000000 | bytes 4194304 | tf_op jit(solution)/shard_map/sender_step/pallas_call | solution.py:375
  19.1 0.0 collective-permute-done.3.m2
  19.1 0.0 copy-start.12
  19.1 0.0 collective-permute-done.2.m0
  19.1 0.0 copy-start.13
  19.2 0.2 collective-permute-start.4
  19.4 0.4 collective-permute-start.6
  19.8 0.0 collective-permute-done.5.m4
  19.8 1.1 collective-permute-done.4.m3
  20.9 0.5 collective-permute-done.6.m5
  21.4 0.2 copy-done.14
  21.6 0.5 copy-done.15
  22.1 18.5 %edge_step.1 = (bf16[16,272,128]{2,1,0:T(8,128)(2,1)}, bf16[1152,256]{1,0:T(8,128)(2,1)}, bf16[1152,256]{1,0:T(8,128)(2,1)}, bf16[1152,256]{1,0:T(8,128)(2,1)}, ...) custom-call(s32[3]{0:T(128)} %pad_add_fusion.where, bf16[576,512]{1,0:T(8,128)(2,1)} %grid_own.3, ...), custom_call_target="tpu_custom_call" | custom-call | flops 8999999488 | bytes 8388608 | tf_op jit(solution)/shard_map/edge_step/pallas_call | solution.py:397
  40.6 0.0 copy-start.2
  40.6 6.2 %all-to-all-start = ((bf16[16,272,128]{2,1,0:T(8,128)(2,1)}), bf16[16,272,128]{2,1,0:T(8,128)(2,1)S(1)}, u32[]{:S(2)}, u32[]{:S(2)}) async-start(bf16[16,272,128]{2,1,0:T(8,128)(2,1)} %get-tuple-element.31), calls=%async_computation | async-start | bytes 2228224 | tf_op jit(solution)/shard_map/all_to_all | solution.py:452
  46.8 0.0 copy-start.1
  46.8 2.0 %collective-permute-start.9 = (bf16[320,256]{1,0:T(8,128)(2,1)}, bf16[320,256]{1,0:T(8,128)(2,1)}, u32[]{:S(2)}, u32[]{:S(2)}) collective-permute-start(bf16[320,256]{1,0:T(8,128)(2,1)} %get-tuple-element.32), channel_id=1, source_target_pairs={{0,2},{4,6},{8,10},{12,14},{16,18},{20,22},{24,26},{28,30},{32,34}... | collective-permute-start | bytes 491528 | tf_op jit(solution)/shard_map/ppermute | solution.py:320
  48.8 5.8 %collective-permute-start.10 = (bf16[320,256]{1,0:T(8,128)(2,1)}, bf16[320,256]{1,0:T(8,128)(2,1)}, u32[]{:S(2)}, u32[]{:S(2)}) collective-permute-start(bf16[320,256]{1,0:T(8,128)(2,1)} %get-tuple-element.33), channel_id=1, source_target_pairs={{2,4},{6,8},{10,12},{14,16},{18,20},{22,24},{26,28},{30,32},{34,36... | collective-permute-start | bytes 491528 | tf_op jit(solution)/shard_map/ppermute | solution.py:320
  54.7 1.6 %convolution_convert_fusion = bf16[1152,512]{1,0:T(8,128)(2,1)S(1)} fusion(bf16[1152,256]{1,0:T(8,128)(2,1)} %get-tuple-element.29, bf16[512,256]{1,0:T(8,128)(2,1)S(1)} %copy-done.2), kind=kOutput, calls=%fused_computation.2 | convolution fusion | flops 302579712 | bytes 2031616 | tf_op jit(solution)/shard_map/dot_general | solution.py:27
  56.2 1.2 %convolution_convert_fusion.1 = bf16[576,512]{1,0:T(8,128)(2,1)} fusion(bf16[512,256]{1,0:T(8,128)(2,1)S(1)} %copy-done.1, bf16[1152,256]{1,0:T(8,128)(2,1)S(1)} %copy-done.4), kind=kOutput, calls=%fused_computation.5 | convolution fusion | flops 151289856 | bytes 1146880 | tf_op jit(solution)/shard_map/dot_general | solution.py:27
  57.4 9.1 %all-to-all-done = bf16[16,272,128]{2,1,0:T(8,128)(2,1)S(1)} async-done(((bf16[16,272,128]{2,1,0:T(8,128)(2,1)}), bf16[16,272,128]{2,1,0:T(8,128)(2,1)S(1)}, u32[]{:S(2)}, u32[]{:S(2)}) %all-to-all-start) | async-done | bytes 1114144 | tf_op jit(solution)/shard_map/all_to_all | solution.py:452
  66.5 0.2 reduce_sum.12
  66.6 0.0 collective-permute-done.9
  66.6 0.1 collective-permute-start.11
  66.8 0.1 collective-permute-start.7
  66.8 0.5 collective-permute-start.8
  67.3 3.7 %collective-permute-done.11 = bf16[272,128]{1,0:T(8,128)(2,1)S(1)} collective-permute-done((bf16[272,128]{1,0:T(8,128)(2,1)S(1)}, bf16[272,128]{1,0:T(8,128)(2,1)S(1)}, u32[]{:S(2)}, u32[]{:S(2)}) %collective-permute-start.11) | collective-permute-done | bytes 69664 | tf_op jit(solution)/shard_map/ppermute | solution.py:328
  71.1 4.6 %collective-permute-start.12 = (bf16[272,128]{1,0:T(8,128)(2,1)S(1)}, bf16[272,128]{1,0:T(8,128)(2,1)S(1)}, u32[]{:S(2)}, u32[]{:S(2)}) collective-permute-start(bf16[272,128]{1,0:T(8,128)(2,1)S(1)} %add_convert_fusion.3), channel_id=1, source_target_pairs={{0,64},{32,96},{64,0},{96,32},{128,192},{160,224},{192,128},{224,1... | collective-permute-start | bytes 208904 | tf_op jit(solution)/shard_map/ppermute | solution.py:328
  75.6 2.3 %collective-permute-done.12 = bf16[272,128]{1,0:T(8,128)(2,1)S(1)} collective-permute-done((bf16[272,128]{1,0:T(8,128)(2,1)S(1)}, bf16[272,128]{1,0:T(8,128)(2,1)S(1)}, u32[]{:S(2)}, u32[]{:S(2)}) %collective-permute-start.12) | collective-permute-done | bytes 69664 | tf_op jit(solution)/shard_map/ppermute | solution.py:328
  78.0 0.0 copy-start.7
  78.0 4.4 %collective-permute-start.13 = (bf16[272,128]{1,0:T(8,128)(2,1)S(1)}, bf16[272,128]{1,0:T(8,128)(2,1)S(1)}, u32[]{:S(2)}, u32[]{:S(2)}) collective-permute-start(bf16[272,128]{1,0:T(8,128)(2,1)S(1)} %add_convert_fusion.2.mine), channel_id=1, source_target_pairs={{0,224},{32,192},{64,160},{96,128},{128,96},{160,64},{192,32},{224... | collective-permute-start | bytes 208904 | tf_op jit(solution)/shard_map/ppermute | solution.py:328
  82.3 0.0 collective-permute-done.7
  82.3 1.2 %fusion.1 = bf16[576,512]{1,0:T(8,128)(2,1)} fusion(bf16[512,256]{1,0:T(8,128)(2,1)S(1)} %copy-done.1, bf16[576,512]{1,0:T(8,128)(2,1)S(1)} %collective-permute-done.7, bf16[1152,256]{1,0:T(8,128)(2,1)S(1)} %copy-done.4), kind=kOutput, calls=%fused_computation.4 | convolution fusion | flops 151879680 | bytes 1736704 | tf_op jit(solution)/shard_map/dot_general | solution.py:27
  83.5 1.9 %collective-permute-done.13.other = bf16[272,128]{1,0:T(8,128)(2,1)S(1)} collective-permute-done((bf16[272,128]{1,0:T(8,128)(2,1)S(1)}, bf16[272,128]{1,0:T(8,128)(2,1)S(1)}, u32[]{:S(2)}, u32[]{:S(2)}) %collective-permute-start.13) | collective-permute-done | bytes 69664 | tf_op jit(solution)/shard_map/ppermute | solution.py:328
  85.4 0.6 copy-done.8
  86.0 2.1 %last_sum.1 = (bf16[16,128,256]{2,1,0:T(8,128)(2,1)}, f32[1,256]{1,0:T(1,128)}) custom-call(bf16[272,128]{1,0:T(8,128)(2,1)} %copy-done.7, bf16[272,128]{1,0:T(8,128)(2,1)} %copy-done.8), custom_call_target="tpu_custom_call" | custom-call | tf_op jit(solution)/shard_map/last_sum/pallas_call | solution.py:460
  88.1 6.0 %all-to-all-start.1 = ((bf16[16,128,256]{2,1,0:T(8,128)(2,1)}), bf16[16,128,256]{2,1,0:T(8,128)(2,1)S(1)}, u32[]{:S(2)}, u32[]{:S(2)}) async-start(bf16[16,128,256]{2,1,0:T(8,128)(2,1)} %get-tuple-element.39), calls=%async_computation.1 | async-start | bytes 2097152 | tf_op jit(solution)/shard_map/all_to_all | solution.py:467
  94.1 0.0 copy-start.3
  94.2 1.2 %add_convert_fusion.1 = bf16[320,256]{1,0:T(8,128)(2,1)S(1)} fusion(bf16[320,256]{1,0:T(8,128)(2,1)} %collective-permute-done.10, f32[320,256]{1,0:T(8,128)} %get-tuple-element.30, bf16[320,256]{1,0:T(8,128)(2,1)} %collective-permute-done.9), kind=kLoop, calls=%fused_computation.9 | loop fusion | flops 409600 | bytes 819200 | tf_op jit(solution)/shard_map/convert_element_type | solution.py:471
  95.4 1.2 %convolution_convert_fusion.2 = bf16[160,512]{1,0:T(8,128)(2,1)S(1)} fusion(bf16[512,256]{1,0:T(8,128)(2,1)} %w_mesh.1, bf16[320,256]{1,0:T(8,128)(2,1)S(1)} %add_convert_fusion.1), kind=kOutput, calls=%fused_computation.6 | convolution fusion | flops 42024960 | bytes 507904 | tf_op jit(solution)/shard_map/dot_general | solution.py:27
  96.6 0.1 collective-permute-start.14
  96.7 0.0 collective-permute-done.8
  96.7 0.0 copy-start
  96.7 1.5 %fusion = bf16[1152,512]{1,0:T(8,128)(2,1)} fusion(bf16[1152,256]{1,0:T(8,128)(2,1)S(1)} %copy-done.5, bf16[512,256]{1,0:T(8,128)(2,1)S(1)} %copy-done.3, bf16[1152,512]{1,0:T(8,128)(2,1)S(1)} %collective-permute-done.8), kind=kOutput, calls=%fused_computation.1 | convolution fusion | flops 303759360 | bytes 3211264 | tf_op jit(solution)/shard_map/dot_general | solution.py:27
  98.2 0.0 collective-permute-done.14
  98.2 0.9 add_convert_fusion
  99.2 9.4 %all-to-all-done.1 = bf16[16,128,256]{2,1,0:T(8,128)(2,1)S(1)} async-done(((bf16[16,128,256]{2,1,0:T(8,128)(2,1)}), bf16[16,128,256]{2,1,0:T(8,128)(2,1)S(1)}, u32[]{:S(2)}, u32[]{:S(2)}) %all-to-all-start.1) | async-done | bytes 1048608 | tf_op jit(solution)/shard_map/all_to_all | solution.py:467
  108.5 0.1 fusion.10
  108.6 0.8 bitcast_convert_fusion.2
  109.5 0.9 maximum_convert_fusion
  110.3 1.1 bitcast_convert_fusion
  (22 shorter events, 0.1 us)
Async XLA Ops:
  0.6 9.8 %collective-permute-start.1 = (bf16[1152,512]{1,0:T(8,128)(2,1)}, bf16[1152,512]{1,0:T(8,128)(2,1)S(1)}, u32[]{:S(2)}, u32[]{:S(2)}) collective-permute-start(bf16[1152,512]{1,0:T(8,128)(2,1)} %edge_own.3), channel_id=1, source_target_pairs={{0,1},{1,0},{2,3},{3,2},{4,5},{5,4},{6,7},{7,6},{8,9},{9,8},{10,11... | collective-permute-start | bytes 3538952 | tf_op jit(solution)/shard_map/ppermute | solution.py:314
  0.7 9.7 %collective-permute-start = (bf16[576,512]{1,0:T(8,128)(2,1)}, bf16[576,512]{1,0:T(8,128)(2,1)S(1)}, u32[]{:S(2)}, u32[]{:S(2)}) collective-permute-start(bf16[576,512]{1,0:T(8,128)(2,1)} %grid_own.3), channel_id=1, source_target_pairs={{0,1},{1,0},{2,3},{3,2},{4,5},{5,4},{6,7},{7,6},{8,9},{9,8},{10,11... | collective-permute-start | bytes 1769480 | tf_op jit(solution)/shard_map/ppermute | solution.py:314
  2.3 16.8 %copy-start.6 = (bf16[2,160,512]{2,1,0:T(8,128)(2,1)}, bf16[2,160,512]{2,1,0:T(8,128)(2,1)S(1)}, u32[]{:S(2)}) copy-start(bf16[2,160,512]{2,1,0:T(8,128)(2,1)S(1)} %pad_maximum_fusion.m1) | copy-start | bytes 983044
  2.3 17.5 %collective-permute-start.5 = (bf16[2,160,512]{2,1,0:T(8,128)(2,1)S(1)}, bf16[2,160,512]{2,1,0:T(8,128)(2,1)S(1)}, u32[]{:S(2)}, u32[]{:S(2)}) collective-permute-start(bf16[2,160,512]{2,1,0:T(8,128)(2,1)S(1)} %pad_maximum_fusion.m1), channel_id=1, source_target_pairs={{0,1},{1,0},{2,3},{3,2},{4,5},{5,4},{6,7},{7,6},{8,9},{9,8},{10,11... | collective-permute-start | bytes 983048 | tf_op jit(solution)/shard_map/ppermute | solution.py:314
  2.5 16.6 %collective-permute-start.3 = (bf16[2,160,512]{2,1,0:T(8,128)(2,1)S(1)}, bf16[2,160,512]{2,1,0:T(8,128)(2,1)S(1)}, u32[]{:S(2)}, u32[]{:S(2)}) collective-permute-start(bf16[2,160,512]{2,1,0:T(8,128)(2,1)S(1)} %pad_maximum_fusion.m1), channel_id=1, source_target_pairs={{2,4},{6,8},{10,12},{14,16},{18,20},{22,24},{26,28},{30,32},{34,36... | collective-permute-start | bytes 983048 | tf_op jit(solution)/shard_map/ppermute | solution.py:320
  9.1 10.0 %collective-permute-start.2 = (bf16[2,160,512]{2,1,0:T(8,128)(2,1)S(1)}, bf16[2,160,512]{2,1,0:T(8,128)(2,1)S(1)}, u32[]{:S(2)}, u32[]{:S(2)}) collective-permute-start(bf16[2,160,512]{2,1,0:T(8,128)(2,1)S(1)} %pad_maximum_fusion.m1), channel_id=1, source_target_pairs={{0,2},{4,6},{8,10},{12,14},{16,18},{20,22},{24,26},{28,30},{32,34}... | collective-permute-start | bytes 983048 | tf_op jit(solution)/shard_map/ppermute | solution.py:320
  10.4 0.8 copy-start.10
  10.4 1.2 %copy-start.9 = (bf16[1152,512]{1,0:T(8,128)(2,1)}, bf16[1152,512]{1,0:T(8,128)(2,1)S(1)}, u32[]{:S(2)}) copy-start(bf16[1152,512]{1,0:T(8,128)(2,1)S(1)} %collective-permute-done.1.edge_far) | copy-start | bytes 3538948
  19.1 2.2 %copy-start.12 = (bf16[2,160,512]{2,1,0:T(8,128)(2,1)}, bf16[2,160,512]{2,1,0:T(8,128)(2,1)S(1)}, u32[]{:S(2)}) copy-start(bf16[2,160,512]{2,1,0:T(8,128)(2,1)S(1)} %collective-permute-done.3.m2) | copy-start | bytes 983044
  19.1 2.2 %copy-start.13 = (bf16[2,160,512]{2,1,0:T(8,128)(2,1)}, bf16[2,160,512]{2,1,0:T(8,128)(2,1)S(1)}, u32[]{:S(2)}) copy-start(bf16[2,160,512]{2,1,0:T(8,128)(2,1)S(1)} %collective-permute-done.2.m0) | copy-start | bytes 983044
  19.2 1.7 %collective-permute-start.4 = (bf16[2,160,512]{2,1,0:T(8,128)(2,1)S(1)}, bf16[2,160,512]{2,1,0:T(8,128)(2,1)S(1)}, u32[]{:S(2)}, u32[]{:S(2)}) collective-permute-start(bf16[2,160,512]{2,1,0:T(8,128)(2,1)S(1)} %collective-permute-done.2.m0), channel_id=1, source_target_pairs={{0,1},{1,0},{2,3},{3,2},{4,5},{5,4},{6,7},{7,6},{8,9},{9,8},{10,11... | collective-permute-start | bytes 983048 | tf_op jit(solution)/shard_map/ppermute | solution.py:314
  19.4 2.0 %collective-permute-start.6 = (bf16[2,160,512]{2,1,0:T(8,128)(2,1)S(1)}, bf16[2,160,512]{2,1,0:T(8,128)(2,1)S(1)}, u32[]{:S(2)}, u32[]{:S(2)}) collective-permute-start(bf16[2,160,512]{2,1,0:T(8,128)(2,1)S(1)} %collective-permute-done.3.m2), channel_id=1, source_target_pairs={{0,1},{1,0},{2,3},{3,2},{4,5},{5,4},{6,7},{7,6},{8,9},{9,8},{10,11... | collective-permute-start | bytes 983048 | tf_op jit(solution)/shard_map/ppermute | solution.py:314
  19.8 1.6 %copy-start.11 = (bf16[2,160,512]{2,1,0:T(8,128)(2,1)}, bf16[2,160,512]{2,1,0:T(8,128)(2,1)S(1)}, u32[]{:S(2)}) copy-start(bf16[2,160,512]{2,1,0:T(8,128)(2,1)S(1)} %collective-permute-done.5.m4) | copy-start | bytes 983044
  20.9 0.7 copy-start.14
  21.3 0.7 copy-start.15
  40.6 14.0 %copy-start.2 = (bf16[512,256]{1,0:T(8,128)(2,1)S(1)}, bf16[512,256]{1,0:T(8,128)(2,1)}, u32[]{:S(2)}) copy-start(bf16[512,256]{1,0:T(8,128)(2,1)} %w_edge.1) | copy-start | bytes 786436
  40.6 25.8 %all-to-all-start = ((bf16[16,272,128]{2,1,0:T(8,128)(2,1)}), bf16[16,272,128]{2,1,0:T(8,128)(2,1)S(1)}, u32[]{:S(2)}, u32[]{:S(2)}) async-start(bf16[16,272,128]{2,1,0:T(8,128)(2,1)} %get-tuple-element.31), calls=%async_computation | async-start | bytes 2228224 | tf_op jit(solution)/shard_map/all_to_all | solution.py:452
  46.8 9.4 %copy-start.1 = (bf16[512,256]{1,0:T(8,128)(2,1)S(1)}, bf16[512,256]{1,0:T(8,128)(2,1)}, u32[]{:S(2)}) copy-start(bf16[512,256]{1,0:T(8,128)(2,1)} %w_grid.1) | copy-start | bytes 786436
  46.8 9.4 %copy-start.4 = (bf16[1152,256]{1,0:T(8,128)(2,1)S(1)}, bf16[1152,256]{1,0:T(8,128)(2,1)}, u32[]{:S(2)}) copy-start(bf16[1152,256]{1,0:T(8,128)(2,1)} %get-tuple-element.27) | copy-start | bytes 1769476
  46.8 19.8 %collective-permute-start.9 = (bf16[320,256]{1,0:T(8,128)(2,1)}, bf16[320,256]{1,0:T(8,128)(2,1)}, u32[]{:S(2)}, u32[]{:S(2)}) collective-permute-start(bf16[320,256]{1,0:T(8,128)(2,1)} %get-tuple-element.32), channel_id=1, source_target_pairs={{0,2},{4,6},{8,10},{12,14},{16,18},{20,22},{24,26},{28,30},{32,34}... | collective-permute-start | bytes 491528 | tf_op jit(solution)/shard_map/ppermute | solution.py:320
  48.8 17.8 %collective-permute-start.10 = (bf16[320,256]{1,0:T(8,128)(2,1)}, bf16[320,256]{1,0:T(8,128)(2,1)}, u32[]{:S(2)}, u32[]{:S(2)}) collective-permute-start(bf16[320,256]{1,0:T(8,128)(2,1)} %get-tuple-element.33), channel_id=1, source_target_pairs={{2,4},{6,8},{10,12},{14,16},{18,20},{22,24},{26,28},{30,32},{34,36... | collective-permute-start | bytes 491528 | tf_op jit(solution)/shard_map/ppermute | solution.py:320
  66.6 4.4 %collective-permute-start.11 = (bf16[272,128]{1,0:T(8,128)(2,1)S(1)}, bf16[272,128]{1,0:T(8,128)(2,1)S(1)}, u32[]{:S(2)}, u32[]{:S(2)}) collective-permute-start(bf16[272,128]{1,0:T(8,128)(2,1)S(1)} %reduce_sum.12), channel_id=1, source_target_pairs={{0,32},{32,0},{64,96},{96,64},{128,160},{160,128},{192,224},{224,1... | collective-permute-start | bytes 208904 | tf_op jit(solution)/shard_map/ppermute | solution.py:328
  66.8 15.6 %collective-permute-start.7 = (bf16[576,512]{1,0:T(8,128)(2,1)}, bf16[576,512]{1,0:T(8,128)(2,1)S(1)}, u32[]{:S(2)}, u32[]{:S(2)}) collective-permute-start(bf16[576,512]{1,0:T(8,128)(2,1)} %convolution_convert_fusion.1), channel_id=1, source_target_pairs={{0,1},{1,0},{2,3},{3,2},{4,5},{5,4},{6,7},{7,6},{8,9},{9,8},{10,11... | collective-permute-start | bytes 1769480 | tf_op jit(solution)/shard_map/ppermute | solution.py:314
  66.8 29.8 %collective-permute-start.8 = (bf16[1152,512]{1,0:T(8,128)(2,1)S(1)}, bf16[1152,512]{1,0:T(8,128)(2,1)S(1)}, u32[]{:S(2)}, u32[]{:S(2)}) collective-permute-start(bf16[1152,512]{1,0:T(8,128)(2,1)S(1)} %convolution_convert_fusion), channel_id=1, source_target_pairs={{0,1},{1,0},{2,3},{3,2},{4,5},{5,4},{6,7},{7,6},{8,9},{9,8},{10,11... | collective-permute-start | bytes 3538952 | tf_op jit(solution)/shard_map/ppermute | solution.py:314
  71.1 6.9 %collective-permute-start.12 = (bf16[272,128]{1,0:T(8,128)(2,1)S(1)}, bf16[272,128]{1,0:T(8,128)(2,1)S(1)}, u32[]{:S(2)}, u32[]{:S(2)}) collective-permute-start(bf16[272,128]{1,0:T(8,128)(2,1)S(1)} %add_convert_fusion.3), channel_id=1, source_target_pairs={{0,64},{32,96},{64,0},{96,32},{128,192},{160,224},{192,128},{224,1... | collective-permute-start | bytes 208904 | tf_op jit(solution)/shard_map/ppermute | solution.py:328
  78.0 7.4 %copy-start.7 = (bf16[272,128]{1,0:T(8,128)(2,1)}, bf16[272,128]{1,0:T(8,128)(2,1)S(1)}, u32[]{:S(2)}) copy-start(bf16[272,128]{1,0:T(8,128)(2,1)S(1)} %add_convert_fusion.2.mine) | copy-start | bytes 208900
  78.0 7.4 %collective-permute-start.13 = (bf16[272,128]{1,0:T(8,128)(2,1)S(1)}, bf16[272,128]{1,0:T(8,128)(2,1)S(1)}, u32[]{:S(2)}, u32[]{:S(2)}) collective-permute-start(bf16[272,128]{1,0:T(8,128)(2,1)S(1)} %add_convert_fusion.2.mine), channel_id=1, source_target_pairs={{0,224},{32,192},{64,160},{96,128},{128,96},{160,64},{192,32},{224... | collective-permute-start | bytes 208904 | tf_op jit(solution)/shard_map/ppermute | solution.py:328
  85.4 0.6 copy-start.8
  88.1 20.4 %all-to-all-start.1 = ((bf16[16,128,256]{2,1,0:T(8,128)(2,1)}), bf16[16,128,256]{2,1,0:T(8,128)(2,1)S(1)}, u32[]{:S(2)}, u32[]{:S(2)}) async-start(bf16[16,128,256]{2,1,0:T(8,128)(2,1)} %get-tuple-element.39), calls=%async_computation.1 | async-start | bytes 2097152 | tf_op jit(solution)/shard_map/all_to_all | solution.py:467
  94.1 2.5 %copy-start.3 = (bf16[512,256]{1,0:T(8,128)(2,1)S(1)}, bf16[512,256]{1,0:T(8,128)(2,1)}, u32[]{:S(2)}) copy-start(bf16[512,256]{1,0:T(8,128)(2,1)} %w_edge.1) | copy-start | bytes 786436
  94.2 2.5 %copy-start.5 = (bf16[1152,256]{1,0:T(8,128)(2,1)S(1)}, bf16[1152,256]{1,0:T(8,128)(2,1)}, u32[]{:S(2)}) copy-start(bf16[1152,256]{1,0:T(8,128)(2,1)} %get-tuple-element.28) | copy-start | bytes 1769476
  96.6 1.7 %collective-permute-start.14 = (bf16[160,512]{1,0:T(8,128)(2,1)S(1)}, bf16[160,512]{1,0:T(8,128)(2,1)S(1)}, u32[]{:S(2)}, u32[]{:S(2)}) collective-permute-start(bf16[160,512]{1,0:T(8,128)(2,1)S(1)} %convolution_convert_fusion.2), channel_id=1, source_target_pairs={{0,1},{1,0},{2,3},{3,2},{4,5},{5,4},{6,7},{7,6},{8,9},{9,8},{10,11... | collective-permute-start | bytes 491528 | tf_op jit(solution)/shard_map/ppermute | solution.py:314
  96.7 1.5 %copy-start = (bf16[512,256]{1,0:T(8,128)(2,1)S(1)}, bf16[512,256]{1,0:T(8,128)(2,1)}, u32[]{:S(2)}) copy-start(bf16[512,256]{1,0:T(8,128)(2,1)} %w_mesh.1) | copy-start | bytes 786436

commit v4 on v3

--- a/solution.py
+++ b/solution.py
@@ -10,11 +10,13 @@
 
 BF = jnp.bfloat16
 F32 = jnp.float32
-BAND = ("z", "y", "x")
-PLANE = ("y", "x")
+BAND = ("zh", "zl", "y", "x")
+GROUP = ("zl", "y", "x")
 LANES = 128
 EDGE_BLOCK = 768
-TAIL = 16
+TAIL = 8
+ROWS = 64
+MEMBERS = 32
 SENDER_FLOPS = 4 * 10**9
 EDGE_FLOPS = 9 * 10**9
 
@@ -67,7 +69,8 @@
 
 
 def sender_kernel(
-    where,
+    band,
+    chan,
     grid_own,
     grid_far,
     edge_own,
@@ -85,6 +88,7 @@
     in_sems,
     out_sems,
 ):
+    where = (band[0], chan[0])
     half_edges = edge_own.shape[0]
     half_grid = grid_own.shape[0]
     n_grid = 2 * half_grid
@@ -130,7 +134,9 @@
 
 
 def edge_kernel(
-    where,
+    band,
+    chan,
+    count,
     grid_own,
     grid_far,
     edge_own,
@@ -174,6 +180,7 @@
     in_sems,
     out_sems,
 ):
+    where = (band[0], chan[0], count[0])
     half_edges = edge_own.shape[0]
     half_grid = grid_own.shape[0]
     n_grid = 2 * half_grid
@@ -242,7 +249,7 @@
         sums[...] += dot(right[...], pre_cot)
         act_sums[...] += dot(right[n_grid:, :], act)
         edge_sum[...] += dot_rows(edge[rows, :], pre_cot)
-        bias_sum[...] += jnp.sum(pre_cot.astype(F32), axis=0, keepdims=True)
+        bias_sum[...] += pre_cot.astype(F32).reshape(block // 8, 8, hidden).sum(axis=0)
         return carry
 
     lax.fori_loop(0, 2 * half_edges // block, step, 0)
@@ -252,62 +259,49 @@
         for h in range(2):
             start = n_grid + (3 * h + o) * piece
             ref[h * piece : (h + 1) * piece] = sums[start : start + piece].astype(kind)
+    rows = ROWS
+    per_grad = w_mesh.shape[0] // rows
+    parts = [slice(k * per_grad, (k + 1) * per_grad) for k in range(4)]
     stores = copies(
-        (
+        [
             (low_v, rim_low),
             (high_v, rim_high),
             (seg_grid, seg_out),
             (cots.at[0:half_edges], cot_own),
             (cots.at[half_edges:], cot_far),
             (mid_v, rim_mid),
-            (wire.at[8:12], wire_out.at[8:12]),
-            (wire.at[0:4], wire_out.at[0:4]),
-            (wire.at[4:8], wire_out.at[4:8]),
-            (wire.at[12:16], wire_out.at[12:16]),
-        ),
+        ]
+        + [(wire.at[p, 0 : 2 * ROWS + TAIL], wire_out.at[p]) for p in parts],
         out_sems,
     )
     for f in stores[0:6]:
         f.start()
-    rows = 128
-    sub = lax.broadcasted_iota(jnp.int32, (TAIL, LANES), 0)
-    low = jnp.broadcast_to(bias_sum[:, :LANES], (TAIL, LANES))
-    high = jnp.broadcast_to(bias_sum[:, LANES:], (TAIL, LANES))
+    sub = lax.broadcasted_iota(jnp.int32, (16, LANES), 0)
+    bias_total = jnp.sum(bias_sum[...], axis=0, keepdims=True)
+    low = jnp.broadcast_to(bias_total[:, :LANES], (16, LANES))
+    high = jnp.broadcast_to(bias_total[:, LANES:], (16, LANES))
     tail = jnp.where(sub == 0, low, jnp.where(sub == 1, high, 0.0)).astype(BF)
     for k in range(wire.shape[0]):
         wire[k, 2 * rows :, :] = tail
 
-    def put(at, value):
-        wire[at, 0:rows, :] = value[:, :LANES].astype(BF)
-        wire[at, rows : 2 * rows, :] = value[:, LANES:].astype(BF)
-
     def put_all(at, g):
         for k in range(g.shape[0] // rows):
-            put(at + k, g[k * rows : (k + 1) * rows])
-
-    put_all(8, edge_sum[...])
+            value = g[k * rows : (k + 1) * rows]
+            wire[at + k, 0:rows, :] = value[:, :LANES].astype(BF)
+            wire[at + k, rows : 2 * rows, :] = value[:, LANES:].astype(BF)
+
+    put_all(parts[2].start, edge_sum[...])
+    stores[8].start()
+    put_all(parts[0].start, dot_rows(grid[...], seg_grid[...]))
     stores[6].start()
-    put_all(0, dot_rows(grid[...], seg_grid[...]))
+    put_all(parts[1].start, dot_rows(lat[...], sums[n_grid:].astype(BF)))
     stores[7].start()
-    put_all(4, dot_rows(lat[...], sums[n_grid:].astype(BF)))
-    stores[8].start()
     g = dot_rows(act_sums[...].astype(BF), cot[...])
-    put_all(12, g[:, 0:hidden])
-    put_all(14, g[:, hidden:])
+    put_all(parts[3].start, g[:, 0:hidden])
+    put_all(parts[3].start + per_grad // 2, g[:, hidden:])
     stores[9].start()
     for f in stores:
         f.wait()
-
-
-def last_sum_kernel(mine, other, spread, bias):
-    total = mine[...].astype(F32) + other[...].astype(F32)
-    rows = spread.shape[1]
-    low, high = (total[:rows].astype(BF), total[rows : 2 * rows].astype(BF))
-    for k in range(spread.shape[0]):
-        spread[k, :, :LANES] = low
-        spread[k, :, LANES:] = high
-    bias[:, :LANES] = total[2 * rows : 2 * rows + 1]
-    bias[:, LANES:] = total[2 * rows + 1 : 2 * rows + 2]
 
 
 def swap(x):
@@ -321,15 +315,16 @@
 
 
 def depth_total(mine):
-    depth = lax.axis_size("z")
+    depth = lax.axis_size("zh")
     step = 1
     while True:
         mask = depth - 1 if 2 * step == depth else step
-        other = lax.ppermute(mine, "z", [(i, i ^ mask) for i in range(depth)])
+        other = lax.ppermute(mine, "zh", [(i, i ^ mask) for i in range(depth)])
+        total = mine.astype(F32) + other.astype(F32)
         step *= 2
         if step == depth:
-            return mine, other
-        mine = (mine.astype(F32) + other.astype(F32)).astype(BF)
+            return total
+        mine = total.astype(BF)
 
 
 def body(
@@ -362,7 +357,6 @@
     grid_far = swap(grid_latent)
     mesh_own_far = swap(mesh_own)
 
-    where = jnp.stack([band, chan, edge_count[0]])
     senders = senders.reshape(-1, LANES)
     receivers = receivers.reshape(-1, LANES)
     shape = jax.ShapeDtypeStruct
@@ -375,7 +369,7 @@
     pre = pl.pallas_call(
         sender_kernel,
         out_shape=shape((n_edges, hidden), F32),
-        in_specs=[smem] + [anywhere] * 4 + [vmem] * 4,
+        in_specs=[smem] * 2 + [anywhere] * 4 + [vmem] * 4,
         out_specs=anywhere,
         scratch_shapes=[
             pltpu.VMEM((n_grid, width), BF),
@@ -389,7 +383,7 @@
         compiler_params=params,
         cost_estimate=pl.CostEstimate(flops=SENDER_FLOPS, transcendentals=0, bytes_accessed=1 << 22),
         name="sender_step",
-    )(where, grid_latent, grid_far, edge_latent, edge_far, w_grid, w_edge, bias.reshape(1, hidden), senders)
+    )(band.reshape(1), chan.reshape(1), grid_latent, grid_far, edge_latent, edge_far, w_grid, w_edge, bias.reshape(1, hidden), senders)
 
     mesh_low, mesh_high, pre = lax.optimization_barrier((mesh_low, mesh_high, pre))
     mesh_near = (mesh_low, mesh_own, mesh_high)
@@ -397,7 +391,7 @@
     wire, cot_own, cot_far, seg_grid, rim_low, rim_mid, rim_high = pl.pallas_call(
         edge_kernel,
         out_shape=(
-            shape((16, 256 + TAIL, LANES), BF),
+            shape((MEMBERS, 2 * ROWS + TAIL, LANES), BF),
             shape((half_edges, hidden), BF),
             shape((half_edges, hidden), BF),
             shape((n_grid, hidden), BF),
@@ -405,7 +399,7 @@
             shape((2 * piece, hidden), F32),
             shape((2 * piece, hidden), BF),
         ),
-        in_specs=[smem] + [anywhere] * 10 + [vmem] * 2 + [anywhere] + [vmem] * 2,
+        in_specs=[smem] * 3 + [anywhere] * 10 + [vmem] * 2 + [anywhere] + [vmem] * 2,
         out_specs=(anywhere,) * 7,
         scratch_shapes=[
             pltpu.VMEM((n_grid, width), BF),
@@ -419,10 +413,10 @@
             pltpu.VMEM((n_grid + pad_mesh, hidden), F32),
             pltpu.VMEM((pad_mesh, hidden), F32),
             pltpu.VMEM((width, hidden), F32),
-            pltpu.VMEM((1, hidden), F32),
+            pltpu.VMEM((8, hidden), F32),
             pltpu.VMEM((n_edges, hidden), BF),
             pltpu.VMEM((n_grid, hidden), BF),
-            pltpu.VMEM((16, 256 + TAIL, LANES), BF),
+            pltpu.VMEM((MEMBERS, 2 * ROWS + 16, LANES), BF),
             pltpu.VMEM((2 * piece, hidden), BF),
             pltpu.VMEM((2 * piece, hidden), F32),
             pltpu.VMEM((2 * piece, hidden), BF),
@@ -433,7 +427,9 @@
         cost_estimate=pl.CostEstimate(flops=EDGE_FLOPS, transcendentals=1 << 20, bytes_accessed=1 << 23),
         name="edge_step",
     )(
-        where,
+        band.reshape(1),
+        chan.reshape(1),
+        edge_count,
         grid_latent,
         grid_far,
         edge_latent,
@@ -449,49 +445,46 @@
 
     from_low = pair_swap(rim_low, 0)
     from_high = pair_swap(rim_high, 1)
-    arrived = lax.all_to_all(wire, PLANE, 0, 0, tiled=True)
+    arrived = lax.all_to_all(wire, GROUP, 0, 0, tiled=True)
     edge_term = dot_t(cot_far, w_edge).astype(BF)
     grid_term = dot_t(seg_grid[half_grid:], w_grid).astype(BF)
     edge_back = swap(edge_term)
     grid_back = swap(grid_term)
     total = arrived.astype(F32).sum(axis=0).astype(BF)
     total, from_low, from_high, _, _ = lax.optimization_barrier((total, from_low, from_high, edge_term, grid_term))
-    mine, other = depth_total(total)
-    spread, grad_bias = pl.pallas_call(
-        last_sum_kernel,
-        out_shape=(shape((16, 128, hidden), BF), shape((1, hidden), F32)),
-        in_specs=[vmem] * 2,
-        out_specs=(vmem,) * 2,
-        name="last_sum",
-    )(mine, other)
-    everyone = lax.all_to_all(spread, PLANE, 0, 0, tiled=True)
+    total = depth_total(total)
+    grad_bias = total[2 * ROWS : 2 * ROWS + 2].reshape(hidden)
+    chunk = jnp.concatenate([total[:ROWS], total[ROWS : 2 * ROWS]], axis=1).astype(BF)
+    spread = jnp.broadcast_to(chunk[None], (MEMBERS, ROWS, hidden))
+    everyone = lax.all_to_all(spread, GROUP, 0, 0, tiled=True)
 
     grad_edge = (dot_t(cot_own, w_edge) + edge_back.astype(F32)).astype(BF)
     grad_grid = (dot_t(seg_grid[:half_grid], w_grid) + grid_back.astype(F32)).astype(BF)
     seg_mesh = (rim_mid + from_low.astype(F32) + from_high.astype(F32)).astype(BF)
-    seg_mesh, _ = lax.optimization_barrier((seg_mesh, grad_bias))
+    seg_mesh, _ = lax.optimization_barrier((seg_mesh, chunk))
     mesh_back = swap(dot_t(seg_mesh[piece:], w_mesh).astype(BF))
     grad_mesh = (dot_t(seg_mesh[:piece], w_mesh) + mesh_back.astype(F32)).astype(BF)
 
     def rows_of(start, stop):
         return everyone[start:stop].astype(F32).reshape(-1, hidden)
 
+    q = MEMBERS // 4
     return (
         grad_grid,
         grad_edge,
         grad_mesh,
-        rows_of(0, 4),
-        rows_of(4, 8),
-        rows_of(8, 12),
-        grad_bias.reshape(hidden),
-        jnp.concatenate([rows_of(12, 14), rows_of(14, 16)], axis=1),
+        rows_of(0, q),
+        rows_of(q, 2 * q),
+        rows_of(2 * q, 3 * q),
+        grad_bias,
+        jnp.concatenate([rows_of(3 * q, 3 * q + q // 2), rows_of(3 * q + q // 2, 4 * q)], axis=1),
     )
 
 
 def solution(mesh):
     bands, chans = (mesh.shape["band"], mesh.shape["chan"])
     side = 4
-    inner = Mesh(np.asarray(mesh.devices).reshape(bands // side**2, side, side, chans), (*BAND, "chan"))
+    inner = Mesh(np.asarray(mesh.devices).reshape(bands // (2 * side**2), 2, side, side, chans), (*BAND, "chan"))
     every = P((*BAND, "chan"), None)
     return jax.shard_map(
         body,

time: 112 us -> 106 us (0.946)
  waiting for transfers between devices: 27.9 us -> 25.6 us
  Pallas kernels: 28.1 us -> 26 us
  other arithmetic: 5.78 us -> 4.05 us
    ppermute x3 -> x2, waiting for transfers between devices: 7.85 us -> 4.05 us  [depth_total(): other = lax.ppermute(mine, 'zh', [(i, i ^ mask) for i in range(depth)])]
    ppermute x4, waiting for transfers between devices: 0.01 us -> 3.59 us  [pair_swap(): return lax.ppermute(x, BAND, pairs + [(j, i) for i, j in pairs])]
    all_to_all x2, waiting for transfers between devices: 18.4 us -> 16.2 us  [the longest x1 8.51 us: body(): arrived = lax.all_to_all(wire, GROUP, 0, 0, tiled=True)]
    pallas_call x2 -> x1, Pallas kernels: 20.6 us -> 18.5 us  [body(): pl.pallas_call(edge_kernel, out_shape=(shape((MEMBERS, 2 * ROWS + TAIL, L...]
    convert_element_type x1, other arithmetic: 1.22 us -> 0.05 us  [body(): (rim_mid + from_low.astype(F32) + from_high.astype(F32)).astype(BF)]
    ppermute x3 -> x2, starting transfers between devices: 9.04 us -> 7.95 us  [depth_total(): other = lax.ppermute(mine, 'zh', [(i, i ^ mask) for i in range(depth)])]
    unnamed x32 -> x40, local copies, waits for them, and re-layouts: 2.6 us -> 1.99 us
  transfers between devices with their start and end apart: 17 -> 16, of which waited for: 7 -> 11; matrix products, arithmetic and copies ran while one was open for 9% -> 9% of each run, Pallas kernels for 9% -> 7%
where the time goes in v4:
time: 106 us; the launch traced here: 105 us
  starting transfers between devices  37.4 us (35%)
  Pallas kernels  26 us (25%)
  waiting for transfers between devices  25.6 us (24%)
  matrix products  6.79 us (6%)
  other arithmetic  4.05 us (4%)
  local copies, waits for them, and re-layouts  3.74 us (4%)
  between operations  1.64 us (2%)
    pallas_call x1, Pallas kernels, body(): pl.pallas_call(edge_kernel, out_shape=(shape((MEMBERS, 2 * ROWS + TAIL, L...  18.5 us
    ppermute x4, starting transfers between devices, pair_swap(): return lax.ppermute(x, BAND, pairs + [(j, i) for i, j in pairs])  14.5 us
    all_to_all x1, waiting for transfers between devices, body(): arrived = lax.all_to_all(wire, GROUP, 0, 0, tiled=True)  8.51 us
    all_to_all x1, starting transfers between devices, body(): arrived = lax.all_to_all(wire, GROUP, 0, 0, tiled=True)  7.98 us
    ppermute x2, starting transfers between devices, depth_total(): other = lax.ppermute(mine, 'zh', [(i, i ^ mask) for i in range(depth)])  7.95 us
    all_to_all x1, waiting for transfers between devices, body(): everyone = lax.all_to_all(spread, GROUP, 0, 0, tiled=True)  7.66 us
    pallas_call x1, Pallas kernels, body(): pl.pallas_call(sender_kernel, out_shape=shape((n_edges, hidden), F32), in...  7.43 us
    dot_general x6, matrix products, dot_t(): lax.dot_general(a, b, (((1,), (1,)), ((), ())), preferred_element_type=F32)  6.79 us
  transfers between devices with their start and end apart: 16, of which 11 were waited for; matrix products, arithmetic and copies ran while one was open for 9% of the time, Pallas kernels for 7%

profile of v4, /device:TPU:32, one launch (start us, length us, event | category | flops | bytes accessed | tf_op | source)
XLA Modules:
  0.0 105.1 jit_solution(2147761309936084986)
XLA Ops:
  0.6 0.1 collective-permute-start.1
  0.7 0.5 collective-permute-start
  1.2 1.0 pad_maximum_fusion.m1
  2.3 0.0 copy-start.8
  2.3 0.2 collective-permute-start.5
  2.5 6.7 %collective-permute-start.3 = (bf16[2,160,512]{2,1,0:T(8,128)(2,1)S(1)}, bf16[2,160,512]{2,1,0:T(8,128)(2,1)S(1)}, u32[]{:S(2)}, u32[]{:S(2)}) collective-permute-start(bf16[2,160,512]{2,1,0:T(8,128)(2,1)S(1)} %pad_maximum_fusion.m1), channel_id=1, source_target_pairs={{2,4},{6,8},{10,12},{14,16},{18,20},{22,24},{26,28},{30,32},{34,36... | collective-permute-start | bytes 983048 | tf_op jit(solution)/shard_map/ppermute | solution.py:314
  9.1 0.1 collective-permute-start.2
  9.2 0.0 collective-permute-done.grid_far
  9.2 0.0 copy-start.14
  9.3 0.0 collective-permute-done.1.edge_far
  9.3 0.0 copy-start.13
  9.3 0.8 copy-done.14
  10.1 0.4 copy-done.13
  10.5 7.4 %sender_step.1.pre_in = f32[2304,256]{1,0:T(8,128)} custom-call(s32[1]{0:T(128)} %bitcast.band, s32[1]{0:T(128)} %bitcast.1.chan, bf16[576,512]{1,0:T(8,128)(2,1)} %grid_own.3, bf16[576,512]{1,0:T(8,128)(2,1)} %copy-done.14, bf16[1152,512]{1,0:T(8,128)(2,1)} %edge_own.3, bf16[1152,512]{1,0:T(8,128)(2,1)} %copy-done.13, bf16[512,256]{1,0:T(8,128)(2,1)} %w_grid.1, ...), custom_call_target="tpu_custom_call" | custom-call | flops 4000000000 | bytes 4194304 | tf_op jit(solution)/shard_map/sender_step/pallas_call | solution.py:369
  17.9 0.7 collective-permute-done.3.m2
  18.6 0.4 collective-permute-done.2.m0
  19.0 0.0 collective-permute-start.4
  19.0 0.5 collective-permute-start.6
  20.1 0.0 collective-permute-done.5.m4
  20.1 0.4 collective-permute-done.4.m3
  20.6 0.5 collective-permute-done.6.m5
  21.1 0.2 copy-done.18
  21.3 0.5 copy-done.19
  21.8 18.5 %edge_step.1 = (bf16[32,136,128]{2,1,0:T(8,128)(2,1)}, bf16[1152,256]{1,0:T(8,128)(2,1)}, bf16[1152,256]{1,0:T(8,128)(2,1)}, bf16[1152,256]{1,0:T(8,128)(2,1)}, ...) custom-call(s32[1]{0:T(128)} %bitcast.band, s32[1]{0:T(128)} %bitcast.1.chan, ...), custom_call_target="tpu_custom_call" | custom-call | flops 8999999488 | bytes 8388608 | tf_op jit(solution)/shard_map/edge_step/pallas_call | solution.py:391
  40.3 0.0 copy-start.2
  40.4 8.0 %all-to-all-start = ((bf16[32,136,128]{2,1,0:T(8,128)(2,1)}), bf16[32,136,128]{2,1,0:T(8,128)(2,1)S(1)}, u32[]{:S(2)}, u32[]{:S(2)}) async-start(bf16[32,136,128]{2,1,0:T(8,128)(2,1)} %get-tuple-element.28), calls=%async_computation | async-start | bytes 2228224 | tf_op jit(solution)/shard_map/all_to_all | solution.py:448
  48.3 0.0 copy-start.1
  48.4 1.6 %collective-permute-start.9 = (bf16[320,256]{1,0:T(8,128)(2,1)}, bf16[320,256]{1,0:T(8,128)(2,1)S(1)}, u32[]{:S(2)}, u32[]{:S(2)}) collective-permute-start(bf16[320,256]{1,0:T(8,128)(2,1)} %get-tuple-element.29), channel_id=1, source_target_pairs={{0,2},{4,6},{8,10},{12,14},{16,18},{20,22},{24,26},{28,30},{32,34}... | collective-permute-start | bytes 491528 | tf_op jit(solution)/shard_map/ppermute | solution.py:314
  49.9 6.3 %collective-permute-start.10 = (bf16[320,256]{1,0:T(8,128)(2,1)}, bf16[320,256]{1,0:T(8,128)(2,1)S(1)}, u32[]{:S(2)}, u32[]{:S(2)}) collective-permute-start(bf16[320,256]{1,0:T(8,128)(2,1)} %get-tuple-element.30), channel_id=1, source_target_pairs={{2,4},{6,8},{10,12},{14,16},{18,20},{22,24},{26,28},{30,32},{34,36... | collective-permute-start | bytes 491528 | tf_op jit(solution)/shard_map/ppermute | solution.py:314
  56.2 0.0 copy-done.2
  56.2 0.0 copy-done.6
  56.2 0.5 convolution_convert_fusion
  56.7 1.2 %convolution_convert_fusion.1 = bf16[576,512]{1,0:T(8,128)(2,1)} fusion(bf16[512,256]{1,0:T(8,128)(2,1)S(1)} %copy-done.1, bf16[1152,256]{1,0:T(8,128)(2,1)S(1)} %copy-done.4), kind=kOutput, calls=%fused_computation.5 | convolution fusion | flops 151289856 | bytes 1146880 | tf_op jit(solution)/shard_map/dot_general | solution.py:29
  57.9 8.5 %all-to-all-done = bf16[32,136,128]{2,1,0:T(8,128)(2,1)S(1)} async-done(((bf16[32,136,128]{2,1,0:T(8,128)(2,1)}), bf16[32,136,128]{2,1,0:T(8,128)(2,1)S(1)}, u32[]{:S(2)}, u32[]{:S(2)}) %all-to-all-start) | async-done | bytes 1114144 | tf_op jit(solution)/shard_map/all_to_all | solution.py:448
  66.4 0.2 reduce_sum.12
  66.6 0.3 collective-permute-done.9
  66.9 2.2 %collective-permute-done.10 = bf16[320,256]{1,0:T(8,128)(2,1)S(1)} collective-permute-done((bf16[320,256]{1,0:T(8,128)(2,1)}, bf16[320,256]{1,0:T(8,128)(2,1)S(1)}, u32[]{:S(2)}, u32[]{:S(2)}) %collective-permute-start.10) | collective-permute-done | bytes 163872 | tf_op jit(solution)/shard_map/ppermute | solution.py:314
  69.1 4.5 %collective-permute-start.12 = (bf16[136,128]{1,0:T(8,128)(2,1)S(1)}, bf16[136,128]{1,0:T(8,128)(2,1)S(1)}, u32[]{:S(2)}, u32[]{:S(2)}) collective-permute-start(bf16[136,128]{1,0:T(8,128)(2,1)S(1)} %reduce_sum.12), channel_id=1, source_target_pairs={{0,64},{64,0},{128,192},{192,128},{1,65},{65,1},{129,193},{193,129... | collective-permute-start | bytes 104456 | tf_op jit(solution)/shard_map/ppermute | solution.py:322
  73.6 1.9 %collective-permute-done.12 = bf16[136,128]{1,0:T(8,128)(2,1)S(1)} collective-permute-done((bf16[136,128]{1,0:T(8,128)(2,1)S(1)}, bf16[136,128]{1,0:T(8,128)(2,1)S(1)}, u32[]{:S(2)}, u32[]{:S(2)}) %collective-permute-start.12) | collective-permute-done | bytes 34848 | tf_op jit(solution)/shard_map/ppermute | solution.py:322
  75.5 3.5 %collective-permute-start.13 = (bf16[136,128]{1,0:T(8,128)(2,1)S(1)}, bf16[136,128]{1,0:T(8,128)(2,1)S(1)}, u32[]{:S(2)}, u32[]{:S(2)}) collective-permute-start(bf16[136,128]{1,0:T(8,128)(2,1)S(1)} %add_convert_fusion.2), channel_id=1, source_target_pairs={{0,192},{64,128},{128,64},{192,0},{1,193},{65,129},{129,65},{193,1... | collective-permute-start | bytes 104456 | tf_op jit(solution)/shard_map/ppermute | solution.py:322
  79.0 0.0 collective-permute-start.7
  79.0 0.5 collective-permute-start.8
  79.5 2.1 %collective-permute-done.13 = bf16[136,128]{1,0:T(8,128)(2,1)S(1)} collective-permute-done((bf16[136,128]{1,0:T(8,128)(2,1)S(1)}, bf16[136,128]{1,0:T(8,128)(2,1)S(1)}, u32[]{:S(2)}, u32[]{:S(2)}) %collective-permute-start.13) | collective-permute-done | bytes 34848 | tf_op jit(solution)/shard_map/ppermute | solution.py:322
  81.7 1.1 %broadcast_in_dim.2 = bf16[32,64,256]{2,1,0:T(8,128)(2,1)} broadcast(bf16[64,256]{1,0:T(8,128)(2,1)S(1)} %pad_maximum_fusion.1), dimensions={1,2} | broadcast | bytes 1081344 | tf_op jit(solution)/shard_map/broadcast_in_dim | solution.py:458
  82.8 5.0 %all-to-all-start.1 = ((bf16[32,64,256]{2,1,0:T(8,128)(2,1)}), bf16[32,64,256]{2,1,0:T(8,128)(2,1)S(1)}, u32[]{:S(2)}, u32[]{:S(2)}) async-start(bf16[32,64,256]{2,1,0:T(8,128)(2,1)} %broadcast_in_dim.2), calls=%async_computation.1 | async-start | bytes 2097152 | tf_op jit(solution)/shard_map/all_to_all | solution.py:459
  87.8 0.0 copy-start.3
  87.9 0.0 collective-permute-done.7
  87.9 2.5 %fusion.1 = bf16[576,512]{1,0:T(8,128)(2,1)} fusion(bf16[512,256]{1,0:T(8,128)(2,1)} %w_grid.1, bf16[576,512]{1,0:T(8,128)(2,1)} %collective-permute-done.7, bf16[1152,256]{1,0:T(8,128)(2,1)} %get-tuple-element.24), kind=kOutput, calls=%fused_computation.4 | convolution fusion | flops 151879680 | bytes 1736704 | tf_op jit(solution)/shard_map/dot_general | solution.py:29
  90.4 0.0 collective-permute-done.8
  90.4 0.0 copy-start.10
  90.4 0.0 copy-start.12
  90.4 0.0 copy-start
  90.4 1.5 %fusion = bf16[1152,512]{1,0:T(8,128)(2,1)} fusion(bf16[1152,256]{1,0:T(8,128)(2,1)S(1)} %copy-done.5, bf16[512,256]{1,0:T(8,128)(2,1)S(1)} %copy-done.3, bf16[1152,512]{1,0:T(8,128)(2,1)S(1)} %collective-permute-done.8), kind=kOutput, calls=%fused_computation.1 | convolution fusion | flops 303759360 | bytes 3211264 | tf_op jit(solution)/shard_map/dot_general | solution.py:29
  91.9 0.1 add_convert_fusion.1
  92.0 0.2 convolution_convert_fusion.2
  92.2 0.1 collective-permute-start.11
  92.3 0.6 slice_bitcast_fusion
  92.9 0.8 collective-permute-done.11
  93.7 0.9 add_convert_fusion
  94.6 7.7 %all-to-all-done.1 = bf16[32,64,256]{2,1,0:T(8,128)(2,1)S(1)} async-done(((bf16[32,64,256]{2,1,0:T(8,128)(2,1)}), bf16[32,64,256]{2,1,0:T(8,128)(2,1)S(1)}, u32[]{:S(2)}, u32[]{:S(2)}) %all-to-all-start.1) | async-done | bytes 1048608 | tf_op jit(solution)/shard_map/all_to_all | solution.py:459
  102.3 0.1 fusion.11
  102.3 0.8 bitcast_convert_fusion.2
  103.2 0.9 maximum_convert_fusion
  104.1 1.1 %bitcast_convert_fusion = (f32[512,256]{1,0:T(8,128)}, f32[512,256]{1,0:T(8,128)}) fusion(bf16[8,64,256]{2,1,0:T(8,128)(2,1)S(1)} %get-tuple-element.36, bf16[8,64,256]{2,1,0:T(8,128)(2,1)S(1)} %get-tuple-element.37), kind=kLoop, calls=%fused_computation.13 | loop fusion | flops 262144 | bytes 1572864 | tf_op jit(solution)/shard_map/reshape | solution.py:469
  (30 shorter events, 0.1 us)
Async XLA Ops:
  0.6 8.6 %collective-permute-start.1 = (bf16[1152,512]{1,0:T(8,128)(2,1)}, bf16[1152,512]{1,0:T(8,128)(2,1)S(1)}, u32[]{:S(2)}, u32[]{:S(2)}) collective-permute-start(bf16[1152,512]{1,0:T(8,128)(2,1)} %edge_own.3), channel_id=1, source_target_pairs={{0,1},{1,0},{2,3},{3,2},{4,5},{5,4},{6,7},{7,6},{8,9},{9,8},{10,11... | collective-permute-start | bytes 3538952 | tf_op jit(solution)/shard_map/ppermute | solution.py:308
  0.7 8.5 %collective-permute-start = (bf16[576,512]{1,0:T(8,128)(2,1)}, bf16[576,512]{1,0:T(8,128)(2,1)S(1)}, u32[]{:S(2)}, u32[]{:S(2)}) collective-permute-start(bf16[576,512]{1,0:T(8,128)(2,1)} %grid_own.3), channel_id=1, source_target_pairs={{0,1},{1,0},{2,3},{3,2},{4,5},{5,4},{6,7},{7,6},{8,9},{9,8},{10,11... | collective-permute-start | bytes 1769480 | tf_op jit(solution)/shard_map/ppermute | solution.py:308
  2.3 15.6 %copy-start.8 = (bf16[2,160,512]{2,1,0:T(8,128)(2,1)}, bf16[2,160,512]{2,1,0:T(8,128)(2,1)S(1)}, u32[]{:S(2)}) copy-start(bf16[2,160,512]{2,1,0:T(8,128)(2,1)S(1)} %pad_maximum_fusion.m1) | copy-start | bytes 983044
  2.3 17.8 %collective-permute-start.5 = (bf16[2,160,512]{2,1,0:T(8,128)(2,1)S(1)}, bf16[2,160,512]{2,1,0:T(8,128)(2,1)S(1)}, u32[]{:S(2)}, u32[]{:S(2)}) collective-permute-start(bf16[2,160,512]{2,1,0:T(8,128)(2,1)S(1)} %pad_maximum_fusion.m1), channel_id=1, source_target_pairs={{0,1},{1,0},{2,3},{3,2},{4,5},{5,4},{6,7},{7,6},{8,9},{9,8},{10,11... | collective-permute-start | bytes 983048 | tf_op jit(solution)/shard_map/ppermute | solution.py:308
  2.5 16.1 %collective-permute-start.3 = (bf16[2,160,512]{2,1,0:T(8,128)(2,1)S(1)}, bf16[2,160,512]{2,1,0:T(8,128)(2,1)S(1)}, u32[]{:S(2)}, u32[]{:S(2)}) collective-permute-start(bf16[2,160,512]{2,1,0:T(8,128)(2,1)S(1)} %pad_maximum_fusion.m1), channel_id=1, source_target_pairs={{2,4},{6,8},{10,12},{14,16},{18,20},{22,24},{26,28},{30,32},{34,36... | collective-permute-start | bytes 983048 | tf_op jit(solution)/shard_map/ppermute | solution.py:314
  9.1 9.8 %collective-permute-start.2 = (bf16[2,160,512]{2,1,0:T(8,128)(2,1)S(1)}, bf16[2,160,512]{2,1,0:T(8,128)(2,1)S(1)}, u32[]{:S(2)}, u32[]{:S(2)}) collective-permute-start(bf16[2,160,512]{2,1,0:T(8,128)(2,1)S(1)} %pad_maximum_fusion.m1), channel_id=1, source_target_pairs={{0,2},{4,6},{8,10},{12,14},{16,18},{20,22},{24,26},{28,30},{32,34}... | collective-permute-start | bytes 983048 | tf_op jit(solution)/shard_map/ppermute | solution.py:314
  9.2 0.8 copy-start.14
  9.3 1.2 %copy-start.13 = (bf16[1152,512]{1,0:T(8,128)(2,1)}, bf16[1152,512]{1,0:T(8,128)(2,1)S(1)}, u32[]{:S(2)}) copy-start(bf16[1152,512]{1,0:T(8,128)(2,1)S(1)} %collective-permute-done.1.edge_far) | copy-start | bytes 3538948
  18.6 2.5 %copy-start.16 = (bf16[2,160,512]{2,1,0:T(8,128)(2,1)}, bf16[2,160,512]{2,1,0:T(8,128)(2,1)S(1)}, u32[]{:S(2)}) copy-start(bf16[2,160,512]{2,1,0:T(8,128)(2,1)S(1)} %collective-permute-done.3.m2) | copy-start | bytes 983044
  18.9 2.1 %copy-start.17 = (bf16[2,160,512]{2,1,0:T(8,128)(2,1)}, bf16[2,160,512]{2,1,0:T(8,128)(2,1)S(1)}, u32[]{:S(2)}) copy-start(bf16[2,160,512]{2,1,0:T(8,128)(2,1)S(1)} %collective-permute-done.2.m0) | copy-start | bytes 983044
  19.0 1.6 %collective-permute-start.4 = (bf16[2,160,512]{2,1,0:T(8,128)(2,1)S(1)}, bf16[2,160,512]{2,1,0:T(8,128)(2,1)S(1)}, u32[]{:S(2)}, u32[]{:S(2)}) collective-permute-start(bf16[2,160,512]{2,1,0:T(8,128)(2,1)S(1)} %collective-permute-done.2.m0), channel_id=1, source_target_pairs={{0,1},{1,0},{2,3},{3,2},{4,5},{5,4},{6,7},{7,6},{8,9},{9,8},{10,11... | collective-permute-start | bytes 983048 | tf_op jit(solution)/shard_map/ppermute | solution.py:308
  19.0 2.1 %collective-permute-start.6 = (bf16[2,160,512]{2,1,0:T(8,128)(2,1)S(1)}, bf16[2,160,512]{2,1,0:T(8,128)(2,1)S(1)}, u32[]{:S(2)}, u32[]{:S(2)}) collective-permute-start(bf16[2,160,512]{2,1,0:T(8,128)(2,1)S(1)} %collective-permute-done.3.m2), channel_id=1, source_target_pairs={{0,1},{1,0},{2,3},{3,2},{4,5},{5,4},{6,7},{7,6},{8,9},{9,8},{10,11... | collective-permute-start | bytes 983048 | tf_op jit(solution)/shard_map/ppermute | solution.py:308
  20.1 0.9 copy-start.15
  20.6 0.7 copy-start.18
  21.1 0.7 copy-start.19
  40.3 15.8 %copy-start.2 = (bf16[512,256]{1,0:T(8,128)(2,1)S(1)}, bf16[512,256]{1,0:T(8,128)(2,1)}, u32[]{:S(2)}) copy-start(bf16[512,256]{1,0:T(8,128)(2,1)} %w_edge.1) | copy-start | bytes 786436
  40.3 15.8 %copy-start.6 = (bf16[1152,256]{1,0:T(8,128)(2,1)S(1)}, bf16[1152,256]{1,0:T(8,128)(2,1)}, u32[]{:S(2)}) copy-start(bf16[1152,256]{1,0:T(8,128)(2,1)} %get-tuple-element.26) | copy-start | bytes 1769476
  40.4 26.0 %all-to-all-start = ((bf16[32,136,128]{2,1,0:T(8,128)(2,1)}), bf16[32,136,128]{2,1,0:T(8,128)(2,1)S(1)}, u32[]{:S(2)}, u32[]{:S(2)}) async-start(bf16[32,136,128]{2,1,0:T(8,128)(2,1)} %get-tuple-element.28), calls=%async_computation | async-start | bytes 2228224 | tf_op jit(solution)/shard_map/all_to_all | solution.py:448
  48.3 8.4 %copy-start.1 = (bf16[512,256]{1,0:T(8,128)(2,1)S(1)}, bf16[512,256]{1,0:T(8,128)(2,1)}, u32[]{:S(2)}) copy-start(bf16[512,256]{1,0:T(8,128)(2,1)} %w_grid.1) | copy-start | bytes 786436
  48.4 8.4 %copy-start.4 = (bf16[1152,256]{1,0:T(8,128)(2,1)S(1)}, bf16[1152,256]{1,0:T(8,128)(2,1)}, u32[]{:S(2)}) copy-start(bf16[1152,256]{1,0:T(8,128)(2,1)} %get-tuple-element.24) | copy-start | bytes 1769476
  48.4 18.5 %collective-permute-start.9 = (bf16[320,256]{1,0:T(8,128)(2,1)}, bf16[320,256]{1,0:T(8,128)(2,1)S(1)}, u32[]{:S(2)}, u32[]{:S(2)}) collective-permute-start(bf16[320,256]{1,0:T(8,128)(2,1)} %get-tuple-element.29), channel_id=1, source_target_pairs={{0,2},{4,6},{8,10},{12,14},{16,18},{20,22},{24,26},{28,30},{32,34}... | collective-permute-start | bytes 491528 | tf_op jit(solution)/shard_map/ppermute | solution.py:314
  49.9 19.2 %collective-permute-start.10 = (bf16[320,256]{1,0:T(8,128)(2,1)}, bf16[320,256]{1,0:T(8,128)(2,1)S(1)}, u32[]{:S(2)}, u32[]{:S(2)}) collective-permute-start(bf16[320,256]{1,0:T(8,128)(2,1)} %get-tuple-element.30), channel_id=1, source_target_pairs={{2,4},{6,8},{10,12},{14,16},{18,20},{22,24},{26,28},{30,32},{34,36... | collective-permute-start | bytes 491528 | tf_op jit(solution)/shard_map/ppermute | solution.py:314
  66.9 12.1 %copy-start.9 = (bf16[320,256]{1,0:T(8,128)(2,1)}, bf16[320,256]{1,0:T(8,128)(2,1)S(1)}, u32[]{:S(2)}) copy-start(bf16[320,256]{1,0:T(8,128)(2,1)S(1)} %collective-permute-done.9) | copy-start | bytes 491524
  69.1 9.9 %copy-start.11 = (bf16[320,256]{1,0:T(8,128)(2,1)}, bf16[320,256]{1,0:T(8,128)(2,1)S(1)}, u32[]{:S(2)}) copy-start(bf16[320,256]{1,0:T(8,128)(2,1)S(1)} %collective-permute-done.10) | copy-start | bytes 491524
  69.1 6.4 %collective-permute-start.12 = (bf16[136,128]{1,0:T(8,128)(2,1)S(1)}, bf16[136,128]{1,0:T(8,128)(2,1)S(1)}, u32[]{:S(2)}, u32[]{:S(2)}) collective-permute-start(bf16[136,128]{1,0:T(8,128)(2,1)S(1)} %reduce_sum.12), channel_id=1, source_target_pairs={{0,64},{64,0},{128,192},{192,128},{1,65},{65,1},{129,193},{193,129... | collective-permute-start | bytes 104456 | tf_op jit(solution)/shard_map/ppermute | solution.py:322
  75.5 6.1 %collective-permute-start.13 = (bf16[136,128]{1,0:T(8,128)(2,1)S(1)}, bf16[136,128]{1,0:T(8,128)(2,1)S(1)}, u32[]{:S(2)}, u32[]{:S(2)}) collective-permute-start(bf16[136,128]{1,0:T(8,128)(2,1)S(1)} %add_convert_fusion.2), channel_id=1, source_target_pairs={{0,192},{64,128},{128,64},{192,0},{1,193},{65,129},{129,65},{193,1... | collective-permute-start | bytes 104456 | tf_op jit(solution)/shard_map/ppermute | solution.py:322
  79.0 8.9 %collective-permute-start.7 = (bf16[576,512]{1,0:T(8,128)(2,1)}, bf16[576,512]{1,0:T(8,128)(2,1)}, u32[]{:S(2)}, u32[]{:S(2)}) collective-permute-start(bf16[576,512]{1,0:T(8,128)(2,1)} %convolution_convert_fusion.1), channel_id=1, source_target_pairs={{0,1},{1,0},{2,3},{3,2},{4,5},{5,4},{6,7},{7,6},{8,9},{9,8},{10,11... | collective-permute-start | bytes 1769480 | tf_op jit(solution)/shard_map/ppermute | solution.py:308
  79.0 11.4 %collective-permute-start.8 = (bf16[1152,512]{1,0:T(8,128)(2,1)S(1)}, bf16[1152,512]{1,0:T(8,128)(2,1)S(1)}, u32[]{:S(2)}, u32[]{:S(2)}) collective-permute-start(bf16[1152,512]{1,0:T(8,128)(2,1)S(1)} %convolution_convert_fusion), channel_id=1, source_target_pairs={{0,1},{1,0},{2,3},{3,2},{4,5},{5,4},{6,7},{7,6},{8,9},{9,8},{10,11... | collective-permute-start | bytes 3538952 | tf_op jit(solution)/shard_map/ppermute | solution.py:308
  82.8 19.5 %all-to-all-start.1 = ((bf16[32,64,256]{2,1,0:T(8,128)(2,1)}), bf16[32,64,256]{2,1,0:T(8,128)(2,1)S(1)}, u32[]{:S(2)}, u32[]{:S(2)}) async-start(bf16[32,64,256]{2,1,0:T(8,128)(2,1)} %broadcast_in_dim.2), calls=%async_computation.1 | async-start | bytes 2097152 | tf_op jit(solution)/shard_map/all_to_all | solution.py:459
  87.8 2.5 %copy-start.3 = (bf16[512,256]{1,0:T(8,128)(2,1)S(1)}, bf16[512,256]{1,0:T(8,128)(2,1)}, u32[]{:S(2)}) copy-start(bf16[512,256]{1,0:T(8,128)(2,1)} %w_edge.1) | copy-start | bytes 786436
  87.9 2.5 %copy-start.5 = (bf16[1152,256]{1,0:T(8,128)(2,1)S(1)}, bf16[1152,256]{1,0:T(8,128)(2,1)}, u32[]{:S(2)}) copy-start(bf16[1152,256]{1,0:T(8,128)(2,1)} %get-tuple-element.25) | copy-start | bytes 1769476
  90.4 1.6 %copy-start.7 = (f32[320,256]{1,0:T(8,128)S(1)}, f32[320,256]{1,0:T(8,128)}, u32[]{:S(2)}) copy-start(f32[320,256]{1,0:T(8,128)} %get-tuple-element.27) | copy-start | bytes 983044
  90.4 1.6 %copy-start.10 = (bf16[320,256]{1,0:T(8,128)(2,1)S(1)}, bf16[320,256]{1,0:T(8,128)(2,1)}, u32[]{:S(2)}) copy-start(bf16[320,256]{1,0:T(8,128)(2,1)} %copy-done.9) | copy-start | bytes 491524
  90.4 1.5 %copy-start.12 = (bf16[320,256]{1,0:T(8,128)(2,1)S(1)}, bf16[320,256]{1,0:T(8,128)(2,1)}, u32[]{:S(2)}) copy-start(bf16[320,256]{1,0:T(8,128)(2,1)} %copy-done.11) | copy-start | bytes 491524
  90.4 1.6 %copy-start = (bf16[512,256]{1,0:T(8,128)(2,1)S(1)}, bf16[512,256]{1,0:T(8,128)(2,1)}, u32[]{:S(2)}) copy-start(bf16[512,256]{1,0:T(8,128)(2,1)} %w_mesh.1) | copy-start | bytes 786436
  92.2 1.5 %collective-permute-start.11 = (bf16[160,512]{1,0:T(8,128)(2,1)S(1)}, bf16[160,512]{1,0:T(8,128)(2,1)S(1)}, u32[]{:S(2)}, u32[]{:S(2)}) collective-permute-start(bf16[160,512]{1,0:T(8,128)(2,1)S(1)} %convolution_convert_fusion.2), channel_id=1, source_target_pairs={{0,1},{1,0},{2,3},{3,2},{4,5},{5,4},{6,7},{7,6},{8,9},{9,8},{10,11... | collective-permute-start | bytes 491528 | tf_op jit(solution)/shard_map/ppermute | solution.py:308

commit v5 on v4

--- a/solution.py
+++ b/solution.py
@@ -14,6 +14,7 @@
 GROUP = ("zl", "y", "x")
 LANES = 128
 EDGE_BLOCK = 768
+UNIT = 384
 TAIL = 8
 ROWS = 64
 MEMBERS = 32
@@ -79,58 +80,55 @@
     w_edge,
     bias,
     senders,
-    pre_out,
+    pre,
     grid,
     edge,
-    pre,
     table,
     left,
     in_sems,
-    out_sems,
 ):
     where = (band[0], chan[0])
     half_edges = edge_own.shape[0]
     half_grid = grid_own.shape[0]
     n_grid = 2 * half_grid
     block = left.shape[0]
-    fetches = copies(
-        (
-            (grid_own, grid.at[0:half_grid]),
-            (grid_far, grid.at[half_grid:]),
-            (edge_own, edge.at[0:half_edges]),
-            (edge_far, edge.at[half_edges:]),
-        ),
-        in_sems,
-    )
+    fetches = copies(((grid_own, grid), (edge_own, edge)), in_sems)
     for f in fetches:
         f.start()
     table[n_grid:] = w_edge[...]
+    table[half_grid:n_grid] = dot(grid_far[...], w_grid[...]).astype(BF)
     fetches[0].wait()
+    table[0:half_grid] = dot(grid[...], w_grid[...]).astype(BF)
     fetches[1].wait()
-    table[0:n_grid] = dot(grid[...], w_grid[...]).astype(BF)
-    fetches[2].wait()
-    fetches[3].wait()
     groups = 2 * half_edges // LANES
     per = block // LANES
-    steps = 2 * half_edges // block
+    units = block // UNIT
+    near = half_edges // UNIT
 
     def step(i, carry):
         rows = pl.ds(pl.multiple_of(i * block, block), block)
+        for h in range(units):
+            at = i * units + h
+            mine = slice(h * UNIT, (h + 1) * UNIT)
+
+            @pl.when(at < near)
+            def _():
+                left[mine, n_grid:] = edge[pl.ds(pl.multiple_of(at * UNIT, UNIT), UNIT), :]
+
+            @pl.when(at >= near)
+            def _():
+                left[mine, n_grid:] = edge_far[pl.ds(pl.multiple_of((at - near) * UNIT, UNIT), UNIT), :]
+
         for c in range(per):
             at = index_row(i * per + c, groups, where)
             row = local_senders(senders[pl.ds(at, 1), :], where, half_grid)
             column = jnp.broadcast_to(row, (LANES, LANES)).T
             for k in range(n_grid // LANES):
                 left[c * LANES : (c + 1) * LANES, k * LANES : (k + 1) * LANES] = one_hot(column, k * LANES)
-        left[:, n_grid:] = edge[rows, :]
         pre[rows, :] = dot(left[...], table[...]) + bias[...]
-        pltpu.make_async_copy(pre.at[rows], pre_out.at[rows], out_sems.at[i]).start()
         return carry
 
-    lax.fori_loop(0, steps, step, 0)
-    for k in range(steps):
-        rows = pl.ds(k * block, block)
-        pltpu.make_async_copy(pre.at[rows], pre_out.at[rows], out_sems.at[k]).wait()
+    lax.fori_loop(0, 2 * half_edges // block, step, 0)
 
 
 def edge_kernel(
@@ -149,19 +147,17 @@
     m5,
     w_mesh,
     w_out,
-    pre_in,
+    pre_part,
     senders,
     receivers,
     wire_out,
-    cot_own,
-    cot_far,
-    seg_out,
+    cots,
+    seg_grid,
     rim_low,
     rim_mid,
     rim_high,
     grid,
     edge,
-    pre_part,
     lat,
     cot,
     table,
@@ -171,13 +167,11 @@
     act_sums,
     edge_sum,
     bias_sum,
-    cots,
-    seg_grid,
     wire,
     low_v,
-    mid_v,
     high_v,
     in_sems,
+    edge_sems,
     out_sems,
 ):
     where = (band[0], chan[0], count[0])
@@ -190,19 +184,22 @@
     n_rows = n_grid + pad_mesh
     block = left.shape[0]
     hidden = w_mesh.shape[1]
-    pieces = (m0, m1, m2, m3, m4, m5)
-    lats = [(m.at[0], lat.at[k * piece : (k + 1) * piece]) for k, m in enumerate(pieces)]
-    cot_pairs = [(m.at[1], cot.at[k * piece : (k + 1) * piece]) for k, m in enumerate(pieces)]
-    rest = [
-        (pre_in, pre_part),
-        (edge_own, edge.at[0:half_edges]),
-        (edge_far, edge.at[half_edges:]),
-        (grid_own, grid.at[0:half_grid]),
-        (grid_far, grid.at[half_grid:]),
+    near = half_edges // UNIT
+    apart = ((0, m0), (1, m1), (2, m2), (4, m4))
+    lats = [(m.at[0], lat.at[k * piece : (k + 1) * piece]) for k, m in apart]
+    cot_pairs = [(m.at[1], cot.at[k * piece : (k + 1) * piece]) for k, m in apart]
+    grids = [(grid_own, grid.at[0:half_grid]), (grid_far, grid.at[half_grid:])]
+    fetches = copies(lats + cot_pairs + grids, in_sems)
+    edges = [
+        (source.at[k * UNIT : (k + 1) * UNIT], edge.at[(k + off) * UNIT : (k + off + 1) * UNIT])
+        for source, off in ((edge_own, 0), (edge_far, near))
+        for k in range(near)
     ]
-    fetches = copies(lats + cot_pairs + rest, in_sems)
-    for f in fetches:
+    for f in fetches[0:8] + copies(edges, edge_sems) + fetches[8:]:
         f.start()
+    for k, m in ((3, m3), (5, m5)):
+        lat[k * piece : (k + 1) * piece] = m[0]
+        cot[k * piece : (k + 1) * piece] = m[1]
     if pad_mesh > n_mesh:
         lat[n_mesh:] = jnp.zeros((pad_mesh - n_mesh, lat.shape[1]), BF)
         cot[n_mesh:] = jnp.zeros((pad_mesh - n_mesh, cot.shape[1]), BF)
@@ -210,15 +207,13 @@
     act_sums[...] = jnp.zeros_like(act_sums)
     edge_sum[...] = jnp.zeros_like(edge_sum)
     bias_sum[...] = jnp.zeros_like(bias_sum)
-    for f in fetches[0:12]:
+    for f in fetches[0:8]:
         f.wait()
     table[:, 0:hidden] = dot(lat[...], w_mesh[...]).astype(BF)
     cot_terms = dot_t(cot[...], w_out[...])
     high = cot_terms.astype(BF)
     table[:, hidden : 2 * hidden] = high
     table[:, 2 * hidden :] = (cot_terms - high.astype(F32)).astype(BF)
-    for f in fetches[12:]:
-        f.wait()
     groups = 2 * half_edges // LANES
     per = block // LANES
 
@@ -248,6 +243,10 @@
         cots[rows, :] = pre_cot
         sums[...] += dot(right[...], pre_cot)
         act_sums[...] += dot(right[n_grid:, :], act)
+        for h in range(block // UNIT):
+            at = i * (block // UNIT) + h
+            unit = pl.ds(pl.multiple_of(at * UNIT, UNIT), UNIT)
+            pltpu.make_async_copy(edge_own.at[0:UNIT], edge.at[unit], edge_sems.at[at]).wait()
         edge_sum[...] += dot_rows(edge[rows, :], pre_cot)
         bias_sum[...] += pre_cot.astype(F32).reshape(block // 8, 8, hidden).sum(axis=0)
         return carry
@@ -255,7 +254,7 @@
     lax.fori_loop(0, 2 * half_edges // block, step, 0)
 
     seg_grid[...] = sums[:n_grid].astype(BF)
-    for ref, o, kind in ((low_v, 0, BF), (mid_v, 1, F32), (high_v, 2, BF)):
+    for ref, o, kind in ((low_v, 0, BF), (rim_mid, 1, F32), (high_v, 2, BF)):
         for h in range(2):
             start = n_grid + (3 * h + o) * piece
             ref[h * piece : (h + 1) * piece] = sums[start : start + piece].astype(kind)
@@ -263,19 +262,13 @@
     per_grad = w_mesh.shape[0] // rows
     parts = [slice(k * per_grad, (k + 1) * per_grad) for k in range(4)]
     stores = copies(
-        [
-            (low_v, rim_low),
-            (high_v, rim_high),
-            (seg_grid, seg_out),
-            (cots.at[0:half_edges], cot_own),
-            (cots.at[half_edges:], cot_far),
-            (mid_v, rim_mid),
-        ]
-        + [(wire.at[p, 0 : 2 * ROWS + TAIL], wire_out.at[p]) for p in parts],
+        [(low_v, rim_low), (high_v, rim_high)] + [(wire.at[p, 0 : 2 * ROWS + TAIL], wire_out.at[p]) for p in parts],
         out_sems,
     )
-    for f in stores[0:6]:
+    for f in stores[0:2]:
         f.start()
+    for f in fetches[8:]:
+        f.wait()
     sub = lax.broadcasted_iota(jnp.int32, (16, LANES), 0)
     bias_total = jnp.sum(bias_sum[...], axis=0, keepdims=True)
     low = jnp.broadcast_to(bias_total[:, :LANES], (16, LANES))
@@ -291,15 +284,15 @@
             wire[at + k, rows : 2 * rows, :] = value[:, LANES:].astype(BF)
 
     put_all(parts[2].start, edge_sum[...])
-    stores[8].start()
+    stores[4].start()
     put_all(parts[0].start, dot_rows(grid[...], seg_grid[...]))
-    stores[6].start()
+    stores[2].start()
     put_all(parts[1].start, dot_rows(lat[...], sums[n_grid:].astype(BF)))
-    stores[7].start()
+    stores[3].start()
     g = dot_rows(act_sums[...].astype(BF), cot[...])
     put_all(parts[3].start, g[:, 0:hidden])
     put_all(parts[3].start + per_grad // 2, g[:, hidden:])
-    stores[9].start()
+    stores[5].start()
     for f in stores:
         f.wait()
 
@@ -359,52 +352,64 @@
 
     senders = senders.reshape(-1, LANES)
     receivers = receivers.reshape(-1, LANES)
-    shape = jax.ShapeDtypeStruct
     vmem = pl.BlockSpec(memory_space=pltpu.VMEM)
     smem = pl.BlockSpec(memory_space=pltpu.SMEM)
-    params = pltpu.CompilerParams(vmem_limit_bytes=56 * 1024 * 1024)
+    small, large = [pltpu.CompilerParams(vmem_limit_bytes=n * 2**20) for n in (16, 32)]
+
+    def near(x):
+        return pltpu.with_memory_space_constraint(x, pltpu.VMEM)
+
+    def wide(*arrays):
+        return [pltpu.with_memory_space_constraint(x, pltpu.HBM) for x in arrays]
+
+    def scalars(*arrays):
+        return [pltpu.with_memory_space_constraint(x, pltpu.SMEM) for x in arrays]
+
     anywhere = pl.BlockSpec(memory_space=pl.ANY)
     dma = pltpu.SemaphoreType.DMA
     n_edges = 2 * half_edges
     pre = pl.pallas_call(
         sender_kernel,
-        out_shape=shape((n_edges, hidden), F32),
-        in_specs=[smem] * 2 + [anywhere] * 4 + [vmem] * 4,
-        out_specs=anywhere,
+        out_shape=pltpu.VMEM((n_edges, hidden), F32),
+        in_specs=[smem] * 2 + [anywhere, vmem] * 2 + [vmem] * 4,
+        out_specs=vmem,
+        scratch_shapes=[
+            pltpu.VMEM((half_grid, width), BF),
+            pltpu.VMEM((half_edges, width), BF),
+            pltpu.VMEM((n_grid + width, hidden), BF),
+            pltpu.VMEM((EDGE_BLOCK, n_grid + width), BF),
+            dma((2,)),
+        ],
+        compiler_params=small,
+        cost_estimate=pl.CostEstimate(flops=SENDER_FLOPS, transcendentals=0, bytes_accessed=1 << 22),
+        name="sender_step",
+    )(
+        *scalars(band.reshape(1), chan.reshape(1)),
+        *wide(grid_latent),
+        near(grid_far),
+        *wide(edge_latent),
+        near(edge_far),
+        *wide(w_grid, w_edge, bias.reshape(1, hidden), senders),
+    )
+
+    mesh_low, mesh_high, pre = lax.optimization_barrier((mesh_low, mesh_high, pre))
+    mesh_near = (mesh_low, mesh_own, mesh_high)
+    mesh_far = [near(swap(mesh_low)), *wide(mesh_own_far), near(swap(mesh_high))]
+    wire, cots, seg_grid, rim_low, rim_mid, rim_high = pl.pallas_call(
+        edge_kernel,
+        out_shape=(
+            pltpu.HBM((MEMBERS, 2 * ROWS + TAIL, LANES), BF),
+            pltpu.VMEM((n_edges, hidden), BF),
+            pltpu.VMEM((n_grid, hidden), BF),
+            pltpu.HBM((2 * piece, hidden), BF),
+            pltpu.VMEM((2 * piece, hidden), F32),
+            pltpu.HBM((2 * piece, hidden), BF),
+        ),
+        in_specs=[smem] * 3 + [anywhere] * 7 + [vmem] * 8,
+        out_specs=(anywhere, vmem, vmem, anywhere, vmem, anywhere),
         scratch_shapes=[
             pltpu.VMEM((n_grid, width), BF),
             pltpu.VMEM((n_edges, width), BF),
-            pltpu.VMEM((n_edges, hidden), F32),
-            pltpu.VMEM((n_grid + width, hidden), BF),
-            pltpu.VMEM((EDGE_BLOCK, n_grid + width), BF),
-            dma((4,)),
-            dma((n_edges // EDGE_BLOCK,)),
-        ],
-        compiler_params=params,
-        cost_estimate=pl.CostEstimate(flops=SENDER_FLOPS, transcendentals=0, bytes_accessed=1 << 22),
-        name="sender_step",
-    )(band.reshape(1), chan.reshape(1), grid_latent, grid_far, edge_latent, edge_far, w_grid, w_edge, bias.reshape(1, hidden), senders)
-
-    mesh_low, mesh_high, pre = lax.optimization_barrier((mesh_low, mesh_high, pre))
-    mesh_near = (mesh_low, mesh_own, mesh_high)
-    mesh_far = (swap(mesh_low), mesh_own_far, swap(mesh_high))
-    wire, cot_own, cot_far, seg_grid, rim_low, rim_mid, rim_high = pl.pallas_call(
-        edge_kernel,
-        out_shape=(
-            shape((MEMBERS, 2 * ROWS + TAIL, LANES), BF),
-            shape((half_edges, hidden), BF),
-            shape((half_edges, hidden), BF),
-            shape((n_grid, hidden), BF),
-            shape((2 * piece, hidden), BF),
-            shape((2 * piece, hidden), F32),
-            shape((2 * piece, hidden), BF),
-        ),
-        in_specs=[smem] * 3 + [anywhere] * 10 + [vmem] * 2 + [anywhere] + [vmem] * 2,
-        out_specs=(anywhere,) * 7,
-        scratch_shapes=[
-            pltpu.VMEM((n_grid, width), BF),
-            pltpu.VMEM((n_edges, width), BF),
-            pltpu.VMEM((n_edges, hidden), F32),
             pltpu.VMEM((pad_mesh, width), BF),
             pltpu.VMEM((pad_mesh, width), BF),
             pltpu.VMEM((pad_mesh, 3 * hidden), BF),
@@ -414,35 +419,26 @@
             pltpu.VMEM((pad_mesh, hidden), F32),
             pltpu.VMEM((width, hidden), F32),
             pltpu.VMEM((8, hidden), F32),
-            pltpu.VMEM((n_edges, hidden), BF),
-            pltpu.VMEM((n_grid, hidden), BF),
             pltpu.VMEM((MEMBERS, 2 * ROWS + 16, LANES), BF),
             pltpu.VMEM((2 * piece, hidden), BF),
-            pltpu.VMEM((2 * piece, hidden), F32),
             pltpu.VMEM((2 * piece, hidden), BF),
-            dma((17,)),
             dma((10,)),
+            dma((n_edges // UNIT,)),
+            dma((6,)),
         ],
-        compiler_params=params,
+        compiler_params=large,
         cost_estimate=pl.CostEstimate(flops=EDGE_FLOPS, transcendentals=1 << 20, bytes_accessed=1 << 23),
         name="edge_step",
     )(
-        band.reshape(1),
-        chan.reshape(1),
-        edge_count,
-        grid_latent,
-        grid_far,
-        edge_latent,
-        edge_far,
-        *mesh_near,
+        *scalars(band.reshape(1), chan.reshape(1), edge_count),
+        *wide(grid_latent, grid_far, edge_latent, edge_far, *mesh_near),
         *mesh_far,
-        w_mesh,
-        w_out,
-        pre,
-        senders,
-        receivers,
+        *wide(w_mesh, w_out),
+        near(pre),
+        *wide(senders, receivers),
     )
 
+    cot_own, cot_far = (cots[:half_edges], cots[half_edges:])
     from_low = pair_swap(rim_low, 0)
     from_high = pair_swap(rim_high, 1)
     arrived = lax.all_to_all(wire, GROUP, 0, 0, tiled=True)

time: 106 us -> 105 us (level)
  matrix products: 6.79 us -> 9.87 us
  waiting for transfers between devices: 25.6 us -> 23.5 us
  local copies, waits for them, and re-layouts: 3.74 us -> 1.79 us
    dot_general x6, matrix products: 6.79 us -> 9.87 us  [dot_t(): lax.dot_general(a, b, (((1,), (1,)), ((), ())), preferred_element_type=F32)]
    all_to_all x1, waiting for transfers between devices: 7.66 us -> 5.55 us  [body(): everyone = lax.all_to_all(spread, GROUP, 0, 0, tiled=True)]
    unnamed x40 -> x18, local copies, waits for them, and re-layouts: 1.99 us -> 0.05 us
    ppermute x4, waiting for transfers between devices: 3.59 us -> 5.35 us  [pair_swap(): return lax.ppermute(x, BAND, pairs + [(j, i) for i, j in pairs])]
    all_to_all x1, waiting for transfers between devices: 8.51 us -> 6.81 us  [body(): arrived = lax.all_to_all(wire, GROUP, 0, 0, tiled=True)]
  transfers between devices with their start and end apart: 16 -> 16, of which waited for: 11 -> 11; matrix products, arithmetic and copies ran while one was open for 9% -> 13% of each run, Pallas kernels for 7% -> 7%
where the time goes in v5:
time: 105 us
  starting transfers between devices  37 us (35%)
  Pallas kernels  25.8 us (25%)
  waiting for transfers between devices  23.5 us (22%)
  matrix products  9.87 us (9%)
  other arithmetic  5.05 us (5%)
  local copies, waits for them, and re-layouts  1.79 us (2%)
  between operations  1.54 us (1%)
    pallas_call x1, Pallas kernels, body(): pl.pallas_call(edge_kernel, out_shape=(pltpu.HBM((MEMBERS, 2 * ROWS + TAI...  19 us
    ppermute x4, starting transfers between devices, pair_swap(): return lax.ppermute(x, BAND, pairs + [(j, i) for i, j in pairs])  14.4 us
    dot_general x6, matrix products, dot_t(): lax.dot_general(a, b, (((1,), (1,)), ((), ())), preferred_element_type=F32)  9.87 us
    ppermute x2, starting transfers between devices, depth_total(): other = lax.ppermute(mine, 'zh', [(i, i ^ mask) for i in range(depth)])  7.96 us
    all_to_all x1, starting transfers between devices, body(): arrived = lax.all_to_all(wire, GROUP, 0, 0, tiled=True)  7.85 us
    pallas_call x1, Pallas kernels, body(): pl.pallas_call(sender_kernel, out_shape=pltpu.VMEM((n_edges, hidden), F32...  6.87 us
    all_to_all x1, waiting for transfers between devices, body(): arrived = lax.all_to_all(wire, GROUP, 0, 0, tiled=True)  6.81 us
    all_to_all x1, waiting for transfers between devices, body(): everyone = lax.all_to_all(spread, GROUP, 0, 0, tiled=True)  5.55 us
  transfers between devices with their start and end apart: 16, of which 11 were waited for; matrix products, arithmetic and copies ran while one was open for 13% of the time, Pallas kernels for 7%

profile of v5, /device:TPU:32, one launch (start us, length us, event | category | flops | bytes accessed | tf_op | source)
XLA Modules:
  0.0 104.6 jit_solution(3644961887611472160)
XLA Ops:
  0.6 0.1 collective-permute-start.1
  0.7 0.5 collective-permute-start
  1.2 1.0 pad_maximum_fusion.m1
  2.3 0.0 copy-start.5
  2.3 0.2 collective-permute-start.5
  2.5 6.7 %collective-permute-start.3 = (bf16[2,160,512]{2,1,0:T(8,128)(2,1)S(1)}, bf16[2,160,512]{2,1,0:T(8,128)(2,1)S(1)}, u32[]{:S(2)}, u32[]{:S(2)}) collective-permute-start(bf16[2,160,512]{2,1,0:T(8,128)(2,1)S(1)} %pad_maximum_fusion.m1), channel_id=1, source_target_pairs={{2,4},{6,8},{10,12},{14,16},{18,20},{22,24},{26,28},{30,32},{34,36... | collective-permute-start | bytes 983048 | tf_op jit(solution)/shard_map/ppermute | solution.py:307
  9.1 0.1 collective-permute-start.2
  9.2 0.0 collective-permute-done.grid_far
  9.2 0.0 copy-start.1
  9.3 0.0 collective-permute-done.1.edge_far
  9.3 0.0 copy-start
  9.3 6.9 %sender_step.1.pre_part = f32[2304,256]{1,0:T(8,128)S(1)} custom-call(s32[1]{0:T(128)} %bitcast.band, s32[1]{0:T(128)} %bitcast.1.chan, bf16[576,512]{1,0:T(8,128)(2,1)} %grid_own.3, bf16[576,512]{1,0:T(8,128)(2,1)S(1)} %collective-permute-done.grid_far, bf16[1152,512]{1,0:T(8,128)(2,1)} %edge_own.3, bf16[1152,512]{1,0:T(8,128)(2,1)S(1)} %collective-permute-done.1.edge_far, ...), custom_call_target="tpu_custom_call" | custom-call | flops 4000000000 | bytes 4194304 | tf_op jit(solution)/shard_map/sender_step/pallas_call | solution.py:371
  16.2 0.0 copy-done.5
  16.2 0.0 copy-done.1
  16.2 0.0 copy-done
  16.2 2.4 %collective-permute-done.3.m2 = bf16[2,160,512]{2,1,0:T(8,128)(2,1)S(1)} collective-permute-done((bf16[2,160,512]{2,1,0:T(8,128)(2,1)S(1)}, bf16[2,160,512]{2,1,0:T(8,128)(2,1)S(1)}, u32[]{:S(2)}, u32[]{:S(2)}) %collective-permute-start.3) | collective-permute-done | bytes 327712 | tf_op jit(solution)/shard_map/ppermute | solution.py:307
  18.6 0.4 collective-permute-done.2.m0
  19.0 0.0 collective-permute-start.4
  19.0 0.5 collective-permute-start.6
  20.1 0.0 collective-permute-done.5.m4
  20.1 0.0 copy-start.6
  20.1 0.4 collective-permute-done.4.m3
  20.6 0.5 collective-permute-done.6.m5
  21.1 0.0 copy-done.7
  21.1 0.0 copy-done.8
  21.1 0.0 copy-done.6
  21.1 19.0 %edge_step.1 = (bf16[32,136,128]{2,1,0:T(8,128)(2,1)}, bf16[2304,256]{1,0:T(8,128)(2,1)S(1)}, bf16[1152,256]{1,0:T(8,128)(2,1)S(1)}, bf16[320,256]{1,0:T(8,128)(...) custom-call(s32[1]{0:T(128)} %bitcast.band, s32[1]{0:T(128)} %bitcast.1.chan, s32[1]{0:T(128)S(6)} %copy.20.count, ...), custom_call_target="tpu_custom_call" | custom-call | flops 8999999488 | bytes 8388608 | tf_op jit(solution)/shard_map/edge_step/pallas_call | solution.py:398
  40.0 7.8 %all-to-all-start = ((bf16[32,136,128]{2,1,0:T(8,128)(2,1)}), bf16[32,136,128]{2,1,0:T(8,128)(2,1)S(1)}, u32[]{:S(2)}, u32[]{:S(2)}) async-start(bf16[32,136,128]{2,1,0:T(8,128)(2,1)} %get-tuple-element.26), calls=%async_computation | async-start | bytes 2228224 | tf_op jit(solution)/shard_map/all_to_all | solution.py:444
  47.9 0.0 copy-start.3
  47.9 1.6 %collective-permute-start.9 = (bf16[320,256]{1,0:T(8,128)(2,1)}, bf16[320,256]{1,0:T(8,128)(2,1)}, u32[]{:S(2)}, u32[]{:S(2)}) collective-permute-start(bf16[320,256]{1,0:T(8,128)(2,1)} %get-tuple-element.27), channel_id=1, source_target_pairs={{0,2},{4,6},{8,10},{12,14},{16,18},{20,22},{24,26},{28,30},{32,34}... | collective-permute-start | bytes 491528 | tf_op jit(solution)/shard_map/ppermute | solution.py:307
  49.4 6.1 %collective-permute-start.10 = (bf16[320,256]{1,0:T(8,128)(2,1)}, bf16[320,256]{1,0:T(8,128)(2,1)}, u32[]{:S(2)}, u32[]{:S(2)}) collective-permute-start(bf16[320,256]{1,0:T(8,128)(2,1)} %get-tuple-element.28), channel_id=1, source_target_pairs={{2,4},{6,8},{10,12},{14,16},{18,20},{22,24},{26,28},{30,32},{34,36... | collective-permute-start | bytes 491528 | tf_op jit(solution)/shard_map/ppermute | solution.py:307
  55.5 2.5 %convolution_convert_fusion = bf16[1152,512]{1,0:T(8,128)(2,1)} fusion(bf16[512,256]{1,0:T(8,128)(2,1)} %w_edge.1, bf16[2304,256]{1,0:T(8,128)(2,1)S(1)} %get-tuple-element.24), kind=kOutput, calls=%fused_computation.2 | convolution fusion | flops 302579712 | bytes 2031616 | tf_op jit(solution)/shard_map/dot_general | solution.py:30
  58.0 0.0 copy-done.3
  58.0 1.2 %convolution_convert_fusion.1 = bf16[576,512]{1,0:T(8,128)(2,1)} fusion(bf16[512,256]{1,0:T(8,128)(2,1)S(1)} %copy-done.3, bf16[1152,256]{1,0:T(8,128)(2,1)S(1)} %get-tuple-element.23), kind=kOutput, calls=%fused_computation.5 | convolution fusion | flops 151289856 | bytes 1146880 | tf_op jit(solution)/shard_map/dot_general | solution.py:30
  59.2 6.8 %all-to-all-done = bf16[32,136,128]{2,1,0:T(8,128)(2,1)S(1)} async-done(((bf16[32,136,128]{2,1,0:T(8,128)(2,1)}), bf16[32,136,128]{2,1,0:T(8,128)(2,1)S(1)}, u32[]{:S(2)}, u32[]{:S(2)}) %all-to-all-start) | async-done | bytes 1114144 | tf_op jit(solution)/shard_map/all_to_all | solution.py:444
  66.0 0.2 reduce_sum.12
  66.1 0.4 collective-permute-done.9
  66.5 2.2 %collective-permute-done.10 = bf16[320,256]{1,0:T(8,128)(2,1)} collective-permute-done((bf16[320,256]{1,0:T(8,128)(2,1)}, bf16[320,256]{1,0:T(8,128)(2,1)}, u32[]{:S(2)}, u32[]{:S(2)}) %collective-permute-start.10) | collective-permute-done | bytes 163872 | tf_op jit(solution)/shard_map/ppermute | solution.py:307
  68.7 4.5 %collective-permute-start.12 = (bf16[136,128]{1,0:T(8,128)(2,1)S(1)}, bf16[136,128]{1,0:T(8,128)(2,1)S(1)}, u32[]{:S(2)}, u32[]{:S(2)}) collective-permute-start(bf16[136,128]{1,0:T(8,128)(2,1)S(1)} %reduce_sum.12), channel_id=1, source_target_pairs={{0,64},{64,0},{128,192},{192,128},{1,65},{65,1},{129,193},{193,129... | collective-permute-start | bytes 104456 | tf_op jit(solution)/shard_map/ppermute | solution.py:315
  73.2 1.9 %collective-permute-done.12 = bf16[136,128]{1,0:T(8,128)(2,1)S(1)} collective-permute-done((bf16[136,128]{1,0:T(8,128)(2,1)S(1)}, bf16[136,128]{1,0:T(8,128)(2,1)S(1)}, u32[]{:S(2)}, u32[]{:S(2)}) %collective-permute-start.12) | collective-permute-done | bytes 34848 | tf_op jit(solution)/shard_map/ppermute | solution.py:315
  75.1 3.5 %collective-permute-start.13 = (bf16[136,128]{1,0:T(8,128)(2,1)S(1)}, bf16[136,128]{1,0:T(8,128)(2,1)S(1)}, u32[]{:S(2)}, u32[]{:S(2)}) collective-permute-start(bf16[136,128]{1,0:T(8,128)(2,1)S(1)} %add_convert_fusion.2), channel_id=1, source_target_pairs={{0,192},{64,128},{128,64},{192,0},{1,193},{65,129},{129,65},{193,1... | collective-permute-start | bytes 104456 | tf_op jit(solution)/shard_map/ppermute | solution.py:315
  78.6 0.0 collective-permute-start.7
  78.6 0.5 collective-permute-start.8
  79.1 2.1 %collective-permute-done.13 = bf16[136,128]{1,0:T(8,128)(2,1)S(1)} collective-permute-done((bf16[136,128]{1,0:T(8,128)(2,1)S(1)}, bf16[136,128]{1,0:T(8,128)(2,1)S(1)}, u32[]{:S(2)}, u32[]{:S(2)}) %collective-permute-start.13) | collective-permute-done | bytes 34848 | tf_op jit(solution)/shard_map/ppermute | solution.py:315
  81.3 1.1 %broadcast_in_dim.2 = bf16[32,64,256]{2,1,0:T(8,128)(2,1)} broadcast(bf16[64,256]{1,0:T(8,128)(2,1)S(1)} %pad_maximum_fusion.1), dimensions={1,2} | broadcast | bytes 1081344 | tf_op jit(solution)/shard_map/broadcast_in_dim | solution.py:454
  82.4 4.9 %all-to-all-start.1 = ((bf16[32,64,256]{2,1,0:T(8,128)(2,1)}), bf16[32,64,256]{2,1,0:T(8,128)(2,1)S(1)}, u32[]{:S(2)}, u32[]{:S(2)}) async-start(bf16[32,64,256]{2,1,0:T(8,128)(2,1)} %broadcast_in_dim.2), calls=%async_computation.1 | async-start | bytes 2097152 | tf_op jit(solution)/shard_map/all_to_all | solution.py:455
  87.4 0.0 copy-start.4
  87.4 0.0 collective-permute-done.7
  87.4 2.3 %fusion.1 = bf16[576,512]{1,0:T(8,128)(2,1)} fusion(bf16[512,256]{1,0:T(8,128)(2,1)S(1)} %copy-done.3, bf16[576,512]{1,0:T(8,128)(2,1)} %collective-permute-done.7, bf16[1152,256]{1,0:T(8,128)(2,1)S(1)} %get-tuple-element.23), kind=kOutput, calls=%fused_computation.4 | convolution fusion | flops 151879680 | bytes 1736704 | tf_op jit(solution)/shard_map/dot_general | solution.py:30
  89.7 0.0 collective-permute-done.8
  89.7 0.0 copy-done.4
  89.7 2.8 %fusion = bf16[1152,512]{1,0:T(8,128)(2,1)} fusion(bf16[512,256]{1,0:T(8,128)(2,1)S(1)} %copy-done.4, bf16[1152,512]{1,0:T(8,128)(2,1)} %collective-permute-done.8, bf16[2304,256]{1,0:T(8,128)(2,1)S(1)} %get-tuple-element.24), kind=kOutput, calls=%fused_computation.1 | convolution fusion | flops 303759360 | bytes 3211264 | tf_op jit(solution)/shard_map/dot_general | solution.py:30
  92.5 1.0 add_convert_fusion.1
  93.5 0.0 copy-done.2
  93.6 0.2 convolution_convert_fusion.2
  93.8 0.1 collective-permute-start.11
  93.9 0.6 slice_bitcast_fusion
  94.5 0.8 collective-permute-done.11
  95.3 0.9 add_convert_fusion
  96.2 5.6 %all-to-all-done.1 = bf16[32,64,256]{2,1,0:T(8,128)(2,1)S(1)} async-done(((bf16[32,64,256]{2,1,0:T(8,128)(2,1)}), bf16[32,64,256]{2,1,0:T(8,128)(2,1)S(1)}, u32[]{:S(2)}, u32[]{:S(2)}) %all-to-all-start.1) | async-done | bytes 1048608 | tf_op jit(solution)/shard_map/all_to_all | solution.py:455
  101.7 0.1 fusion.13
  101.8 0.8 bitcast_convert_fusion.2
  102.7 0.9 maximum_convert_fusion
  103.5 1.1 %bitcast_convert_fusion = (f32[512,256]{1,0:T(8,128)}, f32[512,256]{1,0:T(8,128)}) fusion(bf16[8,64,256]{2,1,0:T(8,128)(2,1)S(1)} %get-tuple-element.34, bf16[8,64,256]{2,1,0:T(8,128)(2,1)S(1)} %get-tuple-element.35), kind=kLoop, calls=%fused_computation.15 | loop fusion | flops 262144 | bytes 1572864 | tf_op jit(solution)/shard_map/reshape | solution.py:465
  (8 shorter events, 0.1 us)
Async XLA Ops:
  0.6 8.6 %collective-permute-start.1 = (bf16[1152,512]{1,0:T(8,128)(2,1)}, bf16[1152,512]{1,0:T(8,128)(2,1)S(1)}, u32[]{:S(2)}, u32[]{:S(2)}) collective-permute-start(bf16[1152,512]{1,0:T(8,128)(2,1)} %edge_own.3), channel_id=1, source_target_pairs={{0,1},{1,0},{2,3},{3,2},{4,5},{5,4},{6,7},{7,6},{8,9},{9,8},{10,11... | collective-permute-start | bytes 3538952 | tf_op jit(solution)/shard_map/ppermute | solution.py:301
  0.7 8.5 %collective-permute-start = (bf16[576,512]{1,0:T(8,128)(2,1)}, bf16[576,512]{1,0:T(8,128)(2,1)S(1)}, u32[]{:S(2)}, u32[]{:S(2)}) collective-permute-start(bf16[576,512]{1,0:T(8,128)(2,1)} %grid_own.3), channel_id=1, source_target_pairs={{0,1},{1,0},{2,3},{3,2},{4,5},{5,4},{6,7},{7,6},{8,9},{9,8},{10,11... | collective-permute-start | bytes 1769480 | tf_op jit(solution)/shard_map/ppermute | solution.py:301
  2.3 13.9 %copy-start.5 = (bf16[2,160,512]{2,1,0:T(8,128)(2,1)}, bf16[2,160,512]{2,1,0:T(8,128)(2,1)S(1)}, u32[]{:S(2)}) copy-start(bf16[2,160,512]{2,1,0:T(8,128)(2,1)S(1)} %pad_maximum_fusion.m1) | copy-start | bytes 983044
  2.3 17.8 %collective-permute-start.5 = (bf16[2,160,512]{2,1,0:T(8,128)(2,1)S(1)}, bf16[2,160,512]{2,1,0:T(8,128)(2,1)S(1)}, u32[]{:S(2)}, u32[]{:S(2)}) collective-permute-start(bf16[2,160,512]{2,1,0:T(8,128)(2,1)S(1)} %pad_maximum_fusion.m1), channel_id=1, source_target_pairs={{0,1},{1,0},{2,3},{3,2},{4,5},{5,4},{6,7},{7,6},{8,9},{9,8},{10,11... | collective-permute-start | bytes 983048 | tf_op jit(solution)/shard_map/ppermute | solution.py:301
  2.5 16.1 %collective-permute-start.3 = (bf16[2,160,512]{2,1,0:T(8,128)(2,1)S(1)}, bf16[2,160,512]{2,1,0:T(8,128)(2,1)S(1)}, u32[]{:S(2)}, u32[]{:S(2)}) collective-permute-start(bf16[2,160,512]{2,1,0:T(8,128)(2,1)S(1)} %pad_maximum_fusion.m1), channel_id=1, source_target_pairs={{2,4},{6,8},{10,12},{14,16},{18,20},{22,24},{26,28},{30,32},{34,36... | collective-permute-start | bytes 983048 | tf_op jit(solution)/shard_map/ppermute | solution.py:307
  9.1 9.8 %collective-permute-start.2 = (bf16[2,160,512]{2,1,0:T(8,128)(2,1)S(1)}, bf16[2,160,512]{2,1,0:T(8,128)(2,1)S(1)}, u32[]{:S(2)}, u32[]{:S(2)}) collective-permute-start(bf16[2,160,512]{2,1,0:T(8,128)(2,1)S(1)} %pad_maximum_fusion.m1), channel_id=1, source_target_pairs={{0,2},{4,6},{8,10},{12,14},{16,18},{20,22},{24,26},{28,30},{32,34}... | collective-permute-start | bytes 983048 | tf_op jit(solution)/shard_map/ppermute | solution.py:307
  9.2 6.9 %copy-start.1 = (bf16[576,512]{1,0:T(8,128)(2,1)}, bf16[576,512]{1,0:T(8,128)(2,1)S(1)}, u32[]{:S(2)}) copy-start(bf16[576,512]{1,0:T(8,128)(2,1)S(1)} %collective-permute-done.grid_far) | copy-start | bytes 1769476
  9.3 6.9 %copy-start = (bf16[1152,512]{1,0:T(8,128)(2,1)}, bf16[1152,512]{1,0:T(8,128)(2,1)S(1)}, u32[]{:S(2)}) copy-start(bf16[1152,512]{1,0:T(8,128)(2,1)S(1)} %collective-permute-done.1.edge_far) | copy-start | bytes 3538948
  18.6 2.5 %copy-start.7 = (bf16[2,160,512]{2,1,0:T(8,128)(2,1)}, bf16[2,160,512]{2,1,0:T(8,128)(2,1)S(1)}, u32[]{:S(2)}) copy-start(bf16[2,160,512]{2,1,0:T(8,128)(2,1)S(1)} %collective-permute-done.3.m2) | copy-start | bytes 983044
  18.9 2.1 %copy-start.8 = (bf16[2,160,512]{2,1,0:T(8,128)(2,1)}, bf16[2,160,512]{2,1,0:T(8,128)(2,1)S(1)}, u32[]{:S(2)}) copy-start(bf16[2,160,512]{2,1,0:T(8,128)(2,1)S(1)} %collective-permute-done.2.m0) | copy-start | bytes 983044
  19.0 1.6 %collective-permute-start.4 = (bf16[2,160,512]{2,1,0:T(8,128)(2,1)S(1)}, bf16[2,160,512]{2,1,0:T(8,128)(2,1)S(1)}, u32[]{:S(2)}, u32[]{:S(2)}) collective-permute-start(bf16[2,160,512]{2,1,0:T(8,128)(2,1)S(1)} %collective-permute-done.2.m0), channel_id=1, source_target_pairs={{0,1},{1,0},{2,3},{3,2},{4,5},{5,4},{6,7},{7,6},{8,9},{9,8},{10,11... | collective-permute-start | bytes 983048 | tf_op jit(solution)/shard_map/ppermute | solution.py:301
  19.0 2.1 %collective-permute-start.6 = (bf16[2,160,512]{2,1,0:T(8,128)(2,1)S(1)}, bf16[2,160,512]{2,1,0:T(8,128)(2,1)S(1)}, u32[]{:S(2)}, u32[]{:S(2)}) collective-permute-start(bf16[2,160,512]{2,1,0:T(8,128)(2,1)S(1)} %collective-permute-done.3.m2), channel_id=1, source_target_pairs={{0,1},{1,0},{2,3},{3,2},{4,5},{5,4},{6,7},{7,6},{8,9},{9,8},{10,11... | collective-permute-start | bytes 983048 | tf_op jit(solution)/shard_map/ppermute | solution.py:301
  20.1 0.9 copy-start.6
  40.0 25.9 %all-to-all-start = ((bf16[32,136,128]{2,1,0:T(8,128)(2,1)}), bf16[32,136,128]{2,1,0:T(8,128)(2,1)S(1)}, u32[]{:S(2)}, u32[]{:S(2)}) async-start(bf16[32,136,128]{2,1,0:T(8,128)(2,1)} %get-tuple-element.26), calls=%async_computation | async-start | bytes 2228224 | tf_op jit(solution)/shard_map/all_to_all | solution.py:444
  47.9 10.1 %copy-start.3 = (bf16[512,256]{1,0:T(8,128)(2,1)S(1)}, bf16[512,256]{1,0:T(8,128)(2,1)}, u32[]{:S(2)}) copy-start(bf16[512,256]{1,0:T(8,128)(2,1)} %w_grid.1) | copy-start | bytes 786436
  47.9 18.6 %collective-permute-start.9 = (bf16[320,256]{1,0:T(8,128)(2,1)}, bf16[320,256]{1,0:T(8,128)(2,1)}, u32[]{:S(2)}, u32[]{:S(2)}) collective-permute-start(bf16[320,256]{1,0:T(8,128)(2,1)} %get-tuple-element.27), channel_id=1, source_target_pairs={{0,2},{4,6},{8,10},{12,14},{16,18},{20,22},{24,26},{28,30},{32,34}... | collective-permute-start | bytes 491528 | tf_op jit(solution)/shard_map/ppermute | solution.py:307
  49.4 19.3 %collective-permute-start.10 = (bf16[320,256]{1,0:T(8,128)(2,1)}, bf16[320,256]{1,0:T(8,128)(2,1)}, u32[]{:S(2)}, u32[]{:S(2)}) collective-permute-start(bf16[320,256]{1,0:T(8,128)(2,1)} %get-tuple-element.28), channel_id=1, source_target_pairs={{2,4},{6,8},{10,12},{14,16},{18,20},{22,24},{26,28},{30,32},{34,36... | collective-permute-start | bytes 491528 | tf_op jit(solution)/shard_map/ppermute | solution.py:307
  68.7 6.4 %collective-permute-start.12 = (bf16[136,128]{1,0:T(8,128)(2,1)S(1)}, bf16[136,128]{1,0:T(8,128)(2,1)S(1)}, u32[]{:S(2)}, u32[]{:S(2)}) collective-permute-start(bf16[136,128]{1,0:T(8,128)(2,1)S(1)} %reduce_sum.12), channel_id=1, source_target_pairs={{0,64},{64,0},{128,192},{192,128},{1,65},{65,1},{129,193},{193,129... | collective-permute-start | bytes 104456 | tf_op jit(solution)/shard_map/ppermute | solution.py:315
  75.1 6.1 %collective-permute-start.13 = (bf16[136,128]{1,0:T(8,128)(2,1)S(1)}, bf16[136,128]{1,0:T(8,128)(2,1)S(1)}, u32[]{:S(2)}, u32[]{:S(2)}) collective-permute-start(bf16[136,128]{1,0:T(8,128)(2,1)S(1)} %add_convert_fusion.2), channel_id=1, source_target_pairs={{0,192},{64,128},{128,64},{192,0},{1,193},{65,129},{129,65},{193,1... | collective-permute-start | bytes 104456 | tf_op jit(solution)/shard_map/ppermute | solution.py:315
  78.6 8.8 %collective-permute-start.7 = (bf16[576,512]{1,0:T(8,128)(2,1)}, bf16[576,512]{1,0:T(8,128)(2,1)}, u32[]{:S(2)}, u32[]{:S(2)}) collective-permute-start(bf16[576,512]{1,0:T(8,128)(2,1)} %convolution_convert_fusion.1), channel_id=1, source_target_pairs={{0,1},{1,0},{2,3},{3,2},{4,5},{5,4},{6,7},{7,6},{8,9},{9,8},{10,11... | collective-permute-start | bytes 1769480 | tf_op jit(solution)/shard_map/ppermute | solution.py:301
  78.6 11.0 %collective-permute-start.8 = (bf16[1152,512]{1,0:T(8,128)(2,1)}, bf16[1152,512]{1,0:T(8,128)(2,1)}, u32[]{:S(2)}, u32[]{:S(2)}) collective-permute-start(bf16[1152,512]{1,0:T(8,128)(2,1)} %convolution_convert_fusion), channel_id=1, source_target_pairs={{0,1},{1,0},{2,3},{3,2},{4,5},{5,4},{6,7},{7,6},{8,9},{9,8},{10,11... | collective-permute-start | bytes 3538952 | tf_op jit(solution)/shard_map/ppermute | solution.py:301
  82.4 19.3 %all-to-all-start.1 = ((bf16[32,64,256]{2,1,0:T(8,128)(2,1)}), bf16[32,64,256]{2,1,0:T(8,128)(2,1)S(1)}, u32[]{:S(2)}, u32[]{:S(2)}) async-start(bf16[32,64,256]{2,1,0:T(8,128)(2,1)} %broadcast_in_dim.2), calls=%async_computation.1 | async-start | bytes 2097152 | tf_op jit(solution)/shard_map/all_to_all | solution.py:455
  87.4 2.3 %copy-start.4 = (bf16[512,256]{1,0:T(8,128)(2,1)S(1)}, bf16[512,256]{1,0:T(8,128)(2,1)}, u32[]{:S(2)}) copy-start(bf16[512,256]{1,0:T(8,128)(2,1)} %w_edge.1) | copy-start | bytes 786436
  89.7 3.9 %copy-start.2 = (bf16[512,256]{1,0:T(8,128)(2,1)S(1)}, bf16[512,256]{1,0:T(8,128)(2,1)}, u32[]{:S(2)}) copy-start(bf16[512,256]{1,0:T(8,128)(2,1)} %w_mesh.1) | copy-start | bytes 786436
  93.8 1.5 %collective-permute-start.11 = (bf16[160,512]{1,0:T(8,128)(2,1)S(1)}, bf16[160,512]{1,0:T(8,128)(2,1)S(1)}, u32[]{:S(2)}, u32[]{:S(2)}) collective-permute-start(bf16[160,512]{1,0:T(8,128)(2,1)S(1)} %convolution_convert_fusion.2), channel_id=1, source_target_pairs={{0,1},{1,0},{2,3},{3,2},{4,5},{5,4},{6,7},{7,6},{8,9},{9,8},{10,11... | collective-permute-start | bytes 491528 | tf_op jit(solution)/shard_map/ppermute | solution.py:301

commit v6 on v5

--- a/solution.py
+++ b/solution.py
@@ -78,11 +78,14 @@
     edge_far,
     w_grid,
     w_edge,
-    bias,
-    senders,
+    bias_in,
+    send_in,
     pre,
     grid,
     edge,
+    weights,
+    bias_row,
+    senders,
     table,
     left,
     in_sems,
@@ -92,14 +95,25 @@
     half_grid = grid_own.shape[0]
     n_grid = 2 * half_grid
     block = left.shape[0]
-    fetches = copies(((grid_own, grid), (edge_own, edge)), in_sems)
+    fetches = copies(
+        (
+            (w_grid, weights),
+            (grid_own, grid),
+            (send_in, senders),
+            (w_edge, table.at[n_grid:]),
+            (bias_in, bias_row),
+            (edge_own, edge),
+        ),
+        in_sems,
+    )
     for f in fetches:
         f.start()
-    table[n_grid:] = w_edge[...]
-    table[half_grid:n_grid] = dot(grid_far[...], w_grid[...]).astype(BF)
     fetches[0].wait()
-    table[0:half_grid] = dot(grid[...], w_grid[...]).astype(BF)
+    table[half_grid:n_grid] = dot(grid_far[...], weights[...]).astype(BF)
     fetches[1].wait()
+    table[0:half_grid] = dot(grid[...], weights[...]).astype(BF)
+    for f in fetches[2:]:
+        f.wait()
     groups = 2 * half_edges // LANES
     per = block // LANES
     units = block // UNIT
@@ -125,7 +139,7 @@
             column = jnp.broadcast_to(row, (LANES, LANES)).T
             for k in range(n_grid // LANES):
                 left[c * LANES : (c + 1) * LANES, k * LANES : (k + 1) * LANES] = one_hot(column, k * LANES)
-        pre[rows, :] = dot(left[...], table[...]) + bias[...]
+        pre[rows, :] = dot(left[...], table[...]) + bias_row[...]
         return carry
 
     lax.fori_loop(0, 2 * half_edges // block, step, 0)
@@ -145,11 +159,11 @@
     m3,
     m4,
     m5,
-    w_mesh,
-    w_out,
+    w_mesh_in,
+    w_out_in,
     pre_part,
-    senders,
-    receivers,
+    send_in,
+    recv_in,
     wire_out,
     cots,
     seg_grid,
@@ -163,10 +177,12 @@
     table,
     left,
     right,
+    both,
     sums,
-    act_sums,
-    edge_sum,
-    bias_sum,
+    w_mesh,
+    w_out,
+    senders,
+    receivers,
     wire,
     low_v,
     high_v,
@@ -189,13 +205,14 @@
     lats = [(m.at[0], lat.at[k * piece : (k + 1) * piece]) for k, m in apart]
     cot_pairs = [(m.at[1], cot.at[k * piece : (k + 1) * piece]) for k, m in apart]
     grids = [(grid_own, grid.at[0:half_grid]), (grid_far, grid.at[half_grid:])]
-    fetches = copies(lats + cot_pairs + grids, in_sems)
+    small = [(w_mesh_in, w_mesh), (w_out_in, w_out), (send_in, senders), (recv_in, receivers)]
+    fetches = copies(small + lats + cot_pairs + grids, in_sems)
     edges = [
         (source.at[k * UNIT : (k + 1) * UNIT], edge.at[(k + off) * UNIT : (k + off + 1) * UNIT])
         for source, off in ((edge_own, 0), (edge_far, near))
         for k in range(near)
     ]
-    for f in fetches[0:8] + copies(edges, edge_sems) + fetches[8:]:
+    for f in fetches[0:12] + copies(edges, edge_sems) + fetches[12:]:
         f.start()
     for k, m in ((3, m3), (5, m5)):
         lat[k * piece : (k + 1) * piece] = m[0]
@@ -203,11 +220,7 @@
     if pad_mesh > n_mesh:
         lat[n_mesh:] = jnp.zeros((pad_mesh - n_mesh, lat.shape[1]), BF)
         cot[n_mesh:] = jnp.zeros((pad_mesh - n_mesh, cot.shape[1]), BF)
-    sums[...] = jnp.zeros_like(sums)
-    act_sums[...] = jnp.zeros_like(act_sums)
-    edge_sum[...] = jnp.zeros_like(edge_sum)
-    bias_sum[...] = jnp.zeros_like(bias_sum)
-    for f in fetches[0:8]:
+    for f in fetches[0:12]:
         f.wait()
     table[:, 0:hidden] = dot(lat[...], w_mesh[...]).astype(BF)
     cot_terms = dot_t(cot[...], w_out[...])
@@ -222,6 +235,7 @@
         for c in range(per):
             at = index_row(i * per + c, groups, where)
             mine = slice(c * LANES, (c + 1) * LANES)
+            edge_lanes = pl.ds(pl.multiple_of(i * block + c * LANES, LANES), LANES)
             slot = at * LANES + lax.broadcasted_iota(jnp.int32, (1, LANES), 1)
             row = local_receivers(receivers[pl.ds(at, 1), :], slot, where, piece)
             row = jnp.broadcast_to(row, (LANES, LANES))
@@ -229,11 +243,11 @@
             for k in range(pad_mesh // LANES):
                 left[mine, k * LANES : (k + 1) * LANES] = one_hot(column, k * LANES)
                 at_row = n_grid + k * LANES
-                right[at_row : at_row + LANES, mine] = one_hot_rows(row, k * LANES)
+                right[at_row : at_row + LANES, edge_lanes] = one_hot_rows(row, k * LANES)
             row = local_senders(senders[pl.ds(at, 1), :], where, half_grid)
             row = jnp.broadcast_to(row, (LANES, LANES))
             for k in range(n_grid // LANES):
-                right[k * LANES : (k + 1) * LANES, mine] = one_hot_rows(row, k * LANES)
+                right[k * LANES : (k + 1) * LANES, edge_lanes] = one_hot_rows(row, k * LANES)
         got = dot(left[...], table[...])
         pre = pre_part[rows, :] + got[:, 0:hidden]
         hidden_cot = got[:, hidden : 2 * hidden] + got[:, 2 * hidden :]
@@ -241,23 +255,31 @@
         act = (pre * sig).astype(BF)
         pre_cot = (hidden_cot * sig * (1.0 + pre * (1.0 - sig))).astype(BF)
         cots[rows, :] = pre_cot
-        sums[...] += dot(right[...], pre_cot)
-        act_sums[...] += dot(right[n_grid:, :], act)
-        for h in range(block // UNIT):
-            at = i * (block // UNIT) + h
-            unit = pl.ds(pl.multiple_of(at * UNIT, UNIT), UNIT)
-            pltpu.make_async_copy(edge_own.at[0:UNIT], edge.at[unit], edge_sems.at[at]).wait()
-        edge_sum[...] += dot_rows(edge[rows, :], pre_cot)
-        bias_sum[...] += pre_cot.astype(F32).reshape(block // 8, 8, hidden).sum(axis=0)
+        both[rows, 0:hidden] = pre_cot
+        both[rows, hidden:] = act
         return carry
 
     lax.fori_loop(0, 2 * half_edges // block, step, 0)
 
-    seg_grid[...] = sums[:n_grid].astype(BF)
+    grid_tile = n_grid // 3
+    mesh_tile = pad_mesh // 2
+
+    def sum_grid(t, carry):
+        at = pl.ds(pl.multiple_of(t * grid_tile, grid_tile), grid_tile)
+        seg_grid[at, :] = dot(right[at, :], both[:, 0:hidden]).astype(BF)
+        return carry
+
+    def sum_mesh(t, carry):
+        at = pl.multiple_of(t * mesh_tile, mesh_tile)
+        sums[pl.ds(at, mesh_tile), :] = dot(right[pl.ds(n_grid + at, mesh_tile), :], both[...])
+        return carry
+
+    lax.fori_loop(0, 2, sum_mesh, 0)
+    lax.fori_loop(0, 3, sum_grid, 0)
     for ref, o, kind in ((low_v, 0, BF), (rim_mid, 1, F32), (high_v, 2, BF)):
         for h in range(2):
-            start = n_grid + (3 * h + o) * piece
-            ref[h * piece : (h + 1) * piece] = sums[start : start + piece].astype(kind)
+            start = (3 * h + o) * piece
+            ref[h * piece : (h + 1) * piece] = sums[start : start + piece, 0:hidden].astype(kind)
     rows = ROWS
     per_grad = w_mesh.shape[0] // rows
     parts = [slice(k * per_grad, (k + 1) * per_grad) for k in range(4)]
@@ -267,13 +289,11 @@
     )
     for f in stores[0:2]:
         f.start()
-    for f in fetches[8:]:
+    for f in fetches[12:] + copies(edges, edge_sems):
         f.wait()
     sub = lax.broadcasted_iota(jnp.int32, (16, LANES), 0)
-    bias_total = jnp.sum(bias_sum[...], axis=0, keepdims=True)
-    low = jnp.broadcast_to(bias_total[:, :LANES], (16, LANES))
-    high = jnp.broadcast_to(bias_total[:, LANES:], (16, LANES))
-    tail = jnp.where(sub == 0, low, jnp.where(sub == 1, high, 0.0)).astype(BF)
+    bias_total = dot(jnp.ones((16, 2 * half_edges), BF), both[:, 0:hidden])
+    tail = jnp.where(sub == 0, bias_total[:, :LANES], jnp.where(sub == 1, bias_total[:, LANES:], 0.0)).astype(BF)
     for k in range(wire.shape[0]):
         wire[k, 2 * rows :, :] = tail
 
@@ -283,13 +303,13 @@
             wire[at + k, 0:rows, :] = value[:, :LANES].astype(BF)
             wire[at + k, rows : 2 * rows, :] = value[:, LANES:].astype(BF)
 
-    put_all(parts[2].start, edge_sum[...])
+    put_all(parts[2].start, dot_rows(edge[...], both[:, 0:hidden]))
     stores[4].start()
     put_all(parts[0].start, dot_rows(grid[...], seg_grid[...]))
     stores[2].start()
-    put_all(parts[1].start, dot_rows(lat[...], sums[n_grid:].astype(BF)))
+    put_all(parts[1].start, dot_rows(lat[...], sums[:, 0:hidden].astype(BF)))
     stores[3].start()
-    g = dot_rows(act_sums[...].astype(BF), cot[...])
+    g = dot_rows(sums[:, hidden:].astype(BF), cot[...])
     put_all(parts[3].start, g[:, 0:hidden])
     put_all(parts[3].start + per_grad // 2, g[:, hidden:])
     stores[5].start()
@@ -354,7 +374,7 @@
     receivers = receivers.reshape(-1, LANES)
     vmem = pl.BlockSpec(memory_space=pltpu.VMEM)
     smem = pl.BlockSpec(memory_space=pltpu.SMEM)
-    small, large = [pltpu.CompilerParams(vmem_limit_bytes=n * 2**20) for n in (16, 32)]
+    small, large = [pltpu.CompilerParams(vmem_limit_bytes=n * 2**20) for n in (16, 40)]
 
     def near(x):
         return pltpu.with_memory_space_constraint(x, pltpu.VMEM)
@@ -371,14 +391,17 @@
     pre = pl.pallas_call(
         sender_kernel,
         out_shape=pltpu.VMEM((n_edges, hidden), F32),
-        in_specs=[smem] * 2 + [anywhere, vmem] * 2 + [vmem] * 4,
+        in_specs=[smem] * 2 + [anywhere, vmem] * 2 + [anywhere] * 4,
         out_specs=vmem,
         scratch_shapes=[
             pltpu.VMEM((half_grid, width), BF),
             pltpu.VMEM((half_edges, width), BF),
+            pltpu.VMEM((width, hidden), BF),
+            pltpu.VMEM((1, hidden), F32),
+            pltpu.VMEM(senders.shape, jnp.int32),
             pltpu.VMEM((n_grid + width, hidden), BF),
             pltpu.VMEM((EDGE_BLOCK, n_grid + width), BF),
-            dma((2,)),
+            dma((6,)),
         ],
         compiler_params=small,
         cost_estimate=pl.CostEstimate(flops=SENDER_FLOPS, transcendentals=0, bytes_accessed=1 << 22),
@@ -405,7 +428,7 @@
             pltpu.VMEM((2 * piece, hidden), F32),
             pltpu.HBM((2 * piece, hidden), BF),
         ),
-        in_specs=[smem] * 3 + [anywhere] * 7 + [vmem] * 8,
+        in_specs=[smem] * 3 + [anywhere] * 7 + [vmem, anywhere, vmem, anywhere, anywhere, vmem, anywhere, anywhere],
         out_specs=(anywhere, vmem, vmem, anywhere, vmem, anywhere),
         scratch_shapes=[
             pltpu.VMEM((n_grid, width), BF),
@@ -414,15 +437,17 @@
             pltpu.VMEM((pad_mesh, width), BF),
             pltpu.VMEM((pad_mesh, 3 * hidden), BF),
             pltpu.VMEM((EDGE_BLOCK, pad_mesh), BF),
-            pltpu.VMEM((n_grid + pad_mesh, EDGE_BLOCK), BF),
-            pltpu.VMEM((n_grid + pad_mesh, hidden), F32),
-            pltpu.VMEM((pad_mesh, hidden), F32),
-            pltpu.VMEM((width, hidden), F32),
-            pltpu.VMEM((8, hidden), F32),
+            pltpu.VMEM((n_grid + pad_mesh, n_edges), BF),
+            pltpu.VMEM((n_edges, 2 * hidden), BF),
+            pltpu.VMEM((pad_mesh, 2 * hidden), F32),
+            pltpu.VMEM((width, hidden), BF),
+            pltpu.VMEM((hidden, width), BF),
+            pltpu.VMEM(senders.shape, jnp.int32),
+            pltpu.VMEM(receivers.shape, jnp.int32),
             pltpu.VMEM((MEMBERS, 2 * ROWS + 16, LANES), BF),
             pltpu.VMEM((2 * piece, hidden), BF),
             pltpu.VMEM((2 * piece, hidden), BF),
-            dma((10,)),
+            dma((14,)),
             dma((n_edges // UNIT,)),
             dma((6,)),
         ],

time: 105 us -> 104 us (level)
  Pallas kernels: 25.8 us -> 23.4 us
    pallas_call x1, Pallas kernels: 19 us -> 17.4 us  [body(): pl.pallas_call(edge_kernel, out_shape=(pltpu.HBM((MEMBERS, 2 * ROWS + TAI...]
  transfers between devices with their start and end apart: 16 -> 16, of which waited for: 11 -> 11; matrix products, arithmetic and copies ran while one was open for 13% -> 13% of each run, Pallas kernels for 7% -> 6%
where the time goes in v6:
time: 104 us; the launch traced here: 103 us
  starting transfers between devices  37.2 us (36%)
  waiting for transfers between devices  24.3 us (23%)
  Pallas kernels  23.4 us (22%)
  matrix products  9.87 us (9%)
  other arithmetic  5.05 us (5%)
  local copies, waits for them, and re-layouts  1.79 us (2%)
  between operations  1.54 us (1%)
    pallas_call x1, Pallas kernels, body(): pl.pallas_call(edge_kernel, out_shape=(pltpu.HBM((MEMBERS, 2 * ROWS + TAI...  17.4 us
    ppermute x4, starting transfers between devices, pair_swap(): return lax.ppermute(x, BAND, pairs + [(j, i) for i, j in pairs])  14.5 us
    dot_general x6, matrix products, dot_t(): lax.dot_general(a, b, (((1,), (1,)), ((), ())), preferred_element_type=F32)  9.87 us
    ppermute x2, starting transfers between devices, depth_total(): other = lax.ppermute(mine, 'zh', [(i, i ^ mask) for i in range(depth)])  7.96 us
    all_to_all x1, starting transfers between devices, body(): arrived = lax.all_to_all(wire, GROUP, 0, 0, tiled=True)  7.85 us
    all_to_all x1, waiting for transfers between devices, body(): arrived = lax.all_to_all(wire, GROUP, 0, 0, tiled=True)  6.61 us
    ppermute x4, waiting for transfers between devices, pair_swap(): return lax.ppermute(x, BAND, pairs + [(j, i) for i, j in pairs])  6.34 us
    pallas_call x1, Pallas kernels, body(): pl.pallas_call(sender_kernel, out_shape=pltpu.VMEM((n_edges, hidden), F32...  5.91 us
  transfers between devices with their start and end apart: 16, of which 11 were waited for; matrix products, arithmetic and copies ran while one was open for 13% of the time, Pallas kernels for 6%

profile of v6, /device:TPU:32, one launch (start us, length us, event | category | flops | bytes accessed | tf_op | source)
XLA Modules:
  0.0 103.1 jit_solution(5574898852716253412)
XLA Ops:
  0.6 0.1 collective-permute-start.1
  0.7 0.5 collective-permute-start
  1.2 1.0 pad_maximum_fusion.m1
  2.3 0.0 copy-start.5
  2.3 0.2 collective-permute-start.5
  2.5 6.7 %collective-permute-start.3 = (bf16[2,160,512]{2,1,0:T(8,128)(2,1)S(1)}, bf16[2,160,512]{2,1,0:T(8,128)(2,1)S(1)}, u32[]{:S(2)}, u32[]{:S(2)}) collective-permute-start(bf16[2,160,512]{2,1,0:T(8,128)(2,1)S(1)} %pad_maximum_fusion.m1), channel_id=1, source_target_pairs={{2,4},{6,8},{10,12},{14,16},{18,20},{22,24},{26,28},{30,32},{34,36... | collective-permute-start | bytes 983048 | tf_op jit(solution)/shard_map/ppermute | solution.py:327
  9.1 0.1 collective-permute-start.2
  9.2 0.0 collective-permute-done.grid_far
  9.2 0.0 copy-start.1
  9.3 0.0 collective-permute-done.1.edge_far
  9.3 0.0 copy-start
  9.3 5.9 %sender_step.1.pre_part = f32[2304,256]{1,0:T(8,128)S(1)} custom-call(s32[1]{0:T(128)} %bitcast.band, s32[1]{0:T(128)} %bitcast.1.chan, bf16[576,512]{1,0:T(8,128)(2,1)} %grid_own.3, bf16[576,512]{1,0:T(8,128)(2,1)S(1)} %collective-permute-done.grid_far, bf16[1152,512]{1,0:T(8,128)(2,1)} %edge_own.3, bf16[1152,512]{1,0:T(8,128)(2,1)S(1)} %collective-permute-done.1.edge_far, ...), custom_call_target="tpu_custom_call" | custom-call | flops 4000000000 | bytes 4194304 | tf_op jit(solution)/shard_map/sender_step/pallas_call | solution.py:391
  15.2 0.0 copy-done.5
  15.2 0.0 copy-done.1
  15.2 0.0 copy-done
  15.2 3.4 %collective-permute-done.3.m2 = bf16[2,160,512]{2,1,0:T(8,128)(2,1)S(1)} collective-permute-done((bf16[2,160,512]{2,1,0:T(8,128)(2,1)S(1)}, bf16[2,160,512]{2,1,0:T(8,128)(2,1)S(1)}, u32[]{:S(2)}, u32[]{:S(2)}) %collective-permute-start.3) | collective-permute-done | bytes 327712 | tf_op jit(solution)/shard_map/ppermute | solution.py:327
  18.6 0.4 collective-permute-done.2.m0
  19.0 0.0 collective-permute-start.4
  19.0 0.5 collective-permute-start.6
  20.1 0.0 collective-permute-done.5.m4
  20.1 0.0 copy-start.6
  20.1 0.4 collective-permute-done.4.m3
  20.6 0.5 collective-permute-done.6.m5
  21.1 0.0 copy-done.7
  21.1 0.0 copy-done.8
  21.1 0.0 copy-done.6
  21.1 17.4 %edge_step.1 = (bf16[32,136,128]{2,1,0:T(8,128)(2,1)}, bf16[2304,256]{1,0:T(8,128)(2,1)S(1)}, bf16[1152,256]{1,0:T(8,128)(2,1)S(1)}, bf16[320,256]{1,0:T(8,128)(...) custom-call(s32[1]{0:T(128)} %bitcast.band, s32[1]{0:T(128)} %bitcast.1.chan, s32[1]{0:T(128)S(6)} %copy.20.count, ...), custom_call_target="tpu_custom_call" | custom-call | flops 8999999488 | bytes 8388608 | tf_op jit(solution)/shard_map/edge_step/pallas_call | solution.py:421
  38.5 7.8 %all-to-all-start = ((bf16[32,136,128]{2,1,0:T(8,128)(2,1)}), bf16[32,136,128]{2,1,0:T(8,128)(2,1)S(1)}, u32[]{:S(2)}, u32[]{:S(2)}) async-start(bf16[32,136,128]{2,1,0:T(8,128)(2,1)} %get-tuple-element.26), calls=%async_computation | async-start | bytes 2228224 | tf_op jit(solution)/shard_map/all_to_all | solution.py:469
  46.4 0.0 copy-start.3
  46.4 1.6 %collective-permute-start.9 = (bf16[320,256]{1,0:T(8,128)(2,1)}, bf16[320,256]{1,0:T(8,128)(2,1)}, u32[]{:S(2)}, u32[]{:S(2)}) collective-permute-start(bf16[320,256]{1,0:T(8,128)(2,1)} %get-tuple-element.27), channel_id=1, source_target_pairs={{0,2},{4,6},{8,10},{12,14},{16,18},{20,22},{24,26},{28,30},{32,34}... | collective-permute-start | bytes 491528 | tf_op jit(solution)/shard_map/ppermute | solution.py:327
  47.9 6.3 %collective-permute-start.10 = (bf16[320,256]{1,0:T(8,128)(2,1)}, bf16[320,256]{1,0:T(8,128)(2,1)}, u32[]{:S(2)}, u32[]{:S(2)}) collective-permute-start(bf16[320,256]{1,0:T(8,128)(2,1)} %get-tuple-element.28), channel_id=1, source_target_pairs={{2,4},{6,8},{10,12},{14,16},{18,20},{22,24},{26,28},{30,32},{34,36... | collective-permute-start | bytes 491528 | tf_op jit(solution)/shard_map/ppermute | solution.py:327
  54.2 2.5 %convolution_convert_fusion = bf16[1152,512]{1,0:T(8,128)(2,1)} fusion(bf16[512,256]{1,0:T(8,128)(2,1)} %w_edge.1, bf16[2304,256]{1,0:T(8,128)(2,1)S(1)} %get-tuple-element.24), kind=kOutput, calls=%fused_computation.2 | convolution fusion | flops 302579712 | bytes 2031616 | tf_op jit(solution)/shard_map/dot_general | solution.py:30
  56.7 0.0 copy-done.3
  56.7 1.2 %convolution_convert_fusion.1 = bf16[576,512]{1,0:T(8,128)(2,1)} fusion(bf16[512,256]{1,0:T(8,128)(2,1)S(1)} %copy-done.3, bf16[1152,256]{1,0:T(8,128)(2,1)S(1)} %get-tuple-element.23), kind=kOutput, calls=%fused_computation.5 | convolution fusion | flops 151289856 | bytes 1146880 | tf_op jit(solution)/shard_map/dot_general | solution.py:30
  57.8 6.6 %all-to-all-done = bf16[32,136,128]{2,1,0:T(8,128)(2,1)S(1)} async-done(((bf16[32,136,128]{2,1,0:T(8,128)(2,1)}), bf16[32,136,128]{2,1,0:T(8,128)(2,1)S(1)}, u32[]{:S(2)}, u32[]{:S(2)}) %all-to-all-start) | async-done | bytes 1114144 | tf_op jit(solution)/shard_map/all_to_all | solution.py:469
  64.4 0.2 reduce_sum.12
  64.6 0.4 collective-permute-done.9
  65.0 2.2 %collective-permute-done.10 = bf16[320,256]{1,0:T(8,128)(2,1)} collective-permute-done((bf16[320,256]{1,0:T(8,128)(2,1)}, bf16[320,256]{1,0:T(8,128)(2,1)}, u32[]{:S(2)}, u32[]{:S(2)}) %collective-permute-start.10) | collective-permute-done | bytes 163872 | tf_op jit(solution)/shard_map/ppermute | solution.py:327
  67.2 4.5 %collective-permute-start.12 = (bf16[136,128]{1,0:T(8,128)(2,1)S(1)}, bf16[136,128]{1,0:T(8,128)(2,1)S(1)}, u32[]{:S(2)}, u32[]{:S(2)}) collective-permute-start(bf16[136,128]{1,0:T(8,128)(2,1)S(1)} %reduce_sum.12), channel_id=1, source_target_pairs={{0,64},{64,0},{128,192},{192,128},{1,65},{65,1},{129,193},{193,129... | collective-permute-start | bytes 104456 | tf_op jit(solution)/shard_map/ppermute | solution.py:335
  71.7 1.9 %collective-permute-done.12 = bf16[136,128]{1,0:T(8,128)(2,1)S(1)} collective-permute-done((bf16[136,128]{1,0:T(8,128)(2,1)S(1)}, bf16[136,128]{1,0:T(8,128)(2,1)S(1)}, u32[]{:S(2)}, u32[]{:S(2)}) %collective-permute-start.12) | collective-permute-done | bytes 34848 | tf_op jit(solution)/shard_map/ppermute | solution.py:335
  73.6 3.5 %collective-permute-start.13 = (bf16[136,128]{1,0:T(8,128)(2,1)S(1)}, bf16[136,128]{1,0:T(8,128)(2,1)S(1)}, u32[]{:S(2)}, u32[]{:S(2)}) collective-permute-start(bf16[136,128]{1,0:T(8,128)(2,1)S(1)} %add_convert_fusion.2), channel_id=1, source_target_pairs={{0,192},{64,128},{128,64},{192,0},{1,193},{65,129},{129,65},{193,1... | collective-permute-start | bytes 104456 | tf_op jit(solution)/shard_map/ppermute | solution.py:335
  77.1 0.0 collective-permute-start.7
  77.1 0.5 collective-permute-start.8
  77.6 2.1 %collective-permute-done.13 = bf16[136,128]{1,0:T(8,128)(2,1)S(1)} collective-permute-done((bf16[136,128]{1,0:T(8,128)(2,1)S(1)}, bf16[136,128]{1,0:T(8,128)(2,1)S(1)}, u32[]{:S(2)}, u32[]{:S(2)}) %collective-permute-start.13) | collective-permute-done | bytes 34848 | tf_op jit(solution)/shard_map/ppermute | solution.py:335
  79.8 1.1 %broadcast_in_dim.2 = bf16[32,64,256]{2,1,0:T(8,128)(2,1)} broadcast(bf16[64,256]{1,0:T(8,128)(2,1)S(1)} %pad_maximum_fusion.1), dimensions={1,2} | broadcast | bytes 1081344 | tf_op jit(solution)/shard_map/broadcast_in_dim | solution.py:479
  80.9 4.9 %all-to-all-start.1 = ((bf16[32,64,256]{2,1,0:T(8,128)(2,1)}), bf16[32,64,256]{2,1,0:T(8,128)(2,1)S(1)}, u32[]{:S(2)}, u32[]{:S(2)}) async-start(bf16[32,64,256]{2,1,0:T(8,128)(2,1)} %broadcast_in_dim.2), calls=%async_computation.1 | async-start | bytes 2097152 | tf_op jit(solution)/shard_map/all_to_all | solution.py:480
  85.8 0.0 copy-start.4
  85.9 0.0 collective-permute-done.7
  85.9 2.3 %fusion.1 = bf16[576,512]{1,0:T(8,128)(2,1)} fusion(bf16[512,256]{1,0:T(8,128)(2,1)S(1)} %copy-done.3, bf16[576,512]{1,0:T(8,128)(2,1)} %collective-permute-done.7, bf16[1152,256]{1,0:T(8,128)(2,1)S(1)} %get-tuple-element.23), kind=kOutput, calls=%fused_computation.4 | convolution fusion | flops 151879680 | bytes 1736704 | tf_op jit(solution)/shard_map/dot_general | solution.py:30
  88.1 0.0 collective-permute-done.8
  88.1 0.0 copy-done.4
  88.2 2.8 %fusion = bf16[1152,512]{1,0:T(8,128)(2,1)} fusion(bf16[512,256]{1,0:T(8,128)(2,1)S(1)} %copy-done.4, bf16[1152,512]{1,0:T(8,128)(2,1)} %collective-permute-done.8, bf16[2304,256]{1,0:T(8,128)(2,1)S(1)} %get-tuple-element.24), kind=kOutput, calls=%fused_computation.1 | convolution fusion | flops 303759360 | bytes 3211264 | tf_op jit(solution)/shard_map/dot_general | solution.py:30
  91.0 1.0 %add_convert_fusion.1 = bf16[320,256]{1,0:T(8,128)(2,1)S(1)} fusion(bf16[320,256]{1,0:T(8,128)(2,1)} %collective-permute-done.10, f32[320,256]{1,0:T(8,128)S(1)} %get-tuple-element.25, bf16[320,256]{1,0:T(8,128)(2,1)} %collective-permute-done.9), kind=kLoop, calls=%fused_computation.11 | loop fusion | flops 409600 | bytes 819200 | tf_op jit(solution)/shard_map/convert_element_type | solution.py:484
  92.0 0.0 copy-done.2
  92.0 0.2 convolution_convert_fusion.2
  92.3 0.1 collective-permute-start.11
  92.4 0.6 slice_bitcast_fusion
  92.9 0.8 collective-permute-done.11
  93.8 0.9 add_convert_fusion
  94.7 5.6 %all-to-all-done.1 = bf16[32,64,256]{2,1,0:T(8,128)(2,1)S(1)} async-done(((bf16[32,64,256]{2,1,0:T(8,128)(2,1)}), bf16[32,64,256]{2,1,0:T(8,128)(2,1)S(1)}, u32[]{:S(2)}, u32[]{:S(2)}) %all-to-all-start.1) | async-done | bytes 1048608 | tf_op jit(solution)/shard_map/all_to_all | solution.py:480
  100.2 0.1 fusion.13
  100.3 0.8 bitcast_convert_fusion.2
  101.2 0.9 maximum_convert_fusion
  102.0 1.1 %bitcast_convert_fusion = (f32[512,256]{1,0:T(8,128)}, f32[512,256]{1,0:T(8,128)}) fusion(bf16[8,64,256]{2,1,0:T(8,128)(2,1)S(1)} %get-tuple-element.34, bf16[8,64,256]{2,1,0:T(8,128)(2,1)S(1)} %get-tuple-element.35), kind=kLoop, calls=%fused_computation.15 | loop fusion | flops 262144 | bytes 1572864 | tf_op jit(solution)/shard_map/reshape | solution.py:490
  (8 shorter events, 0.1 us)
Async XLA Ops:
  0.6 8.6 %collective-permute-start.1 = (bf16[1152,512]{1,0:T(8,128)(2,1)}, bf16[1152,512]{1,0:T(8,128)(2,1)S(1)}, u32[]{:S(2)}, u32[]{:S(2)}) collective-permute-start(bf16[1152,512]{1,0:T(8,128)(2,1)} %edge_own.3), channel_id=1, source_target_pairs={{0,1},{1,0},{2,3},{3,2},{4,5},{5,4},{6,7},{7,6},{8,9},{9,8},{10,11... | collective-permute-start | bytes 3538952 | tf_op jit(solution)/shard_map/ppermute | solution.py:321
  0.7 8.5 %collective-permute-start = (bf16[576,512]{1,0:T(8,128)(2,1)}, bf16[576,512]{1,0:T(8,128)(2,1)S(1)}, u32[]{:S(2)}, u32[]{:S(2)}) collective-permute-start(bf16[576,512]{1,0:T(8,128)(2,1)} %grid_own.3), channel_id=1, source_target_pairs={{0,1},{1,0},{2,3},{3,2},{4,5},{5,4},{6,7},{7,6},{8,9},{9,8},{10,11... | collective-permute-start | bytes 1769480 | tf_op jit(solution)/shard_map/ppermute | solution.py:321
  2.3 12.9 %copy-start.5 = (bf16[2,160,512]{2,1,0:T(8,128)(2,1)}, bf16[2,160,512]{2,1,0:T(8,128)(2,1)S(1)}, u32[]{:S(2)}) copy-start(bf16[2,160,512]{2,1,0:T(8,128)(2,1)S(1)} %pad_maximum_fusion.m1) | copy-start | bytes 983044
  2.3 17.8 %collective-permute-start.5 = (bf16[2,160,512]{2,1,0:T(8,128)(2,1)S(1)}, bf16[2,160,512]{2,1,0:T(8,128)(2,1)S(1)}, u32[]{:S(2)}, u32[]{:S(2)}) collective-permute-start(bf16[2,160,512]{2,1,0:T(8,128)(2,1)S(1)} %pad_maximum_fusion.m1), channel_id=1, source_target_pairs={{0,1},{1,0},{2,3},{3,2},{4,5},{5,4},{6,7},{7,6},{8,9},{9,8},{10,11... | collective-permute-start | bytes 983048 | tf_op jit(solution)/shard_map/ppermute | solution.py:321
  2.5 16.1 %collective-permute-start.3 = (bf16[2,160,512]{2,1,0:T(8,128)(2,1)S(1)}, bf16[2,160,512]{2,1,0:T(8,128)(2,1)S(1)}, u32[]{:S(2)}, u32[]{:S(2)}) collective-permute-start(bf16[2,160,512]{2,1,0:T(8,128)(2,1)S(1)} %pad_maximum_fusion.m1), channel_id=1, source_target_pairs={{2,4},{6,8},{10,12},{14,16},{18,20},{22,24},{26,28},{30,32},{34,36... | collective-permute-start | bytes 983048 | tf_op jit(solution)/shard_map/ppermute | solution.py:327
  9.1 9.8 %collective-permute-start.2 = (bf16[2,160,512]{2,1,0:T(8,128)(2,1)S(1)}, bf16[2,160,512]{2,1,0:T(8,128)(2,1)S(1)}, u32[]{:S(2)}, u32[]{:S(2)}) collective-permute-start(bf16[2,160,512]{2,1,0:T(8,128)(2,1)S(1)} %pad_maximum_fusion.m1), channel_id=1, source_target_pairs={{0,2},{4,6},{8,10},{12,14},{16,18},{20,22},{24,26},{28,30},{32,34}... | collective-permute-start | bytes 983048 | tf_op jit(solution)/shard_map/ppermute | solution.py:327
  9.2 6.0 %copy-start.1 = (bf16[576,512]{1,0:T(8,128)(2,1)}, bf16[576,512]{1,0:T(8,128)(2,1)S(1)}, u32[]{:S(2)}) copy-start(bf16[576,512]{1,0:T(8,128)(2,1)S(1)} %collective-permute-done.grid_far) | copy-start | bytes 1769476
  9.3 5.9 %copy-start = (bf16[1152,512]{1,0:T(8,128)(2,1)}, bf16[1152,512]{1,0:T(8,128)(2,1)S(1)}, u32[]{:S(2)}) copy-start(bf16[1152,512]{1,0:T(8,128)(2,1)S(1)} %collective-permute-done.1.edge_far) | copy-start | bytes 3538948
  18.6 2.5 %copy-start.7 = (bf16[2,160,512]{2,1,0:T(8,128)(2,1)}, bf16[2,160,512]{2,1,0:T(8,128)(2,1)S(1)}, u32[]{:S(2)}) copy-start(bf16[2,160,512]{2,1,0:T(8,128)(2,1)S(1)} %collective-permute-done.3.m2) | copy-start | bytes 983044
  18.9 2.1 %copy-start.8 = (bf16[2,160,512]{2,1,0:T(8,128)(2,1)}, bf16[2,160,512]{2,1,0:T(8,128)(2,1)S(1)}, u32[]{:S(2)}) copy-start(bf16[2,160,512]{2,1,0:T(8,128)(2,1)S(1)} %collective-permute-done.2.m0) | copy-start | bytes 983044
  19.0 1.6 %collective-permute-start.4 = (bf16[2,160,512]{2,1,0:T(8,128)(2,1)S(1)}, bf16[2,160,512]{2,1,0:T(8,128)(2,1)S(1)}, u32[]{:S(2)}, u32[]{:S(2)}) collective-permute-start(bf16[2,160,512]{2,1,0:T(8,128)(2,1)S(1)} %collective-permute-done.2.m0), channel_id=1, source_target_pairs={{0,1},{1,0},{2,3},{3,2},{4,5},{5,4},{6,7},{7,6},{8,9},{9,8},{10,11... | collective-permute-start | bytes 983048 | tf_op jit(solution)/shard_map/ppermute | solution.py:321
  19.0 2.1 %collective-permute-start.6 = (bf16[2,160,512]{2,1,0:T(8,128)(2,1)S(1)}, bf16[2,160,512]{2,1,0:T(8,128)(2,1)S(1)}, u32[]{:S(2)}, u32[]{:S(2)}) collective-permute-start(bf16[2,160,512]{2,1,0:T(8,128)(2,1)S(1)} %collective-permute-done.3.m2), channel_id=1, source_target_pairs={{0,1},{1,0},{2,3},{3,2},{4,5},{5,4},{6,7},{7,6},{8,9},{9,8},{10,11... | collective-permute-start | bytes 983048 | tf_op jit(solution)/shard_map/ppermute | solution.py:321
  20.1 0.9 copy-start.6
  38.5 25.9 %all-to-all-start = ((bf16[32,136,128]{2,1,0:T(8,128)(2,1)}), bf16[32,136,128]{2,1,0:T(8,128)(2,1)S(1)}, u32[]{:S(2)}, u32[]{:S(2)}) async-start(bf16[32,136,128]{2,1,0:T(8,128)(2,1)} %get-tuple-element.26), calls=%async_computation | async-start | bytes 2228224 | tf_op jit(solution)/shard_map/all_to_all | solution.py:469
  46.4 10.3 %copy-start.3 = (bf16[512,256]{1,0:T(8,128)(2,1)S(1)}, bf16[512,256]{1,0:T(8,128)(2,1)}, u32[]{:S(2)}) copy-start(bf16[512,256]{1,0:T(8,128)(2,1)} %w_grid.1) | copy-start | bytes 786436
  46.4 18.6 %collective-permute-start.9 = (bf16[320,256]{1,0:T(8,128)(2,1)}, bf16[320,256]{1,0:T(8,128)(2,1)}, u32[]{:S(2)}, u32[]{:S(2)}) collective-permute-start(bf16[320,256]{1,0:T(8,128)(2,1)} %get-tuple-element.27), channel_id=1, source_target_pairs={{0,2},{4,6},{8,10},{12,14},{16,18},{20,22},{24,26},{28,30},{32,34}... | collective-permute-start | bytes 491528 | tf_op jit(solution)/shard_map/ppermute | solution.py:327
  47.9 19.3 %collective-permute-start.10 = (bf16[320,256]{1,0:T(8,128)(2,1)}, bf16[320,256]{1,0:T(8,128)(2,1)}, u32[]{:S(2)}, u32[]{:S(2)}) collective-permute-start(bf16[320,256]{1,0:T(8,128)(2,1)} %get-tuple-element.28), channel_id=1, source_target_pairs={{2,4},{6,8},{10,12},{14,16},{18,20},{22,24},{26,28},{30,32},{34,36... | collective-permute-start | bytes 491528 | tf_op jit(solution)/shard_map/ppermute | solution.py:327
  67.2 6.4 %collective-permute-start.12 = (bf16[136,128]{1,0:T(8,128)(2,1)S(1)}, bf16[136,128]{1,0:T(8,128)(2,1)S(1)}, u32[]{:S(2)}, u32[]{:S(2)}) collective-permute-start(bf16[136,128]{1,0:T(8,128)(2,1)S(1)} %reduce_sum.12), channel_id=1, source_target_pairs={{0,64},{64,0},{128,192},{192,128},{1,65},{65,1},{129,193},{193,129... | collective-permute-start | bytes 104456 | tf_op jit(solution)/shard_map/ppermute | solution.py:335
  73.6 6.1 %collective-permute-start.13 = (bf16[136,128]{1,0:T(8,128)(2,1)S(1)}, bf16[136,128]{1,0:T(8,128)(2,1)S(1)}, u32[]{:S(2)}, u32[]{:S(2)}) collective-permute-start(bf16[136,128]{1,0:T(8,128)(2,1)S(1)} %add_convert_fusion.2), channel_id=1, source_target_pairs={{0,192},{64,128},{128,64},{192,0},{1,193},{65,129},{129,65},{193,1... | collective-permute-start | bytes 104456 | tf_op jit(solution)/shard_map/ppermute | solution.py:335
  77.1 8.8 %collective-permute-start.7 = (bf16[576,512]{1,0:T(8,128)(2,1)}, bf16[576,512]{1,0:T(8,128)(2,1)}, u32[]{:S(2)}, u32[]{:S(2)}) collective-permute-start(bf16[576,512]{1,0:T(8,128)(2,1)} %convolution_convert_fusion.1), channel_id=1, source_target_pairs={{0,1},{1,0},{2,3},{3,2},{4,5},{5,4},{6,7},{7,6},{8,9},{9,8},{10,11... | collective-permute-start | bytes 1769480 | tf_op jit(solution)/shard_map/ppermute | solution.py:321
  77.1 11.0 %collective-permute-start.8 = (bf16[1152,512]{1,0:T(8,128)(2,1)}, bf16[1152,512]{1,0:T(8,128)(2,1)}, u32[]{:S(2)}, u32[]{:S(2)}) collective-permute-start(bf16[1152,512]{1,0:T(8,128)(2,1)} %convolution_convert_fusion), channel_id=1, source_target_pairs={{0,1},{1,0},{2,3},{3,2},{4,5},{5,4},{6,7},{7,6},{8,9},{9,8},{10,11... | collective-permute-start | bytes 3538952 | tf_op jit(solution)/shard_map/ppermute | solution.py:321
  80.9 19.3 %all-to-all-start.1 = ((bf16[32,64,256]{2,1,0:T(8,128)(2,1)}), bf16[32,64,256]{2,1,0:T(8,128)(2,1)S(1)}, u32[]{:S(2)}, u32[]{:S(2)}) async-start(bf16[32,64,256]{2,1,0:T(8,128)(2,1)} %broadcast_in_dim.2), calls=%async_computation.1 | async-start | bytes 2097152 | tf_op jit(solution)/shard_map/all_to_all | solution.py:480
  85.8 2.3 %copy-start.4 = (bf16[512,256]{1,0:T(8,128)(2,1)S(1)}, bf16[512,256]{1,0:T(8,128)(2,1)}, u32[]{:S(2)}) copy-start(bf16[512,256]{1,0:T(8,128)(2,1)} %w_edge.1) | copy-start | bytes 786436
  88.1 3.9 %copy-start.2 = (bf16[512,256]{1,0:T(8,128)(2,1)S(1)}, bf16[512,256]{1,0:T(8,128)(2,1)}, u32[]{:S(2)}) copy-start(bf16[512,256]{1,0:T(8,128)(2,1)} %w_mesh_in.1) | copy-start | bytes 786436
  92.3 1.5 %collective-permute-start.11 = (bf16[160,512]{1,0:T(8,128)(2,1)S(1)}, bf16[160,512]{1,0:T(8,128)(2,1)S(1)}, u32[]{:S(2)}, u32[]{:S(2)}) collective-permute-start(bf16[160,512]{1,0:T(8,128)(2,1)S(1)} %convolution_convert_fusion.2), channel_id=1, source_target_pairs={{0,1},{1,0},{2,3},{3,2},{4,5},{5,4},{6,7},{7,6},{8,9},{9,8},{10,11... | collective-permute-start | bytes 491528 | tf_op jit(solution)/shard_map/ppermute | solution.py:321

commit v7 on v6

--- a/solution.py
+++ b/solution.py
@@ -70,8 +70,10 @@
 
 
 def sender_kernel(
+    piece,
     band,
     chan,
+    count,
     grid_own,
     grid_far,
     edge_own,
@@ -80,17 +82,21 @@
     w_edge,
     bias_in,
     send_in,
+    recv_in,
     pre,
+    left_mesh,
+    right,
     grid,
     edge,
     weights,
     bias_row,
     senders,
+    receivers,
     table,
     left,
     in_sems,
 ):
-    where = (band[0], chan[0])
+    where = (band[0], chan[0], count[0])
     half_edges = edge_own.shape[0]
     half_grid = grid_own.shape[0]
     n_grid = 2 * half_grid
@@ -100,6 +106,7 @@
             (w_grid, weights),
             (grid_own, grid),
             (send_in, senders),
+            (recv_in, receivers),
             (w_edge, table.at[n_grid:]),
             (bias_in, bias_row),
             (edge_own, edge),
@@ -135,10 +142,21 @@
 
         for c in range(per):
             at = index_row(i * per + c, groups, where)
+            mine = pl.ds(pl.multiple_of(i * block + c * LANES, LANES), LANES)
             row = local_senders(senders[pl.ds(at, 1), :], where, half_grid)
-            column = jnp.broadcast_to(row, (LANES, LANES)).T
+            row = jnp.broadcast_to(row, (LANES, LANES))
+            column = row.T
             for k in range(n_grid // LANES):
                 left[c * LANES : (c + 1) * LANES, k * LANES : (k + 1) * LANES] = one_hot(column, k * LANES)
+                right[k * LANES : (k + 1) * LANES, mine] = one_hot_rows(row, k * LANES)
+            slot = at * LANES + lax.broadcasted_iota(jnp.int32, (1, LANES), 1)
+            row = local_receivers(receivers[pl.ds(at, 1), :], slot, where, piece)
+            row = jnp.broadcast_to(row, (LANES, LANES))
+            column = row.T
+            for k in range(left_mesh.shape[1] // LANES):
+                left_mesh[mine, k * LANES : (k + 1) * LANES] = one_hot(column, k * LANES)
+                at_row = n_grid + k * LANES
+                right[at_row : at_row + LANES, mine] = one_hot_rows(row, k * LANES)
         pre[rows, :] = dot(left[...], table[...]) + bias_row[...]
         return carry
 
@@ -146,9 +164,6 @@
 
 
 def edge_kernel(
-    band,
-    chan,
-    count,
     grid_own,
     grid_far,
     edge_own,
@@ -162,8 +177,8 @@
     w_mesh_in,
     w_out_in,
     pre_part,
-    send_in,
-    recv_in,
+    left,
+    right,
     wire_out,
     cots,
     seg_grid,
@@ -175,14 +190,10 @@
     lat,
     cot,
     table,
-    left,
-    right,
     both,
     sums,
     w_mesh,
     w_out,
-    senders,
-    receivers,
     wire,
     low_v,
     high_v,
@@ -190,7 +201,6 @@
     edge_sems,
     out_sems,
 ):
-    where = (band[0], chan[0], count[0])
     half_edges = edge_own.shape[0]
     half_grid = grid_own.shape[0]
     n_grid = 2 * half_grid
@@ -198,21 +208,21 @@
     n_mesh = 6 * piece
     pad_mesh = lat.shape[0]
     n_rows = n_grid + pad_mesh
-    block = left.shape[0]
+    block = EDGE_BLOCK
     hidden = w_mesh.shape[1]
     near = half_edges // UNIT
     apart = ((0, m0), (1, m1), (2, m2), (4, m4))
     lats = [(m.at[0], lat.at[k * piece : (k + 1) * piece]) for k, m in apart]
     cot_pairs = [(m.at[1], cot.at[k * piece : (k + 1) * piece]) for k, m in apart]
     grids = [(grid_own, grid.at[0:half_grid]), (grid_far, grid.at[half_grid:])]
-    small = [(w_mesh_in, w_mesh), (w_out_in, w_out), (send_in, senders), (recv_in, receivers)]
+    small = [(w_mesh_in, w_mesh), (w_out_in, w_out)]
     fetches = copies(small + lats + cot_pairs + grids, in_sems)
     edges = [
         (source.at[k * UNIT : (k + 1) * UNIT], edge.at[(k + off) * UNIT : (k + off + 1) * UNIT])
         for source, off in ((edge_own, 0), (edge_far, near))
         for k in range(near)
     ]
-    for f in fetches[0:12] + copies(edges, edge_sems) + fetches[12:]:
+    for f in fetches[0:10] + copies(edges, edge_sems) + fetches[10:]:
         f.start()
     for k, m in ((3, m3), (5, m5)):
         lat[k * piece : (k + 1) * piece] = m[0]
@@ -220,35 +230,16 @@
     if pad_mesh > n_mesh:
         lat[n_mesh:] = jnp.zeros((pad_mesh - n_mesh, lat.shape[1]), BF)
         cot[n_mesh:] = jnp.zeros((pad_mesh - n_mesh, cot.shape[1]), BF)
-    for f in fetches[0:12]:
+    for f in fetches[0:10]:
         f.wait()
     table[:, 0:hidden] = dot(lat[...], w_mesh[...]).astype(BF)
     cot_terms = dot_t(cot[...], w_out[...])
     high = cot_terms.astype(BF)
     table[:, hidden : 2 * hidden] = high
     table[:, 2 * hidden :] = (cot_terms - high.astype(F32)).astype(BF)
-    groups = 2 * half_edges // LANES
-    per = block // LANES
-
     def step(i, carry):
         rows = pl.ds(pl.multiple_of(i * block, block), block)
-        for c in range(per):
-            at = index_row(i * per + c, groups, where)
-            mine = slice(c * LANES, (c + 1) * LANES)
-            edge_lanes = pl.ds(pl.multiple_of(i * block + c * LANES, LANES), LANES)
-            slot = at * LANES + lax.broadcasted_iota(jnp.int32, (1, LANES), 1)
-            row = local_receivers(receivers[pl.ds(at, 1), :], slot, where, piece)
-            row = jnp.broadcast_to(row, (LANES, LANES))
-            column = row.T
-            for k in range(pad_mesh // LANES):
-                left[mine, k * LANES : (k + 1) * LANES] = one_hot(column, k * LANES)
-                at_row = n_grid + k * LANES
-                right[at_row : at_row + LANES, edge_lanes] = one_hot_rows(row, k * LANES)
-            row = local_senders(senders[pl.ds(at, 1), :], where, half_grid)
-            row = jnp.broadcast_to(row, (LANES, LANES))
-            for k in range(n_grid // LANES):
-                right[k * LANES : (k + 1) * LANES, edge_lanes] = one_hot_rows(row, k * LANES)
-        got = dot(left[...], table[...])
+        got = dot(left[rows, :], table[...])
         pre = pre_part[rows, :] + got[:, 0:hidden]
         hidden_cot = got[:, hidden : 2 * hidden] + got[:, 2 * hidden :]
         sig = jax.nn.sigmoid(pre)
@@ -289,7 +280,7 @@
     )
     for f in stores[0:2]:
         f.start()
-    for f in fetches[12:] + copies(edges, edge_sems):
+    for f in fetches[10:] + copies(edges, edge_sems):
         f.wait()
     sub = lax.broadcasted_iota(jnp.int32, (16, LANES), 0)
     bias_total = dot(jnp.ones((16, 2 * half_edges), BF), both[:, 0:hidden])
@@ -374,7 +365,7 @@
     receivers = receivers.reshape(-1, LANES)
     vmem = pl.BlockSpec(memory_space=pltpu.VMEM)
     smem = pl.BlockSpec(memory_space=pltpu.SMEM)
-    small, large = [pltpu.CompilerParams(vmem_limit_bytes=n * 2**20) for n in (16, 40)]
+    small, large = [pltpu.CompilerParams(vmem_limit_bytes=n * 2**20) for n in (12, 26)]
 
     def near(x):
         return pltpu.with_memory_space_constraint(x, pltpu.VMEM)
@@ -388,34 +379,39 @@
     anywhere = pl.BlockSpec(memory_space=pl.ANY)
     dma = pltpu.SemaphoreType.DMA
     n_edges = 2 * half_edges
-    pre = pl.pallas_call(
-        sender_kernel,
-        out_shape=pltpu.VMEM((n_edges, hidden), F32),
-        in_specs=[smem] * 2 + [anywhere, vmem] * 2 + [anywhere] * 4,
-        out_specs=vmem,
+    pre, left, right = pl.pallas_call(
+        functools.partial(sender_kernel, piece),
+        out_shape=(
+            pltpu.VMEM((n_edges, hidden), F32),
+            pltpu.VMEM((n_edges, pad_mesh), BF),
+            pltpu.VMEM((n_grid + pad_mesh, n_edges), BF),
+        ),
+        in_specs=[smem] * 3 + [anywhere, vmem] * 2 + [anywhere] * 5,
+        out_specs=(vmem,) * 3,
         scratch_shapes=[
             pltpu.VMEM((half_grid, width), BF),
             pltpu.VMEM((half_edges, width), BF),
             pltpu.VMEM((width, hidden), BF),
             pltpu.VMEM((1, hidden), F32),
             pltpu.VMEM(senders.shape, jnp.int32),
+            pltpu.VMEM(receivers.shape, jnp.int32),
             pltpu.VMEM((n_grid + width, hidden), BF),
             pltpu.VMEM((EDGE_BLOCK, n_grid + width), BF),
-            dma((6,)),
+            dma((7,)),
         ],
         compiler_params=small,
         cost_estimate=pl.CostEstimate(flops=SENDER_FLOPS, transcendentals=0, bytes_accessed=1 << 22),
         name="sender_step",
     )(
-        *scalars(band.reshape(1), chan.reshape(1)),
+        *scalars(band.reshape(1), chan.reshape(1), edge_count),
         *wide(grid_latent),
         near(grid_far),
         *wide(edge_latent),
         near(edge_far),
-        *wide(w_grid, w_edge, bias.reshape(1, hidden), senders),
+        *wide(w_grid, w_edge, bias.reshape(1, hidden), senders, receivers),
     )
 
-    mesh_low, mesh_high, pre = lax.optimization_barrier((mesh_low, mesh_high, pre))
+    mesh_low, mesh_high, pre, left, right = lax.optimization_barrier((mesh_low, mesh_high, pre, left, right))
     mesh_near = (mesh_low, mesh_own, mesh_high)
     mesh_far = [near(swap(mesh_low)), *wide(mesh_own_far), near(swap(mesh_high))]
     wire, cots, seg_grid, rim_low, rim_mid, rim_high = pl.pallas_call(
@@ -428,7 +424,7 @@
             pltpu.VMEM((2 * piece, hidden), F32),
             pltpu.HBM((2 * piece, hidden), BF),
         ),
-        in_specs=[smem] * 3 + [anywhere] * 7 + [vmem, anywhere, vmem, anywhere, anywhere, vmem, anywhere, anywhere],
+        in_specs=[anywhere] * 7 + [vmem, anywhere, vmem, anywhere, anywhere, vmem, vmem, vmem],
         out_specs=(anywhere, vmem, vmem, anywhere, vmem, anywhere),
         scratch_shapes=[
             pltpu.VMEM((n_grid, width), BF),
@@ -436,18 +432,14 @@
             pltpu.VMEM((pad_mesh, width), BF),
             pltpu.VMEM((pad_mesh, width), BF),
             pltpu.VMEM((pad_mesh, 3 * hidden), BF),
-            pltpu.VMEM((EDGE_BLOCK, pad_mesh), BF),
-            pltpu.VMEM((n_grid + pad_mesh, n_edges), BF),
             pltpu.VMEM((n_edges, 2 * hidden), BF),
             pltpu.VMEM((pad_mesh, 2 * hidden), F32),
             pltpu.VMEM((width, hidden), BF),
             pltpu.VMEM((hidden, width), BF),
-            pltpu.VMEM(senders.shape, jnp.int32),
-            pltpu.VMEM(receivers.shape, jnp.int32),
             pltpu.VMEM((MEMBERS, 2 * ROWS + 16, LANES), BF),
             pltpu.VMEM((2 * piece, hidden), BF),
             pltpu.VMEM((2 * piece, hidden), BF),
-            dma((14,)),
+            dma((12,)),
             dma((n_edges // UNIT,)),
             dma((6,)),
         ],
@@ -455,12 +447,12 @@
         cost_estimate=pl.CostEstimate(flops=EDGE_FLOPS, transcendentals=1 << 20, bytes_accessed=1 << 23),
         name="edge_step",
     )(
-        *scalars(band.reshape(1), chan.reshape(1), edge_count),
         *wide(grid_latent, grid_far, edge_latent, edge_far, *mesh_near),
         *mesh_far,
         *wide(w_mesh, w_out),
         near(pre),
-        *wide(senders, receivers),
+        near(left),
+        near(right),
     )
 
     cot_own, cot_far = (cots[:half_edges], cots[half_edges:])

time: 104 us -> 100 us (0.962)
  waiting for transfers between devices: 24.3 us -> 21.3 us
    ppermute x4, waiting for transfers between devices: 6.34 us -> 2.64 us  [pair_swap(): return lax.ppermute(x, BAND, pairs + [(j, i) for i, j in pairs])]
    pallas_call x1, Pallas kernels: 5.91 us -> 9.2 us  [body(): pl.pallas_call(functools.partial(sender_kernel, piece), out_shape=(pltpu....]
    pallas_call x1, Pallas kernels: 17.4 us -> 14.3 us  [body(): pl.pallas_call(edge_kernel, out_shape=(pltpu.HBM((MEMBERS, 2 * ROWS + TAI...]
  transfers between devices with their start and end apart: 16 -> 16, of which waited for: 11 -> 9; matrix products, arithmetic and copies ran while one was open for 13% -> 14% of each run, Pallas kernels for 6% -> 9%
where the time goes in v7:
time: 100 us; the launch traced here: 99.9 us
  starting transfers between devices  36.9 us (37%)
  Pallas kernels  23.5 us (24%)
  waiting for transfers between devices  21.3 us (21%)
  matrix products  9.86 us (10%)
  other arithmetic  5.05 us (5%)
  local copies, waits for them, and re-layouts  1.79 us (2%)
  between operations  1.55 us (2%)
    ppermute x4, starting transfers between devices, pair_swap(): return lax.ppermute(x, BAND, pairs + [(j, i) for i, j in pairs])  14.5 us
    pallas_call x1, Pallas kernels, body(): pl.pallas_call(edge_kernel, out_shape=(pltpu.HBM((MEMBERS, 2 * ROWS + TAI...  14.3 us
    dot_general x6, matrix products, dot_t(): lax.dot_general(a, b, (((1,), (1,)), ((), ())), preferred_element_type=F32)  9.86 us
    pallas_call x1, Pallas kernels, body(): pl.pallas_call(functools.partial(sender_kernel, piece), out_shape=(pltpu....  9.2 us
    ppermute x2, starting transfers between devices, depth_total(): other = lax.ppermute(mine, 'zh', [(i, i ^ mask) for i in range(depth)])  7.95 us
    all_to_all x1, starting transfers between devices, body(): arrived = lax.all_to_all(wire, GROUP, 0, 0, tiled=True)  7.5 us
    all_to_all x1, waiting for transfers between devices, body(): arrived = lax.all_to_all(wire, GROUP, 0, 0, tiled=True)  6.6 us
    all_to_all x1, waiting for transfers between devices, body(): everyone = lax.all_to_all(spread, GROUP, 0, 0, tiled=True)  5.56 us
  transfers between devices with their start and end apart: 16, of which 9 were waited for; matrix products, arithmetic and copies ran while one was open for 14% of the time, Pallas kernels for 9%

profile of v7, /device:TPU:32, one launch (start us, length us, event | category | flops | bytes accessed | tf_op | source)
XLA Modules:
  0.0 99.9 jit_solution(3330011658253317533)
XLA Ops:
  0.6 0.1 collective-permute-start.1
  0.7 0.5 collective-permute-start
  1.2 1.0 %pad_maximum_fusion.m1 = bf16[2,160,512]{2,1,0:T(8,128)(2,1)S(1)} fusion(bf16[1,160,512]{2,1,0:T(8,128)(2,1)} %bitcast.28, bf16[1,160,512]{2,1,0:T(8,128)(2,1)} %bitcast.29), kind=kLoop, calls=%fused_computation.9 | loop fusion | flops 163840 | bytes 655360 | tf_op jit(solution)/shard_map/stack | solution.py:357
  2.3 0.0 copy-start.5
  2.3 0.2 collective-permute-start.5
  2.5 6.7 %collective-permute-start.3 = (bf16[2,160,512]{2,1,0:T(8,128)(2,1)S(1)}, bf16[2,160,512]{2,1,0:T(8,128)(2,1)S(1)}, u32[]{:S(2)}, u32[]{:S(2)}) collective-permute-start(bf16[2,160,512]{2,1,0:T(8,128)(2,1)S(1)} %pad_maximum_fusion.m1), channel_id=1, source_target_pairs={{2,4},{6,8},{10,12},{14,16},{18,20},{22,24},{26,28},{30,32},{34,36... | collective-permute-start | bytes 983048 | tf_op jit(solution)/shard_map/ppermute | solution.py:318
  9.1 0.1 collective-permute-start.2
  9.9 0.0 collective-permute-done.grid_far
  9.9 0.0 copy-start.1
  9.9 0.0 collective-permute-done.1.edge_far
  9.9 0.0 copy-start
  9.9 9.2 %sender_step.1 = (f32[2304,256]{1,0:T(8,128)S(1)}, bf16[2304,1024]{1,0:T(8,128)(2,1)S(1)}, bf16[2176,2304]{1,0:T(8,128)(2,1)S(1)}) custom-call(s32[1]{0:T(128)} %bitcast.2.band, s32[1]{0:T(128)} %bitcast.3.chan, s32[1]{0:T(128)S(6)} %copy.20.count, bf16[576,512]{1,0:T(8,128)(2,1)} %grid_own.3, bf16[576,512]{1,0:T(8,128)(2,1)S(1)} %collective-permute-done.grid_far, ...), custom_call_target="tpu_custom_call" | custom-call | flops 4000000000 | bytes 4194304 | tf_op jit(solution)/shard_map/sender_step/pallas_call | solution.py:382
  19.1 0.0 copy-done.5
  19.1 0.0 copy-done.1
  19.1 0.0 copy-done
  19.2 0.0 collective-permute-done.3.m2
  19.2 0.0 copy-start.7
  19.2 0.0 collective-permute-done.2.m0
  19.2 0.0 copy-start.8
  19.2 0.2 collective-permute-start.4
  19.4 0.4 collective-permute-start.6
  19.8 0.0 collective-permute-done.5.m4
  19.8 1.1 %collective-permute-done.4.m3 = bf16[2,160,512]{2,1,0:T(8,128)(2,1)S(1)} collective-permute-done((bf16[2,160,512]{2,1,0:T(8,128)(2,1)S(1)}, bf16[2,160,512]{2,1,0:T(8,128)(2,1)S(1)}, u32[]{:S(2)}, u32[]{:S(2)}) %collective-permute-start.4) | collective-permute-done | bytes 327712 | tf_op jit(solution)/shard_map/ppermute | solution.py:312
  20.9 0.5 collective-permute-done.6.m5
  21.4 0.0 copy-done.7
  21.4 0.0 copy-done.8
  21.4 0.0 copy-done.6
  21.4 14.3 %edge_step.1 = (bf16[32,136,128]{2,1,0:T(8,128)(2,1)}, bf16[2304,256]{1,0:T(8,128)(2,1)S(1)}, bf16[1152,256]{1,0:T(8,128)(2,1)S(1)}, bf16[320,256]{1,0:T(8,128)(...) custom-call(bf16[576,512]{1,0:T(8,128)(2,1)} %grid_own.3, bf16[576,512]{1,0:T(8,128)(2,1)} %copy-done.1, ...), custom_call_target="tpu_custom_call" | custom-call | flops 8999999488 | bytes 8388608 | tf_op jit(solution)/shard_map/edge_step/pallas_call | solution.py:417
  35.7 7.5 %all-to-all-start = ((bf16[32,136,128]{2,1,0:T(8,128)(2,1)}), bf16[32,136,128]{2,1,0:T(8,128)(2,1)S(1)}, u32[]{:S(2)}, u32[]{:S(2)}) async-start(bf16[32,136,128]{2,1,0:T(8,128)(2,1)} %get-tuple-element.36), calls=%async_computation | async-start | bytes 2228224 | tf_op jit(solution)/shard_map/all_to_all | solution.py:461
  43.2 0.0 copy-start.3
  43.2 1.6 %collective-permute-start.9 = (bf16[320,256]{1,0:T(8,128)(2,1)}, bf16[320,256]{1,0:T(8,128)(2,1)}, u32[]{:S(2)}, u32[]{:S(2)}) collective-permute-start(bf16[320,256]{1,0:T(8,128)(2,1)} %get-tuple-element.37), channel_id=1, source_target_pairs={{0,2},{4,6},{8,10},{12,14},{16,18},{20,22},{24,26},{28,30},{32,34}... | collective-permute-start | bytes 491528 | tf_op jit(solution)/shard_map/ppermute | solution.py:318
  44.8 6.3 %collective-permute-start.10 = (bf16[320,256]{1,0:T(8,128)(2,1)}, bf16[320,256]{1,0:T(8,128)(2,1)}, u32[]{:S(2)}, u32[]{:S(2)}) collective-permute-start(bf16[320,256]{1,0:T(8,128)(2,1)} %get-tuple-element.38), channel_id=1, source_target_pairs={{2,4},{6,8},{10,12},{14,16},{18,20},{22,24},{26,28},{30,32},{34,36... | collective-permute-start | bytes 491528 | tf_op jit(solution)/shard_map/ppermute | solution.py:318
  51.0 2.5 %convolution_convert_fusion = bf16[1152,512]{1,0:T(8,128)(2,1)} fusion(bf16[512,256]{1,0:T(8,128)(2,1)} %w_edge.1, bf16[2304,256]{1,0:T(8,128)(2,1)S(1)} %get-tuple-element.34), kind=kOutput, calls=%fused_computation.2 | convolution fusion | flops 302579712 | bytes 2031616 | tf_op jit(solution)/shard_map/dot_general | solution.py:30
  53.5 0.0 copy-done.3
  53.5 1.2 %convolution_convert_fusion.1 = bf16[576,512]{1,0:T(8,128)(2,1)} fusion(bf16[512,256]{1,0:T(8,128)(2,1)S(1)} %copy-done.3, bf16[1152,256]{1,0:T(8,128)(2,1)S(1)} %get-tuple-element.33), kind=kOutput, calls=%fused_computation.5 | convolution fusion | flops 151289856 | bytes 1146880 | tf_op jit(solution)/shard_map/dot_general | solution.py:30
  54.7 6.6 %all-to-all-done = bf16[32,136,128]{2,1,0:T(8,128)(2,1)S(1)} async-done(((bf16[32,136,128]{2,1,0:T(8,128)(2,1)}), bf16[32,136,128]{2,1,0:T(8,128)(2,1)S(1)}, u32[]{:S(2)}, u32[]{:S(2)}) %all-to-all-start) | async-done | bytes 1114144 | tf_op jit(solution)/shard_map/all_to_all | solution.py:461
  61.3 0.2 reduce_sum.12
  61.4 0.4 collective-permute-done.9
  61.9 2.2 %collective-permute-done.10 = bf16[320,256]{1,0:T(8,128)(2,1)} collective-permute-done((bf16[320,256]{1,0:T(8,128)(2,1)}, bf16[320,256]{1,0:T(8,128)(2,1)}, u32[]{:S(2)}, u32[]{:S(2)}) %collective-permute-start.10) | collective-permute-done | bytes 163872 | tf_op jit(solution)/shard_map/ppermute | solution.py:318
  64.1 4.5 %collective-permute-start.12 = (bf16[136,128]{1,0:T(8,128)(2,1)S(1)}, bf16[136,128]{1,0:T(8,128)(2,1)S(1)}, u32[]{:S(2)}, u32[]{:S(2)}) collective-permute-start(bf16[136,128]{1,0:T(8,128)(2,1)S(1)} %reduce_sum.12), channel_id=1, source_target_pairs={{0,64},{64,0},{128,192},{192,128},{1,65},{65,1},{129,193},{193,129... | collective-permute-start | bytes 104456 | tf_op jit(solution)/shard_map/ppermute | solution.py:326
  68.6 1.9 %collective-permute-done.12 = bf16[136,128]{1,0:T(8,128)(2,1)S(1)} collective-permute-done((bf16[136,128]{1,0:T(8,128)(2,1)S(1)}, bf16[136,128]{1,0:T(8,128)(2,1)S(1)}, u32[]{:S(2)}, u32[]{:S(2)}) %collective-permute-start.12) | collective-permute-done | bytes 34848 | tf_op jit(solution)/shard_map/ppermute | solution.py:326
  70.5 3.5 %collective-permute-start.13 = (bf16[136,128]{1,0:T(8,128)(2,1)S(1)}, bf16[136,128]{1,0:T(8,128)(2,1)S(1)}, u32[]{:S(2)}, u32[]{:S(2)}) collective-permute-start(bf16[136,128]{1,0:T(8,128)(2,1)S(1)} %add_convert_fusion.2), channel_id=1, source_target_pairs={{0,192},{64,128},{128,64},{192,0},{1,193},{65,129},{129,65},{193,1... | collective-permute-start | bytes 104456 | tf_op jit(solution)/shard_map/ppermute | solution.py:326
  74.0 0.0 collective-permute-start.7
  74.0 0.5 collective-permute-start.8
  74.5 2.2 %collective-permute-done.13 = bf16[136,128]{1,0:T(8,128)(2,1)S(1)} collective-permute-done((bf16[136,128]{1,0:T(8,128)(2,1)S(1)}, bf16[136,128]{1,0:T(8,128)(2,1)S(1)}, u32[]{:S(2)}, u32[]{:S(2)}) %collective-permute-start.13) | collective-permute-done | bytes 34848 | tf_op jit(solution)/shard_map/ppermute | solution.py:326
  76.7 1.1 %broadcast_in_dim.2 = bf16[32,64,256]{2,1,0:T(8,128)(2,1)} broadcast(bf16[64,256]{1,0:T(8,128)(2,1)S(1)} %pad_maximum_fusion.1), dimensions={1,2} | broadcast | bytes 1081344 | tf_op jit(solution)/shard_map/broadcast_in_dim | solution.py:471
  77.8 4.9 %all-to-all-start.1 = ((bf16[32,64,256]{2,1,0:T(8,128)(2,1)}), bf16[32,64,256]{2,1,0:T(8,128)(2,1)S(1)}, u32[]{:S(2)}, u32[]{:S(2)}) async-start(bf16[32,64,256]{2,1,0:T(8,128)(2,1)} %broadcast_in_dim.2), calls=%async_computation.1 | async-start | bytes 2097152 | tf_op jit(solution)/shard_map/all_to_all | solution.py:472
  82.7 0.0 copy-start.4
  82.7 0.0 collective-permute-done.7
  82.7 2.3 %fusion.1 = bf16[576,512]{1,0:T(8,128)(2,1)} fusion(bf16[512,256]{1,0:T(8,128)(2,1)S(1)} %copy-done.3, bf16[576,512]{1,0:T(8,128)(2,1)} %collective-permute-done.7, bf16[1152,256]{1,0:T(8,128)(2,1)S(1)} %get-tuple-element.33), kind=kOutput, calls=%fused_computation.4 | convolution fusion | flops 151879680 | bytes 1736704 | tf_op jit(solution)/shard_map/dot_general | solution.py:30
  85.0 0.0 collective-permute-done.8
  85.0 0.0 copy-done.4
  85.0 2.8 %fusion = bf16[1152,512]{1,0:T(8,128)(2,1)} fusion(bf16[512,256]{1,0:T(8,128)(2,1)S(1)} %copy-done.4, bf16[1152,512]{1,0:T(8,128)(2,1)} %collective-permute-done.8, bf16[2304,256]{1,0:T(8,128)(2,1)S(1)} %get-tuple-element.34), kind=kOutput, calls=%fused_computation.1 | convolution fusion | flops 303759360 | bytes 3211264 | tf_op jit(solution)/shard_map/dot_general | solution.py:30
  87.8 1.0 %add_convert_fusion.1 = bf16[320,256]{1,0:T(8,128)(2,1)S(1)} fusion(bf16[320,256]{1,0:T(8,128)(2,1)} %collective-permute-done.10, f32[320,256]{1,0:T(8,128)S(1)} %get-tuple-element.35, bf16[320,256]{1,0:T(8,128)(2,1)} %collective-permute-done.9), kind=kLoop, calls=%fused_computation.11 | loop fusion | flops 409600 | bytes 819200 | tf_op jit(solution)/shard_map/convert_element_type | solution.py:476
  88.9 0.2 convolution_convert_fusion.2
  89.1 0.1 collective-permute-start.11
  89.2 0.6 slice_bitcast_fusion
  89.8 0.8 collective-permute-done.11
  90.6 0.9 add_convert_fusion
  91.5 5.6 %all-to-all-done.1 = bf16[32,64,256]{2,1,0:T(8,128)(2,1)S(1)} async-done(((bf16[32,64,256]{2,1,0:T(8,128)(2,1)}), bf16[32,64,256]{2,1,0:T(8,128)(2,1)S(1)}, u32[]{:S(2)}, u32[]{:S(2)}) %all-to-all-start.1) | async-done | bytes 1048608 | tf_op jit(solution)/shard_map/all_to_all | solution.py:472
  97.1 0.1 fusion.13
  97.1 0.8 bitcast_convert_fusion.2
  98.0 0.9 maximum_convert_fusion
  98.9 1.1 %bitcast_convert_fusion = (f32[512,256]{1,0:T(8,128)}, f32[512,256]{1,0:T(8,128)}) fusion(bf16[8,64,256]{2,1,0:T(8,128)(2,1)S(1)} %get-tuple-element.44, bf16[8,64,256]{2,1,0:T(8,128)(2,1)S(1)} %get-tuple-element.45), kind=kLoop, calls=%fused_computation.15 | loop fusion | flops 262144 | bytes 1572864 | tf_op jit(solution)/shard_map/reshape | solution.py:482
  (8 shorter events, 0.1 us)
Async XLA Ops:
  0.6 9.3 %collective-permute-start.1 = (bf16[1152,512]{1,0:T(8,128)(2,1)}, bf16[1152,512]{1,0:T(8,128)(2,1)S(1)}, u32[]{:S(2)}, u32[]{:S(2)}) collective-permute-start(bf16[1152,512]{1,0:T(8,128)(2,1)} %edge_own.3), channel_id=1, source_target_pairs={{0,1},{1,0},{2,3},{3,2},{4,5},{5,4},{6,7},{7,6},{8,9},{9,8},{10,11... | collective-permute-start | bytes 3538952 | tf_op jit(solution)/shard_map/ppermute | solution.py:312
  0.7 9.1 %collective-permute-start = (bf16[576,512]{1,0:T(8,128)(2,1)}, bf16[576,512]{1,0:T(8,128)(2,1)S(1)}, u32[]{:S(2)}, u32[]{:S(2)}) collective-permute-start(bf16[576,512]{1,0:T(8,128)(2,1)} %grid_own.3), channel_id=1, source_target_pairs={{0,1},{1,0},{2,3},{3,2},{4,5},{5,4},{6,7},{7,6},{8,9},{9,8},{10,11... | collective-permute-start | bytes 1769480 | tf_op jit(solution)/shard_map/ppermute | solution.py:312
  2.3 16.9 %copy-start.5 = (bf16[2,160,512]{2,1,0:T(8,128)(2,1)}, bf16[2,160,512]{2,1,0:T(8,128)(2,1)S(1)}, u32[]{:S(2)}) copy-start(bf16[2,160,512]{2,1,0:T(8,128)(2,1)S(1)} %pad_maximum_fusion.m1) | copy-start | bytes 983044
  2.3 17.5 %collective-permute-start.5 = (bf16[2,160,512]{2,1,0:T(8,128)(2,1)S(1)}, bf16[2,160,512]{2,1,0:T(8,128)(2,1)S(1)}, u32[]{:S(2)}, u32[]{:S(2)}) collective-permute-start(bf16[2,160,512]{2,1,0:T(8,128)(2,1)S(1)} %pad_maximum_fusion.m1), channel_id=1, source_target_pairs={{0,1},{1,0},{2,3},{3,2},{4,5},{5,4},{6,7},{7,6},{8,9},{9,8},{10,11... | collective-permute-start | bytes 983048 | tf_op jit(solution)/shard_map/ppermute | solution.py:312
  2.5 16.7 %collective-permute-start.3 = (bf16[2,160,512]{2,1,0:T(8,128)(2,1)S(1)}, bf16[2,160,512]{2,1,0:T(8,128)(2,1)S(1)}, u32[]{:S(2)}, u32[]{:S(2)}) collective-permute-start(bf16[2,160,512]{2,1,0:T(8,128)(2,1)S(1)} %pad_maximum_fusion.m1), channel_id=1, source_target_pairs={{2,4},{6,8},{10,12},{14,16},{18,20},{22,24},{26,28},{30,32},{34,36... | collective-permute-start | bytes 983048 | tf_op jit(solution)/shard_map/ppermute | solution.py:318
  9.1 10.1 %collective-permute-start.2 = (bf16[2,160,512]{2,1,0:T(8,128)(2,1)S(1)}, bf16[2,160,512]{2,1,0:T(8,128)(2,1)S(1)}, u32[]{:S(2)}, u32[]{:S(2)}) collective-permute-start(bf16[2,160,512]{2,1,0:T(8,128)(2,1)S(1)} %pad_maximum_fusion.m1), channel_id=1, source_target_pairs={{0,2},{4,6},{8,10},{12,14},{16,18},{20,22},{24,26},{28,30},{32,34}... | collective-permute-start | bytes 983048 | tf_op jit(solution)/shard_map/ppermute | solution.py:318
  9.9 9.3 %copy-start.1 = (bf16[576,512]{1,0:T(8,128)(2,1)}, bf16[576,512]{1,0:T(8,128)(2,1)S(1)}, u32[]{:S(2)}) copy-start(bf16[576,512]{1,0:T(8,128)(2,1)S(1)} %collective-permute-done.grid_far) | copy-start | bytes 1769476
  9.9 9.2 %copy-start = (bf16[1152,512]{1,0:T(8,128)(2,1)}, bf16[1152,512]{1,0:T(8,128)(2,1)S(1)}, u32[]{:S(2)}) copy-start(bf16[1152,512]{1,0:T(8,128)(2,1)S(1)} %collective-permute-done.1.edge_far) | copy-start | bytes 3538948
  19.2 2.2 %copy-start.7 = (bf16[2,160,512]{2,1,0:T(8,128)(2,1)}, bf16[2,160,512]{2,1,0:T(8,128)(2,1)S(1)}, u32[]{:S(2)}) copy-start(bf16[2,160,512]{2,1,0:T(8,128)(2,1)S(1)} %collective-permute-done.3.m2) | copy-start | bytes 983044
  19.2 2.2 %copy-start.8 = (bf16[2,160,512]{2,1,0:T(8,128)(2,1)}, bf16[2,160,512]{2,1,0:T(8,128)(2,1)S(1)}, u32[]{:S(2)}) copy-start(bf16[2,160,512]{2,1,0:T(8,128)(2,1)S(1)} %collective-permute-done.2.m0) | copy-start | bytes 983044
  19.2 1.7 %collective-permute-start.4 = (bf16[2,160,512]{2,1,0:T(8,128)(2,1)S(1)}, bf16[2,160,512]{2,1,0:T(8,128)(2,1)S(1)}, u32[]{:S(2)}, u32[]{:S(2)}) collective-permute-start(bf16[2,160,512]{2,1,0:T(8,128)(2,1)S(1)} %collective-permute-done.2.m0), channel_id=1, source_target_pairs={{0,1},{1,0},{2,3},{3,2},{4,5},{5,4},{6,7},{7,6},{8,9},{9,8},{10,11... | collective-permute-start | bytes 983048 | tf_op jit(solution)/shard_map/ppermute | solution.py:312
  19.4 2.0 %collective-permute-start.6 = (bf16[2,160,512]{2,1,0:T(8,128)(2,1)S(1)}, bf16[2,160,512]{2,1,0:T(8,128)(2,1)S(1)}, u32[]{:S(2)}, u32[]{:S(2)}) collective-permute-start(bf16[2,160,512]{2,1,0:T(8,128)(2,1)S(1)} %collective-permute-done.3.m2), channel_id=1, source_target_pairs={{0,1},{1,0},{2,3},{3,2},{4,5},{5,4},{6,7},{7,6},{8,9},{9,8},{10,11... | collective-permute-start | bytes 983048 | tf_op jit(solution)/shard_map/ppermute | solution.py:312
  19.8 1.6 %copy-start.6 = (bf16[2,160,512]{2,1,0:T(8,128)(2,1)}, bf16[2,160,512]{2,1,0:T(8,128)(2,1)S(1)}, u32[]{:S(2)}) copy-start(bf16[2,160,512]{2,1,0:T(8,128)(2,1)S(1)} %collective-permute-done.5.m4) | copy-start | bytes 983044
  35.7 25.6 %all-to-all-start = ((bf16[32,136,128]{2,1,0:T(8,128)(2,1)}), bf16[32,136,128]{2,1,0:T(8,128)(2,1)S(1)}, u32[]{:S(2)}, u32[]{:S(2)}) async-start(bf16[32,136,128]{2,1,0:T(8,128)(2,1)} %get-tuple-element.36), calls=%async_computation | async-start | bytes 2228224 | tf_op jit(solution)/shard_map/all_to_all | solution.py:461
  43.2 10.3 %copy-start.3 = (bf16[512,256]{1,0:T(8,128)(2,1)S(1)}, bf16[512,256]{1,0:T(8,128)(2,1)}, u32[]{:S(2)}) copy-start(bf16[512,256]{1,0:T(8,128)(2,1)} %w_grid.1) | copy-start | bytes 786436
  43.2 18.6 %collective-permute-start.9 = (bf16[320,256]{1,0:T(8,128)(2,1)}, bf16[320,256]{1,0:T(8,128)(2,1)}, u32[]{:S(2)}, u32[]{:S(2)}) collective-permute-start(bf16[320,256]{1,0:T(8,128)(2,1)} %get-tuple-element.37), channel_id=1, source_target_pairs={{0,2},{4,6},{8,10},{12,14},{16,18},{20,22},{24,26},{28,30},{32,34}... | collective-permute-start | bytes 491528 | tf_op jit(solution)/shard_map/ppermute | solution.py:318
  44.8 19.3 %collective-permute-start.10 = (bf16[320,256]{1,0:T(8,128)(2,1)}, bf16[320,256]{1,0:T(8,128)(2,1)}, u32[]{:S(2)}, u32[]{:S(2)}) collective-permute-start(bf16[320,256]{1,0:T(8,128)(2,1)} %get-tuple-element.38), channel_id=1, source_target_pairs={{2,4},{6,8},{10,12},{14,16},{18,20},{22,24},{26,28},{30,32},{34,36... | collective-permute-start | bytes 491528 | tf_op jit(solution)/shard_map/ppermute | solution.py:318
  64.1 6.4 %collective-permute-start.12 = (bf16[136,128]{1,0:T(8,128)(2,1)S(1)}, bf16[136,128]{1,0:T(8,128)(2,1)S(1)}, u32[]{:S(2)}, u32[]{:S(2)}) collective-permute-start(bf16[136,128]{1,0:T(8,128)(2,1)S(1)} %reduce_sum.12), channel_id=1, source_target_pairs={{0,64},{64,0},{128,192},{192,128},{1,65},{65,1},{129,193},{193,129... | collective-permute-start | bytes 104456 | tf_op jit(solution)/shard_map/ppermute | solution.py:326
  70.5 6.1 %collective-permute-start.13 = (bf16[136,128]{1,0:T(8,128)(2,1)S(1)}, bf16[136,128]{1,0:T(8,128)(2,1)S(1)}, u32[]{:S(2)}, u32[]{:S(2)}) collective-permute-start(bf16[136,128]{1,0:T(8,128)(2,1)S(1)} %add_convert_fusion.2), channel_id=1, source_target_pairs={{0,192},{64,128},{128,64},{192,0},{1,193},{65,129},{129,65},{193,1... | collective-permute-start | bytes 104456 | tf_op jit(solution)/shard_map/ppermute | solution.py:326
  74.0 8.8 %collective-permute-start.7 = (bf16[576,512]{1,0:T(8,128)(2,1)}, bf16[576,512]{1,0:T(8,128)(2,1)}, u32[]{:S(2)}, u32[]{:S(2)}) collective-permute-start(bf16[576,512]{1,0:T(8,128)(2,1)} %convolution_convert_fusion.1), channel_id=1, source_target_pairs={{0,1},{1,0},{2,3},{3,2},{4,5},{5,4},{6,7},{7,6},{8,9},{9,8},{10,11... | collective-permute-start | bytes 1769480 | tf_op jit(solution)/shard_map/ppermute | solution.py:312
  74.0 11.0 %collective-permute-start.8 = (bf16[1152,512]{1,0:T(8,128)(2,1)}, bf16[1152,512]{1,0:T(8,128)(2,1)}, u32[]{:S(2)}, u32[]{:S(2)}) collective-permute-start(bf16[1152,512]{1,0:T(8,128)(2,1)} %convolution_convert_fusion), channel_id=1, source_target_pairs={{0,1},{1,0},{2,3},{3,2},{4,5},{5,4},{6,7},{7,6},{8,9},{9,8},{10,11... | collective-permute-start | bytes 3538952 | tf_op jit(solution)/shard_map/ppermute | solution.py:312
  77.8 19.3 %all-to-all-start.1 = ((bf16[32,64,256]{2,1,0:T(8,128)(2,1)}), bf16[32,64,256]{2,1,0:T(8,128)(2,1)S(1)}, u32[]{:S(2)}, u32[]{:S(2)}) async-start(bf16[32,64,256]{2,1,0:T(8,128)(2,1)} %broadcast_in_dim.2), calls=%async_computation.1 | async-start | bytes 2097152 | tf_op jit(solution)/shard_map/all_to_all | solution.py:472
  82.7 2.3 %copy-start.4 = (bf16[512,256]{1,0:T(8,128)(2,1)S(1)}, bf16[512,256]{1,0:T(8,128)(2,1)}, u32[]{:S(2)}) copy-start(bf16[512,256]{1,0:T(8,128)(2,1)} %w_edge.1) | copy-start | bytes 786436
  85.0 3.9 %copy-start.2 = (bf16[512,256]{1,0:T(8,128)(2,1)S(1)}, bf16[512,256]{1,0:T(8,128)(2,1)}, u32[]{:S(2)}) copy-start(bf16[512,256]{1,0:T(8,128)(2,1)} %w_mesh_in.1) | copy-start | bytes 786436
  89.1 1.5 %collective-permute-start.11 = (bf16[160,512]{1,0:T(8,128)(2,1)S(1)}, bf16[160,512]{1,0:T(8,128)(2,1)S(1)}, u32[]{:S(2)}, u32[]{:S(2)}) collective-permute-start(bf16[160,512]{1,0:T(8,128)(2,1)S(1)} %convolution_convert_fusion.2), channel_id=1, source_target_pairs={{0,1},{1,0},{2,3},{3,2},{4,5},{5,4},{6,7},{7,6},{8,9},{9,8},{10,11... | collective-permute-start | bytes 491528 | tf_op jit(solution)/shard_map/ppermute | solution.py:312

commit v8 on v7

--- a/solution.py
+++ b/solution.py
@@ -464,15 +464,17 @@
     edge_back = swap(edge_term)
     grid_back = swap(grid_term)
     total = arrived.astype(F32).sum(axis=0).astype(BF)
-    total, from_low, from_high, _, _ = lax.optimization_barrier((total, from_low, from_high, edge_term, grid_term))
+    grad_edge = (dot_t(cot_own, w_edge) + edge_back.astype(F32)).astype(BF)
+    grad_grid = (dot_t(seg_grid[:half_grid], w_grid) + grid_back.astype(F32)).astype(BF)
+    total, from_low, from_high, grad_edge, grad_grid = lax.optimization_barrier(
+        (total, from_low, from_high, grad_edge, grad_grid)
+    )
     total = depth_total(total)
     grad_bias = total[2 * ROWS : 2 * ROWS + 2].reshape(hidden)
     chunk = jnp.concatenate([total[:ROWS], total[ROWS : 2 * ROWS]], axis=1).astype(BF)
     spread = jnp.broadcast_to(chunk[None], (MEMBERS, ROWS, hidden))
     everyone = lax.all_to_all(spread, GROUP, 0, 0, tiled=True)
 
-    grad_edge = (dot_t(cot_own, w_edge) + edge_back.astype(F32)).astype(BF)
-    grad_grid = (dot_t(seg_grid[:half_grid], w_grid) + grid_back.astype(F32)).astype(BF)
     seg_mesh = (rim_mid + from_low.astype(F32) + from_high.astype(F32)).astype(BF)
     seg_mesh, _ = lax.optimization_barrier((seg_mesh, chunk))
     mesh_back = swap(dot_t(seg_mesh[piece:], w_mesh).astype(BF))

time: 100 us -> 101 us (1.010)
  matrix products: 9.86 us -> 4.68 us
  waiting for transfers between devices: 21.3 us -> 26.2 us
    dot_general x6, matrix products: 9.86 us -> 4.68 us  [dot_t(): lax.dot_general(a, b, (((1,), (1,)), ((), ())), preferred_element_type=F32)]
    all_to_all x1, waiting for transfers between devices: 5.56 us -> 10.5 us  [body(): everyone = lax.all_to_all(spread, GROUP, 0, 0, tiled=True)]
  transfers between devices with their start and end apart: 16 -> 16, of which waited for: 9 -> 8; matrix products, arithmetic and copies ran while one was open for 14% -> 7% of each run, Pallas kernels for 9% -> 9%
where the time goes in v8:
time: 101 us; the launch traced here: 100 us
  starting transfers between devices  37.2 us (37%)
  waiting for transfers between devices  26.2 us (26%)
  Pallas kernels  23.5 us (23%)
  other arithmetic  5.05 us (5%)
  matrix products  4.68 us (5%)
  local copies, waits for them, and re-layouts  1.93 us (2%)
  between operations  1.58 us (2%)
    pallas_call x1, Pallas kernels, body(): pl.pallas_call(edge_kernel, out_shape=(pltpu.HBM((MEMBERS, 2 * ROWS + TAI...  14.3 us
    ppermute x4, starting transfers between devices, pair_swap(): return lax.ppermute(x, BAND, pairs + [(j, i) for i, j in pairs])  14.3 us
    all_to_all x1, waiting for transfers between devices, body(): everyone = lax.all_to_all(spread, GROUP, 0, 0, tiled=True)  10.5 us
    pallas_call x1, Pallas kernels, body(): pl.pallas_call(functools.partial(sender_kernel, piece), out_shape=(pltpu....  9.2 us
    ppermute x2, starting transfers between devices, depth_total(): other = lax.ppermute(mine, 'zh', [(i, i ^ mask) for i in range(depth)])  7.96 us
    all_to_all x1, starting transfers between devices, body(): arrived = lax.all_to_all(wire, GROUP, 0, 0, tiled=True)  7.64 us
    all_to_all x1, waiting for transfers between devices, body(): arrived = lax.all_to_all(wire, GROUP, 0, 0, tiled=True)  6.06 us
    all_to_all x1, starting transfers between devices, body(): everyone = lax.all_to_all(spread, GROUP, 0, 0, tiled=True)  5.1 us
  transfers between devices with their start and end apart: 16, of which 8 were waited for; matrix products, arithmetic and copies ran while one was open for 7% of the time, Pallas kernels for 9%

profile of v8, /device:TPU:32, one launch (start us, length us, event | category | flops | bytes accessed | tf_op | source)
XLA Modules:
  0.0 100.1 jit_solution(3038592080075245514)
XLA Ops:
  0.6 0.1 collective-permute-start.1
  0.7 0.5 collective-permute-start
  1.2 1.0 %pad_maximum_fusion.m1 = bf16[2,160,512]{2,1,0:T(8,128)(2,1)S(1)} fusion(bf16[1,160,512]{2,1,0:T(8,128)(2,1)} %bitcast.28, bf16[1,160,512]{2,1,0:T(8,128)(2,1)} %bitcast.29), kind=kLoop, calls=%fused_computation.9 | loop fusion | flops 163840 | bytes 655360 | tf_op jit(solution)/shard_map/stack | solution.py:357
  2.3 0.0 copy-start.5
  2.3 0.2 collective-permute-start.5
  2.5 6.7 %collective-permute-start.3 = (bf16[2,160,512]{2,1,0:T(8,128)(2,1)S(1)}, bf16[2,160,512]{2,1,0:T(8,128)(2,1)S(1)}, u32[]{:S(2)}, u32[]{:S(2)}) collective-permute-start(bf16[2,160,512]{2,1,0:T(8,128)(2,1)S(1)} %pad_maximum_fusion.m1), channel_id=1, source_target_pairs={{2,4},{6,8},{10,12},{14,16},{18,20},{22,24},{26,28},{30,32},{34,36... | collective-permute-start | bytes 983048 | tf_op jit(solution)/shard_map/ppermute | solution.py:318
  9.1 0.1 collective-permute-start.2
  9.9 0.0 collective-permute-done.grid_far
  9.9 0.0 copy-start.1
  9.9 0.0 collective-permute-done.1.edge_far
  9.9 0.0 copy-start
  9.9 9.2 %sender_step.1 = (f32[2304,256]{1,0:T(8,128)S(1)}, bf16[2304,1024]{1,0:T(8,128)(2,1)S(1)}, bf16[2176,2304]{1,0:T(8,128)(2,1)S(1)}) custom-call(s32[1]{0:T(128)} %bitcast.2.band, s32[1]{0:T(128)} %bitcast.3.chan, s32[1]{0:T(128)S(6)} %copy.20.count, bf16[576,512]{1,0:T(8,128)(2,1)} %grid_own.3, bf16[576,512]{1,0:T(8,128)(2,1)S(1)} %collective-permute-done.grid_far, ...), custom_call_target="tpu_custom_call" | custom-call | flops 4000000000 | bytes 4194304 | tf_op jit(solution)/shard_map/sender_step/pallas_call | solution.py:382
  19.1 0.0 copy-done.5
  19.1 0.0 copy-done.1
  19.1 0.0 copy-done
  19.2 0.0 collective-permute-done.3.m2
  19.2 0.0 copy-start.7
  19.2 0.0 collective-permute-done.2.m0
  19.2 0.0 copy-start.8
  19.2 0.2 collective-permute-start.4
  19.4 0.4 collective-permute-start.6
  19.8 0.0 collective-permute-done.5.m4
  19.8 1.1 %collective-permute-done.4.m3 = bf16[2,160,512]{2,1,0:T(8,128)(2,1)S(1)} collective-permute-done((bf16[2,160,512]{2,1,0:T(8,128)(2,1)S(1)}, bf16[2,160,512]{2,1,0:T(8,128)(2,1)S(1)}, u32[]{:S(2)}, u32[]{:S(2)}) %collective-permute-start.4) | collective-permute-done | bytes 327712 | tf_op jit(solution)/shard_map/ppermute | solution.py:312
  20.9 0.0 copy-done.7
  20.9 0.5 collective-permute-done.6.m5
  21.4 0.0 copy-done.6
  21.4 14.3 %edge_step.1 = (bf16[32,136,128]{2,1,0:T(8,128)(2,1)}, bf16[2304,256]{1,0:T(8,128)(2,1)S(1)}, bf16[1152,256]{1,0:T(8,128)(2,1)S(1)}, bf16[320,256]{1,0:T(8,128)(...) custom-call(bf16[576,512]{1,0:T(8,128)(2,1)} %grid_own.3, bf16[576,512]{1,0:T(8,128)(2,1)} %copy-done.1, ...), custom_call_target="tpu_custom_call" | custom-call | flops 8999999488 | bytes 8388608 | tf_op jit(solution)/shard_map/edge_step/pallas_call | solution.py:417
  35.7 0.0 copy-start.4
  35.7 7.6 %all-to-all-start = ((bf16[32,136,128]{2,1,0:T(8,128)(2,1)}), bf16[32,136,128]{2,1,0:T(8,128)(2,1)S(1)}, u32[]{:S(2)}, u32[]{:S(2)}) async-start(bf16[32,136,128]{2,1,0:T(8,128)(2,1)} %get-tuple-element.35), calls=%async_computation | async-start | bytes 2228224 | tf_op jit(solution)/shard_map/all_to_all | solution.py:461
  43.4 0.0 copy-start.3
  43.4 0.0 copy-done.4
  43.4 0.5 convolution_convert_fusion
  43.9 0.3 collective-permute-start.9
  44.2 0.1 copy-done.3
  44.3 0.3 convolution_convert_fusion.1
  44.7 0.4 collective-permute-start.10
  45.1 1.5 %collective-permute-start.7 = (bf16[320,256]{1,0:T(8,128)(2,1)}, bf16[320,256]{1,0:T(8,128)(2,1)}, u32[]{:S(2)}, u32[]{:S(2)}) collective-permute-start(bf16[320,256]{1,0:T(8,128)(2,1)} %get-tuple-element.36), channel_id=1, source_target_pairs={{0,2},{4,6},{8,10},{12,14},{16,18},{20,22},{24,26},{28,30},{32,34}... | collective-permute-start | bytes 491528 | tf_op jit(solution)/shard_map/ppermute | solution.py:318
  46.6 6.1 %collective-permute-start.8 = (bf16[320,256]{1,0:T(8,128)(2,1)}, bf16[320,256]{1,0:T(8,128)(2,1)}, u32[]{:S(2)}, u32[]{:S(2)}) collective-permute-start(bf16[320,256]{1,0:T(8,128)(2,1)} %get-tuple-element.37), channel_id=1, source_target_pairs={{2,4},{6,8},{10,12},{14,16},{18,20},{22,24},{26,28},{30,32},{34,36... | collective-permute-start | bytes 491528 | tf_op jit(solution)/shard_map/ppermute | solution.py:318
  52.6 0.0 collective-permute-done.10
  52.7 1.2 %fusion.1 = bf16[576,512]{1,0:T(8,128)(2,1)} fusion(bf16[512,256]{1,0:T(8,128)(2,1)S(1)} %copy-done.3, bf16[576,512]{1,0:T(8,128)(2,1)S(1)} %collective-permute-done.10, bf16[1152,256]{1,0:T(8,128)(2,1)S(1)} %get-tuple-element.39), kind=kOutput, calls=%fused_computation.4 | convolution fusion | flops 151879680 | bytes 1736704 | tf_op jit(solution)/shard_map/dot_general | solution.py:30
  53.8 0.0 collective-permute-done.9
  53.8 1.5 %fusion = bf16[1152,512]{1,0:T(8,128)(2,1)} fusion(bf16[512,256]{1,0:T(8,128)(2,1)S(1)} %copy-done.4, bf16[1152,512]{1,0:T(8,128)(2,1)S(1)} %collective-permute-done.9, bf16[2304,256]{1,0:T(8,128)(2,1)S(1)} %get-tuple-element.38), kind=kOutput, calls=%fused_computation.1 | convolution fusion | flops 303759360 | bytes 3211264 | tf_op jit(solution)/shard_map/dot_general | solution.py:30
  55.4 6.1 %all-to-all-done = bf16[32,136,128]{2,1,0:T(8,128)(2,1)S(1)} async-done(((bf16[32,136,128]{2,1,0:T(8,128)(2,1)}), bf16[32,136,128]{2,1,0:T(8,128)(2,1)S(1)}, u32[]{:S(2)}, u32[]{:S(2)}) %all-to-all-start) | async-done | bytes 1114144 | tf_op jit(solution)/shard_map/all_to_all | solution.py:461
  61.4 0.2 reduce_sum.12
  61.6 0.0 collective-permute-done.7
  61.6 2.6 %collective-permute-done.8 = bf16[320,256]{1,0:T(8,128)(2,1)} collective-permute-done((bf16[320,256]{1,0:T(8,128)(2,1)}, bf16[320,256]{1,0:T(8,128)(2,1)}, u32[]{:S(2)}, u32[]{:S(2)}) %collective-permute-start.8) | collective-permute-done | bytes 163872 | tf_op jit(solution)/shard_map/ppermute | solution.py:318
  64.2 4.5 %collective-permute-start.12 = (bf16[136,128]{1,0:T(8,128)(2,1)S(1)}, bf16[136,128]{1,0:T(8,128)(2,1)S(1)}, u32[]{:S(2)}, u32[]{:S(2)}) collective-permute-start(bf16[136,128]{1,0:T(8,128)(2,1)S(1)} %reduce_sum.12), channel_id=1, source_target_pairs={{0,64},{64,0},{128,192},{192,128},{1,65},{65,1},{129,193},{193,129... | collective-permute-start | bytes 104456 | tf_op jit(solution)/shard_map/ppermute | solution.py:326
  68.7 1.9 %collective-permute-done.12 = bf16[136,128]{1,0:T(8,128)(2,1)S(1)} collective-permute-done((bf16[136,128]{1,0:T(8,128)(2,1)S(1)}, bf16[136,128]{1,0:T(8,128)(2,1)S(1)}, u32[]{:S(2)}, u32[]{:S(2)}) %collective-permute-start.12) | collective-permute-done | bytes 34848 | tf_op jit(solution)/shard_map/ppermute | solution.py:326
  70.6 3.5 %collective-permute-start.13 = (bf16[136,128]{1,0:T(8,128)(2,1)S(1)}, bf16[136,128]{1,0:T(8,128)(2,1)S(1)}, u32[]{:S(2)}, u32[]{:S(2)}) collective-permute-start(bf16[136,128]{1,0:T(8,128)(2,1)S(1)} %add_convert_fusion.2), channel_id=1, source_target_pairs={{0,192},{64,128},{128,64},{192,0},{1,193},{65,129},{129,65},{193,1... | collective-permute-start | bytes 104456 | tf_op jit(solution)/shard_map/ppermute | solution.py:326
  74.1 2.7 %collective-permute-done.13 = bf16[136,128]{1,0:T(8,128)(2,1)S(1)} collective-permute-done((bf16[136,128]{1,0:T(8,128)(2,1)S(1)}, bf16[136,128]{1,0:T(8,128)(2,1)S(1)}, u32[]{:S(2)}, u32[]{:S(2)}) %collective-permute-start.13) | collective-permute-done | bytes 34848 | tf_op jit(solution)/shard_map/ppermute | solution.py:326
  76.8 1.1 %broadcast_in_dim.2 = bf16[32,64,256]{2,1,0:T(8,128)(2,1)} broadcast(bf16[64,256]{1,0:T(8,128)(2,1)S(1)} %pad_maximum_fusion.1), dimensions={1,2} | broadcast | bytes 1081344 | tf_op jit(solution)/shard_map/broadcast_in_dim | solution.py:475
  77.9 5.1 %all-to-all-start.1 = ((bf16[32,64,256]{2,1,0:T(8,128)(2,1)}), bf16[32,64,256]{2,1,0:T(8,128)(2,1)S(1)}, u32[]{:S(2)}, u32[]{:S(2)}) async-start(bf16[32,64,256]{2,1,0:T(8,128)(2,1)} %broadcast_in_dim.2), calls=%async_computation.1 | async-start | bytes 2097152 | tf_op jit(solution)/shard_map/all_to_all | solution.py:476
  83.0 1.0 %add_convert_fusion.1 = bf16[320,256]{1,0:T(8,128)(2,1)S(1)} fusion(bf16[320,256]{1,0:T(8,128)(2,1)} %collective-permute-done.8, f32[320,256]{1,0:T(8,128)S(1)} %get-tuple-element.42, bf16[320,256]{1,0:T(8,128)(2,1)} %collective-permute-done.7), kind=kLoop, calls=%fused_computation.11 | loop fusion | flops 409600 | bytes 819200 | tf_op jit(solution)/shard_map/convert_element_type | solution.py:478
  84.1 0.0 copy-done.2
  84.1 0.2 convolution_convert_fusion.2
  84.3 0.1 collective-permute-start.11
  84.4 0.6 slice_bitcast_fusion
  85.0 0.8 collective-permute-done.11
  85.8 0.9 add_convert_fusion
  86.7 10.5 %all-to-all-done.1 = bf16[32,64,256]{2,1,0:T(8,128)(2,1)S(1)} async-done(((bf16[32,64,256]{2,1,0:T(8,128)(2,1)}), bf16[32,64,256]{2,1,0:T(8,128)(2,1)S(1)}, u32[]{:S(2)}, u32[]{:S(2)}) %all-to-all-start.1) | async-done | bytes 1048608 | tf_op jit(solution)/shard_map/all_to_all | solution.py:476
  97.2 0.1 fusion.13
  97.3 0.8 bitcast_convert_fusion.2
  98.1 0.9 maximum_convert_fusion
  99.0 1.1 %bitcast_convert_fusion = (f32[512,256]{1,0:T(8,128)}, f32[512,256]{1,0:T(8,128)}) fusion(bf16[8,64,256]{2,1,0:T(8,128)(2,1)S(1)} %get-tuple-element.48, bf16[8,64,256]{2,1,0:T(8,128)(2,1)S(1)} %get-tuple-element.49), kind=kLoop, calls=%fused_computation.15 | loop fusion | flops 262144 | bytes 1572864 | tf_op jit(solution)/shard_map/reshape | solution.py:484
  (8 shorter events, 0.1 us)
Async XLA Ops:
  0.6 9.3 %collective-permute-start.1 = (bf16[1152,512]{1,0:T(8,128)(2,1)}, bf16[1152,512]{1,0:T(8,128)(2,1)S(1)}, u32[]{:S(2)}, u32[]{:S(2)}) collective-permute-start(bf16[1152,512]{1,0:T(8,128)(2,1)} %edge_own.3), channel_id=1, source_target_pairs={{0,1},{1,0},{2,3},{3,2},{4,5},{5,4},{6,7},{7,6},{8,9},{9,8},{10,11... | collective-permute-start | bytes 3538952 | tf_op jit(solution)/shard_map/ppermute | solution.py:312
  0.7 9.1 %collective-permute-start = (bf16[576,512]{1,0:T(8,128)(2,1)}, bf16[576,512]{1,0:T(8,128)(2,1)S(1)}, u32[]{:S(2)}, u32[]{:S(2)}) collective-permute-start(bf16[576,512]{1,0:T(8,128)(2,1)} %grid_own.3), channel_id=1, source_target_pairs={{0,1},{1,0},{2,3},{3,2},{4,5},{5,4},{6,7},{7,6},{8,9},{9,8},{10,11... | collective-permute-start | bytes 1769480 | tf_op jit(solution)/shard_map/ppermute | solution.py:312
  2.3 16.9 %copy-start.5 = (bf16[2,160,512]{2,1,0:T(8,128)(2,1)}, bf16[2,160,512]{2,1,0:T(8,128)(2,1)S(1)}, u32[]{:S(2)}) copy-start(bf16[2,160,512]{2,1,0:T(8,128)(2,1)S(1)} %pad_maximum_fusion.m1) | copy-start | bytes 983044
  2.3 17.5 %collective-permute-start.5 = (bf16[2,160,512]{2,1,0:T(8,128)(2,1)S(1)}, bf16[2,160,512]{2,1,0:T(8,128)(2,1)S(1)}, u32[]{:S(2)}, u32[]{:S(2)}) collective-permute-start(bf16[2,160,512]{2,1,0:T(8,128)(2,1)S(1)} %pad_maximum_fusion.m1), channel_id=1, source_target_pairs={{0,1},{1,0},{2,3},{3,2},{4,5},{5,4},{6,7},{7,6},{8,9},{9,8},{10,11... | collective-permute-start | bytes 983048 | tf_op jit(solution)/shard_map/ppermute | solution.py:312
  2.5 16.7 %collective-permute-start.3 = (bf16[2,160,512]{2,1,0:T(8,128)(2,1)S(1)}, bf16[2,160,512]{2,1,0:T(8,128)(2,1)S(1)}, u32[]{:S(2)}, u32[]{:S(2)}) collective-permute-start(bf16[2,160,512]{2,1,0:T(8,128)(2,1)S(1)} %pad_maximum_fusion.m1), channel_id=1, source_target_pairs={{2,4},{6,8},{10,12},{14,16},{18,20},{22,24},{26,28},{30,32},{34,36... | collective-permute-start | bytes 983048 | tf_op jit(solution)/shard_map/ppermute | solution.py:318
  9.1 10.1 %collective-permute-start.2 = (bf16[2,160,512]{2,1,0:T(8,128)(2,1)S(1)}, bf16[2,160,512]{2,1,0:T(8,128)(2,1)S(1)}, u32[]{:S(2)}, u32[]{:S(2)}) collective-permute-start(bf16[2,160,512]{2,1,0:T(8,128)(2,1)S(1)} %pad_maximum_fusion.m1), channel_id=1, source_target_pairs={{0,2},{4,6},{8,10},{12,14},{16,18},{20,22},{24,26},{28,30},{32,34}... | collective-permute-start | bytes 983048 | tf_op jit(solution)/shard_map/ppermute | solution.py:318
  9.9 9.3 %copy-start.1 = (bf16[576,512]{1,0:T(8,128)(2,1)}, bf16[576,512]{1,0:T(8,128)(2,1)S(1)}, u32[]{:S(2)}) copy-start(bf16[576,512]{1,0:T(8,128)(2,1)S(1)} %collective-permute-done.grid_far) | copy-start | bytes 1769476
  9.9 9.2 %copy-start = (bf16[1152,512]{1,0:T(8,128)(2,1)}, bf16[1152,512]{1,0:T(8,128)(2,1)S(1)}, u32[]{:S(2)}) copy-start(bf16[1152,512]{1,0:T(8,128)(2,1)S(1)} %collective-permute-done.1.edge_far) | copy-start | bytes 3538948
  19.2 1.8 %copy-start.7 = (bf16[2,160,512]{2,1,0:T(8,128)(2,1)}, bf16[2,160,512]{2,1,0:T(8,128)(2,1)S(1)}, u32[]{:S(2)}) copy-start(bf16[2,160,512]{2,1,0:T(8,128)(2,1)S(1)} %collective-permute-done.3.m2) | copy-start | bytes 983044
  19.2 1.7 %copy-start.8 = (bf16[2,160,512]{2,1,0:T(8,128)(2,1)}, bf16[2,160,512]{2,1,0:T(8,128)(2,1)S(1)}, u32[]{:S(2)}) copy-start(bf16[2,160,512]{2,1,0:T(8,128)(2,1)S(1)} %collective-permute-done.2.m0) | copy-start | bytes 983044
  19.2 1.7 %collective-permute-start.4 = (bf16[2,160,512]{2,1,0:T(8,128)(2,1)S(1)}, bf16[2,160,512]{2,1,0:T(8,128)(2,1)S(1)}, u32[]{:S(2)}, u32[]{:S(2)}) collective-permute-start(bf16[2,160,512]{2,1,0:T(8,128)(2,1)S(1)} %collective-permute-done.2.m0), channel_id=1, source_target_pairs={{0,1},{1,0},{2,3},{3,2},{4,5},{5,4},{6,7},{7,6},{8,9},{9,8},{10,11... | collective-permute-start | bytes 983048 | tf_op jit(solution)/shard_map/ppermute | solution.py:312
  19.4 2.0 %collective-permute-start.6 = (bf16[2,160,512]{2,1,0:T(8,128)(2,1)S(1)}, bf16[2,160,512]{2,1,0:T(8,128)(2,1)S(1)}, u32[]{:S(2)}, u32[]{:S(2)}) collective-permute-start(bf16[2,160,512]{2,1,0:T(8,128)(2,1)S(1)} %collective-permute-done.3.m2), channel_id=1, source_target_pairs={{0,1},{1,0},{2,3},{3,2},{4,5},{5,4},{6,7},{7,6},{8,9},{9,8},{10,11... | collective-permute-start | bytes 983048 | tf_op jit(solution)/shard_map/ppermute | solution.py:312
  19.8 1.6 %copy-start.6 = (bf16[2,160,512]{2,1,0:T(8,128)(2,1)}, bf16[2,160,512]{2,1,0:T(8,128)(2,1)S(1)}, u32[]{:S(2)}) copy-start(bf16[2,160,512]{2,1,0:T(8,128)(2,1)S(1)} %collective-permute-done.5.m4) | copy-start | bytes 983044
  35.7 7.7 %copy-start.4 = (bf16[512,256]{1,0:T(8,128)(2,1)S(1)}, bf16[512,256]{1,0:T(8,128)(2,1)}, u32[]{:S(2)}) copy-start(bf16[512,256]{1,0:T(8,128)(2,1)} %w_edge.1) | copy-start | bytes 786436
  35.7 25.7 %all-to-all-start = ((bf16[32,136,128]{2,1,0:T(8,128)(2,1)}), bf16[32,136,128]{2,1,0:T(8,128)(2,1)S(1)}, u32[]{:S(2)}, u32[]{:S(2)}) async-start(bf16[32,136,128]{2,1,0:T(8,128)(2,1)} %get-tuple-element.35), calls=%async_computation | async-start | bytes 2228224 | tf_op jit(solution)/shard_map/all_to_all | solution.py:461
  43.4 1.0 copy-start.3
  43.9 9.9 %collective-permute-start.9 = (bf16[1152,512]{1,0:T(8,128)(2,1)S(1)}, bf16[1152,512]{1,0:T(8,128)(2,1)S(1)}, u32[]{:S(2)}, u32[]{:S(2)}) collective-permute-start(bf16[1152,512]{1,0:T(8,128)(2,1)S(1)} %convolution_convert_fusion), channel_id=1, source_target_pairs={{0,1},{1,0},{2,3},{3,2},{4,5},{5,4},{6,7},{7,6},{8,9},{9,8},{10,11... | collective-permute-start | bytes 3538952 | tf_op jit(solution)/shard_map/ppermute | solution.py:312
  44.7 8.0 %collective-permute-start.10 = (bf16[576,512]{1,0:T(8,128)(2,1)S(1)}, bf16[576,512]{1,0:T(8,128)(2,1)S(1)}, u32[]{:S(2)}, u32[]{:S(2)}) collective-permute-start(bf16[576,512]{1,0:T(8,128)(2,1)S(1)} %convolution_convert_fusion.1), channel_id=1, source_target_pairs={{0,1},{1,0},{2,3},{3,2},{4,5},{5,4},{6,7},{7,6},{8,9},{9,8},{10,11... | collective-permute-start | bytes 1769480 | tf_op jit(solution)/shard_map/ppermute | solution.py:312
  45.1 16.5 %collective-permute-start.7 = (bf16[320,256]{1,0:T(8,128)(2,1)}, bf16[320,256]{1,0:T(8,128)(2,1)}, u32[]{:S(2)}, u32[]{:S(2)}) collective-permute-start(bf16[320,256]{1,0:T(8,128)(2,1)} %get-tuple-element.36), channel_id=1, source_target_pairs={{0,2},{4,6},{8,10},{12,14},{16,18},{20,22},{24,26},{28,30},{32,34}... | collective-permute-start | bytes 491528 | tf_op jit(solution)/shard_map/ppermute | solution.py:318
  46.6 17.6 %collective-permute-start.8 = (bf16[320,256]{1,0:T(8,128)(2,1)}, bf16[320,256]{1,0:T(8,128)(2,1)}, u32[]{:S(2)}, u32[]{:S(2)}) collective-permute-start(bf16[320,256]{1,0:T(8,128)(2,1)} %get-tuple-element.37), channel_id=1, source_target_pairs={{2,4},{6,8},{10,12},{14,16},{18,20},{22,24},{26,28},{30,32},{34,36... | collective-permute-start | bytes 491528 | tf_op jit(solution)/shard_map/ppermute | solution.py:318
  64.2 6.4 %collective-permute-start.12 = (bf16[136,128]{1,0:T(8,128)(2,1)S(1)}, bf16[136,128]{1,0:T(8,128)(2,1)S(1)}, u32[]{:S(2)}, u32[]{:S(2)}) collective-permute-start(bf16[136,128]{1,0:T(8,128)(2,1)S(1)} %reduce_sum.12), channel_id=1, source_target_pairs={{0,64},{64,0},{128,192},{192,128},{1,65},{65,1},{129,193},{193,129... | collective-permute-start | bytes 104456 | tf_op jit(solution)/shard_map/ppermute | solution.py:326
  70.6 6.1 %collective-permute-start.13 = (bf16[136,128]{1,0:T(8,128)(2,1)S(1)}, bf16[136,128]{1,0:T(8,128)(2,1)S(1)}, u32[]{:S(2)}, u32[]{:S(2)}) collective-permute-start(bf16[136,128]{1,0:T(8,128)(2,1)S(1)} %add_convert_fusion.2), channel_id=1, source_target_pairs={{0,192},{64,128},{128,64},{192,0},{1,193},{65,129},{129,65},{193,1... | collective-permute-start | bytes 104456 | tf_op jit(solution)/shard_map/ppermute | solution.py:326
  77.9 6.2 %copy-start.2 = (bf16[512,256]{1,0:T(8,128)(2,1)S(1)}, bf16[512,256]{1,0:T(8,128)(2,1)}, u32[]{:S(2)}) copy-start(bf16[512,256]{1,0:T(8,128)(2,1)} %w_mesh_in.1) | copy-start | bytes 786436
  77.9 19.3 %all-to-all-start.1 = ((bf16[32,64,256]{2,1,0:T(8,128)(2,1)}), bf16[32,64,256]{2,1,0:T(8,128)(2,1)S(1)}, u32[]{:S(2)}, u32[]{:S(2)}) async-start(bf16[32,64,256]{2,1,0:T(8,128)(2,1)} %broadcast_in_dim.2), calls=%async_computation.1 | async-start | bytes 2097152 | tf_op jit(solution)/shard_map/all_to_all | solution.py:476
  84.3 1.5 %collective-permute-start.11 = (bf16[160,512]{1,0:T(8,128)(2,1)S(1)}, bf16[160,512]{1,0:T(8,128)(2,1)S(1)}, u32[]{:S(2)}, u32[]{:S(2)}) collective-permute-start(bf16[160,512]{1,0:T(8,128)(2,1)S(1)} %convolution_convert_fusion.2), channel_id=1, source_target_pairs={{0,1},{1,0},{2,3},{3,2},{4,5},{5,4},{6,7},{7,6},{8,9},{9,8},{10,11... | collective-permute-start | bytes 491528 | tf_op jit(solution)/shard_map/ppermute | solution.py:312

commit v9 on v8

--- a/solution.py
+++ b/solution.py
@@ -7,6 +7,7 @@
 from jax.experimental import pallas as pl
 from jax.experimental.pallas import tpu as pltpu
 from jax.sharding import Mesh, PartitionSpec as P
+
 
 BF = jnp.bfloat16
 F32 = jnp.float32
@@ -207,7 +208,6 @@
     piece = m0.shape[1]
     n_mesh = 6 * piece
     pad_mesh = lat.shape[0]
-    n_rows = n_grid + pad_mesh
     block = EDGE_BLOCK
     hidden = w_mesh.shape[1]
     near = half_edges // UNIT
@@ -237,6 +237,7 @@
     high = cot_terms.astype(BF)
     table[:, hidden : 2 * hidden] = high
     table[:, 2 * hidden :] = (cot_terms - high.astype(F32)).astype(BF)
+
     def step(i, carry):
         rows = pl.ds(pl.multiple_of(i * block, block), block)
         got = dot(left[rows, :], table[...])
@@ -456,8 +457,6 @@
     )
 
     cot_own, cot_far = (cots[:half_edges], cots[half_edges:])
-    from_low = pair_swap(rim_low, 0)
-    from_high = pair_swap(rim_high, 1)
     arrived = lax.all_to_all(wire, GROUP, 0, 0, tiled=True)
     edge_term = dot_t(cot_far, w_edge).astype(BF)
     grid_term = dot_t(seg_grid[half_grid:], w_grid).astype(BF)
@@ -466,9 +465,11 @@
     total = arrived.astype(F32).sum(axis=0).astype(BF)
     grad_edge = (dot_t(cot_own, w_edge) + edge_back.astype(F32)).astype(BF)
     grad_grid = (dot_t(seg_grid[:half_grid], w_grid) + grid_back.astype(F32)).astype(BF)
-    total, from_low, from_high, grad_edge, grad_grid = lax.optimization_barrier(
-        (total, from_low, from_high, grad_edge, grad_grid)
-    )
+    total, rim_low, rim_high, grad_edge, grad_grid = lax.optimization_barrier(
+        (total, rim_low, rim_high, grad_edge, grad_grid)
+    )
+    from_low = pair_swap(rim_low, 0)
+    from_high = pair_swap(rim_high, 1)
     total = depth_total(total)
     grad_bias = total[2 * ROWS : 2 * ROWS + 2].reshape(hidden)
     chunk = jnp.concatenate([total[:ROWS], total[ROWS : 2 * ROWS]], axis=1).astype(BF)

time: 101 us -> 104 us (1.030)
  waiting for transfers between devices: 26.2 us -> 29.6 us
    all_to_all x1, waiting for transfers between devices: 10.5 us -> 0.01 us  [body(): everyone = lax.all_to_all(spread, GROUP, 0, 0, tiled=True)]
    ppermute x4, waiting for transfers between devices: 2.63 us -> 9.75 us  [pair_swap(): return lax.ppermute(x, BAND, pairs + [(j, i) for i, j in pairs])]
    all_to_all x1, waiting for transfers between devices: 6.06 us -> 10.1 us  [body(): arrived = lax.all_to_all(wire, GROUP, 0, 0, tiled=True)]
    ppermute x8, waiting for transfers between devices: 2.41 us -> 5.15 us  [swap(): return lax.ppermute(x, 'chan', [(0, 1), (1, 0)])]
  transfers between devices with their start and end apart: 16 -> 16, of which waited for: 8 -> 9; matrix products, arithmetic and copies ran while one was open for 7% -> 6% of each run, Pallas kernels for 9% -> 9%
where the time goes in v9:
time: 104 us; the launch traced here: 103 us
  starting transfers between devices  37.8 us (36%)
  waiting for transfers between devices  29.6 us (28%)
  Pallas kernels  23.5 us (23%)
  matrix products  4.67 us (4%)
  other arithmetic  4.05 us (4%)
  local copies, waits for them, and re-layouts  1.93 us (2%)
  between operations  1.59 us (2%)
    ppermute x4, starting transfers between devices, pair_swap(): return lax.ppermute(x, BAND, pairs + [(j, i) for i, j in pairs])  14.4 us
    pallas_call x1, Pallas kernels, body(): pl.pallas_call(edge_kernel, out_shape=(pltpu.HBM((MEMBERS, 2 * ROWS + TAI...  14.3 us
    all_to_all x1, waiting for transfers between devices, body(): arrived = lax.all_to_all(wire, GROUP, 0, 0, tiled=True)  10.1 us
    ppermute x4, waiting for transfers between devices, pair_swap(): return lax.ppermute(x, BAND, pairs + [(j, i) for i, j in pairs])  9.75 us
    pallas_call x1, Pallas kernels, body(): pl.pallas_call(functools.partial(sender_kernel, piece), out_shape=(pltpu....  9.2 us
    ppermute x2, starting transfers between devices, depth_total(): other = lax.ppermute(mine, 'zh', [(i, i ^ mask) for i in range(depth)])  8.25 us
    all_to_all x1, starting transfers between devices, body(): arrived = lax.all_to_all(wire, GROUP, 0, 0, tiled=True)  7.64 us
    all_to_all x1, starting transfers between devices, body(): everyone = lax.all_to_all(spread, GROUP, 0, 0, tiled=True)  5.38 us
  transfers between devices with their start and end apart: 16, of which 9 were waited for; matrix products, arithmetic and copies ran while one was open for 6% of the time, Pallas kernels for 9%

profile of v9, /device:TPU:32, one launch (start us, length us, event | category | flops | bytes accessed | tf_op | source)
XLA Modules:
  0.0 103.2 jit_solution(431395412403712454)
XLA Ops:
  0.6 0.1 collective-permute-start.1
  0.7 0.5 collective-permute-start
  1.2 1.0 pad_maximum_fusion.m1
  2.3 0.0 copy-start.5
  2.3 0.2 collective-permute-start.5
  2.5 6.7 %collective-permute-start.3 = (bf16[2,160,512]{2,1,0:T(8,128)(2,1)S(1)}, bf16[2,160,512]{2,1,0:T(8,128)(2,1)S(1)}, u32[]{:S(2)}, u32[]{:S(2)}) collective-permute-start(bf16[2,160,512]{2,1,0:T(8,128)(2,1)S(1)} %pad_maximum_fusion.m1), channel_id=1, source_target_pairs={{2,4},{6,8},{10,12},{14,16},{18,20},{22,24},{26,28},{30,32},{34,36... | collective-permute-start | bytes 983048 | tf_op jit(solution)/shard_map/ppermute | solution.py:319
  9.1 0.1 collective-permute-start.2
  9.9 0.0 collective-permute-done.grid_far
  9.9 0.0 copy-start.1
  9.9 0.0 collective-permute-done.1.edge_far
  9.9 0.0 copy-start
  9.9 9.2 %sender_step.1 = (f32[2304,256]{1,0:T(8,128)S(1)}, bf16[2304,1024]{1,0:T(8,128)(2,1)S(1)}, bf16[2176,2304]{1,0:T(8,128)(2,1)S(1)}) custom-call(s32[1]{0:T(128)} %bitcast.2.band, s32[1]{0:T(128)} %bitcast.3.chan, s32[1]{0:T(128)S(6)} %copy.20.count, bf16[576,512]{1,0:T(8,128)(2,1)} %grid_own.3, bf16[576,512]{1,0:T(8,128)(2,1)S(1)} %collective-permute-done.grid_far, ...), custom_call_target="tpu_custom_call" | custom-call | flops 4000000000 | bytes 4194304 | tf_op jit(solution)/shard_map/sender_step/pallas_call | solution.py:383
  19.1 0.0 copy-done.5
  19.1 0.0 copy-done.1
  19.1 0.0 copy-done
  19.2 0.0 collective-permute-done.3.m2
  19.2 0.0 copy-start.7
  19.2 0.0 collective-permute-done.2.m0
  19.2 0.0 copy-start.8
  19.2 0.2 collective-permute-start.4
  19.4 0.4 collective-permute-start.6
  19.8 0.0 collective-permute-done.5.m4
  19.8 1.1 %collective-permute-done.4.m3 = bf16[2,160,512]{2,1,0:T(8,128)(2,1)S(1)} collective-permute-done((bf16[2,160,512]{2,1,0:T(8,128)(2,1)S(1)}, bf16[2,160,512]{2,1,0:T(8,128)(2,1)S(1)}, u32[]{:S(2)}, u32[]{:S(2)}) %collective-permute-start.4) | collective-permute-done | bytes 327712 | tf_op jit(solution)/shard_map/ppermute | solution.py:313
  20.9 0.0 copy-done.7
  20.9 0.0 copy-done.8
  20.9 0.5 collective-permute-done.6.m5
  21.4 0.0 copy-done.6
  21.4 14.3 %edge_step.1 = (bf16[32,136,128]{2,1,0:T(8,128)(2,1)}, bf16[2304,256]{1,0:T(8,128)(2,1)S(1)}, bf16[1152,256]{1,0:T(8,128)(2,1)S(1)}, bf16[320,256]{1,0:T(8,128)(...) custom-call(bf16[576,512]{1,0:T(8,128)(2,1)} %grid_own.3, bf16[576,512]{1,0:T(8,128)(2,1)} %copy-done.1, ...), custom_call_target="tpu_custom_call" | custom-call | flops 8999999488 | bytes 8388608 | tf_op jit(solution)/shard_map/edge_step/pallas_call | solution.py:418
  35.7 0.0 copy-start.4
  35.7 7.6 %all-to-all-start = ((bf16[32,136,128]{2,1,0:T(8,128)(2,1)}), bf16[32,136,128]{2,1,0:T(8,128)(2,1)S(1)}, u32[]{:S(2)}, u32[]{:S(2)}) async-start(bf16[32,136,128]{2,1,0:T(8,128)(2,1)} %get-tuple-element.35), calls=%async_computation | async-start | bytes 2228224 | tf_op jit(solution)/shard_map/all_to_all | solution.py:460
  43.4 0.0 copy-start.3
  43.4 0.0 copy-done.4
  43.4 0.5 convolution_convert_fusion
  43.9 0.3 collective-permute-start.7
  44.2 0.1 copy-done.3
  44.3 0.3 convolution_convert_fusion.1
  44.7 0.4 collective-permute-start.8
  45.1 2.7 %collective-permute-done.8 = bf16[576,512]{1,0:T(8,128)(2,1)S(1)} collective-permute-done((bf16[576,512]{1,0:T(8,128)(2,1)S(1)}, bf16[576,512]{1,0:T(8,128)(2,1)S(1)}, u32[]{:S(2)}, u32[]{:S(2)}) %collective-permute-start.8) | collective-permute-done | bytes 589856 | tf_op jit(solution)/shard_map/ppermute | solution.py:313
  47.8 1.2 %fusion.1 = bf16[576,512]{1,0:T(8,128)(2,1)} fusion(bf16[512,256]{1,0:T(8,128)(2,1)S(1)} %copy-done.3, bf16[576,512]{1,0:T(8,128)(2,1)S(1)} %collective-permute-done.8, bf16[1152,256]{1,0:T(8,128)(2,1)S(1)} %get-tuple-element.39), kind=kOutput, calls=%fused_computation.4 | convolution fusion | flops 151879680 | bytes 1736704 | tf_op jit(solution)/shard_map/dot_general | solution.py:31
  49.0 0.0 collective-permute-done.7
  49.0 1.5 %fusion = bf16[1152,512]{1,0:T(8,128)(2,1)} fusion(bf16[512,256]{1,0:T(8,128)(2,1)S(1)} %copy-done.4, bf16[1152,512]{1,0:T(8,128)(2,1)S(1)} %collective-permute-done.7, bf16[2304,256]{1,0:T(8,128)(2,1)S(1)} %get-tuple-element.38), kind=kOutput, calls=%fused_computation.1 | convolution fusion | flops 303759360 | bytes 3211264 | tf_op jit(solution)/shard_map/dot_general | solution.py:31
  50.5 10.1 %all-to-all-done = bf16[32,136,128]{2,1,0:T(8,128)(2,1)S(1)} async-done(((bf16[32,136,128]{2,1,0:T(8,128)(2,1)}), bf16[32,136,128]{2,1,0:T(8,128)(2,1)S(1)}, u32[]{:S(2)}, u32[]{:S(2)}) %all-to-all-start) | async-done | bytes 1114144 | tf_op jit(solution)/shard_map/all_to_all | solution.py:460
  60.7 0.2 reduce_sum.12
  60.9 4.6 %collective-permute-start.12 = (bf16[136,128]{1,0:T(8,128)(2,1)S(1)}, bf16[136,128]{1,0:T(8,128)(2,1)S(1)}, u32[]{:S(2)}, u32[]{:S(2)}) collective-permute-start(bf16[136,128]{1,0:T(8,128)(2,1)S(1)} %reduce_sum.12), channel_id=1, source_target_pairs={{0,64},{64,0},{128,192},{192,128},{1,65},{65,1},{129,193},{193,129... | collective-permute-start | bytes 104456 | tf_op jit(solution)/shard_map/ppermute | solution.py:327
  65.4 1.9 %collective-permute-done.12 = bf16[136,128]{1,0:T(8,128)(2,1)S(1)} collective-permute-done((bf16[136,128]{1,0:T(8,128)(2,1)S(1)}, bf16[136,128]{1,0:T(8,128)(2,1)S(1)}, u32[]{:S(2)}, u32[]{:S(2)}) %collective-permute-start.12) | collective-permute-done | bytes 34848 | tf_op jit(solution)/shard_map/ppermute | solution.py:327
  67.4 3.7 %collective-permute-start.13 = (bf16[136,128]{1,0:T(8,128)(2,1)S(1)}, bf16[136,128]{1,0:T(8,128)(2,1)S(1)}, u32[]{:S(2)}, u32[]{:S(2)}) collective-permute-start(bf16[136,128]{1,0:T(8,128)(2,1)S(1)} %add_convert_fusion.2), channel_id=1, source_target_pairs={{0,192},{64,128},{128,64},{192,0},{1,193},{65,129},{129,65},{193,1... | collective-permute-start | bytes 104456 | tf_op jit(solution)/shard_map/ppermute | solution.py:327
  71.0 2.7 %collective-permute-done.13 = bf16[136,128]{1,0:T(8,128)(2,1)S(1)} collective-permute-done((bf16[136,128]{1,0:T(8,128)(2,1)S(1)}, bf16[136,128]{1,0:T(8,128)(2,1)S(1)}, u32[]{:S(2)}, u32[]{:S(2)}) %collective-permute-start.13) | collective-permute-done | bytes 34848 | tf_op jit(solution)/shard_map/ppermute | solution.py:327
  73.7 1.1 %broadcast_in_dim.2 = bf16[32,64,256]{2,1,0:T(8,128)(2,1)} broadcast(bf16[64,256]{1,0:T(8,128)(2,1)S(1)} %pad_maximum_fusion.1), dimensions={1,2} | broadcast | bytes 1081344 | tf_op jit(solution)/shard_map/broadcast_in_dim | solution.py:476
  74.8 5.4 %all-to-all-start.1 = ((bf16[32,64,256]{2,1,0:T(8,128)(2,1)}), bf16[32,64,256]{2,1,0:T(8,128)(2,1)S(1)}, u32[]{:S(2)}, u32[]{:S(2)}) async-start(bf16[32,64,256]{2,1,0:T(8,128)(2,1)} %broadcast_in_dim.2), calls=%async_computation.1 | async-start | bytes 2097152 | tf_op jit(solution)/shard_map/all_to_all | solution.py:477
  80.2 1.6 %collective-permute-start.9 = (bf16[320,256]{1,0:T(8,128)(2,1)S(1)}, bf16[320,256]{1,0:T(8,128)(2,1)S(1)}, u32[]{:S(2)}, u32[]{:S(2)}) collective-permute-start(bf16[320,256]{1,0:T(8,128)(2,1)S(1)} %copy-done.10), channel_id=1, source_target_pairs={{0,2},{4,6},{8,10},{12,14},{16,18},{20,22},{24,26},{28,30},{32,34}... | collective-permute-start | bytes 491528 | tf_op jit(solution)/shard_map/ppermute | solution.py:319
  81.8 6.1 %collective-permute-start.10 = (bf16[320,256]{1,0:T(8,128)(2,1)S(1)}, bf16[320,256]{1,0:T(8,128)(2,1)S(1)}, u32[]{:S(2)}, u32[]{:S(2)}) collective-permute-start(bf16[320,256]{1,0:T(8,128)(2,1)S(1)} %copy-done.9), channel_id=1, source_target_pairs={{2,4},{6,8},{10,12},{14,16},{18,20},{22,24},{26,28},{30,32},{34,36... | collective-permute-start | bytes 491528 | tf_op jit(solution)/shard_map/ppermute | solution.py:319
  87.9 6.7 %collective-permute-done.9 = bf16[320,256]{1,0:T(8,128)(2,1)S(1)} collective-permute-done((bf16[320,256]{1,0:T(8,128)(2,1)S(1)}, bf16[320,256]{1,0:T(8,128)(2,1)S(1)}, u32[]{:S(2)}, u32[]{:S(2)}) %collective-permute-start.9) | collective-permute-done | bytes 163872 | tf_op jit(solution)/shard_map/ppermute | solution.py:319
  94.6 3.0 %collective-permute-done.10 = bf16[320,256]{1,0:T(8,128)(2,1)S(1)} collective-permute-done((bf16[320,256]{1,0:T(8,128)(2,1)S(1)}, bf16[320,256]{1,0:T(8,128)(2,1)S(1)}, u32[]{:S(2)}, u32[]{:S(2)}) %collective-permute-start.10) | collective-permute-done | bytes 163872 | tf_op jit(solution)/shard_map/ppermute | solution.py:319
  97.6 0.1 add_convert_fusion.1
  97.7 0.2 convolution_convert_fusion.2
  97.9 0.1 collective-permute-start.11
  98.0 0.6 slice_bitcast_fusion
  98.6 0.8 collective-permute-done.11
  99.4 0.9 add_convert_fusion
  100.3 0.0 all-to-all-done.1
  100.3 0.1 fusion.13
  100.4 0.8 bitcast_convert_fusion.2
  101.2 0.9 maximum_convert_fusion
  102.1 1.1 %bitcast_convert_fusion = (f32[512,256]{1,0:T(8,128)}, f32[512,256]{1,0:T(8,128)}) fusion(bf16[8,64,256]{2,1,0:T(8,128)(2,1)S(1)} %get-tuple-element.48, bf16[8,64,256]{2,1,0:T(8,128)(2,1)S(1)} %get-tuple-element.49), kind=kLoop, calls=%fused_computation.15 | loop fusion | flops 262144 | bytes 1572864 | tf_op jit(solution)/shard_map/reshape | solution.py:485
  (12 shorter events, 0.1 us)
Async XLA Ops:
  0.6 9.3 %collective-permute-start.1 = (bf16[1152,512]{1,0:T(8,128)(2,1)}, bf16[1152,512]{1,0:T(8,128)(2,1)S(1)}, u32[]{:S(2)}, u32[]{:S(2)}) collective-permute-start(bf16[1152,512]{1,0:T(8,128)(2,1)} %edge_own.3), channel_id=1, source_target_pairs={{0,1},{1,0},{2,3},{3,2},{4,5},{5,4},{6,7},{7,6},{8,9},{9,8},{10,11... | collective-permute-start | bytes 3538952 | tf_op jit(solution)/shard_map/ppermute | solution.py:313
  0.7 9.1 %collective-permute-start = (bf16[576,512]{1,0:T(8,128)(2,1)}, bf16[576,512]{1,0:T(8,128)(2,1)S(1)}, u32[]{:S(2)}, u32[]{:S(2)}) collective-permute-start(bf16[576,512]{1,0:T(8,128)(2,1)} %grid_own.3), channel_id=1, source_target_pairs={{0,1},{1,0},{2,3},{3,2},{4,5},{5,4},{6,7},{7,6},{8,9},{9,8},{10,11... | collective-permute-start | bytes 1769480 | tf_op jit(solution)/shard_map/ppermute | solution.py:313
  2.3 16.9 %copy-start.5 = (bf16[2,160,512]{2,1,0:T(8,128)(2,1)}, bf16[2,160,512]{2,1,0:T(8,128)(2,1)S(1)}, u32[]{:S(2)}) copy-start(bf16[2,160,512]{2,1,0:T(8,128)(2,1)S(1)} %pad_maximum_fusion.m1) | copy-start | bytes 983044
  2.3 17.5 %collective-permute-start.5 = (bf16[2,160,512]{2,1,0:T(8,128)(2,1)S(1)}, bf16[2,160,512]{2,1,0:T(8,128)(2,1)S(1)}, u32[]{:S(2)}, u32[]{:S(2)}) collective-permute-start(bf16[2,160,512]{2,1,0:T(8,128)(2,1)S(1)} %pad_maximum_fusion.m1), channel_id=1, source_target_pairs={{0,1},{1,0},{2,3},{3,2},{4,5},{5,4},{6,7},{7,6},{8,9},{9,8},{10,11... | collective-permute-start | bytes 983048 | tf_op jit(solution)/shard_map/ppermute | solution.py:313
  2.5 16.7 %collective-permute-start.3 = (bf16[2,160,512]{2,1,0:T(8,128)(2,1)S(1)}, bf16[2,160,512]{2,1,0:T(8,128)(2,1)S(1)}, u32[]{:S(2)}, u32[]{:S(2)}) collective-permute-start(bf16[2,160,512]{2,1,0:T(8,128)(2,1)S(1)} %pad_maximum_fusion.m1), channel_id=1, source_target_pairs={{2,4},{6,8},{10,12},{14,16},{18,20},{22,24},{26,28},{30,32},{34,36... | collective-permute-start | bytes 983048 | tf_op jit(solution)/shard_map/ppermute | solution.py:319
  9.1 10.1 %collective-permute-start.2 = (bf16[2,160,512]{2,1,0:T(8,128)(2,1)S(1)}, bf16[2,160,512]{2,1,0:T(8,128)(2,1)S(1)}, u32[]{:S(2)}, u32[]{:S(2)}) collective-permute-start(bf16[2,160,512]{2,1,0:T(8,128)(2,1)S(1)} %pad_maximum_fusion.m1), channel_id=1, source_target_pairs={{0,2},{4,6},{8,10},{12,14},{16,18},{20,22},{24,26},{28,30},{32,34}... | collective-permute-start | bytes 983048 | tf_op jit(solution)/shard_map/ppermute | solution.py:319
  9.9 9.3 %copy-start.1 = (bf16[576,512]{1,0:T(8,128)(2,1)}, bf16[576,512]{1,0:T(8,128)(2,1)S(1)}, u32[]{:S(2)}) copy-start(bf16[576,512]{1,0:T(8,128)(2,1)S(1)} %collective-permute-done.grid_far) | copy-start | bytes 1769476
  9.9 9.2 %copy-start = (bf16[1152,512]{1,0:T(8,128)(2,1)}, bf16[1152,512]{1,0:T(8,128)(2,1)S(1)}, u32[]{:S(2)}) copy-start(bf16[1152,512]{1,0:T(8,128)(2,1)S(1)} %collective-permute-done.1.edge_far) | copy-start | bytes 3538948
  19.2 1.8 %copy-start.7 = (bf16[2,160,512]{2,1,0:T(8,128)(2,1)}, bf16[2,160,512]{2,1,0:T(8,128)(2,1)S(1)}, u32[]{:S(2)}) copy-start(bf16[2,160,512]{2,1,0:T(8,128)(2,1)S(1)} %collective-permute-done.3.m2) | copy-start | bytes 983044
  19.2 1.7 %copy-start.8 = (bf16[2,160,512]{2,1,0:T(8,128)(2,1)}, bf16[2,160,512]{2,1,0:T(8,128)(2,1)S(1)}, u32[]{:S(2)}) copy-start(bf16[2,160,512]{2,1,0:T(8,128)(2,1)S(1)} %collective-permute-done.2.m0) | copy-start | bytes 983044
  19.2 1.7 %collective-permute-start.4 = (bf16[2,160,512]{2,1,0:T(8,128)(2,1)S(1)}, bf16[2,160,512]{2,1,0:T(8,128)(2,1)S(1)}, u32[]{:S(2)}, u32[]{:S(2)}) collective-permute-start(bf16[2,160,512]{2,1,0:T(8,128)(2,1)S(1)} %collective-permute-done.2.m0), channel_id=1, source_target_pairs={{0,1},{1,0},{2,3},{3,2},{4,5},{5,4},{6,7},{7,6},{8,9},{9,8},{10,11... | collective-permute-start | bytes 983048 | tf_op jit(solution)/shard_map/ppermute | solution.py:313
  19.4 2.0 %collective-permute-start.6 = (bf16[2,160,512]{2,1,0:T(8,128)(2,1)S(1)}, bf16[2,160,512]{2,1,0:T(8,128)(2,1)S(1)}, u32[]{:S(2)}, u32[]{:S(2)}) collective-permute-start(bf16[2,160,512]{2,1,0:T(8,128)(2,1)S(1)} %collective-permute-done.3.m2), channel_id=1, source_target_pairs={{0,1},{1,0},{2,3},{3,2},{4,5},{5,4},{6,7},{7,6},{8,9},{9,8},{10,11... | collective-permute-start | bytes 983048 | tf_op jit(solution)/shard_map/ppermute | solution.py:313
  19.8 1.6 %copy-start.6 = (bf16[2,160,512]{2,1,0:T(8,128)(2,1)}, bf16[2,160,512]{2,1,0:T(8,128)(2,1)S(1)}, u32[]{:S(2)}) copy-start(bf16[2,160,512]{2,1,0:T(8,128)(2,1)S(1)} %collective-permute-done.5.m4) | copy-start | bytes 983044
  35.7 7.7 %copy-start.4 = (bf16[512,256]{1,0:T(8,128)(2,1)S(1)}, bf16[512,256]{1,0:T(8,128)(2,1)}, u32[]{:S(2)}) copy-start(bf16[512,256]{1,0:T(8,128)(2,1)} %w_edge.1) | copy-start | bytes 786436
  35.7 25.0 %all-to-all-start = ((bf16[32,136,128]{2,1,0:T(8,128)(2,1)}), bf16[32,136,128]{2,1,0:T(8,128)(2,1)S(1)}, u32[]{:S(2)}, u32[]{:S(2)}) async-start(bf16[32,136,128]{2,1,0:T(8,128)(2,1)} %get-tuple-element.35), calls=%async_computation | async-start | bytes 2228224 | tf_op jit(solution)/shard_map/all_to_all | solution.py:460
  43.4 1.0 copy-start.3
  43.9 5.1 %collective-permute-start.7 = (bf16[1152,512]{1,0:T(8,128)(2,1)S(1)}, bf16[1152,512]{1,0:T(8,128)(2,1)S(1)}, u32[]{:S(2)}, u32[]{:S(2)}) collective-permute-start(bf16[1152,512]{1,0:T(8,128)(2,1)S(1)} %convolution_convert_fusion), channel_id=1, source_target_pairs={{0,1},{1,0},{2,3},{3,2},{4,5},{5,4},{6,7},{7,6},{8,9},{9,8},{10,11... | collective-permute-start | bytes 3538952 | tf_op jit(solution)/shard_map/ppermute | solution.py:313
  44.7 3.2 %collective-permute-start.8 = (bf16[576,512]{1,0:T(8,128)(2,1)S(1)}, bf16[576,512]{1,0:T(8,128)(2,1)S(1)}, u32[]{:S(2)}, u32[]{:S(2)}) collective-permute-start(bf16[576,512]{1,0:T(8,128)(2,1)S(1)} %convolution_convert_fusion.1), channel_id=1, source_target_pairs={{0,1},{1,0},{2,3},{3,2},{4,5},{5,4},{6,7},{7,6},{8,9},{9,8},{10,11... | collective-permute-start | bytes 1769480 | tf_op jit(solution)/shard_map/ppermute | solution.py:313
  60.9 6.5 %collective-permute-start.12 = (bf16[136,128]{1,0:T(8,128)(2,1)S(1)}, bf16[136,128]{1,0:T(8,128)(2,1)S(1)}, u32[]{:S(2)}, u32[]{:S(2)}) collective-permute-start(bf16[136,128]{1,0:T(8,128)(2,1)S(1)} %reduce_sum.12), channel_id=1, source_target_pairs={{0,64},{64,0},{128,192},{192,128},{1,65},{65,1},{129,193},{193,129... | collective-permute-start | bytes 104456 | tf_op jit(solution)/shard_map/ppermute | solution.py:327
  67.4 6.3 %collective-permute-start.13 = (bf16[136,128]{1,0:T(8,128)(2,1)S(1)}, bf16[136,128]{1,0:T(8,128)(2,1)S(1)}, u32[]{:S(2)}, u32[]{:S(2)}) collective-permute-start(bf16[136,128]{1,0:T(8,128)(2,1)S(1)} %add_convert_fusion.2), channel_id=1, source_target_pairs={{0,192},{64,128},{128,64},{192,0},{1,193},{65,129},{129,65},{193,1... | collective-permute-start | bytes 104456 | tf_op jit(solution)/shard_map/ppermute | solution.py:327
  74.8 5.4 %copy-start.10 = (bf16[320,256]{1,0:T(8,128)(2,1)S(1)}, bf16[320,256]{1,0:T(8,128)(2,1)}, u32[]{:S(2)}) copy-start(bf16[320,256]{1,0:T(8,128)(2,1)} %get-tuple-element.43) | copy-start | bytes 491524
  74.8 7.0 %copy-start.9 = (bf16[320,256]{1,0:T(8,128)(2,1)S(1)}, bf16[320,256]{1,0:T(8,128)(2,1)}, u32[]{:S(2)}) copy-start(bf16[320,256]{1,0:T(8,128)(2,1)} %get-tuple-element.44) | copy-start | bytes 491524
  74.8 22.8 %copy-start.2 = (bf16[512,256]{1,0:T(8,128)(2,1)S(1)}, bf16[512,256]{1,0:T(8,128)(2,1)}, u32[]{:S(2)}) copy-start(bf16[512,256]{1,0:T(8,128)(2,1)} %w_mesh_in.1) | copy-start | bytes 786436
  74.8 25.5 %all-to-all-start.1 = ((bf16[32,64,256]{2,1,0:T(8,128)(2,1)}), bf16[32,64,256]{2,1,0:T(8,128)(2,1)S(1)}, u32[]{:S(2)}, u32[]{:S(2)}) async-start(bf16[32,64,256]{2,1,0:T(8,128)(2,1)} %broadcast_in_dim.2), calls=%async_computation.1 | async-start | bytes 2097152 | tf_op jit(solution)/shard_map/all_to_all | solution.py:477
  80.2 14.3 %collective-permute-start.9 = (bf16[320,256]{1,0:T(8,128)(2,1)S(1)}, bf16[320,256]{1,0:T(8,128)(2,1)S(1)}, u32[]{:S(2)}, u32[]{:S(2)}) collective-permute-start(bf16[320,256]{1,0:T(8,128)(2,1)S(1)} %copy-done.10), channel_id=1, source_target_pairs={{0,2},{4,6},{8,10},{12,14},{16,18},{20,22},{24,26},{28,30},{32,34}... | collective-permute-start | bytes 491528 | tf_op jit(solution)/shard_map/ppermute | solution.py:319
  81.8 15.8 %collective-permute-start.10 = (bf16[320,256]{1,0:T(8,128)(2,1)S(1)}, bf16[320,256]{1,0:T(8,128)(2,1)S(1)}, u32[]{:S(2)}, u32[]{:S(2)}) collective-permute-start(bf16[320,256]{1,0:T(8,128)(2,1)S(1)} %copy-done.9), channel_id=1, source_target_pairs={{2,4},{6,8},{10,12},{14,16},{18,20},{22,24},{26,28},{30,32},{34,36... | collective-permute-start | bytes 491528 | tf_op jit(solution)/shard_map/ppermute | solution.py:319
  97.9 1.5 %collective-permute-start.11 = (bf16[160,512]{1,0:T(8,128)(2,1)S(1)}, bf16[160,512]{1,0:T(8,128)(2,1)S(1)}, u32[]{:S(2)}, u32[]{:S(2)}) collective-permute-start(bf16[160,512]{1,0:T(8,128)(2,1)S(1)} %convolution_convert_fusion.2), channel_id=1, source_target_pairs={{0,1},{1,0},{2,3},{3,2},{4,5},{5,4},{6,7},{7,6},{8,9},{9,8},{10,11... | collective-permute-start | bytes 491528 | tf_op jit(solution)/shard_map/ppermute | solution.py:313
